TPU v7x, 32 devices: a 4x4x1 block of a 4x4x8 slice. The times are simulated.
32 devices in a mesh: data: 1 (over z), tensor: 32 (over y, x, core).
Axes of the slice: x: 4, y: 4, z: 1, core: 2. Of those that a mesh axis runs over, the one named last changes fastest.
The devices are a block of a 4x4x8 slice.
Arguments:
- x_in: bfloat16 [32, 128, 4096], P('data')
- adapter_ids: int32 [32], P('data')
- gain_attn: float32 [4096], replicated
- gain_mlp: float32 [4096], replicated
- w_q: bfloat16 [4096, 32, 128], P(None, 'tensor')
- w_k: bfloat16 [4096, 32, 128], P(None, 'tensor')
- w_v: bfloat16 [4096, 32, 128], P(None, 'tensor')
- w_o: bfloat16 [32, 128, 4096], P('tensor')
- w_gate: bfloat16 [4096, 11008], P(None, 'tensor')
- w_up: bfloat16 [4096, 11008], P(None, 'tensor')
- w_down: bfloat16 [11008, 4096], P('tensor')
- a_q: bfloat16 [2, 4096, 128], P(None, None, 'tensor')
- b_q: bfloat16 [2, 128, 32, 128], P(None, None, 'tensor')
- a_k: bfloat16 [2, 4096, 128], P(None, None, 'tensor')
- b_k: bfloat16 [2, 128, 32, 128], P(None, None, 'tensor')
- a_v: bfloat16 [2, 4096, 128], P(None, None, 'tensor')
- b_v: bfloat16 [2, 128, 32, 128], P(None, None, 'tensor')
- a_o: bfloat16 [2, 32, 128, 128], P(None, 'tensor')
- b_o: bfloat16 [2, 128, 4096], P(None, None, 'tensor')
- a_gate: bfloat16 [2, 4096, 128], P(None, None, 'tensor')
- b_gate: bfloat16 [2, 128, 11008], P(None, None, 'tensor')
- a_up: bfloat16 [2, 4096, 128], P(None, None, 'tensor')
- b_up: bfloat16 [2, 128, 11008], P(None, None, 'tensor')
- a_down: bfloat16 [2, 11008, 128], P(None, 'tensor')
- b_down: bfloat16 [2, 128, 4096], P(None, None, 'tensor')
Outputs:
- output: bfloat16 [32, 128, 4096], P('data')
All inputs are finite; a program needn't handle non-finite values.
Results may differ from a plain program's by a relative error of at most 0.02.
Values are sent between devices in bfloat16 or wider.
A program may use at most 768 MiB of HBM per device.

v0:
```python
import jax
import jax.numpy as jnp
from jax import lax
from jax.sharding import PartitionSpec as P

ALPHA = 16.0
ROPE_BASE = 10000.0
EPSILON = 1e-5


def rms_gain(act_in, gain_vec):
    act_f32 = act_in.astype(jnp.float32)
    inv_rms = lax.rsqrt(jnp.mean(act_f32 * act_f32, axis=-1, keepdims=True) + EPSILON)
    return (act_f32 * inv_rms * gain_vec).astype(jnp.bfloat16)


def rope_rotate(head_vals):
    seq_len = head_vals.shape[1]
    head_dim = head_vals.shape[-1]
    half_dim = head_dim // 2
    inv_freq = ROPE_BASE ** (-2.0 * jnp.arange(half_dim, dtype=jnp.float32) / head_dim)
    angle_tab = jnp.arange(seq_len, dtype=jnp.float32)[:, None] * inv_freq[None, :]
    cos_tab = jnp.cos(angle_tab)[:, None, :]
    sin_tab = jnp.sin(angle_tab)[:, None, :]
    first_half = head_vals[..., :half_dim]
    second_half = head_vals[..., half_dim:]
    return jnp.concatenate([first_half * cos_tab - second_half * sin_tab, second_half * cos_tab + first_half * sin_tab], axis=-1)


def causal_attention(q_heads, k_heads, v_heads):
    batch_size, seq_len, q_count, head_dim = q_heads.shape
    kv_count = k_heads.shape[2]
    q_group = q_heads.reshape(batch_size, seq_len, kv_count, q_count // kv_count, head_dim)
    scores = jnp.einsum('bskgd,btkd->bkgst', q_group, k_heads, preferred_element_type=jnp.float32) * head_dim ** -0.5
    causal = jnp.arange(seq_len)[:, None] >= jnp.arange(seq_len)[None, :]
    attn_prob = jax.nn.softmax(jnp.where(causal, scores, -1e30), axis=-1).astype(jnp.bfloat16)
    mixed_out = jnp.einsum('bkgst,btkd->bskgd', attn_prob, v_heads, preferred_element_type=jnp.float32)
    return mixed_out.astype(jnp.bfloat16).reshape(batch_size, seq_len, q_count, head_dim)


def solution(mesh):
    tp_size = mesh.shape['tensor']
    head_split = P(None, 'tensor', None)
    last_split = P(None, None, 'tensor')
    b_head_split = P(None, None, 'tensor', None)
    in_specs = (P('data', None, None), P('data'), P(None), P(None),
                head_split, head_split, head_split, P('tensor', None, None),
                P(None, 'tensor'), P(None, 'tensor'), P('tensor', None),
                last_split, b_head_split, last_split, b_head_split, last_split, b_head_split,
                P(None, 'tensor', None, None), last_split,
                last_split, last_split, last_split, last_split,
                P(None, 'tensor', None), last_split)

    def local_layer(x_in, adapter_ids, gain_attn, gain_mlp, w_q, w_k, w_v, w_o, w_gate, w_up, w_down, a_q, b_q, a_k, b_k, a_v, b_v, a_o, b_o, a_gate, b_gate, a_up, b_up, a_down, b_down):
        value_a10 = ALPHA / b_q.shape[1]
        shard_width = x_in.shape[2] // tp_size
        my_index = lax.axis_index('tensor')

        def per_sequence(table_stack):
            return jnp.take(table_stack, adapter_ids, axis=0)

        def column_proj(act_in, weight, a_stack, b_stack, base_form, up_form):
            low_part = jnp.einsum('bsd,bdr->bsr', act_in, per_sequence(a_stack), preferred_element_type=jnp.float32)
            low_rank = lax.all_gather(low_part.astype(jnp.bfloat16), 'tensor', axis=2, tiled=True)
            base_out = jnp.einsum(base_form, act_in, weight, preferred_element_type=jnp.float32)
            return base_out + value_a10 * jnp.einsum(up_form, low_rank, per_sequence(b_stack), preferred_element_type=jnp.float32)

        def row_proj(act_in, weight, a_stack, b_stack, base_form, low_form, resid_shard):
            base_part = jnp.einsum(base_form, act_in, weight, preferred_element_type=jnp.float32).astype(jnp.bfloat16)
            low_part = jnp.einsum(low_form, act_in, per_sequence(a_stack), preferred_element_type=jnp.float32).astype(jnp.bfloat16)
            low_rank = lax.psum(low_part, 'tensor')
            base_shard = lax.psum_scatter(base_part, 'tensor', scatter_dimension=2, tiled=True)
            delta_out = jnp.einsum('bsr,brd->bsd', low_rank, per_sequence(b_stack), preferred_element_type=jnp.float32)
            out_shard = (resid_shard.astype(jnp.float32) + base_shard.astype(jnp.float32) + value_a10 * delta_out).astype(jnp.bfloat16)
            return out_shard, lax.all_gather(out_shard, 'tensor', axis=2, tiled=True)

        h_attn = rms_gain(x_in, gain_attn)
        z_q = column_proj(h_attn, w_q, a_q, b_q, 'bsd,dhe->bshe', 'bsr,brhe->bshe')
        z_k = column_proj(h_attn, w_k, a_k, b_k, 'bsd,dhe->bshe', 'bsr,brhe->bshe')
        z_v = column_proj(h_attn, w_v, a_v, b_v, 'bsd,dhe->bshe', 'bsr,brhe->bshe')
        attn_out = causal_attention(rope_rotate(z_q).astype(jnp.bfloat16), rope_rotate(z_k).astype(jnp.bfloat16), z_v.astype(jnp.bfloat16))
        x_shard = lax.dynamic_slice_in_dim(x_in, my_index * shard_width, shard_width, axis=2)
        mid_shard, x_mid = row_proj(attn_out, w_o, a_o, b_o, 'bshe,hed->bsd', 'bshe,bher->bsr', x_shard)
        h_mlp = rms_gain(x_mid, gain_mlp)
        z_gate = column_proj(h_mlp, w_gate, a_gate, b_gate, 'bsd,df->bsf', 'bsr,brf->bsf')
        z_up = column_proj(h_mlp, w_up, a_up, b_up, 'bsd,df->bsf', 'bsr,brf->bsf')
        hidden = (jax.nn.silu(z_gate) * z_up).astype(jnp.bfloat16)
        return row_proj(hidden, w_down, a_down, b_down, 'bsf,fd->bsd', 'bsf,bfr->bsr', mid_shard)[1]

    return jax.shard_map(local_layer, mesh=mesh, in_specs=in_specs, out_specs=P('data', None, None), check_vma=False)
```

profile of v0, /device:TPU:97, one launch (start us, length us, event | category | flops | bytes accessed | tf_op | source)
XLA Modules:
  0.0 1113.2 jit_solution(9193980474475360344)
XLA Ops:
  8.1 11.4 %fusion = f32[32,128]{1,0:T(8,128)S(1)} fusion(bf16[32,128,4096]{2,1,0:T(8,128)(2,1)} %param.33), kind=kLoop, calls=%fused_computation.18 | loop fusion | flops 50327552 | bytes 33570816 | tf_op jit(solution)/shard_map/reduce_sum | solution.py:13
  21.9 15.2 %fusion.60 = bf16[32,128,4]{1,2,0:T(4,128)(2,1)S(1)} fusion(bf16[32,4096,4]{1,2,0:T(4,128)(2,1)} %gather_fusion.6, pred[32]{0:T(512)(128)(4,1)S(1)} %compare_and_fusion, bf16[32,128,4096]{2,1,0:T(8,128)(2,1)} %param.33, f32[4096]{0:T(1024)S(1)} %copy-done.19, f32[32,128]{1,0:T(8,128)S(1)} %add_rsqrt_fusion.1), kind=kOutput, calls=%fused_computation.88 | convolution fusion | flops 201850880 | bytes 34668576 | tf_op jit(solution)/shard_map/bsd,bdr->bsr/dot_general | solution.py:63
  40.2 15.2 %fusion.62 = bf16[32,128,4]{1,2,0:T(4,128)(2,1)S(1)} fusion(bf16[32,4096,4]{1,2,0:T(4,128)(2,1)} %gather_fusion.4, pred[32]{0:T(512)(128)(4,1)S(1)} %compare_and_fusion, bf16[32,128,4096]{2,1,0:T(8,128)(2,1)} %param.33, f32[4096]{0:T(1024)S(1)} %copy-done.19, f32[32,128]{1,0:T(8,128)S(1)} %add_rsqrt_fusion.1), kind=kOutput, calls=%fused_computation.90 | convolution fusion | flops 201850880 | bytes 34668576 | tf_op jit(solution)/shard_map/bsd,bdr->bsr/dot_general | solution.py:63
  58.7 15.2 %fusion.64 = bf16[32,128,4]{1,2,0:T(4,128)(2,1)S(1)} fusion(bf16[32,4096,4]{1,2,0:T(4,128)(2,1)} %gather_fusion.2, pred[32]{0:T(512)(128)(4,1)S(1)} %compare_and_fusion, bf16[32,128,4096]{2,1,0:T(8,128)(2,1)} %param.33, f32[4096]{0:T(1024)S(1)} %copy-done.19, f32[32,128]{1,0:T(8,128)S(1)} %add_rsqrt_fusion.1), kind=kOutput, calls=%fused_computation.92 | convolution fusion | flops 201850880 | bytes 34668576 | tf_op jit(solution)/shard_map/bsd,bdr->bsr/dot_general | solution.py:63
  74.6 17.0 %fusion.36 = f32[32,128,128]{1,2,0:T(8,128)} fusion(bf16[4096,1,128]{2,0,1:T(8,128)(2,1)} %param.37, bf16[32,128,4096]{2,1,0:T(8,128)(2,1)} %param.33, f32[4096]{0:T(1024)S(1)} %copy-done.19, f32[32,128]{1,0:T(8,128)S(1)} %add_rsqrt_fusion.1), kind=kOutput, calls=%fused_computation.63 | convolution fusion | flops 4362076160 | bytes 36732928 | tf_op jit(solution)/shard_map/bsd,dhe->bshe/dot_general | solution.py:65
  91.6 16.7 %fusion.38 = f32[32,128,128]{1,2,0:T(8,128)} fusion(bf16[4096,1,128]{2,0,1:T(8,128)(2,1)S(1)} %copy-done.18, bf16[32,128,4096]{2,1,0:T(8,128)(2,1)} %param.33, f32[4096]{0:T(1024)S(1)} %copy-done.19, f32[32,128]{1,0:T(8,128)S(1)} %add_rsqrt_fusion.1), kind=kOutput, calls=%fused_computation.65 | convolution fusion | flops 4362076160 | bytes 36732928 | tf_op jit(solution)/shard_map/bsd,dhe->bshe/dot_general | solution.py:65
  108.3 17.1 %fusion.46 = f32[32,128,128]{1,2,0:T(8,128)} fusion(bf16[4096,1,128]{2,0,1:T(8,128)(2,1)} %param.39, bf16[32,128,4096]{2,1,0:T(8,128)(2,1)} %param.33, f32[4096]{0:T(1024)S(1)} %copy-done.19, f32[32,128]{1,0:T(8,128)S(1)} %add_rsqrt_fusion.1), kind=kOutput, calls=%fused_computation.75 | convolution fusion | flops 4362076160 | bytes 36732928 | tf_op jit(solution)/shard_map/bsd,dhe->bshe/dot_general | solution.py:65
  132.3 4.4 add_bitcast_fusion
  136.8 3.2 add_bitcast_fusion.1
  143.0 14.3 %all-gather.8.cloned.1.call-done = bf16[32,128,128]{1,0,2:T(8,128)(2,1)} async-done(((bf16[32,128,4]{1,0,2:T(8,128)(2,1)}), bf16[32,128,128]{1,0,2:T(8,128)(2,1)}) %all-gather.8.cloned.1.call-update) | async-done | bytes 1048592 | tf_op jit(solution)/shard_map/all_gather | solution.py:64
  157.3 5.3 fusion.29
  165.8 16.3 %convolution_convert_fusion.1 = bf16[32,128,4096]{1,2,0:T(8,128)(2,1)} fusion(bf16[32,128,128]{1,2,0:T(8,128)(2,1)} %fusion.29, bf16[1,128,4096]{2,1,0:T(8,128)(2,1)} %param.40), kind=kOutput, calls=%fused_computation.25 | convolution fusion | flops 4311744512 | bytes 35651584 | tf_op jit(solution)/shard_map/bshe,hed->bsd/dot_general | solution.py:69
  189.3 70.6 %all-reduce.3.cloned.1.call-done = bf16[32,128,128]{2,1,0:T(8,128)(2,1)} async-done(((bf16[32,128,128]{2,1,0:T(8,128)(2,1)}), bf16[32,128,128]{2,1,0:T(8,128)(2,1)}) %all-reduce.3.cloned.1.call-update) | async-done | bytes 1048592 | tf_op jit(solution)/shard_map/psum | solution.py:71
  259.9 159.1 %reduce-scatter.3.cloned.1.call-done = bf16[32,128,128]{1,2,0:T(8,128)(2,1)} async-done(((bf16[32,128,4096]{1,2,0:T(8,128)(2,1)}), bf16[32,128,128]{1,2,0:T(8,128)(2,1)}) %reduce-scatter.3.cloned.1.call-update) | async-done | bytes 1048592 | tf_op jit(solution)/shard_map/reduce_scatter | solution.py:72
  418.9 4.2 add_convert_fusion.1
  425.6 106.5 %all-gather.14.cloned.1.call-done = bf16[32,128,4096]{1,2,0:T(8,128)(2,1)} async-done(((bf16[32,128,128]{1,2,0:T(8,128)(2,1)}), bf16[32,128,4096]{1,2,0:T(8,128)(2,1)}) %all-gather.14.cloned.1.call-update) | async-done | bytes 33554448 | tf_op jit(solution)/shard_map/all_gather | solution.py:75
  532.1 11.8 %fusion.3 = f32[32,128]{1,0:T(8,128)S(1)} fusion(bf16[32,128,4096]{1,2,0:T(8,128)(2,1)} %all-gather.14.cloned.1.call-done), kind=kLoop, calls=%fused_computation.21 | loop fusion | flops 50327552 | bytes 33570816 | tf_op jit(solution)/shard_map/reduce_sum | solution.py:13
  543.9 22.7 %fusion.5 = bf16[32,128,4096]{1,2,0:T(8,128)(2,1)} fusion(bf16[32,128,4096]{1,2,0:T(8,128)(2,1)} %all-gather.14.cloned.1.call-done, f32[4096]{0:T(1024)S(1)} %copy-done.17, f32[32,128]{1,0:T(8,128)S(1)} %add_rsqrt_fusion), kind=kLoop, calls=%fused_computation.23 | loop fusion | flops 67108864 | bytes 67141632 | tf_op jit(solution)/shard_map/convert_element_type | solution.py:14
  566.6 12.9 %fusion.57 = bf16[32,128,4]{1,2,0:T(4,128)(2,1)S(1)} fusion(bf16[32,128,4096]{1,2,0:T(8,128)(2,1)} %fusion.5, bf16[32,4096,4]{1,2,0:T(4,128)(2,1)} %gather_fusion.9, pred[32]{0:T(512)(128)(4,1)S(1)} %compare_and_fusion), kind=kOutput, calls=%fused_computation.85 | convolution fusion | flops 134742016 | bytes 34635808 | tf_op jit(solution)/shard_map/bsd,bdr->bsr/dot_general | solution.py:63
  590.1 12.8 %fusion.55 = bf16[32,128,4]{1,2,0:T(4,128)(2,1)S(1)} fusion(bf16[32,128,4096]{1,2,0:T(8,128)(2,1)} %fusion.5, bf16[32,4096,4]{1,2,0:T(4,128)(2,1)} %gather_fusion.11, pred[32]{0:T(512)(128)(4,1)S(1)} %compare_and_fusion), kind=kOutput, calls=%fused_computation.83 | convolution fusion | flops 134742016 | bytes 34635808 | tf_op jit(solution)/shard_map/bsd,bdr->bsr/dot_general | solution.py:63
  603.7 20.3 %fusion.11 = f32[32,128,344]{1,2,0:T(8,128)} fusion(bf16[32,128,4096]{1,2,0:T(8,128)(2,1)} %fusion.5, bf16[4096,344]{0,1:T(8,128)(2,1)} %param.41), kind=kOutput, calls=%fused_computation.30 | convolution fusion | flops 11542724608 | bytes 42008576 | tf_op jit(solution)/shard_map/bsd,df->bsf/dot_general | solution.py:65
  624.0 6.3 fusion.15
  630.3 25.4 %all-gather.18.cloned.1.call-done = bf16[32,128,128]{1,0,2:T(8,128)(2,1)} async-done(((bf16[32,128,4]{1,0,2:T(8,128)(2,1)}), bf16[32,128,128]{1,0,2:T(8,128)(2,1)}) %all-gather.18.cloned.1.call-update) | async-done | bytes 1048592 | tf_op jit(solution)/shard_map/all_gather | solution.py:64
  655.7 6.2 fusion.13
  661.9 28.9 %multiply_convert_fusion = bf16[32,128,344]{1,2,0:T(8,128)(2,1)} fusion(f32[32,128,344]{1,2,0:T(8,128)} %fusion.13, f32[32,128,344]{1,2,0:T(8,128)} %fusion.11, f32[32,128,344]{1,2,0:T(8,128)} %fusion.15, bf16[32,128,4096]{1,2,0:T(8,128)(2,1)} %fusion.5, bf16[4096,344]{0,1:T(8,128)(2,1)} %param.42), kind=kOutput, calls=%fused_computation.26 | convolution fusion | flops 11556814848 | bytes 56098816 | tf_op jit(solution)/shard_map/bsd,df->bsf/dot_general | solution.py:65
  690.8 5.0 fusion.23
  695.9 23.5 %convolution_convert_fusion = bf16[32,128,4096]{1,2,0:T(8,128)(2,1)} fusion(bf16[32,128,344]{1,2,0:T(8,128)(2,1)} %multiply_convert_fusion, bf16[344,4096]{1,0:T(8,128)(2,1)S(1)} %copy-done), kind=kOutput, calls=%fused_computation.24 | convolution fusion | flops 11559501824 | bytes 39190528 | tf_op jit(solution)/shard_map/bsf,fd->bsd/dot_general | solution.py:69
  722.0 68.0 %all-reduce.5.cloned.1.call-done = bf16[32,128,128]{2,1,0:T(8,128)(2,1)} async-done(((bf16[32,128,128]{2,1,0:T(8,128)(2,1)}), bf16[32,128,128]{2,1,0:T(8,128)(2,1)}) %all-reduce.5.cloned.1.call-update) | async-done | bytes 1048592 | tf_op jit(solution)/shard_map/psum | solution.py:71
  790.0 159.1 %reduce-scatter.5.cloned.1.call-done = bf16[32,128,128]{1,2,0:T(8,128)(2,1)} async-done(((bf16[32,128,4096]{1,2,0:T(8,128)(2,1)}), bf16[32,128,128]{1,2,0:T(8,128)(2,1)}) %reduce-scatter.5.cloned.1.call-update) | async-done | bytes 1048592 | tf_op jit(solution)/shard_map/reduce_scatter | solution.py:72
  949.1 4.1 add_convert_fusion
  953.3 108.9 %all-gather.20.cloned.1.call-done = bf16[32,128,4096]{1,2,0:T(8,128)(2,1)} async-done(((bf16[32,128,128]{1,2,0:T(8,128)(2,1)}), bf16[32,128,4096]{1,2,0:T(8,128)(2,1)}) %all-gather.20.cloned.1.call-update) | async-done | bytes 33554448 | tf_op jit(solution)/shard_map/all_gather | solution.py:75
  1062.2 44.2 %copy.61 = bf16[32,128,4096]{2,1,0:T(8,128)(2,1)} copy(bf16[32,128,4096]{1,2,0:T(8,128)(2,1)} %all-gather.20.cloned.1.call-done) | data formatting | bytes 67108864 | tf_op jit(solution)/shard_map/all_gather | solution.py:75
  (98 shorter events, 47.8 us)
Async XLA Ops:
  6.5 689.4 %copy-start = (bf16[344,4096]{1,0:T(8,128)(2,1)S(1)}, bf16[344,4096]{1,0:T(8,128)(2,1)}, u32[]{:S(2)}) copy-start(bf16[344,4096]{1,0:T(8,128)(2,1)} %param.43) | copy-start | bytes 8454148
  6.6 125.8 %all-gather.12.cloned.1.call-start = ((), (), s32[]{:S(2)}) async-start(), calls=%async_computation.4 | async-start | bytes 1081344 | tf_op jit(solution)/shard_map/all_gather | solution.py:64
  8.1 11.4 %copy-start.1 = (bf16[2,4096,4]{1,2,0:T(4,128)(2,1)S(1)}, bf16[2,4096,4]{1,2,0:T(4,128)(2,1)}, u32[]{:S(2)}) copy-start(bf16[2,4096,4]{1,2,0:T(4,128)(2,1)} %param.44) | copy-start | bytes 196612
  19.5 2.4 copy-start.19
  37.0 0.9 copy-start.2
  37.7 99.1 %all-gather.10.cloned.1.call-start = ((), (), s32[]{:S(2)}) async-start(), calls=%async_computation.3 | async-start | bytes 1081344 | tf_op jit(solution)/shard_map/all_gather | solution.py:64
  55.4 0.9 copy-start.3
  56.1 101.2 %all-gather.8.cloned.1.call-start = ((), (), s32[]{:S(2)}) async-start(), calls=%async_computation.2 | async-start | bytes 1081344 | tf_op jit(solution)/shard_map/all_gather | solution.py:64
  74.5 185.3 %all-reduce.3.cloned.1.call-start = ((), (), s32[]{:S(2)}) async-start(), calls=%async_computation.6 | async-start | bytes 2097152 | tf_op jit(solution)/shard_map/psum | solution.py:71
  74.6 17.0 %copy-start.18 = (bf16[4096,1,128]{2,0,1:T(8,128)(2,1)S(1)}, bf16[4096,1,128]{2,0,1:T(8,128)(2,1)}, u32[]{:S(2)}) copy-start(bf16[4096,1,128]{2,0,1:T(8,128)(2,1)} %param.38) | copy-start | bytes 3145732
  108.3 17.1 %copy-start.9 = (bf16[2,128,1,128]{3,1,2,0:T(8,128)(2,1)S(1)}, bf16[2,128,1,128]{3,1,2,0:T(8,128)(2,1)}, u32[]{:S(2)}) copy-start(bf16[2,128,1,128]{3,1,2,0:T(8,128)(2,1)} %param.45) | copy-start | bytes 196612
  108.3 18.8 %copy-start.10 = (bf16[2,128,1,128]{3,1,2,0:T(8,128)(2,1)S(1)}, bf16[2,128,1,128]{3,1,2,0:T(8,128)(2,1)}, u32[]{:S(2)}) copy-start(bf16[2,128,1,128]{3,1,2,0:T(8,128)(2,1)} %param.47) | copy-start | bytes 196612
  108.3 20.5 %copy-start.11 = (bf16[2,128,1,128]{3,1,2,0:T(8,128)(2,1)S(1)}, bf16[2,128,1,128]{3,1,2,0:T(8,128)(2,1)}, u32[]{:S(2)}) copy-start(bf16[2,128,1,128]{3,1,2,0:T(8,128)(2,1)} %param.49) | copy-start | bytes 196612
  125.4 5.0 copy-start.12
  136.8 3.2 copy-start.15
  141.2 1.4 copy-start.16
  165.8 253.2 %reduce-scatter.3.cloned.1.call-start = ((), (), s32[]{:S(2)}) async-start(), calls=%async_computation.5 | async-start | bytes 34603008 | tf_op jit(solution)/shard_map/reduce_scatter | solution.py:72
  182.1 0.8 copy-start.13
  182.2 349.9 %all-gather.14.cloned.1.call-start = ((), (), s32[]{:S(2)}) async-start(), calls=%async_computation.7 | async-start | bytes 34603008 | tf_op jit(solution)/shard_map/all_gather | solution.py:75
  184.6 238.6 %copy-start.4 = (bf16[2,4096,4]{1,2,0:T(4,128)(2,1)S(1)}, bf16[2,4096,4]{1,2,0:T(4,128)(2,1)}, u32[]{:S(2)}) copy-start(bf16[2,4096,4]{1,2,0:T(4,128)(2,1)} %param.52) | copy-start | bytes 196612
  423.2 200.9 %all-gather.16.cloned.1.call-start = ((), (), s32[]{:S(2)}) async-start(), calls=%async_computation.8 | async-start | bytes 1081344 | tf_op jit(solution)/shard_map/all_gather | solution.py:64
  425.6 118.3 %copy-start.17 = (f32[4096]{0:T(1024)S(1)}, f32[4096]{0:T(1024)}, u32[]{:S(2)}) copy-start(f32[4096]{0:T(1024)} %param.36) | copy-start | bytes 49156
  566.6 13.6 %copy-start.6 = (bf16[2,128,344]{1,2,0:T(8,128)(2,1)S(1)}, bf16[2,128,344]{1,2,0:T(8,128)(2,1)}, u32[]{:S(2)}) copy-start(bf16[2,128,344]{1,2,0:T(8,128)(2,1)} %param.53) | copy-start | bytes 528388
  579.4 3.3 copy-start.5
  580.1 75.6 %all-gather.18.cloned.1.call-start = ((), (), s32[]{:S(2)}) async-start(), calls=%async_computation.9 | async-start | bytes 1081344 | tf_op jit(solution)/shard_map/all_gather | solution.py:64
  582.7 2.4 copy-start.7
  585.1 2.5 copy-start.8
  603.6 186.4 %all-reduce.5.cloned.1.call-start = ((), (), s32[]{:S(2)}) async-start(), calls=%async_computation.11 | async-start | bytes 2097152 | tf_op jit(solution)/shard_map/psum | solution.py:71
  695.8 253.2 %reduce-scatter.5.cloned.1.call-start = ((), (), s32[]{:S(2)}) async-start(), calls=%async_computation.10 | async-start | bytes 34603008 | tf_op jit(solution)/shard_map/reduce_scatter | solution.py:72
  719.5 0.8 copy-start.14
  719.5 342.7 %all-gather.20.cloned.1.call-start = ((), (), s32[]{:S(2)}) async-start(), calls=%async_computation.12 | async-start | bytes 34603008 | tf_op jit(solution)/shard_map/all_gather | solution.py:75
Sparse Core Ops, SparseCore 0:
  37.8 41.6 all-gather.11
  81.6 36.7 all-gather.9
  120.5 36.6 all-gather.7
  165.9 93.9 all-reduce.2
  263.4 155.4 reduce-scatter.2
  423.3 108.7 all-gather.13
  580.2 36.6 all-gather.15
  619.0 36.6 all-gather.17
  696.0 93.9 all-reduce.4
  793.6 155.4 reduce-scatter.4
  953.4 108.7 all-gather.19
where the time goes:
time: 1120 us; the launch traced here: 1110 us
  waiting for transfers between devices  713 us (64%)
  matrix products  253 us (23%)
  local copies, waits for them, and re-layouts  84.1 us (8%)
  other arithmetic  48.6 us (4%)
  between operations  13.8 us (1%)
    reduce_scatter x2, waiting for transfers between devices, row_proj(): lax.psum_scatter(base_part, 'tensor', scatter_dimension=2, tiled=True)  318 us
    all_gather x2, waiting for transfers between devices, row_proj(): return (out_shard, lax.all_gather(out_shard, 'tensor', axis=2, tiled=True))  215 us
    psum x2, waiting for transfers between devices, row_proj(): low_rank = lax.psum(low_part, 'tensor')  139 us
    dot_general x5, matrix products, column_proj(): jnp.einsum(base_form, act_in, weight, preferred_element_type=jnp.float32)  100 us
    dot_general x5, matrix products, column_proj(): jnp.einsum('bsd,bdr->bsr', act_in, per_sequence(a_stack), preferred_eleme...  71.1 us
    all_gather x1, local copies, waits for them, and re-layouts, row_proj(): return (out_shard, lax.all_gather(out_shard, 'tensor', axis=2, tiled=True))  44.2 us
    dot_general x2, matrix products, row_proj(): jnp.einsum(base_form, act_in, weight, preferred_element_type=jnp.float32)  39.8 us
    all_gather x5, waiting for transfers between devices, column_proj(): lax.all_gather(low_part.astype(jnp.bfloat16), 'tensor', axis=2, tiled=True)  39.7 us
  transfers between devices with their start and end apart: 11, of which 8 were waited for; matrix products, arithmetic and copies ran while one was open for 18% of the time, Pallas kernels for 0%

commit v1 on v0

v1 whole, which is shorter than its diff:
```python
import functools
import math

import jax
import jax.numpy as jnp
from jax import lax
from jax.experimental import pallas as pl
from jax.experimental.pallas import tpu as pltpu
from jax.sharding import PartitionSpec as P

ALPHA = 16.0
ROPE_BASE = 10000.0
EPSILON = 1e-5
BF = jnp.bfloat16
F32 = jnp.float32
LANE = 128
VMEM_MOST = 67043328
MESH = pl.DeviceIdType.MESH
HBM = pl.BlockSpec(memory_space=pltpu.HBM)
SMEM = pl.BlockSpec(memory_space=pltpu.SMEM)


def round_up(size, unit):
    return (size + unit - 1) // unit * unit


def fit(size, most):
    return max(c for c in range(LANE, most + 1, LANE) if size % c == 0)


class Place:
    def __init__(self, side):
        index = lax.axis_index('tensor')
        self.side = side
        self.core = lax.rem(index, 2)
        chip = index // 2
        self.y, self.x = chip // side, lax.rem(chip, side)

    def device(self, y, x):
        return (lax.rem(y + self.side, self.side) * self.side + lax.rem(x + self.side, self.side)) * 2 + self.core

    def fast(self, part, step):
        return self.device(self.y, self.x + step) if part == 0 else self.device(self.y + step, self.x)

    def slow(self, part, step):
        return self.fast(1 - part, step)

    def sequence(self, part, slow_step, fast_step):
        fast_is_x = part == 0
        dy = jnp.where(fast_is_x, slow_step, fast_step)
        dx = jnp.where(fast_is_x, fast_step, slow_step)
        return self.device(self.y + dy, self.x + dx)

    def barrier(self):
        sem = pltpu.get_barrier_semaphore()
        for part in (0, 1):
            for step in (1, -1):
                pl.semaphore_signal(sem, inc=1, device_id={'tensor': self.fast(part, step)}, device_id_type=MESH)
        pl.semaphore_wait(sem, 4)


def remote(src, dst, send_sem, recv_sem, to):
    return pltpu.make_async_remote_copy(src_ref=src, dst_ref=dst, send_sem=send_sem, recv_sem=recv_sem, device_id={'tensor': to}, device_id_type=MESH)


def gather_messages(place, gbuf, send_sem, recv_sem):
    def message(part, slot):
        sems = (send_sem.at[part, slot], recv_sem.at[part, slot])
        if slot < 4:
            src = (gbuf.at[part, 0, 0], gbuf.at[part, 0, 0], gbuf.at[part, 0, 3, 0], gbuf.at[part, 0, 1, 1])[slot]
            dst = (gbuf.at[part, 0, 3], gbuf.at[part, 0, 1], gbuf.at[part, 0, 2, 0], gbuf.at[part, 0, 2, 1])[slot]
            to = place.fast(part, (1, -1, 1, -1)[slot])
        else:
            j, kind = divmod(slot - 4, 4)
            src = (gbuf.at[part, 0, j], gbuf.at[part, 0, j], gbuf.at[part, 3, j, 0], gbuf.at[part, 1, j, 1])[kind]
            dst = (gbuf.at[part, 3, j], gbuf.at[part, 1, j], gbuf.at[part, 2, j, 0], gbuf.at[part, 2, j, 1])[kind]
            to = place.slow(part, (1, -1, 1, -1)[kind])
        return remote(src, dst, *sems, to)

    return message


GATHER_SLOTS = 20


def gather(message, on_near, on_sides, on_far):
    def start(*slots):
        for slot in slots:
            for part in (0, 1):
                message(part, slot).start()

    def then(part, slot, *nexts):
        message(part, slot).wait_recv()
        for n in nexts:
            message(part, n).start()

    start(0, 1)
    start(4, 5)
    for part in (0, 1):
        then(part, 0, 2, 16, 17)
        then(part, 1, 3, 8, 9)
    for part in (0, 1):
        then(part, 2)
        then(part, 3, 12, 13)
    for part in (0, 1):
        then(part, 4, 6)
        then(part, 5, 7)
    on_near()
    for j in (3, 1, 2):
        for part in (0, 1):
            then(part, 4 + 4 * j, 6 + 4 * j)
            then(part, 5 + 4 * j, 7 + 4 * j)
    on_sides()
    for j in (0, 3, 1, 2):
        for part in (0, 1):
            then(part, 6 + 4 * j)
            then(part, 7 + 4 * j)
    on_far()
    for part in (0, 1):
        for slot in range(GATHER_SLOTS):
            message(part, slot).wait_send()


def gather_scratch(rows, cols):
    return [
        pltpu.VMEM((2, 4, 4, 2, rows, cols), BF),
        pltpu.SemaphoreType.DMA((2, GATHER_SLOTS)),
        pltpu.SemaphoreType.DMA((2, GATHER_SLOTS)),
    ]


def small_gather_kernel(side, own_ref, out_ref, gbuf, send_sem, recv_sem, copy_sem):
    place = Place(side)
    load = pltpu.make_async_copy(own_ref, gbuf.at[:, 0, 0], copy_sem.at[0])
    load.start()
    place.barrier()
    load.wait()
    nothing = lambda: None
    gather(gather_messages(place, gbuf, send_sem, recv_sem), nothing, nothing, nothing)
    stores = []
    for part in (0, 1):
        mine = (place.y, place.x) if part == 0 else (place.x, place.y)
        for ds in range(4):
            for df in range(4):
                slow, fast = lax.rem(mine[0] + ds, side), lax.rem(mine[1] + df, side)
                stores.append(pltpu.make_async_copy(gbuf.at[part, ds, df], out_ref.at[part, slow, fast], copy_sem.at[1]))
    for s in stores:
        s.start()
    for s in stores:
        s.wait()


def small_gather(own, side, collective_id):
    _, _, rows, cols = own.shape
    return pl.pallas_call(
        functools.partial(small_gather_kernel, side),
        out_shape=jax.ShapeDtypeStruct((2, 4, 4, 2, rows, cols), BF),
        in_specs=[HBM],
        out_specs=HBM,
        scratch_shapes=gather_scratch(rows, cols) + [pltpu.SemaphoreType.DMA((2,))],
        compiler_params=pltpu.CompilerParams(collective_id=collective_id, has_side_effects=True, vmem_limit_bytes=VMEM_MOST),
        name='small_gather',
    )(own)


def adapter_of_rows(place, ids_ref, part, ds, shape):
    block = lax.broadcasted_iota(jnp.int32, shape, 0) // (shape[0] // 4)
    chosen = jnp.zeros(shape, jnp.int32)
    for df in range(4):
        chosen = jnp.where(block == df, ids_ref[place.sequence(part, ds, df)], chosen)
    return chosen


def gate_up_kernel(side, adapters, rank, scale, ids_ref, own_ref, wg_own, wg_par, wu_own, wu_par, bg_own, bg_par, bu_own, bu_par, hid_ref,
                   gbuf, send_sem, recv_sem, wg, wu, bg, bu, hid, load_sem, store_sem):
    place = Place(side)
    half = wg_own.shape[1]
    width = gbuf.shape[-1] - 2 * rank
    own_load = pltpu.make_async_copy(own_ref, gbuf.at[:, 0, 0], load_sem.at[0])
    own_load.start()
    loads = []
    for dst, own, par in ((wg, wg_own, wg_par), (wu, wu_own, wu_par), (bg, bg_own, bg_par), (bu, bu_own, bu_par)):
        loads.append(pltpu.make_async_copy(own, dst.at[:, pl.ds(0, half)], load_sem.at[1]))
        loads.append(pltpu.make_async_copy(par, dst.at[:, pl.ds(half, half)], load_sem.at[1]))
    for load in loads:
        load.start()
    place.barrier()
    own_load.wait()
    chunk = fit(2 * half, 256)
    rows = 8 * gbuf.shape[4]

    def unit(part, ds):
        low = gbuf[part, ds, :, :, :, width:].reshape(rows, 2 * rank).astype(F32)
        chosen = adapter_of_rows(place, ids_ref, part, ds, (rows, rank))
        low_g, low_u = (jnp.concatenate([jnp.where(chosen == a, v, 0.0) for a in range(adapters)], axis=1).astype(BF) for v in (low[:, :rank], low[:, rank:]))

        def columns(n, carry):
            at = pl.ds(pl.multiple_of(n * chunk, chunk), chunk)
            act = gbuf[part, ds, :, :, :, :width].reshape(rows, width)
            z_g = jnp.dot(act, wg[:, at], preferred_element_type=F32) + scale * jnp.dot(low_g, bg[:, at], preferred_element_type=F32)
            z_u = jnp.dot(act, wu[:, at], preferred_element_type=F32) + scale * jnp.dot(low_u, bu[:, at], preferred_element_type=F32)
            hid[part, ds, :, at] = (z_g * jax.nn.sigmoid(z_g) * z_u).astype(BF)
            return carry

        lax.fori_loop(0, 2 * half // chunk, columns, 0)
        pltpu.make_async_copy(hid.at[part, ds], hid_ref.at[part, ds], store_sem).start()

    def on_near():
        for load in loads:
            load.wait()
        lax.fori_loop(0, 2, lambda part, c: (unit(part, 0), c)[1], 0)

    def on_sides():
        lax.fori_loop(0, 4, lambda i, c: (unit(lax.rem(i, 2), 1 + 2 * (i // 2)), c)[1], 0)

    def on_far():
        lax.fori_loop(0, 2, lambda part, c: (unit(part, 2), c)[1], 0)

    gather(gather_messages(place, gbuf, send_sem, recv_sem), on_near, on_sides, on_far)
    pltpu.make_async_copy(hid, hid_ref, store_sem).wait()


def gate_up(ids, own, w, side, adapters, rank, scale, collective_id):
    _, _, rows, cols = own.shape
    half = w[0].shape[1]
    depth = w[0].shape[0]
    hidden = jax.ShapeDtypeStruct((2, 4, 8 * rows, 2 * half), BF)
    return pl.pallas_call(
        functools.partial(gate_up_kernel, side, adapters, rank, scale),
        out_shape=hidden,
        in_specs=[SMEM] + [HBM] * 9,
        out_specs=HBM,
        scratch_shapes=gather_scratch(rows, cols) + [
            pltpu.VMEM((depth, 2 * half), BF),
            pltpu.VMEM((depth, 2 * half), BF),
            pltpu.VMEM((adapters * rank, 2 * half), BF),
            pltpu.VMEM((adapters * rank, 2 * half), BF),
            pltpu.VMEM(hidden.shape, BF),
            pltpu.SemaphoreType.DMA((2,)),
            pltpu.SemaphoreType.DMA,
        ],
        compiler_params=pltpu.CompilerParams(collective_id=collective_id, has_side_effects=True, vmem_limit_bytes=VMEM_MOST),
        name='gate_up',
    )(ids, own, *w)


SCATTER_SLOTS = 18


def row_proj_kernel(side, adapters, ids_ref, act_ref, w_own, w_par, a_own, a_par, out_ref,
                    act, w, stage, near, landed, fast_near, fast_landed, send_sem, recv_sem, load_sem):
    place = Place(side)
    half, width = w_own.shape
    rank = a_own.shape[2]
    rows = stage.shape[3]
    quarter = rows // 2
    loads = [pltpu.make_async_copy(act_ref, act, load_sem)]
    for at, w_part, a_part in ((0, w_own, a_own), (half, w_par, a_par)):
        loads.append(pltpu.make_async_copy(w_part, w.at[pl.ds(at, half), pl.ds(0, width)], load_sem))
        for a in range(adapters):
            loads.append(pltpu.make_async_copy(a_part.at[a], w.at[pl.ds(at, half), pl.ds(width + a * rank, rank)], load_sem))
    for load in loads:
        load.start()
    place.barrier()
    for load in loads:
        load.wait()
    chunk = fit(width, 512)

    def unit(part, ds):
        def columns(n, carry):
            at = pl.ds(pl.multiple_of(n * chunk, chunk), chunk)
            sums = jnp.dot(act[part, ds], w[:, at], preferred_element_type=F32)
            stage[part, ds, :, :, at] = sums.reshape(4, rows, chunk).astype(BF)
            return carry

        lax.fori_loop(0, width // chunk, columns, 0)
        low = jnp.dot(act[part, ds], w[:, width:], preferred_element_type=F32)
        chosen = adapter_of_rows(place, ids_ref, part, ds, (4 * rows, rank))
        kept = low[:, :rank]
        for a in range(1, adapters):
            kept = jnp.where(chosen == a, low[:, a * rank:(a + 1) * rank], kept)
        stage[part, ds, :, :, width:] = kept.reshape(4, rows, rank).astype(BF)

    def message(part, slot):
        sems = (send_sem.at[part, slot], recv_sem.at[part, slot])
        lo, hi = pl.ds(0, quarter), pl.ds(quarter, quarter)
        table = (
            (stage.at[part, 2, 2], near.at[part, 0], 's', 1),
            (stage.at[part, 2, 3], near.at[part, 1], 's', 1),
            (stage.at[part, 2, 0], near.at[part, 2], 's', -1),
            (stage.at[part, 2, 1], near.at[part, 3], 's', -1),
            (stage.at[part, 1, 0], landed.at[part, 0, 0], 's', 1),
            (stage.at[part, 1, 1], landed.at[part, 0, 1], 's', 1),
            (stage.at[part, 3, 2], landed.at[part, 1, 2], 's', -1),
            (stage.at[part, 3, 3], landed.at[part, 1, 3], 's', -1),
            (stage.at[part, 1, 2], landed.at[part, 0, 2], 's', 1),
            (stage.at[part, 1, 3], landed.at[part, 0, 3], 's', 1),
            (stage.at[part, 3, 0], landed.at[part, 1, 0], 's', -1),
            (stage.at[part, 3, 1], landed.at[part, 1, 1], 's', -1),
            (stage.at[part, 0, 2, lo], fast_near.at[part, 0], 'f', 1),
            (stage.at[part, 0, 2, hi], fast_near.at[part, 1], 'f', -1),
            (stage.at[part, 0, 1, hi], fast_landed.at[part, 0, hi], 'f', 1),
            (stage.at[part, 0, 3, lo], fast_landed.at[part, 1, lo], 'f', -1),
            (stage.at[part, 0, 1, lo], fast_landed.at[part, 0, lo], 'f', 1),
            (stage.at[part, 0, 3, hi], fast_landed.at[part, 1, hi], 'f', -1),
        )
        src, dst, ring, step = table[slot]
        return remote(src, dst, *sems, place.slow(part, step) if ring == 's' else place.fast(part, step))

    def add(into, *others):
        def some(i, carry):
            at = pl.ds(pl.multiple_of(i * 16, 16), 16)
            total = into[at, :].astype(F32)
            for other in others:
                total += other[at, :].astype(F32)
            into[at, :] = total.astype(BF)
            return carry

        lax.fori_loop(0, into.shape[0] // 16, some, 0)

    def start(slot, parts=(0, 1)):
        for part in parts:
            message(part, slot).start()

    def arrived(slot, parts=(0, 1)):
        for part in parts:
            message(part, slot).wait_recv()

    for part in (0, 1):
        unit(part, 2)
        for slot in (0, 2, 1, 3):
            start(slot, (part,))
    lax.fori_loop(0, 4, lambda i, c: (unit(lax.rem(i, 2), 1 + 2 * (i // 2)), c)[1], 0)
    for slot in (4, 6, 5, 7):
        start(slot)
    lax.fori_loop(0, 2, lambda part, c: (unit(part, 0), c)[1], 0)
    for near_slot, ds, df, slot in ((0, 1, 2, 8), (2, 3, 0, 10), (1, 1, 3, 9), (3, 3, 1, 11)):
        for part in (0, 1):
            arrived(near_slot, (part,))
            add(stage.at[part, ds, df], near.at[part, near_slot])
            start(slot, (part,))
    for df, slots, nexts in ((2, (6, 8), (12, 13)), (0, (4, 10), ()), (3, (7, 9), (15,)), (1, (5, 11), (14,))):
        for part in (0, 1):
            for slot in slots:
                arrived(slot, (part,))
            add(stage.at[part, 0, df], landed.at[part, 0, df], landed.at[part, 1, df])
            for slot in nexts:
                start(slot, (part,))
    for part in (0, 1):
        arrived(12, (part,))
        add(stage.at[part, 0, 1, pl.ds(0, quarter)], fast_near.at[part, 0])
        start(16, (part,))
        arrived(13, (part,))
        add(stage.at[part, 0, 3, pl.ds(quarter, quarter)], fast_near.at[part, 1])
        start(17, (part,))
    for part in (0, 1):
        for slot in (14, 15, 16, 17):
            arrived(slot, (part,))
        add(stage.at[part, 0, 0], fast_landed.at[part, 0], fast_landed.at[part, 1])
    out = [pltpu.make_async_copy(stage.at[part, 0, 0], out_ref.at[pl.ds(part * rows, rows)], load_sem) for part in (0, 1)]
    for copy in out:
        copy.start()
    for copy in out:
        copy.wait()
    for part in (0, 1):
        for slot in range(SCATTER_SLOTS):
            message(part, slot).wait_send()


def row_proj(ids, act, w_own, w_par, a_own, a_par, side, collective_id):
    adapters, _, rank = a_own.shape
    half, width = w_own.shape
    rows = act.shape[2] // 4
    cols = width + rank
    return pl.pallas_call(
        functools.partial(row_proj_kernel, side, adapters),
        out_shape=jax.ShapeDtypeStruct((2 * rows, cols), BF),
        in_specs=[SMEM] + [HBM] * 5,
        out_specs=HBM,
        scratch_shapes=[
            pltpu.VMEM(act.shape, BF),
            pltpu.VMEM((2 * half, width + adapters * rank), BF),
            pltpu.VMEM((2, 4, 4, rows, cols), BF),
            pltpu.VMEM((2, 4, rows, cols), BF),
            pltpu.VMEM((2, 2, 4, rows, cols), BF),
            pltpu.VMEM((2, 2, rows // 2, cols), BF),
            pltpu.VMEM((2, 2, rows, cols), BF),
            pltpu.SemaphoreType.DMA((2, SCATTER_SLOTS)),
            pltpu.SemaphoreType.DMA((2, SCATTER_SLOTS)),
            pltpu.SemaphoreType.DMA,
        ],
        compiler_params=pltpu.CompilerParams(collective_id=collective_id, has_side_effects=True, vmem_limit_bytes=VMEM_MOST),
        name='row_proj',
    )(ids, act, w_own, w_par, a_own, a_par)


def qkv_kernel(where_ref, ids_ref, xa_ref, xb_ref, gain_ref, at_ref, *rest):
    weights, (z_ref, low_ref, w, h, sem) = rest[:6], rest[6:]
    step = pl.program_id(0)
    head = weights[0].shape[1]
    seq_len = xa_ref.shape[1]

    @pl.when(step == 0)
    def _():
        copies = [pltpu.make_async_copy(weights[i], w.at[:, pl.ds(i * head, head)], sem) for i in range(6)]
        for c in copies:
            c.start()
        for c in copies:
            c.wait()

    for i, x_ref in enumerate((xa_ref, xb_ref)):
        act = x_ref[0].astype(F32)
        inv_rms = lax.rsqrt(jnp.mean(act * act, axis=-1, keepdims=True) + EPSILON)
        h[i * seq_len:(i + 1) * seq_len, :] = (act * inv_rms * gain_ref[...]).astype(BF)
    chunk = fit(6 * head, 256)
    for n in range(6 * head // chunk):
        z_ref[:, n * chunk:(n + 1) * chunk] = jnp.dot(h[...], w[:, n * chunk:(n + 1) * chunk], preferred_element_type=F32)
    low = lax.dot_general(at_ref[...], h[...], (((1,), (1,)), ((), ())), preferred_element_type=F32)
    adapters = at_ref.shape[0] // 32
    pieces = []
    for i in range(2):
        chosen = ids_ref[2 * step + i]
        piece = low[:32, i * seq_len:(i + 1) * seq_len]
        for a in range(1, adapters):
            piece = jnp.where(chosen == a, low[32 * a:32 * (a + 1), i * seq_len:(i + 1) * seq_len], piece)
        pieces.append(piece)
    low_sel = jnp.concatenate(pieces, axis=1).astype(BF)
    low_ref[0, 0] = low_sel[:16]
    low_ref[1, 0] = low_sel[16:]


def qkv(where, plane_ids, x_in, gain, a_rows, weights):
    depth = x_in.shape[2]
    seq_len = x_in.shape[1]
    head = weights[0].shape[1]
    seqs = x_in.shape[0] // 2
    steps = seqs // 2
    grid_spec = pltpu.PrefetchScalarGridSpec(
        num_scalar_prefetch=2,
        grid=(steps,),
        in_specs=[
            pl.BlockSpec((1, seq_len, depth), lambda i, where, ids: (4 * i + where[0], 0, 0)),
            pl.BlockSpec((1, seq_len, depth), lambda i, where, ids: (4 * i + 2 + where[0], 0, 0)),
            pl.BlockSpec((1, depth), lambda i, where, ids: (0, 0)),
            pl.BlockSpec(a_rows.shape, lambda i, where, ids: (0, 0)),
        ] + [HBM] * 6,
        out_specs=[
            pl.BlockSpec((2 * seq_len, 6 * head), lambda i, where, ids: (i, 0)),
            pl.BlockSpec((2, 1, 16, 2 * seq_len), lambda i, where, ids: (0, i // (steps // 2), 0, lax.rem(i, steps // 2))),
        ],
        scratch_shapes=[pltpu.VMEM((depth, 6 * head), BF), pltpu.VMEM((2 * seq_len, depth), BF), pltpu.SemaphoreType.DMA],
    )
    tokens = seqs * seq_len
    return pl.pallas_call(
        qkv_kernel,
        grid_spec=grid_spec,
        out_shape=[jax.ShapeDtypeStruct((tokens, 6 * head), F32), jax.ShapeDtypeStruct((2, 2, 16, tokens // 2), BF)],
        compiler_params=pltpu.CompilerParams(dimension_semantics=('arbitrary',), vmem_limit_bytes=VMEM_MOST),
        cost_estimate=pl.CostEstimate(flops=2 * tokens * depth * 7 * head, bytes_accessed=2 * tokens * depth * 2, transcendentals=0),
        name='qkv',
    )(where, plane_ids, x_in, x_in, gain.reshape(1, depth), a_rows, *weights)


def attention_kernel(scale, where_ref, ids_ref, z_ref, low_ref, bqk_ref, bv_ref, cos_ref, sin_ref, out_a_ref, out_b_ref):
    head = cos_ref.shape[1]
    seq_len = z_ref.shape[0]
    c = where_ref[1 + pl.program_id(0)]
    adapter = ids_ref[c]
    parts = [low_ref[p, :, 0].reshape(-1, seq_len) for p in (0, 1)]
    across = (((0,), (0,)), ((), ()))
    z_qk = z_ref[:, :4 * head] + scale * lax.dot_general(parts[0], bqk_ref[adapter], across, preferred_element_type=F32)
    z_v = z_ref[:, 4 * head:] + scale * lax.dot_general(parts[1], bv_ref[adapter], across, preferred_element_type=F32)
    cos, sin = cos_ref[...], sin_ref[...]
    rotated = []
    for i in range(4):
        z = z_qk[:, i * head:(i + 1) * head]
        rotated.append((z * cos + pltpu.roll(z, head // 2, axis=1) * sin).astype(BF))
    values = z_v.astype(BF)
    causal = lax.broadcasted_iota(jnp.int32, (seq_len, seq_len), 0) >= lax.broadcasted_iota(jnp.int32, (seq_len, seq_len), 1)
    for i in range(2):
        scores = lax.dot_general(rotated[i], rotated[2 + i], (((1,), (1,)), ((), ())), preferred_element_type=F32) * head ** -0.5
        scores = jnp.where(causal, scores, -1e30)
        e = jnp.exp(scores - jnp.max(scores, axis=-1, keepdims=True))
        prob = (e / jnp.sum(e, axis=-1, keepdims=True)).astype(BF)
        mixed = jnp.dot(prob, values[:, i * head:(i + 1) * head], preferred_element_type=F32).astype(BF)
        out_a_ref[0, :, i * head:(i + 1) * head] = mixed[:seq_len // 2]
        out_b_ref[0, :, i * head:(i + 1) * head] = mixed[seq_len // 2:]


def attention(where, plane_ids, z, low, b_qk, b_v, scale):
    tokens, cols = z.shape
    head = cols // 6
    chips = 16
    seq_len = tokens // chips
    half_dim = head // 2
    inv_freq = ROPE_BASE ** (-2.0 * jnp.arange(half_dim, dtype=F32) / head)
    angle = jnp.arange(seq_len, dtype=F32)[:, None] * inv_freq[None, :]
    cos = jnp.concatenate([jnp.cos(angle)] * 2, axis=1)
    sin = jnp.concatenate([-jnp.sin(angle), jnp.sin(angle)], axis=1)
    whole = lambda a: pl.BlockSpec(a.shape, lambda i, where, ids: (0,) * a.ndim)
    chip_of = lambda i, where: where[1 + i]
    grid_spec = pltpu.PrefetchScalarGridSpec(
        num_scalar_prefetch=2,
        grid=(chips,),
        in_specs=[
            pl.BlockSpec((seq_len, cols), lambda i, where, ids: (chip_of(i, where), 0)),
            pl.BlockSpec((2, chips, 1, 16, seq_len), lambda i, where, ids: (0, 0, chip_of(i, where) // (chips // 2), 0, lax.rem(chip_of(i, where), chips // 2))),
            whole(b_qk), whole(b_v), whole(cos), whole(sin),
        ],
        out_specs=[
            pl.BlockSpec((1, seq_len // 2, 2 * head), lambda i, where, ids: (i, 0, 0)),
            pl.BlockSpec((1, seq_len // 2, 2 * head), lambda i, where, ids: (lax.rem(i, 4) * 4 + i // 4, 0, 0)),
        ],
    )
    one = jax.ShapeDtypeStruct((chips, seq_len // 2, 2 * head), BF)
    return pl.pallas_call(
        functools.partial(attention_kernel, scale),
        grid_spec=grid_spec,
        out_shape=[one, one],
        compiler_params=pltpu.CompilerParams(dimension_semantics=('arbitrary',), vmem_limit_bytes=VMEM_MOST),
        cost_estimate=pl.CostEstimate(flops=16 * tokens * head * head, bytes_accessed=tokens * cols * 4, transcendentals=tokens * seq_len * 2),
        name='attention',
    )(where, plane_ids, z, low.reshape(2, chips, 2, 16, tokens // 2), b_qk, b_v, cos, sin)


def solution(mesh):
    tp_size = mesh.shape['tensor']
    side = math.isqrt(tp_size // 2)
    partner = [(i, i ^ 1) for i in range(tp_size)]
    head_split = P(None, 'tensor', None)
    last_split = P(None, None, 'tensor')
    b_head_split = P(None, None, 'tensor', None)
    in_specs = (P('data', None, None), P('data'), P(None), P(None),
                head_split, head_split, head_split, P('tensor', None, None),
                P(None, 'tensor'), P(None, 'tensor'), P('tensor', None),
                last_split, b_head_split, last_split, b_head_split, last_split, b_head_split,
                P(None, 'tensor', None, None), last_split,
                last_split, last_split, last_split, last_split,
                P(None, 'tensor', None), last_split)

    def local_layer(x_in, adapter_ids, gain_attn, gain_mlp, w_q, w_k, w_v, w_o, w_gate, w_up, w_down, a_q, b_q, a_k, b_k, a_v, b_v, a_o, b_o, a_gate, b_gate, a_up, b_up, a_down, b_down):
        depth = x_in.shape[2]
        seq_len = x_in.shape[1]
        adapters, rank = b_q.shape[0], b_q.shape[1]
        scale = ALPHA / rank
        index = lax.axis_index('tensor')
        core = lax.rem(index, 2)
        my_y, my_x = index // 2 // side, lax.rem(index // 2, side)

        def other(a):
            return lax.ppermute(a, 'tensor', partner)

        plane_ids = lax.dynamic_index_in_dim(adapter_ids.reshape(-1, 2), core, axis=1, keepdims=False)
        steps = jnp.arange(side)
        chips = (lax.rem(my_y + steps, side)[:, None] * side + lax.rem(my_x + steps, side)[None, :]).reshape(-1)
        where = jnp.concatenate([core[None], chips]).astype(jnp.int32)

        own_qkv = [w_q[:, 0], w_k[:, 0], w_v[:, 0]]
        par_qkv = [other(w) for w in own_qkv]
        own_a = jnp.stack([a.swapaxes(1, 2) for a in (a_q, a_k, a_v)], axis=1)
        par_a = other(own_a)
        first = jnp.where(core == 0, own_a, par_a)
        second = jnp.where(core == 0, par_a, own_a)
        a_rows = jnp.concatenate([first, second], axis=2)
        a_rows = jnp.pad(a_rows, ((0, 0), (0, 1), (0, 0), (0, 0))).reshape(adapters * 32, depth)
        z, low = qkv(where, plane_ids, x_in, gain_attn, a_rows, [w for pair in zip(own_qkv, par_qkv) for w in pair])

        def both_heads(b):
            return jnp.concatenate([b[:, :, 0], other(b)[:, :, 0]], axis=-1).reshape(adapters, side * side, 8, -1)

        bq2, bk2, bv2 = both_heads(b_q), both_heads(b_k), both_heads(b_v)
        blank = jnp.zeros_like(bq2)
        b_qk = jnp.concatenate([jnp.concatenate([bq2, blank], axis=-1), jnp.concatenate([blank, bk2], axis=-1)], axis=2).reshape(adapters, 2 * rank, -1)
        bv2 = bv2.reshape(adapters, side, side, 8, -1).swapaxes(1, 2).reshape(bv2.shape)
        b_v2 = jnp.concatenate([bv2, blank], axis=2).reshape(adapters, 2 * rank, -1)
        low_all = small_gather(low, side, 0)
        attn_a, attn_b = attention(where, plane_ids, z, low_all, b_qk, b_v2, scale)
        attn = jnp.stack([attn_a, attn_b]).reshape(2, 4, 4 * (seq_len // 2), -1)

        my_id = adapter_ids[index]

        def pick(a):
            return lax.dynamic_index_in_dim(a, my_id, axis=0, keepdims=False)

        full_b = lax.all_gather(jnp.stack([b_o, b_down], axis=1), 'tensor', axis=0)
        full_a = lax.all_gather(jnp.stack([a_gate.swapaxes(1, 2), a_up.swapaxes(1, 2)], axis=1), 'tensor', axis=0)
        my_b = lax.dynamic_index_in_dim(full_b, my_id, axis=1, keepdims=False)
        my_a = lax.dynamic_index_in_dim(full_a, my_id, axis=1, keepdims=False)

        def finish(sums, b_mine, resid):
            base, low_rank = sums[:, :depth].astype(F32), sums[:, depth:]
            delta = jnp.einsum('sr,jrc->sjc', low_rank, b_mine, preferred_element_type=F32).reshape(seq_len, depth)
            return (resid.astype(F32) + (base + scale * delta)).astype(BF)

        x_own = lax.dynamic_index_in_dim(x_in, index, axis=0, keepdims=False)
        a_o2 = a_o[:, 0]
        sums = row_proj(adapter_ids, attn, w_o[0], other(w_o[0]), a_o2, other(a_o2), side, 1)
        x_mid = finish(sums, my_b[:, 0], x_own)
        mid_f32 = x_mid.astype(F32)
        h_mlp = (mid_f32 * lax.rsqrt(jnp.mean(mid_f32 * mid_f32, axis=-1, keepdims=True) + EPSILON) * gain_mlp).astype(BF)
        low_gu = jnp.einsum('sd,jprd->spjr', h_mlp, my_a, preferred_element_type=F32).astype(BF).reshape(seq_len, 2 * rank)
        payload = jnp.concatenate([h_mlp, low_gu], axis=1).reshape(2, 2, seq_len // 4, depth + 2 * rank)

        ffn = w_gate.shape[1]
        half = round_up(ffn, LANE)
        pad_cols = lambda w: jnp.pad(w, ((0, 0),) * (w.ndim - 1) + ((0, half - ffn),))
        gate_up_w = []
        for w in (w_gate, w_up, b_gate.reshape(adapters * rank, ffn), b_up.reshape(adapters * rank, ffn)):
            w = pad_cols(w)
            gate_up_w += [w, other(w)]
        hidden = gate_up(adapter_ids, payload, gate_up_w, side, adapters, rank, scale, 2)
        w_d = jnp.pad(w_down, ((0, half - ffn), (0, 0)))
        a_d = jnp.pad(a_down, ((0, 0), (0, half - ffn), (0, 0)))
        sums = row_proj(adapter_ids, hidden, w_d, other(w_d), a_d, other(a_d), side, 3)
        y_own = finish(sums, my_b[:, 1], x_mid)
        return lax.all_gather(y_own, 'tensor', axis=0)

    return jax.shard_map(local_layer, mesh=mesh, in_specs=in_specs, out_specs=P('data', None, None), check_vma=False)
```

time: 1120 us -> 592 us (0.53)
  waiting for transfers between devices: 713 us -> 112 us
  Pallas kernels: 0 us -> 378 us
  matrix products: 253 us -> 7.3 us
  other arithmetic: 48.6 us -> 11.9 us
  local copies, waits for them, and re-layouts: 84.1 us -> 57.7 us
    pallas_call x0 -> x6, Pallas kernels: none -> 378 us  [the longest x2 200 us: row_proj(): pl.pallas_call(functools.partial(row_proj_kernel, side, adapters), out_sh...]
    reduce_scatter x2 -> x0, waiting for transfers between devices: 318 us -> none  [row_proj(): lax.psum_scatter(base_part, 'tensor', scatter_dimension=2, tiled=True)]
    dot_general x22 -> x3, matrix products: 253 us -> 7.3 us  [the longest x2 5.73 us: finish(): jnp.einsum('sr,jrc->sjc', low_rank, b_mine, preferred_element_type=F32)]
    all_gather x7 -> x3, waiting for transfers between devices: 255 us -> 110 us  [the longest x1 109 us: local_layer(): return lax.all_gather(y_own, 'tensor', axis=0)]
    psum x2 -> x0, waiting for transfers between devices: 139 us -> none  [row_proj(): low_rank = lax.psum(low_part, 'tensor')]
    all_gather x1 -> x0, local copies, waits for them, and re-layouts: 44.2 us -> none  [row_proj(): return (out_shard, lax.all_gather(out_shard, 'tensor', axis=2, tiled=True))]
    unnamed x41 -> x35, local copies, waits for them, and re-layouts: 5.2 us -> 34.9 us
    gather x14 -> x0, local copies, waits for them, and re-layouts: 29.3 us -> none  [per_sequence(): return jnp.take(table_stack, adapter_ids, axis=0)]
  transfers between devices with their start and end apart: 11 -> 18, of which waited for: 8 -> 3; matrix products, arithmetic and copies ran while one was open for 18% -> 8% of each run, Pallas kernels for 0% -> 47%
where the time goes in v1:
time: 592 us; the launch traced here: 591 us
  Pallas kernels  378 us (64%)
  waiting for transfers between devices  112 us (19%)
  local copies, waits for them, and re-layouts  57.7 us (10%)
  between operations  15.6 us (3%)
  other arithmetic  11.9 us (2%)
  starting transfers between devices  8.89 us (2%)
  matrix products  7.3 us (1%)
    pallas_call x2, Pallas kernels, row_proj(): pl.pallas_call(functools.partial(row_proj_kernel, side, adapters), out_sh...  200 us
    all_gather x1, waiting for transfers between devices, local_layer(): return lax.all_gather(y_own, 'tensor', axis=0)  109 us
    pallas_call x1, Pallas kernels, gate_up(): pl.pallas_call(functools.partial(gate_up_kernel, side, adapters, rank, sc...  104 us
    unnamed x35, local copies, waits for them, and re-layouts  34.9 us
    pallas_call x1, Pallas kernels, qkv(): pl.pallas_call(qkv_kernel, grid_spec=grid_spec, out_shape=[jax.ShapeDtype...  28.8 us
    pallas_call x1, Pallas kernels, small_gather(): pl.pallas_call(functools.partial(small_gather_kernel, side), out_shape=ja...  28 us
    pallas_call x1, Pallas kernels, attention(): pl.pallas_call(functools.partial(attention_kernel, scale), grid_spec=grid...  17.3 us
  transfers between devices with their start and end apart: 18, of which 3 were waited for; matrix products, arithmetic and copies ran while one was open for 8% of the time, Pallas kernels for 47%

profile of v1, /device:TPU:97, one launch (start us, length us, event | category | flops | bytes accessed | tf_op | source)
XLA Modules:
  0.0 590.7 jit_solution(17479262988681600290)
XLA Ops:
  6.6 1.6 pad_maximum_fusion.5
  8.3 1.6 pad_maximum_fusion.6
  10.0 2.1 collective-permute-start.8
  12.8 1.1 copy.43
  15.0 1.2 dynamic_slice.21
  18.4 1.6 pad.35.a_own
  20.9 3.8 pad.34.w_own
  24.8 3.4 copy.40
  28.1 2.0 pad.30.wg_own
  30.2 3.4 copy.41
  33.6 2.0 pad.31.wu_own
  42.3 0.9 pad_maximum_fusion.2
  46.0 1.4 collective-permute-done.3.rest_5_
  48.4 28.8 %qkv.1 = (f32[2048,768]{1,0:T(8,128)}, bf16[2,2,16,1024]{3,2,1,0:T(8,128)(2,1)}) custom-call(s32[17]{0:T(128)} %pad_add_fusion.where_ref, s32[16]{0:T(128)} %dynamic-slice_reduce_fusion.ids_ref, bf16[32,128,4096]{2,1,0:T(8,128)(2,1)} %xb_ref.1, bf16[32,128,4096]{2,1,0:T(8,128)(2,1)} %xb_ref.1, f32[1,4096]{1,0:T(1,128)} %bitcast.116, ...), custom_call_target="tpu_custom_call" | custom-call | flops 15032385536 | bytes 33554432 | tf_op jit(solution)/shard_map/qkv/pallas_call | solution.py:454
  77.2 28.0 %small_gather.1 = bf16[2,4,4,2,16,1024]{5,4,3,2,1,0:T(8,128)(2,1)} custom-call(bf16[2,2,16,1024]{3,2,1,0:T(8,128)(2,1)} %get-tuple-element.10.own_ref), custom_call_target="tpu_custom_call" | custom-call | tf_op jit(solution)/shard_map/small_gather/pallas_call | solution.py:155
  105.2 17.3 %attention.1 = (bf16[16,64,256]{2,1,0:T(8,128)(2,1)}, bf16[16,64,256]{2,1,0:T(8,128)(2,1)}) custom-call(s32[17]{0:T(128)} %pad_add_fusion.where_ref, s32[16]{0:T(128)} %dynamic-slice_reduce_fusion.ids_ref, f32[2048,768]{1,0:T(8,128)} %get-tuple-element.9.z_ref, bf16[2,16,2,16,1024]{4,3,2,1,0:T(8,128)(2,1)} %bitcast.79, bf16[2,256,512]{2,1,0:T(8,128)(2,1)} %bitcast.83, ...), custom_call_target="tpu_custom_call" | custom-call | flops 536870912 | bytes 6291456 | tf_op jit(solution)/shard_map/attention/pallas_call | solution.py:516
  122.5 2.3 pad_maximum_fusion.1.act_ref
  124.7 2.4 collective-permute-start.9
  127.3 98.7 %row_proj.2 = bf16[128,4224]{1,0:T(8,128)(2,1)} custom-call(s32[32]{0:T(128)} %ids_ref.5, bf16[2,4,256,256]{3,2,1,0:T(8,128)(2,1)} %pad_maximum_fusion.1.act_ref, bf16[128,4096]{1,0:T(8,128)(2,1)} %bitcast.26.w_own, bf16[128,4096]{1,0:T(8,128)(2,1)} %collective-permute-done.7.w_par, bf16[2,128,128]{2,1,0:T(8,128)(2,1)} %bitcast.107, ...), custom_call_target="tpu_custom_call" | custom-call | tf_op jit(solution)/shard_map/row_proj/pallas_call | solution.py:375
  226.0 3.2 constant_dynamic-slice_fusion.1
  229.2 3.3 copy.45
  232.5 1.2 fusion.23
  233.7 2.3 fusion
  236.1 2.8 constant_dynamic-slice_fusion
  239.3 1.6 fusion.7
  241.2 1.1 collective-permute-start.14
  242.3 1.1 pad_maximum_fusion.own_ref
  243.4 103.9 %gate_up.1.act_ref = bf16[2,4,256,768]{3,2,1,0:T(8,128)(2,1)} custom-call(s32[32]{0:T(128)} %ids_ref.5, bf16[2,2,32,4352]{3,2,1,0:T(8,128)(2,1)} %pad_maximum_fusion.own_ref, bf16[4096,384]{1,0:T(8,128)(2,1)} %pad.30.wg_own, bf16[4096,384]{1,0:T(8,128)(2,1)} %collective-permute-done.9.wg_par, bf16[4096,384]{1,0:T(8,128)(2,1)} %pad.31.wu_own, ...), custom_call_target="tpu_custom_call" | custom-call | tf_op jit(solution)/shard_map/gate_up/pallas_call | solution.py:228
  347.3 101.0 %row_proj.3 = bf16[128,4224]{1,0:T(8,128)(2,1)} custom-call(s32[32]{0:T(128)} %ids_ref.5, bf16[2,4,256,768]{3,2,1,0:T(8,128)(2,1)} %gate_up.1.act_ref, bf16[384,4096]{1,0:T(8,128)(2,1)} %pad.34.w_own, bf16[384,4096]{1,0:T(8,128)(2,1)} %collective-permute-done.13.w_par, bf16[2,384,128]{2,1,0:T(8,128)(2,1)} %pad.35.a_own, ...), custom_call_target="tpu_custom_call" | custom-call | tf_op jit(solution)/shard_map/row_proj/pallas_call | solution.py:375
  448.3 3.4 fusion.3
  451.8 109.5 %all-gather.11.cloned.1.call-done = bf16[4096,4096]{1,0:T(8,128)(2,1)} async-done(((bf16[128,4096]{1,0:T(8,128)(2,1)}), bf16[4096,4096]{1,0:T(8,128)(2,1)}) %all-gather.11.cloned.1.call-update) | async-done | bytes 33554448 | tf_op jit(solution)/shard_map/all_gather | solution.py:616
  561.3 22.9 %copy.55 = bf16[32,128,4096]{2,1,0:T(8,128)(2,1)} copy(bf16[32,128,4096]{2,1,0:T(8,128)(2,1)} %bitcast.78) | data formatting | bytes 67108864
  (89 shorter events, 14.3 us)
Async XLA Ops:
  6.5 13.5 %copy-start.9 = (bf16[2,128,344]{1,2,0:T(8,128)(2,1)S(1)}, bf16[2,128,344]{1,2,0:T(8,128)(2,1)}, u32[]{:S(2)}) copy-start(bf16[2,128,344]{1,2,0:T(8,128)(2,1)} %param.45) | copy-start | bytes 528388
  6.5 219.5 %all-gather.7.cloned.1.call-start = ((), (), s32[]{:S(2)}) async-start(), calls=%async_computation | async-start | bytes 4325376 | tf_op jit(solution)/shard_map/all_gather | solution.py:585
  8.2 227.9 %all-gather.9.cloned.1.call-start = ((), (), s32[]{:S(2)}) async-start(), calls=%async_computation.1 | async-start | bytes 4325376 | tf_op jit(solution)/shard_map/all_gather | solution.py:586
  9.9 551.3 %all-gather.11.cloned.1.call-start = ((), (), s32[]{:S(2)}) async-start(), calls=%async_computation.2 | async-start | bytes 34603008 | tf_op jit(solution)/shard_map/all_gather | solution.py:616
  10.0 114.7 %collective-permute-start.8 = (bf16[2,128,128]{2,1,0:T(8,128)(2,1)}, bf16[2,128,128]{2,1,0:T(8,128)(2,1)}, u32[]{:S(2)}, u32[]{:S(2)}) collective-permute-start(bf16[2,128,128]{2,1,0:T(8,128)(2,1)} %bitcast.106), channel_id=1, source_target_pairs={{0,1},{1,0},{2,3},{3,2},{4,5},{5,4},{6,7},{7,6},{8,9},{9,8},{10,11... | collective-permute-start | bytes 196616 | tf_op jit(solution)/shard_map/ppermute | solution.py:551
  12.2 29.8 %collective-permute-start.4 = (bf16[2,128,1,128]{3,1,2,0:T(8,128)(2,1)}, bf16[2,128,1,128]{3,1,2,0:T(8,128)(2,1)S(1)}, u32[]{:S(2)}, u32[]{:S(2)}) collective-permute-start(bf16[2,128,1,128]{3,1,2,0:T(8,128)(2,1)} %param.37), channel_id=1, source_target_pairs={{0,1},{1,0},{2,3},{3,2},{4,5},{5,4},{6,7},{7,6},{8,9},{9,8},{10,11... | collective-permute-start | bytes 196616 | tf_op jit(solution)/shard_map/ppermute | solution.py:551
  12.3 28.4 %collective-permute-start.5 = (bf16[2,128,1,128]{3,1,2,0:T(8,128)(2,1)}, bf16[2,128,1,128]{3,1,2,0:T(8,128)(2,1)}, u32[]{:S(2)}, u32[]{:S(2)}) collective-permute-start(bf16[2,128,1,128]{3,1,2,0:T(8,128)(2,1)} %param.39), channel_id=1, source_target_pairs={{0,1},{1,0},{2,3},{3,2},{4,5},{5,4},{6,7},{7,6},{8,9},{9,8},{10,11... | collective-permute-start | bytes 196616 | tf_op jit(solution)/shard_map/ppermute | solution.py:551
  12.7 26.3 %collective-permute-start.6 = (bf16[2,128,1,128]{3,1,2,0:T(8,128)(2,1)}, bf16[2,128,1,128]{3,1,2,0:T(8,128)(2,1)}, u32[]{:S(2)}, u32[]{:S(2)}) collective-permute-start(bf16[2,128,1,128]{3,1,2,0:T(8,128)(2,1)} %param.41), channel_id=1, source_target_pairs={{0,1},{1,0},{2,3},{3,2},{4,5},{5,4},{6,7},{7,6},{8,9},{9,8},{10,11... | collective-permute-start | bytes 196616 | tf_op jit(solution)/shard_map/ppermute | solution.py:551
  14.6 226.7 %collective-permute-start.12 = (bf16[256,384]{1,0:T(8,128)(2,1)}, bf16[256,384]{1,0:T(8,128)(2,1)}, u32[]{:S(2)}, u32[]{:S(2)}) collective-permute-start(bf16[256,384]{1,0:T(8,128)(2,1)} %pad.33.bu_own), channel_id=1, source_target_pairs={{0,1},{1,0},{2,3},{3,2},{4,5},{5,4},{6,7},{7,6},{8,9},{9,8},{10,11... | collective-permute-start | bytes 589832 | tf_op jit(solution)/shard_map/ppermute | solution.py:551
  33.5 4.6 copy-start.6
  33.5 4.6 copy-start.7
  33.6 4.6 copy-start.8
  33.6 5.5 copy-start.10
  33.6 7.5 %copy-start.11 = (bf16[2,128,1,128]{3,1,2,0:T(8,128)(2,1)S(1)}, bf16[2,128,1,128]{3,1,2,0:T(8,128)(2,1)}, u32[]{:S(2)}) copy-start(bf16[2,128,1,128]{3,1,2,0:T(8,128)(2,1)} %param.39) | copy-start | bytes 196612
  35.6 6.4 %copy-start = (bf16[4096,1,128]{2,0,1:T(8,128)(2,1)S(1)}, bf16[4096,1,128]{2,0,1:T(8,128)(2,1)}, u32[]{:S(2)}) copy-start(bf16[4096,1,128]{2,0,1:T(8,128)(2,1)} %param.30) | copy-start | bytes 3145732
  35.6 6.7 %copy-start.12 = (bf16[2,128,1,128]{3,1,2,0:T(8,128)(2,1)S(1)}, bf16[2,128,1,128]{3,1,2,0:T(8,128)(2,1)}, u32[]{:S(2)}) copy-start(bf16[2,128,1,128]{3,1,2,0:T(8,128)(2,1)} %param.37) | copy-start | bytes 196612
  35.6 7.6 %copy-start.1 = (bf16[4096,1,128]{2,0,1:T(8,128)(2,1)S(1)}, bf16[4096,1,128]{2,0,1:T(8,128)(2,1)}, u32[]{:S(2)}) copy-start(bf16[4096,1,128]{2,0,1:T(8,128)(2,1)} %param.31) | copy-start | bytes 3145732
  39.0 4.2 collective-permute-start
  40.7 4.2 collective-permute-start.1
  42.0 3.7 collective-permute-start.2
  43.2 4.2 collective-permute-start.3
  44.9 2.5 copy-start.2
  44.9 198.5 %collective-permute-start.11 = (bf16[256,384]{1,0:T(8,128)(2,1)}, bf16[256,384]{1,0:T(8,128)(2,1)}, u32[]{:S(2)}, u32[]{:S(2)}) collective-permute-start(bf16[256,384]{1,0:T(8,128)(2,1)} %pad.32.bg_own), channel_id=1, source_target_pairs={{0,1},{1,0},{2,3},{3,2},{4,5},{5,4},{6,7},{7,6},{8,9},{9,8},{10,11... | collective-permute-start | bytes 589832 | tf_op jit(solution)/shard_map/ppermute | solution.py:551
  45.6 2.1 copy-start.3
  45.6 81.5 %collective-permute-start.7 = (bf16[128,4096]{1,0:T(8,128)(2,1)}, bf16[128,4096]{1,0:T(8,128)(2,1)}, u32[]{:S(2)}, u32[]{:S(2)}) collective-permute-start(bf16[128,4096]{1,0:T(8,128)(2,1)} %bitcast.26.w_own), channel_id=1, source_target_pairs={{0,1},{1,0},{2,3},{3,2},{4,5},{5,4},{6,7},{7,6},{8,9},{9,8},{10,11... | collective-permute-start | bytes 3145736 | tf_op jit(solution)/shard_map/ppermute | solution.py:551
  47.4 1.0 copy-start.4
  47.4 196.0 %collective-permute-start.10 = (bf16[4096,384]{1,0:T(8,128)(2,1)}, bf16[4096,384]{1,0:T(8,128)(2,1)}, u32[]{:S(2)}, u32[]{:S(2)}) collective-permute-start(bf16[4096,384]{1,0:T(8,128)(2,1)} %pad.31.wu_own), channel_id=1, source_target_pairs={{0,1},{1,0},{2,3},{3,2},{4,5},{5,4},{6,7},{7,6},{8,9},{9,8},{10,11... | collective-permute-start | bytes 9437192 | tf_op jit(solution)/shard_map/ppermute | solution.py:551
  124.7 118.7 %collective-permute-start.9 = (bf16[4096,384]{1,0:T(8,128)(2,1)}, bf16[4096,384]{1,0:T(8,128)(2,1)}, u32[]{:S(2)}, u32[]{:S(2)}) collective-permute-start(bf16[4096,384]{1,0:T(8,128)(2,1)} %pad.30.wg_own), channel_id=1, source_target_pairs={{0,1},{1,0},{2,3},{3,2},{4,5},{5,4},{6,7},{7,6},{8,9},{9,8},{10,11... | collective-permute-start | bytes 9437192 | tf_op jit(solution)/shard_map/ppermute | solution.py:551
  127.2 220.1 %collective-permute-start.13 = (bf16[384,4096]{1,0:T(8,128)(2,1)}, bf16[384,4096]{1,0:T(8,128)(2,1)}, u32[]{:S(2)}, u32[]{:S(2)}) collective-permute-start(bf16[384,4096]{1,0:T(8,128)(2,1)} %pad.34.w_own), channel_id=1, source_target_pairs={{0,1},{1,0},{2,3},{3,2},{4,5},{5,4},{6,7},{7,6},{8,9},{9,8},{10,11... | collective-permute-start | bytes 9437192 | tf_op jit(solution)/shard_map/ppermute | solution.py:551
  236.0 2.9 copy-start.5
  236.1 2.9 copy-start.13
  241.2 106.0 %collective-permute-start.14 = (bf16[2,384,128]{2,1,0:T(8,128)(2,1)}, bf16[2,384,128]{2,1,0:T(8,128)(2,1)}, u32[]{:S(2)}, u32[]{:S(2)}) collective-permute-start(bf16[2,384,128]{2,1,0:T(8,128)(2,1)} %pad.35.a_own), channel_id=1, source_target_pairs={{0,1},{1,0},{2,3},{3,2},{4,5},{5,4},{6,7},{7,6},{8,9},{9,8},{10,11... | collective-permute-start | bytes 589832 | tf_op jit(solution)/shard_map/ppermute | solution.py:551
Sparse Core Ops, SparseCore 0:
  9.5 45.2 all-gather.6
  56.9 45.7 all-gather.8
  451.9 109.3 all-gather.10

commit v2 on v0

v2 whole, which is shorter than its diff:
```python
import functools
import math

import jax
import jax.numpy as jnp
import numpy as np
from jax import lax
from jax.experimental import pallas as pl
from jax.experimental.pallas import tpu as pltpu
from jax.sharding import PartitionSpec as P

ALPHA = 16.0
ROPE_BASE = 10000.0
EPSILON = 1e-5
BF = jnp.bfloat16
F32 = jnp.float32
LANE = 128
TILE = 16
VMEM_MOST = 67043328
MESH = pl.DeviceIdType.MESH
HBM = pl.BlockSpec(memory_space=pltpu.HBM)
VMEM = pl.BlockSpec(memory_space=pltpu.VMEM)
SMEM = pl.BlockSpec(memory_space=pltpu.SMEM)
DMA = pltpu.SemaphoreType.DMA

OWN, NEXT, FAR, LAST = RING = range(4)
UP, DOWN = BOTH = range(2)
STEP = (NEXT, -NEXT)
FROM = (LAST, NEXT)
TOWARD = (NEXT, LAST)
FAST, SLOW = BOTH


def fit(size, most):
    return max(c for c in range(LANE, most + 1, LANE) if size % c == 0)


def first(size):
    return pl.ds(0, size)


def dot(a, b):
    return jnp.dot(a, b, preferred_element_type=F32)


def dot_rows(a, b):
    return lax.dot_general(a, b, (((1,), (1,)), ((), ())), preferred_element_type=F32)


def dot_columns(a, b):
    return lax.dot_general(a, b, (((0,), (0,)), ((), ())), preferred_element_type=F32)


def normed(act, gain):
    return (act * lax.rsqrt(jnp.mean(act * act, axis=-1, keepdims=True) + EPSILON) * gain).astype(BF)


def ends(copies):
    for copy in copies:
        copy.start()
    return copies


def wait(copies):
    for copy in copies:
        copy.wait()


def loop(count, body):
    lax.fori_loop(0, count, lambda i, carry: (body(i), carry)[1], 0)


class Place:
    def __init__(self, side):
        index = lax.axis_index('tensor')
        self.side = side
        self.core = lax.rem(index, 2)
        chip = index // 2
        self.y, self.x = chip // side, lax.rem(chip, side)
        self.partner = index + 1 - 2 * self.core

    def turn(self, at, steps):
        return lax.rem(at + steps + self.side, self.side)

    def device(self, dy, dx):
        return (self.turn(self.y, dy) * self.side + self.turn(self.x, dx)) * 2 + self.core

    def neighbour(self, part, ring, step):
        return self.device(0, step) if part == ring else self.device(step, 0)

    def sequence(self, part, ds, df):
        return self.device(jnp.where(part == 0, ds, df), jnp.where(part == 0, df, ds))

    def barrier(self, *more):
        sem = pltpu.get_barrier_semaphore()
        to = [self.neighbour(0, ring, step) for ring in BOTH for step in STEP] + list(more)
        for device in to:
            pl.semaphore_signal(sem, inc=1, device_id={'tensor': device}, device_id_type=MESH)
        pl.semaphore_wait(sem, len(to))


def remote(src, dst, send_sem, recv_sem, to):
    return pltpu.make_async_remote_copy(src_ref=src, dst_ref=dst, send_sem=send_sem, recv_sem=recv_sem, device_id={'tensor': to}, device_id_type=MESH)


GATHER_SEMS = [DMA((2, 2, 2, 2, 4))] * 2


def gather(place, block, send_sem, recv_sem, absolute=False, seen=None, on_near=None, on_sides=None, on_far=None):
    def message(part, ring, passed, d, j=OWN):
        spot = (lambda s: (s, j)) if ring == SLOW else (lambda s: (OWN, s))
        src, dst = (FROM[d], FAR) if passed else (OWN, FROM[d])
        a, b = block(part, *spot(src)), block(part, *spot(src if absolute else dst))
        if passed:
            a, b = a.at[d], b.at[d]
        sems = (part, ring, passed, d, j)
        return remote(a, b, send_sem.at[sems], recv_sem.at[sems], place.neighbour(part, ring, STEP[d]))

    def start(*which):
        for d in BOTH:
            for part in BOTH:
                message(part, *which[:2], d, *which[2:]).start()

    def arrived(part, ring, passed, d, j=OWN):
        message(part, ring, passed, d, j).wait_recv()
        if seen:
            at = FAR if passed else FROM[d]
            seen(part, *((at, j) if ring == SLOW else (OWN, at)), d if passed else None)

    start(FAST, 0)
    start(SLOW, 0, OWN)
    for d in BOTH:
        for part in BOTH:
            arrived(part, FAST, 0, d)
            message(part, FAST, 1, d).start()
            for e in BOTH:
                message(part, SLOW, 0, e, FROM[d]).start()
    for part in BOTH:
        for d in BOTH:
            arrived(part, FAST, 1, d)
        for e in BOTH:
            message(part, SLOW, 0, e, FAR).start()

    def pass_on(j):
        for part in BOTH:
            for d in BOTH:
                arrived(part, SLOW, 0, d, j)
                message(part, SLOW, 1, d, j).start()

    order = (OWN,) + FROM + (FAR,)
    pass_on(OWN)
    if on_near:
        on_near()
    for j in order[1:]:
        pass_on(j)
    if on_sides:
        on_sides()
    for j in order:
        for part in BOTH:
            for d in BOTH:
                arrived(part, SLOW, 1, d, j)
    if on_far:
        on_far()
    for part in BOTH:
        for d in BOTH:
            for passed in BOTH:
                message(part, FAST, passed, d).wait_send()
                for j in RING:
                    message(part, SLOW, passed, d, j).wait_send()


def rows_of_adapter(place, ids_ref, part, ds, shape):
    block = lax.broadcasted_iota(jnp.int32, shape, 0) // (shape[0] // len(RING))
    chosen = jnp.zeros(shape, jnp.int32)
    for df in RING:
        chosen = jnp.where(block == df, ids_ref[place.sequence(part, ds, df)], chosen)
    return chosen


def spread(low, chosen, adapters):
    return jnp.concatenate([jnp.where(chosen == a, low, 0.0) for a in range(adapters)], axis=1).astype(BF)


def comm_params(collective_id):
    return pltpu.CompilerParams(collective_id=collective_id, has_side_effects=True, vmem_limit_bytes=VMEM_MOST)


def attend_kernel(side, adapters, scale, n_keep, ids_ref, x_ref, gain_ref, cos_ref, sin_ref, *rest):
    heads, rest = rest[:5], rest[5:]
    given, rest = rest[:n_keep], rest[n_keep:]
    att_ref, rest = rest[0], rest[1:]
    kept, rest = rest[:n_keep], rest[n_keep:]
    w, a_rows, bx, xbuf, h, z, lows, att, pair_send, pair_recv, load_sem, x_sem, send_sem, recv_sem = rest
    place = Place(side)
    head, seq_len, depth = cos_ref.shape[1], x_ref.shape[1], x_ref.shape[2]
    cols = heads[4].shape[-1]
    chips = side * side
    a_own = a_rows.at[pl.ds(pl.multiple_of(place.core * 2 * TILE, TILE), 2 * TILE)]
    spots = [[w.at[:, pl.ds(at + i * head, head)] for i in range(3)] + [a_own, bx.at[:, :, :, pl.ds(at, cols)]] for at in (0, cols)]
    loads = [pltpu.make_async_copy(src, dst, load_sem) for src, dst in zip(heads, spots[0])]
    ends(loads)

    def x_loads(step):
        slot = lax.rem(step, 2)
        return [pltpu.make_async_copy(x_ref.at[4 * step + 2 * i + place.core], xbuf.at[slot, i], x_sem.at[slot]) for i in BOTH]

    ends(x_loads(0))
    place.barrier(place.partner)
    moves = list(zip(heads, spots[1][:3] + [a_own] + spots[1][4:])) + list(zip(given, kept))
    pair = [remote(src, dst, pair_send.at[i], pair_recv.at[i], place.partner) for i, (src, dst) in enumerate(moves)]
    ends(pair)
    wait(loads)
    for copy in pair[:len(heads)]:
        copy.wait_recv()
    mine = [(place.y, place.x), (place.x, place.y)]
    steps = chips // 2

    def block(part, ds, df):
        return lows.at[part, place.turn(mine[part][0], ds), place.turn(mine[part][1], df)]

    def project(step):
        slot = lax.rem(step, 2)

        @pl.when(step + 1 < steps)
        def _():
            ends(x_loads(step + 1))

        wait(x_loads(step))
        for i in BOTH:
            h[i * seq_len:(i + 1) * seq_len, :] = normed(xbuf[slot, i].astype(F32), gain_ref[...])
        rows = pl.ds(pl.multiple_of(step * 2 * seq_len, LANE), 2 * seq_len)
        chunk = fit(2 * cols, 256)
        for n in range(2 * cols // chunk):
            z[rows, n * chunk:(n + 1) * chunk] = dot(h[...], w[:, n * chunk:(n + 1) * chunk])
        low = dot_rows(a_rows[...], h[...])
        half, at = step // (steps // 2), lax.rem(step, steps // 2) * 2 * seq_len
        for part in BOTH:
            pieces = []
            for i in BOTH:
                options = [low[TILE * (2 * part + a):TILE * (2 * part + a + 1), i * seq_len:(i + 1) * seq_len] for a in range(adapters)]
                piece = options[0]
                for a in range(1, adapters):
                    piece = jnp.where(ids_ref[4 * step + 2 * i + place.core] == a, options[a], piece)
                pieces.append(piece)
            lows[part, mine[part][0], mine[part][1], half, :, pl.ds(pl.multiple_of(at, LANE), 2 * seq_len)] = jnp.concatenate(pieces, axis=1).astype(BF)

    loop(steps, project)
    gather(place, block, send_sem, recv_sem, absolute=True)
    causal = lax.broadcasted_iota(jnp.int32, (seq_len, seq_len), 0) >= lax.broadcasted_iota(jnp.int32, (seq_len, seq_len), 1)

    def attention(i):
        dy, dx = i // side, lax.rem(i, side)
        chip = place.turn(place.y, dy) * side + place.turn(place.x, dx)
        adapter = ids_ref[2 * chip + place.core]
        half, at = chip // steps, pl.ds(pl.multiple_of(lax.rem(chip, steps) * seq_len, LANE), seq_len)
        zs = z[pl.ds(pl.multiple_of(chip * seq_len, LANE), seq_len), :]
        for part in BOTH:
            zs += scale * dot_columns(lows[part, :, :, half, :, at].reshape(-1, seq_len), bx[adapter, part])
        for i_head in BOTH:
            q, k, v = (zs[:, i_head * cols + i * head:i_head * cols + (i + 1) * head] for i in range(3))
            q, k = ((r * cos_ref[...] + pltpu.roll(r, head // 2, axis=1) * sin_ref[...]).astype(BF) for r in (q, k))
            scores = jnp.where(causal, dot_rows(q, k) * head ** -0.5, -1e30)
            e = jnp.exp(scores - jnp.max(scores, axis=-1, keepdims=True))
            prob = (e / jnp.sum(e, axis=-1, keepdims=True)).astype(BF)
            mixed = dot(prob, v.astype(BF)).astype(BF)
            for part, spot in enumerate((i, dx * side + dy)):
                att[part, spot, :, i_head * head:(i_head + 1) * head] = mixed[part * seq_len // 2:(part + 1) * seq_len // 2]

    loop(chips, attention)
    wait(ends([pltpu.make_async_copy(att, att_ref, load_sem)]))
    for copy in pair[len(heads):]:
        copy.wait_recv()
    for copy in pair:
        copy.wait_send()


def attend(ids, x_in, gain, heads, given, side, adapters, scale, collective_id):
    _, seq_len, depth = x_in.shape
    head, cols = heads[0].shape[1], heads[4].shape[-1]
    chips = side * side
    half_dim = head // 2
    inv_freq = ROPE_BASE ** (-2.0 * np.arange(half_dim) / head)
    angle = np.arange(seq_len)[:, None] * inv_freq[None, :]
    cos, sin = np.cos(angle), np.sin(angle)
    tables = [jnp.asarray(np.concatenate(pair, axis=1), F32) for pair in ((cos, cos), (-sin, sin))]
    att = jax.ShapeDtypeStruct((2, chips, seq_len // 2, 2 * head), BF)
    n_moves = len(heads) + len(given)
    return pl.pallas_call(
        functools.partial(attend_kernel, side, adapters, scale, len(given)),
        out_shape=[att] + [jax.ShapeDtypeStruct(g.shape, g.dtype) for g in given],
        in_specs=[SMEM, HBM, VMEM, VMEM, VMEM] + [HBM] * n_moves,
        out_specs=[HBM] * (1 + len(given)),
        scratch_shapes=[
            pltpu.VMEM((depth, 2 * cols), BF),
            pltpu.VMEM((2 * 2 * TILE, depth), BF),
            pltpu.VMEM(heads[4].shape[:3] + (2 * cols,), BF),
            pltpu.VMEM((2, 2, seq_len, depth), BF),
            pltpu.VMEM((2 * seq_len, depth), BF),
            pltpu.VMEM((chips * seq_len, 2 * cols), F32),
            pltpu.VMEM((2, side, side, 2, TILE, chips * seq_len // 2), BF),
            pltpu.VMEM(att.shape, BF),
            DMA((n_moves,)), DMA((n_moves,)), DMA, DMA((2,)),
        ] + GATHER_SEMS,
        compiler_params=comm_params(collective_id),
        name='attend',
    )(ids, x_in, gain.reshape(1, depth), *tables, *heads, *given)


def row_proj_kernel(side, adapters, ids_ref, act_ref, w_own, w_par, a_own, a_par, out_ref,
                    act, w, stage, near, landed, fast_near, fast_landed, slow_send, slow_recv, fast_send, fast_recv, load_sem):
    place = Place(side)
    share, width = w_own.shape
    half = w.shape[0] // 2
    rank = a_own.shape[2]
    rows = stage.shape[3]
    quarter = rows // 2
    if share < half:
        for at in (0, half):
            w[at + share // TILE * TILE:at + half, :] = jnp.zeros((half - share // TILE * TILE, w.shape[1]), BF)
    loads = [pltpu.make_async_copy(act_ref, act, load_sem)]
    for at, w_part, a_part in ((0, w_own, a_own), (half, w_par, a_par)):
        loads.append(pltpu.make_async_copy(w_part, w.at[pl.ds(at, share), first(width)], load_sem))
        for a in range(adapters):
            loads.append(pltpu.make_async_copy(a_part.at[a], w.at[pl.ds(at, share), pl.ds(width + a * rank, rank)], load_sem))
    ends(loads)
    place.barrier()
    wait(loads)
    chunk = fit(width, 512)

    def unit(part, ds):
        def columns(n):
            at = pl.ds(pl.multiple_of(n * chunk, chunk), chunk)
            stage[part, ds, :, :, at] = dot(act[part, ds], w[:, at]).reshape(len(RING), rows, chunk).astype(BF)

        loop(width // chunk, columns)
        low = dot(act[part, ds], w[:, width:])
        chosen = rows_of_adapter(place, ids_ref, part, ds, (len(RING) * rows, rank))
        kept = low[:, :rank]
        for a in range(1, adapters):
            kept = jnp.where(chosen == a, low[:, a * rank:(a + 1) * rank], kept)
        stage[part, ds, :, :, width:] = kept.reshape(len(RING), rows, rank).astype(BF)

    blocks = ((FAR, LAST), (OWN, NEXT))
    halves = (first(quarter), pl.ds(quarter, quarter))
    PASS, FREE, SUM = range(3)

    def slow(part, kind, d, i):
        df = blocks[1 - d][i] if kind == FREE else blocks[d][i]
        sems = (part, kind, d, i)
        src = stage.at[part, FAR if kind == PASS else TOWARD[d], df]
        dst = near.at[part, d, i] if kind == PASS else landed.at[part, d, df]
        return remote(src, dst, slow_send.at[sems], slow_recv.at[sems], place.neighbour(part, SLOW, STEP[d]))

    def fast(part, kind, d):
        at = halves[1 - d] if kind == FREE else halves[d]
        sems = (part, kind, d)
        src = stage.at[part, OWN, FAR if kind == PASS else TOWARD[d], at]
        dst = fast_near.at[part, d] if kind == PASS else fast_landed.at[part, d, at]
        return remote(src, dst, fast_send.at[sems], fast_recv.at[sems], place.neighbour(part, FAST, STEP[d]))

    def add(into, *others):
        def some(i):
            at = pl.ds(pl.multiple_of(i * TILE, TILE), TILE)
            total = into[at, :].astype(F32)
            for other in others:
                total += other[at, :].astype(F32)
            into[at, :] = total.astype(BF)

        loop(into.shape[0] // TILE, some)

    for part in BOTH:
        unit(part, FAR)
        for i in BOTH:
            for d in BOTH:
                slow(part, PASS, d, i).start()
    loop(len(RING), lambda i: unit(lax.rem(i, 2), NEXT + 2 * (i // 2)))
    for i in BOTH:
        for d in BOTH:
            for part in BOTH:
                slow(part, FREE, d, i).start()
    loop(2, lambda part: unit(part, OWN))
    for i in BOTH:
        for d in BOTH:
            for part in BOTH:
                slow(part, PASS, d, i).wait_recv()
                add(stage.at[part, TOWARD[d], blocks[d][i]], near.at[part, d, i])
                slow(part, SUM, d, i).start()
    for i in BOTH:
        for d in BOTH:
            df = blocks[d][i]
            for part in BOTH:
                slow(part, SUM, d, i).wait_recv()
                slow(part, FREE, 1 - d, i).wait_recv()
                add(stage.at[part, OWN, df], landed.at[part, UP, df], landed.at[part, DOWN, df])
                for e in BOTH:
                    if df == FAR:
                        fast(part, PASS, e).start()
                    elif df == TOWARD[e]:
                        fast(part, FREE, e).start()
    for d in BOTH:
        for part in BOTH:
            fast(part, PASS, d).wait_recv()
            add(stage.at[part, OWN, TOWARD[d], halves[d]], fast_near.at[part, d])
            fast(part, SUM, d).start()
    for part in BOTH:
        for d in BOTH:
            fast(part, FREE, d).wait_recv()
            fast(part, SUM, d).wait_recv()
        add(stage.at[part, OWN, OWN], fast_landed.at[part, UP], fast_landed.at[part, DOWN])
    wait(ends([pltpu.make_async_copy(stage.at[part, OWN, OWN], out_ref.at[pl.ds(part * rows, rows)], load_sem) for part in BOTH]))
    for part in BOTH:
        for kind in range(3):
            for d in BOTH:
                fast(part, kind, d).wait_send()
                for i in BOTH:
                    slow(part, kind, d, i).wait_send()


def row_proj(ids, act, w_own, w_par, a_own, a_par, side, collective_id):
    adapters, _, rank = a_own.shape
    width = w_own.shape[1]
    rows = act.shape[2] // side
    cols = width + rank
    blocks = (rows, cols)
    return pl.pallas_call(
        functools.partial(row_proj_kernel, side, adapters),
        out_shape=jax.ShapeDtypeStruct((2 * rows, cols), BF),
        in_specs=[SMEM] + [HBM] * 5,
        out_specs=HBM,
        scratch_shapes=[
            pltpu.VMEM(act.shape, BF),
            pltpu.VMEM((act.shape[3], width + adapters * rank), BF),
            pltpu.VMEM((2, side, side) + blocks, BF),
            pltpu.VMEM((2, 2, 2) + blocks, BF),
            pltpu.VMEM((2, 2, side) + blocks, BF),
            pltpu.VMEM((2, 2, rows // 2, cols), BF),
            pltpu.VMEM((2, 2) + blocks, BF),
            DMA((2, 3, 2, 2)), DMA((2, 3, 2, 2)), DMA((2, 3, 2)), DMA((2, 3, 2)), DMA,
        ],
        compiler_params=comm_params(collective_id),
        name='row_proj',
    )(ids, act, w_own, w_par, a_own, a_par)


def finish(sums_ref, resid, b_ref, chosen, scale, adapters):
    devices, _, rank, part = b_ref.shape
    width = devices * part
    low = spread(sums_ref[:, width:].astype(F32), chosen, adapters)
    delta = [dot(low, b_ref[j].reshape(adapters * rank, part)) for j in range(devices)]
    return resid.astype(F32) + (sums_ref[:, :width].astype(F32) + scale * jnp.concatenate(delta, axis=1))


def gate_up_kernel(side, adapters, scale, ids_ref, sums_ref, x_ref, gain_ref, a_ref, b_all, wg_own, wg_par, wu_own, wu_par, bg_own, bg_par, bu_own, bu_par,
                   hid_ref, mid_ref, gbuf, w, b, b_ref, hid, load_sem, b_sem, store_sem, send_sem, recv_sem):
    place = Place(side)
    b_load = ends([pltpu.make_async_copy(b_all.at[0], b_ref, b_sem)])
    share, width = wg_own.shape
    half = w.shape[1] // 2
    rank = bg_own.shape[2]
    seq_len = sums_ref.shape[0]
    edge = share // TILE * TILE
    for at in (0, half):
        for kind in BOTH:
            w[kind, at + edge:at + half, :] = jnp.zeros((half - edge, width), BF)
            b[kind, at + edge:at + half, :] = jnp.zeros((half - edge, adapters * rank), BF)
    loads = []
    for kind, pieces in enumerate(((wg_own, wg_par, bg_own, bg_par), (wu_own, wu_par, bu_own, bu_par))):
        for i, at in enumerate((0, half)):
            loads.append(pltpu.make_async_copy(pieces[i], w.at[kind, pl.ds(at, share)], load_sem))
            for a in range(adapters):
                loads.append(pltpu.make_async_copy(pieces[2 + i].at[a], b.at[kind, pl.ds(at, share), pl.ds(a * rank, rank)], load_sem))
    ends(loads)
    rows = seq_len // 4
    chosen = jnp.full((seq_len, rank), ids_ref[place.device(0, 0)], jnp.int32)
    wait(b_load)
    mid = finish(sums_ref, x_ref[...], b_ref, chosen, scale, adapters).astype(BF)
    mid_ref[...] = mid
    h2 = normed(mid.astype(F32), gain_ref[...])
    low = dot_rows(h2, a_ref[...]).astype(BF)
    n_low = low.shape[1]
    per = rank // (2 * side * side)
    to = lax.broadcasted_iota(jnp.int32, (n_low, 2 * rank), 1)
    frm = lax.broadcasted_iota(jnp.int32, (n_low, 2 * rank), 0)
    kind, rank_at = to // rank, lax.rem(to, rank)
    pick = (rank_at // per) * (2 * adapters * per) + ids_ref[place.device(0, 0)] * (2 * per) + kind * per + lax.rem(rank_at, per)
    low = dot(low, jnp.where(frm == pick, 1.0, 0.0).astype(BF)).astype(BF)
    for part in BOTH:
        for piece in BOTH:
            at = (2 * part + piece) * rows
            gbuf[part, OWN, OWN, piece, :, :width] = h2[at:at + rows]
            gbuf[part, OWN, OWN, piece, :, width:] = low[at:at + rows]
    place.barrier()
    chunk = fit(2 * half, 256)

    def unit(part, ds):
        unit_rows = len(RING) * 2 * rows
        low = gbuf[part, ds, :, :, :, width:].reshape(unit_rows, 2 * rank).astype(F32)
        chosen = rows_of_adapter(place, ids_ref, part, ds, (unit_rows, rank))
        lows = [spread(low[:, kind * rank:(kind + 1) * rank], chosen, adapters) for kind in BOTH]

        def columns(n):
            at = pl.ds(pl.multiple_of(n * chunk, chunk), chunk)
            act = gbuf[part, ds, :, :, :, :width].reshape(unit_rows, width)
            gate, up = (dot_rows(act, w[kind, at]) + scale * dot_rows(lows[kind], b[kind, at]) for kind in BOTH)
            hid[part, ds, :, at] = (gate * jax.nn.sigmoid(gate) * up).astype(BF)

        loop(2 * half // chunk, columns)
        pltpu.make_async_copy(hid.at[part, ds], hid_ref.at[part, ds], store_sem).start()

    def on_near():
        wait(loads)
        loop(2, lambda part: unit(part, OWN))

    gather(place, lambda part, ds, df: gbuf.at[part, ds, df], send_sem, recv_sem, on_near=on_near,
           on_sides=lambda: loop(len(RING), lambda i: unit(lax.rem(i, 2), NEXT + 2 * (i // 2))),
           on_far=lambda: loop(2, lambda part: unit(part, FAR)))
    pltpu.make_async_copy(hid, hid_ref, store_sem).wait()


def gate_up(ids, sums, x_own, gain, b_all, a_all, w, side, scale, collective_id):
    seq_len, depth = x_own.shape
    share = w[0].shape[0]
    adapters, _, rank = w[4].shape
    half = (share + LANE - 1) // LANE * LANE
    hidden = jax.ShapeDtypeStruct((2, side, side * seq_len // 2, 2 * half), BF)
    return pl.pallas_call(
        functools.partial(gate_up_kernel, side, adapters, scale),
        out_shape=[hidden, jax.ShapeDtypeStruct(x_own.shape, BF)],
        in_specs=[SMEM] + [VMEM] * 4 + [HBM] * (1 + len(w)),
        out_specs=[HBM, VMEM],
        scratch_shapes=[
            pltpu.VMEM((2, side, side, 2, seq_len // 4, depth + 2 * rank), BF),
            pltpu.VMEM((2, 2 * half, depth), BF),
            pltpu.VMEM((2, 2 * half, adapters * rank), BF),
            pltpu.VMEM(b_all.shape[1:], BF),
            pltpu.VMEM(hidden.shape, BF),
            DMA, DMA, DMA,
        ] + GATHER_SEMS,
        compiler_params=comm_params(collective_id),
        name='gate_up',
    )(ids, sums, x_own, gain.reshape(1, depth), a_all, b_all, *w)


def deliver_kernel(side, adapters, scale, ids_ref, sums_ref, x_ref, b_all, out_ref, gbuf, b_ref, b_sem, pair_send, pair_recv, store_sem, send_sem, recv_sem):
    place = Place(side)
    b_load = ends([pltpu.make_async_copy(b_all.at[1], b_ref, b_sem)])
    seq_len = sums_ref.shape[0]
    rows = seq_len // 4
    rank = b_ref.shape[2]
    chosen = jnp.full((seq_len, rank), ids_ref[place.device(0, 0)], jnp.int32)
    wait(b_load)
    y = finish(sums_ref, x_ref[...], b_ref, chosen, scale, adapters).astype(BF)
    for part in BOTH:
        for piece in BOTH:
            at = (2 * part + piece) * rows
            gbuf[part, OWN, OWN, piece] = y[at:at + rows]
    place.barrier(place.partner)

    def block(part, ds, df):
        return gbuf.at[part, ds, df]

    def seen(part, ds, df, half):
        src, dst = block(part, ds, df), out_ref.at[place.sequence(part, ds, df), part]
        if half is not None:
            src, dst = src.at[half], dst.at[half]
        remote(src, dst, pair_send, pair_recv, place.partner).start()
        pltpu.make_async_copy(src, dst, store_sem).start()

    for part in BOTH:
        seen(part, OWN, OWN, None)
    gather(place, block, send_sem, recv_sem, seen=seen)
    every = out_ref.at[first(side * side)]
    for sem in (store_sem, pair_send, pair_recv):
        pltpu.make_async_copy(every, every, sem).wait()


def deliver(ids, sums, x_mid, b_all, side, scale, collective_id):
    seq_len, depth = x_mid.shape
    rows = seq_len // 4
    return pl.pallas_call(
        functools.partial(deliver_kernel, side, b_all.shape[2], scale),
        out_shape=jax.ShapeDtypeStruct((2 * side * side, 2, 2, rows, depth), BF),
        in_specs=[SMEM] + [VMEM] * 2 + [HBM],
        out_specs=HBM,
        scratch_shapes=[pltpu.VMEM((2, side, side, 2, rows, depth), BF), pltpu.VMEM(b_all.shape[1:], BF), DMA, DMA, DMA, DMA] + GATHER_SEMS,
        compiler_params=comm_params(collective_id),
        name='deliver',
    )(ids, sums, x_mid, b_all)


def solution(mesh):
    tp_size = mesh.shape['tensor']
    side = math.isqrt(tp_size // 2)
    rows_only = P('tensor', None)
    head_split = P(None, 'tensor', None)
    last_split = P(None, None, 'tensor')
    b_head_split = P(None, None, 'tensor', None)
    in_specs = (P('data', None, None), P('data'), P(None), P(None),
                head_split, head_split, head_split, P('tensor', None, None),
                P(None, 'tensor'), P(None, 'tensor'), rows_only,
                last_split, b_head_split, last_split, b_head_split, last_split, b_head_split,
                P(None, 'tensor', None, None), last_split,
                last_split, last_split, last_split, last_split,
                head_split, last_split)

    def local_layer(x_in, adapter_ids, gain_attn, gain_mlp, w_q, w_k, w_v, w_o, w_gate, w_up, w_down, a_q, b_q, a_k, b_k, a_v, b_v, a_o, b_o, a_gate, b_gate, a_up, b_up, a_down, b_down):
        depth = x_in.shape[2]
        adapters, rank = b_q.shape[:2]
        scale = ALPHA / rank
        index = lax.axis_index('tensor')

        def across(a):
            return a.swapaxes(-1, -2)

        per = a_q.shape[2]
        own_a = jnp.stack([across(a) for a in (a_q, a_k, a_v)] + [jnp.zeros((adapters, per, depth), BF)], axis=1).reshape(-1, depth)
        spread_b = jnp.stack([jnp.pad(b[:, :, 0].reshape(adapters, side, side, 2, 1, per, -1), ((0, 0),) * 4 + ((i, 3 - i),) + ((0, 0),) * 2)
                              for i, b in enumerate((b_q, b_k, b_v))], axis=-2)
        own_b = jnp.stack([spread_b[:, :, :, 0], spread_b[:, :, :, 1].swapaxes(1, 2)], axis=1).reshape(adapters, 2, 2 * rank, -1)
        heads = [w_q[:, 0], w_k[:, 0], w_v[:, 0], own_a, own_b]
        given = [w_o[0], a_o[:, 0], across(w_gate), across(w_up), w_down, across(b_gate), across(b_up), a_down]
        att, *kept = attend(adapter_ids, x_in, gain_attn, heads, given, side, adapters, scale, 0)

        all_b = lax.all_gather(jnp.stack([b_o, b_down]), 'tensor', axis=1)
        all_a = lax.all_gather(jnp.stack([across(a_gate), across(a_up)], axis=1).reshape(-1, depth), 'tensor', axis=0, tiled=True)
        x_own = lax.dynamic_index_in_dim(x_in, index, axis=0, keepdims=False)
        att = att.reshape(2, side, -1, att.shape[-1])
        sums = row_proj(adapter_ids, att, given[0], kept[0], given[1], kept[1], side, 1)
        w = [piece for i in (2, 3, 5, 6) for piece in (given[i], kept[i])]
        hidden, x_mid = gate_up(adapter_ids, sums, x_own, gain_mlp, all_b, all_a, w, side, scale, 2)
        sums = row_proj(adapter_ids, hidden, given[4], kept[4], given[7], kept[7], side, 3)
        y = deliver(adapter_ids, sums, x_mid, all_b, side, scale, 4)
        return y.reshape(x_in.shape)

    return jax.shard_map(local_layer, mesh=mesh, in_specs=in_specs, out_specs=P('data', None, None), check_vma=False)
```

time: 1120 us -> 526 us (0.47)
  waiting for transfers between devices: 713 us -> 0.11 us
  Pallas kernels: 0 us -> 477 us
  matrix products: 253 us -> 0 us
  local copies, waits for them, and re-layouts: 84.1 us -> 29.4 us
  other arithmetic: 48.6 us -> 5.26 us
    pallas_call x0 -> x5, Pallas kernels: none -> 477 us  [the longest x2 199 us: row_proj(): pl.pallas_call(functools.partial(row_proj_kernel, side, adapters), out_sh...]
    reduce_scatter x2 -> x0, waiting for transfers between devices: 318 us -> none  [row_proj(): lax.psum_scatter(base_part, 'tensor', scatter_dimension=2, tiled=True)]
    all_gather x7 -> x2, waiting for transfers between devices: 255 us -> 0.01 us  [the longest x1 0.01 us: local_layer(): all_b = lax.all_gather(jnp.stack([b_o, b_down]), 'tensor', axis=1)]
    dot_general x22 -> x0, matrix products: 253 us -> none  [the longest x5 100 us: column_proj(): jnp.einsum(base_form, act_in, weight, preferred_element_type=jnp.float32)]
    psum x2 -> x0, waiting for transfers between devices: 139 us -> none  [row_proj(): low_rank = lax.psum(low_part, 'tensor')]
    all_gather x1 -> x0, local copies, waits for them, and re-layouts: 44.2 us -> none  [row_proj(): return (out_shard, lax.all_gather(out_shard, 'tensor', axis=2, tiled=True))]
    gather x14 -> x0, local copies, waits for them, and re-layouts: 29.3 us -> none  [per_sequence(): return jnp.take(table_stack, adapter_ids, axis=0)]
    reduce_sum x3 -> x0, other arithmetic: 23.6 us -> none  [the longest x2 23.2 us: rms_gain(): jnp.mean(act_f32 * act_f32, axis=-1, keepdims=True) + EPSILON]
  transfers between devices with their start and end apart: 11 -> 2, of which waited for: 8 -> 0; matrix products, arithmetic and copies ran while one was open for 18% -> 2% of each run, Pallas kernels for 0% -> 32%
where the time goes in v2:
time: 526 us
  Pallas kernels  477 us (91%)
  local copies, waits for them, and re-layouts  29.4 us (6%)
  between operations  13.6 us (3%)
  other arithmetic  5.26 us (1%)
    pallas_call x2, Pallas kernels, row_proj(): pl.pallas_call(functools.partial(row_proj_kernel, side, adapters), out_sh...  199 us
    pallas_call x1, Pallas kernels, gate_up(): pl.pallas_call(functools.partial(gate_up_kernel, side, adapters, scale),...  113 us
    pallas_call x1, Pallas kernels, deliver(): pl.pallas_call(functools.partial(deliver_kernel, side, b_all.shape[2], sc...  97 us
    pallas_call x1, Pallas kernels, attend(): pl.pallas_call(functools.partial(attend_kernel, side, adapters, scale, le...  67.9 us
    unnamed x7, local copies, waits for them, and re-layouts  22.9 us
  transfers between devices with their start and end apart: 2, of which 0 were waited for; matrix products, arithmetic and copies ran while one was open for 2% of the time, Pallas kernels for 32%

profile of v2, /device:TPU:97, one launch (start us, length us, event | category | flops | bytes accessed | tf_op | source)
XLA Modules:
  0.0 525.8 jit_solution(14094593510632419667)
XLA Ops:
  6.5 0.0 copy-start
  6.5 0.0 copy-start.1
  6.6 0.0 all-gather.6.cloned.1.call-start
  6.6 1.6 pad_maximum_fusion.3
  8.1 0.1 all-gather.6.cloned.1.call-update
  8.2 0.1 all-gather.4.cloned.1.call-start
  8.3 1.0 pad_maximum_fusion.2
  9.3 0.7 reshape.27
  10.0 0.1 all-gather.4.cloned.1.call-update
  10.0 0.1 pad.27.clone
  10.1 1.1 maximum_maximum_fusion
  11.2 0.1 copy.34
  11.3 0.8 reshape.24.rest_3_
  12.1 0.0 copy-done
  12.1 0.1 pad_bitcast_fusion.2
  12.2 0.0 copy-done.1
  12.2 0.0 copy-done.2
  12.2 0.2 pad_bitcast_fusion
  12.4 0.7 pad_maximum_fusion
  13.1 0.4 fusion
  13.5 0.5 copy.38
  14.1 0.3 stack.58
  14.4 0.5 copy.39
  15.0 0.3 stack.59
  15.3 1.0 pad_maximum_fusion.1.rest_4_
  16.3 67.9 %attend.1 = (bf16[2,16,64,256]{3,2,1,0:T(8,128)(2,1)}, bf16[128,4096]{1,0:T(8,128)(2,1)}, bf16[2,128,128]{2,1,0:T(8,128)(2,1)}, bf16[344,4096]{1,0:T(8,128)(2,1)...) custom-call(s32[32]{0:T(128)} %ids_ref.9, ...), custom_call_target="tpu_custom_call" | custom-call | tf_op jit(solution)/shard_map/attend/pallas_call | solution.py:288
  84.2 98.9 %row_proj.2.sums_ref = bf16[128,4224]{1,0:T(8,128)(2,1)} custom-call(s32[32]{0:T(128)} %ids_ref.9, bf16[2,4,256,256]{3,2,1,0:T(8,128)(2,1)} %bitcast.71, bf16[128,4096]{1,0:T(8,128)(2,1)} %bitcast.65, bf16[128,4096]{1,0:T(8,128)(2,1)} %get-tuple-element.17.w_par, bf16[2,128,128]{2,1,0:T(8,128)(2,1)} %bitcast.77, bf16[2,128,128]{2,1,0:T(8,128)(2,1)} %get-tuple-element.18.a_par), custom_call_target="tpu_custom_call" | custom-call | tf_op jit(solution)/shard_map/row_proj/pallas_call | solution.py:425
  183.2 2.3 dynamic-slice_bitcast_fusion.x_ref
  185.5 113.3 %gate_up.1 = (bf16[2,4,256,768]{3,2,1,0:T(8,128)(2,1)}, bf16[128,4096]{1,0:T(8,128)(2,1)}) custom-call(s32[32]{0:T(128)} %ids_ref.9, bf16[128,4224]{1,0:T(8,128)(2,1)} %row_proj.2.sums_ref, bf16[128,4096]{1,0:T(8,128)(2,1)} %dynamic-slice_bitcast_fusion.x_ref, f32[1,4096]{1,0:T(1,128)} %bitcast.89, bf16[512,4096]{1,0:T(8,128)(2,1)} %all-gather.4.cloned.1.call-done.a_ref, ...), custom_call_target="tpu_custom_call" | custom-call | tf_op jit(solution)/shard_map/gate_up/pallas_call | solution.py:526
  298.8 100.2 %row_proj.3.sums_ref = bf16[128,4224]{1,0:T(8,128)(2,1)} custom-call(s32[32]{0:T(128)} %ids_ref.9, bf16[2,4,256,768]{3,2,1,0:T(8,128)(2,1)} %get-tuple-element.23.act_ref, bf16[344,4096]{1,0:T(8,128)(2,1)} %w_own.1, bf16[344,4096]{1,0:T(8,128)(2,1)} %get-tuple-element.24.w_par, bf16[2,344,128]{2,1,0:T(8,128)(2,1)} %a_own.1, ...), custom_call_target="tpu_custom_call" | custom-call | tf_op jit(solution)/shard_map/row_proj/pallas_call | solution.py:425
  399.0 97.0 %deliver.1 = bf16[32,2,2,32,4096]{4,3,2,1,0:T(8,128)(2,1)} custom-call(s32[32]{0:T(128)} %ids_ref.9, bf16[128,4224]{1,0:T(8,128)(2,1)} %row_proj.3.sums_ref, bf16[128,4096]{1,0:T(8,128)(2,1)} %get-tuple-element.26.x_ref, bf16[2,32,2,128,128]{4,3,2,1,0:T(8,128)(2,1)} %bitcast.59), custom_call_target="tpu_custom_call" | custom-call | tf_op jit(solution)/shard_map/deliver/pallas_call | solution.py:580
  496.0 22.9 %copy.44 = bf16[32,128,4096]{2,1,0:T(8,128)(2,1)} copy(bf16[32,128,4096]{2,1,0:T(8,128)(2,1)} %bitcast.57) | data formatting | bytes 67108864
  (4 shorter events, 0.1 us)
Async XLA Ops:
  6.5 5.5 %copy-start = (bf16[2,128,1,128]{3,1,2,0:T(8,128)(2,1)S(1)}, bf16[2,128,1,128]{3,1,2,0:T(8,128)(2,1)}, u32[]{:S(2)}) copy-start(bf16[2,128,1,128]{3,1,2,0:T(8,128)(2,1)} %param.39) | copy-start | bytes 196612
  6.5 5.6 %copy-start.1 = (bf16[2,128,1,128]{3,1,2,0:T(8,128)(2,1)S(1)}, bf16[2,128,1,128]{3,1,2,0:T(8,128)(2,1)}, u32[]{:S(2)}) copy-start(bf16[2,128,1,128]{3,1,2,0:T(8,128)(2,1)} %param.43) | copy-start | bytes 196612
  6.6 5.6 %copy-start.2 = (bf16[2,128,1,128]{3,1,2,0:T(8,128)(2,1)S(1)}, bf16[2,128,1,128]{3,1,2,0:T(8,128)(2,1)}, u32[]{:S(2)}) copy-start(bf16[2,128,1,128]{3,1,2,0:T(8,128)(2,1)} %param.41) | copy-start | bytes 196612
  6.6 178.9 %all-gather.6.cloned.1.call-start = ((), (), s32[]{:S(2)}) async-start(), calls=%async_computation.1 | async-start | bytes 4325376 | tf_op jit(solution)/shard_map/all_gather | solution.py:624
  8.2 177.3 %all-gather.4.cloned.1.call-start = ((), (), s32[]{:S(2)}) async-start(), calls=%async_computation | async-start | bytes 4325376 | tf_op jit(solution)/shard_map/all_gather | solution.py:625
Sparse Core Ops, SparseCore 0:
  9.5 45.1 all-gather.5
  56.7 41.4 all-gather.3

commit v3 on v2

--- a/solution.py
+++ b/solution.py
@@ -177,20 +177,89 @@
     return chosen
 
 
+def pick_columns(low, chosen):
+    rank = chosen.shape[1]
+    kept = low[:, :rank]
+    for a in range(1, low.shape[1] // rank):
+        kept = jnp.where(chosen == a, low[:, a * rank:(a + 1) * rank], kept)
+    return kept
+
+
 def spread(low, chosen, adapters):
     return jnp.concatenate([jnp.where(chosen == a, low, 0.0) for a in range(adapters)], axis=1).astype(BF)
 
 
+PASS, FREE, SUM = range(3)
+FAST_SEMS = [DMA((2, 3, 2))] * 2
+
+
+def add(into, *others):
+    def some(i):
+        at = pl.ds(pl.multiple_of(i * TILE, TILE), TILE)
+        total = into[at, :].astype(F32)
+        for other in others:
+            total += other[at, :].astype(F32)
+        into[at, :] = total.astype(BF)
+
+    loop(into.shape[0] // TILE, some)
+
+
+class FastScatter:
+    def __init__(self, place, stage, near, landed, send_sem, recv_sem):
+        self.place, self.stage, self.near, self.landed, self.sems = place, stage, near, landed, (send_sem, recv_sem)
+        quarter = near.shape[2]
+        self.halves = (first(quarter), pl.ds(quarter, quarter))
+
+    def message(self, part, kind, d):
+        at = self.halves[1 - d] if kind == FREE else self.halves[d]
+        src = self.stage(part, FAR if kind == PASS else TOWARD[d]).at[at]
+        dst = self.near.at[part, d] if kind == PASS else self.landed.at[part, d, at]
+        sems = [sem.at[part, kind, d] for sem in self.sems]
+        return remote(src, dst, *sems, self.place.neighbour(part, FAST, STEP[d]))
+
+    def ready(self, part, df):
+        for d in BOTH:
+            if df == FAR:
+                self.message(part, PASS, d).start()
+            elif df == TOWARD[d]:
+                self.message(part, FREE, d).start()
+
+    def finish(self):
+        for d in BOTH:
+            for part in BOTH:
+                self.message(part, PASS, d).wait_recv()
+                add(self.stage(part, TOWARD[d]).at[self.halves[d]], self.near.at[part, d])
+                self.message(part, SUM, d).start()
+        for part in BOTH:
+            for d in BOTH:
+                self.message(part, FREE, d).wait_recv()
+                self.message(part, SUM, d).wait_recv()
+            add(self.stage(part, OWN), self.landed.at[part, UP], self.landed.at[part, DOWN])
+
+    def store(self, out_ref, sem):
+        rows = self.landed.shape[2]
+        wait(ends([pltpu.make_async_copy(self.stage(part, OWN), out_ref.at[pl.ds(part * rows, rows)], sem) for part in BOTH]))
+        for part in BOTH:
+            for kind in range(3):
+                for d in BOTH:
+                    self.message(part, kind, d).wait_send()
+
+
+def fast_scratch(rows, cols):
+    return [pltpu.VMEM((2, 2, rows // 2, cols), BF), pltpu.VMEM((2, 2, rows, cols), BF)]
+
+
 def comm_params(collective_id):
     return pltpu.CompilerParams(collective_id=collective_id, has_side_effects=True, vmem_limit_bytes=VMEM_MOST)
 
 
-def attend_kernel(side, adapters, scale, n_keep, ids_ref, x_ref, gain_ref, cos_ref, sin_ref, *rest):
+def attend_kernel(side, adapters, scale, n_keep, ids_ref, x_ref, gain_ref, cos_ref, sin_ref, wo_ref, ao_ref, *rest):
     heads, rest = rest[:5], rest[5:]
     given, rest = rest[:n_keep], rest[n_keep:]
-    att_ref, rest = rest[0], rest[1:]
+    out_ref, rest = rest[0], rest[1:]
     kept, rest = rest[:n_keep], rest[n_keep:]
-    w, a_rows, bx, xbuf, h, z, lows, att, pair_send, pair_recv, load_sem, x_sem, send_sem, recv_sem = rest
+    (w, a_rows, bx, xbuf, h, z, lows, att, act, wo, stage, near, landed, pair_send, pair_recv, load_sem, x_sem, wo_load, wo_send, wo_recv,
+     wo_pair_send, wo_pair_recv, swap_send, swap_recv, send_sem, recv_sem, fast_send, fast_recv) = rest
     place = Place(side)
     head, seq_len, depth = cos_ref.shape[1], x_ref.shape[1], x_ref.shape[2]
     cols = heads[4].shape[-1]
@@ -205,10 +274,49 @@
         return [pltpu.make_async_copy(x_ref.at[4 * step + 2 * i + place.core], xbuf.at[slot, i], x_sem.at[slot]) for i in BOTH]
 
     ends(x_loads(0))
-    place.barrier(place.partner)
+    width = wo_ref.shape[1]
+    rank = ao_ref.shape[2]
+    wo_loads = []
+    for part in BOTH:
+        wo_loads.append(pltpu.make_async_copy(wo_ref, wo.at[part, OWN, 0, :, first(width)], wo_load))
+        for a in range(adapters):
+            wo_loads.append(pltpu.make_async_copy(ao_ref.at[a], wo.at[part, OWN, 0, :, pl.ds(width + a * rank, rank)], wo_load))
+    ends(wo_loads)
+    place.barrier(place.partner, place.device(0, FAR), place.device(FAR, 0))
     moves = list(zip(heads, spots[1][:3] + [a_own] + spots[1][4:])) + list(zip(given, kept))
     pair = [remote(src, dst, pair_send.at[i], pair_recv.at[i], place.partner) for i, (src, dst) in enumerate(moves)]
     ends(pair)
+
+    def wo_message(part, passed, d):
+        src, dst = (wo.at[part, s, 0] for s in ((FROM[d], FAR) if passed else (OWN, FROM[d])))
+        if passed:
+            at = pl.ds(d * head // 2, head // 2)
+            src, dst = src.at[at], dst.at[at]
+        return remote(src, dst, wo_send.at[part, passed, d], wo_recv.at[part, passed, d], place.neighbour(part, SLOW, STEP[d]))
+
+    def wo_to_partner(part, s):
+        remote(wo.at[part, s, 0], wo.at[part, s, 1], wo_pair_send, wo_pair_recv, place.partner).start()
+
+    wait(wo_loads)
+    for d in BOTH:
+        for part in BOTH:
+            wo_message(part, 0, d).start()
+    for part in BOTH:
+        wo_to_partner(part, OWN)
+
+    def wo_pass():
+        for d in BOTH:
+            for part in BOTH:
+                wo_message(part, 0, d).wait_recv()
+                wo_message(part, 1, d).start()
+                wo_to_partner(part, FROM[d])
+
+    def wo_last():
+        for part in BOTH:
+            for d in BOTH:
+                wo_message(part, 1, d).wait_recv()
+            wo_to_partner(part, FAR)
+
     wait(loads)
     for copy in pair[:len(heads)]:
         copy.wait_recv()
@@ -244,12 +352,19 @@
                 pieces.append(piece)
             lows[part, mine[part][0], mine[part][1], half, :, pl.ds(pl.multiple_of(at, LANE), 2 * seq_len)] = jnp.concatenate(pieces, axis=1).astype(BF)
 
+        pl.when(step == steps - 3)(wo_pass)
+
     loop(steps, project)
     gather(place, block, send_sem, recv_sem, absolute=True)
     causal = lax.broadcasted_iota(jnp.int32, (seq_len, seq_len), 0) >= lax.broadcasted_iota(jnp.int32, (seq_len, seq_len), 1)
 
+    def swap(part, ds, df):
+        sems = (part, ds, df)
+        to = place.neighbour(part, SLOW, ds)
+        return remote(att.at[sems], act.at[part, lax.rem(len(RING) - ds, len(RING)), df], swap_send.at[sems], swap_recv.at[sems], to)
+
     def attention(i):
-        dy, dx = i // side, lax.rem(i, side)
+        dy, dx = side - 1 - i // side, side - 1 - lax.rem(i, side)
         chip = place.turn(place.y, dy) * side + place.turn(place.x, dx)
         adapter = ids_ref[2 * chip + place.core]
         half, at = chip // steps, pl.ds(pl.multiple_of(lax.rem(chip, steps) * seq_len, LANE), seq_len)
@@ -263,32 +378,76 @@
             e = jnp.exp(scores - jnp.max(scores, axis=-1, keepdims=True))
             prob = (e / jnp.sum(e, axis=-1, keepdims=True)).astype(BF)
             mixed = dot(prob, v.astype(BF)).astype(BF)
-            for part, spot in enumerate((i, dx * side + dy)):
-                att[part, spot, :, i_head * head:(i_head + 1) * head] = mixed[part * seq_len // 2:(part + 1) * seq_len // 2]
-
-    loop(chips, attention)
-    wait(ends([pltpu.make_async_copy(att, att_ref, load_sem)]))
+            for part, (ds, df) in enumerate(((dy, dx), (dx, dy))):
+                att[part, ds, df, :, i_head * head:(i_head + 1) * head] = mixed[part * seq_len // 2:(part + 1) * seq_len // 2]
+
+    def attention_pair(k):
+        for i in BOTH:
+            attention(2 * k + i)
+        for i in BOTH:
+            dy, dx = side - 1 - (2 * k + i) // side, side - 1 - lax.rem(2 * k + i, side)
+            for part, (ds, df) in enumerate(((dy, dx), (dx, dy))):
+                pl.when(ds != OWN)(swap(part, ds, df).start)
+        pl.when(k == 2)(wo_last)
+
+    loop(chips // 2, attention_pair)
+    for part in BOTH:
+        act[part, OWN] = att[part, OWN]
+    pltpu.make_async_copy(wo.at[:, :, 1], wo.at[:, :, 1], wo_pair_recv).wait()
+    chunk = fit(width, 512)
+    rows = seq_len // 2
+    blocks = (len(RING), rows)
+    fast = FastScatter(place, lambda part, df: stage.at[part, df], near, landed, fast_send, fast_recv)
+
+    def sum_heads(part, at):
+        return sum(dot(act[part, s].reshape(-1, 2 * head), wo[part, s, :, :, at].reshape(2 * head, -1)) for s in RING)
+
+    for part in BOTH:
+        for ds in RING[1:]:
+            for df in RING:
+                swap(part, ds, df).wait_recv()
+
+        def columns(n):
+            at = pl.ds(pl.multiple_of(n * chunk, chunk), chunk)
+            stage[part, :, :, at] = sum_heads(part, at).reshape(blocks + (chunk,)).astype(BF)
+
+        loop(width // chunk, columns)
+        chosen = rows_of_adapter(place, ids_ref, part, OWN, (len(RING) * rows, rank))
+        stage[part, :, :, width:] = pick_columns(sum_heads(part, pl.ds(width, adapters * rank)), chosen).reshape(blocks + (rank,)).astype(BF)
+        for df in RING[1:]:
+            fast.ready(part, df)
+    fast.finish()
+    fast.store(out_ref, load_sem)
     for copy in pair[len(heads):]:
         copy.wait_recv()
     for copy in pair:
         copy.wait_send()
-
-
-def attend(ids, x_in, gain, heads, given, side, adapters, scale, collective_id):
+    pltpu.make_async_copy(wo.at[:, :, 1], wo.at[:, :, 1], wo_pair_send).wait()
+    for part in BOTH:
+        for d in BOTH:
+            for passed in BOTH:
+                wo_message(part, passed, d).wait_send()
+        for ds in RING[1:]:
+            for df in RING:
+                swap(part, ds, df).wait_send()
+
+
+def attend(ids, x_in, gain, w_o, a_o, heads, given, side, scale, collective_id):
     _, seq_len, depth = x_in.shape
     head, cols = heads[0].shape[1], heads[4].shape[-1]
+    adapters, _, rank = a_o.shape
     chips = side * side
     half_dim = head // 2
     inv_freq = ROPE_BASE ** (-2.0 * np.arange(half_dim) / head)
     angle = np.arange(seq_len)[:, None] * inv_freq[None, :]
     cos, sin = np.cos(angle), np.sin(angle)
     tables = [jnp.asarray(np.concatenate(pair, axis=1), F32) for pair in ((cos, cos), (-sin, sin))]
-    att = jax.ShapeDtypeStruct((2, chips, seq_len // 2, 2 * head), BF)
     n_moves = len(heads) + len(given)
+    rows, out_cols = seq_len // 2, depth + rank
     return pl.pallas_call(
         functools.partial(attend_kernel, side, adapters, scale, len(given)),
-        out_shape=[att] + [jax.ShapeDtypeStruct(g.shape, g.dtype) for g in given],
-        in_specs=[SMEM, HBM, VMEM, VMEM, VMEM] + [HBM] * n_moves,
+        out_shape=[jax.ShapeDtypeStruct((seq_len, out_cols), BF)] + [jax.ShapeDtypeStruct(g.shape, g.dtype) for g in given],
+        in_specs=[SMEM, HBM, VMEM, VMEM, VMEM] + [HBM] * (2 + n_moves),
         out_specs=[HBM] * (1 + len(given)),
         scratch_shapes=[
             pltpu.VMEM((depth, 2 * cols), BF),
@@ -298,12 +457,16 @@
             pltpu.VMEM((2 * seq_len, depth), BF),
             pltpu.VMEM((chips * seq_len, 2 * cols), F32),
             pltpu.VMEM((2, side, side, 2, TILE, chips * seq_len // 2), BF),
-            pltpu.VMEM(att.shape, BF),
-            DMA((n_moves,)), DMA((n_moves,)), DMA, DMA((2,)),
-        ] + GATHER_SEMS,
+            pltpu.VMEM((2, side, side, rows, 2 * head), BF),
+            pltpu.VMEM((2, side, side, rows, 2 * head), BF),
+            pltpu.VMEM((2, side, 2, head, depth + adapters * rank), BF),
+            pltpu.VMEM((2, side, rows, out_cols), BF),
+        ] + fast_scratch(rows, out_cols) + [
+            DMA((n_moves,)), DMA((n_moves,)), DMA, DMA((2,)), DMA, DMA((2, 2, 2)), DMA((2, 2, 2)), DMA, DMA, DMA((2, 4, 4)), DMA((2, 4, 4)),
+        ] + GATHER_SEMS + FAST_SEMS,
         compiler_params=comm_params(collective_id),
         name='attend',
-    )(ids, x_in, gain.reshape(1, depth), *tables, *heads, *given)
+    )(ids, x_in, gain.reshape(1, depth), *tables, w_o, a_o, *heads, *given)
 
 
 def row_proj_kernel(side, adapters, ids_ref, act_ref, w_own, w_par, a_own, a_par, out_ref,
@@ -333,16 +496,10 @@
             stage[part, ds, :, :, at] = dot(act[part, ds], w[:, at]).reshape(len(RING), rows, chunk).astype(BF)
 
         loop(width // chunk, columns)
-        low = dot(act[part, ds], w[:, width:])
         chosen = rows_of_adapter(place, ids_ref, part, ds, (len(RING) * rows, rank))
-        kept = low[:, :rank]
-        for a in range(1, adapters):
-            kept = jnp.where(chosen == a, low[:, a * rank:(a + 1) * rank], kept)
-        stage[part, ds, :, :, width:] = kept.reshape(len(RING), rows, rank).astype(BF)
+        stage[part, ds, :, :, width:] = pick_columns(dot(act[part, ds], w[:, width:]), chosen).reshape(len(RING), rows, rank).astype(BF)
 
     blocks = ((FAR, LAST), (OWN, NEXT))
-    halves = (first(quarter), pl.ds(quarter, quarter))
-    PASS, FREE, SUM = range(3)
 
     def slow(part, kind, d, i):
         df = blocks[1 - d][i] if kind == FREE else blocks[d][i]
@@ -351,23 +508,7 @@
         dst = near.at[part, d, i] if kind == PASS else landed.at[part, d, df]
         return remote(src, dst, slow_send.at[sems], slow_recv.at[sems], place.neighbour(part, SLOW, STEP[d]))
 
-    def fast(part, kind, d):
-        at = halves[1 - d] if kind == FREE else halves[d]
-        sems = (part, kind, d)
-        src = stage.at[part, OWN, FAR if kind == PASS else TOWARD[d], at]
-        dst = fast_near.at[part, d] if kind == PASS else fast_landed.at[part, d, at]
-        return remote(src, dst, fast_send.at[sems], fast_recv.at[sems], place.neighbour(part, FAST, STEP[d]))
-
-    def add(into, *others):
-        def some(i):
-            at = pl.ds(pl.multiple_of(i * TILE, TILE), TILE)
-            total = into[at, :].astype(F32)
-            for other in others:
-                total += other[at, :].astype(F32)
-            into[at, :] = total.astype(BF)
-
-        loop(into.shape[0] // TILE, some)
-
+    fast = FastScatter(place, lambda part, df: stage.at[part, OWN, df], fast_near, fast_landed, fast_send, fast_recv)
     for part in BOTH:
         unit(part, FAR)
         for i in BOTH:
@@ -392,26 +533,12 @@
                 slow(part, SUM, d, i).wait_recv()
                 slow(part, FREE, 1 - d, i).wait_recv()
                 add(stage.at[part, OWN, df], landed.at[part, UP, df], landed.at[part, DOWN, df])
-                for e in BOTH:
-                    if df == FAR:
-                        fast(part, PASS, e).start()
-                    elif df == TOWARD[e]:
-                        fast(part, FREE, e).start()
-    for d in BOTH:
-        for part in BOTH:
-            fast(part, PASS, d).wait_recv()
-            add(stage.at[part, OWN, TOWARD[d], halves[d]], fast_near.at[part, d])
-            fast(part, SUM, d).start()
-    for part in BOTH:
-        for d in BOTH:
-            fast(part, FREE, d).wait_recv()
-            fast(part, SUM, d).wait_recv()
-        add(stage.at[part, OWN, OWN], fast_landed.at[part, UP], fast_landed.at[part, DOWN])
-    wait(ends([pltpu.make_async_copy(stage.at[part, OWN, OWN], out_ref.at[pl.ds(part * rows, rows)], load_sem) for part in BOTH]))
+                fast.ready(part, df)
+    fast.finish()
+    fast.store(out_ref, load_sem)
     for part in BOTH:
         for kind in range(3):
             for d in BOTH:
-                fast(part, kind, d).wait_send()
                 for i in BOTH:
                     slow(part, kind, d, i).wait_send()
 
@@ -433,10 +560,7 @@
             pltpu.VMEM((2, side, side) + blocks, BF),
             pltpu.VMEM((2, 2, 2) + blocks, BF),
             pltpu.VMEM((2, 2, side) + blocks, BF),
-            pltpu.VMEM((2, 2, rows // 2, cols), BF),
-            pltpu.VMEM((2, 2) + blocks, BF),
-            DMA((2, 3, 2, 2)), DMA((2, 3, 2, 2)), DMA((2, 3, 2)), DMA((2, 3, 2)), DMA,
-        ],
+        ] + fast_scratch(rows, cols) + [DMA((2, 3, 2, 2))] * 2 + FAST_SEMS + [DMA],
         compiler_params=comm_params(collective_id),
         name='row_proj',
     )(ids, act, w_own, w_par, a_own, a_par)
@@ -618,18 +742,16 @@
                               for i, b in enumerate((b_q, b_k, b_v))], axis=-2)
         own_b = jnp.stack([spread_b[:, :, :, 0], spread_b[:, :, :, 1].swapaxes(1, 2)], axis=1).reshape(adapters, 2, 2 * rank, -1)
         heads = [w_q[:, 0], w_k[:, 0], w_v[:, 0], own_a, own_b]
-        given = [w_o[0], a_o[:, 0], across(w_gate), across(w_up), w_down, across(b_gate), across(b_up), a_down]
-        att, *kept = attend(adapter_ids, x_in, gain_attn, heads, given, side, adapters, scale, 0)
+        given = [across(w_gate), across(w_up), across(b_gate), across(b_up), w_down, a_down]
+        sums, *kept = attend(adapter_ids, x_in, gain_attn, w_o[0], a_o[:, 0], heads, given, side, scale, 0)
 
         all_b = lax.all_gather(jnp.stack([b_o, b_down]), 'tensor', axis=1)
         all_a = lax.all_gather(jnp.stack([across(a_gate), across(a_up)], axis=1).reshape(-1, depth), 'tensor', axis=0, tiled=True)
         x_own = lax.dynamic_index_in_dim(x_in, index, axis=0, keepdims=False)
-        att = att.reshape(2, side, -1, att.shape[-1])
-        sums = row_proj(adapter_ids, att, given[0], kept[0], given[1], kept[1], side, 1)
-        w = [piece for i in (2, 3, 5, 6) for piece in (given[i], kept[i])]
-        hidden, x_mid = gate_up(adapter_ids, sums, x_own, gain_mlp, all_b, all_a, w, side, scale, 2)
-        sums = row_proj(adapter_ids, hidden, given[4], kept[4], given[7], kept[7], side, 3)
-        y = deliver(adapter_ids, sums, x_mid, all_b, side, scale, 4)
+        w = [piece for pair in zip(given[:4], kept[:4]) for piece in pair]
+        hidden, x_mid = gate_up(adapter_ids, sums, x_own, gain_mlp, all_b, all_a, w, side, scale, 1)
+        sums = row_proj(adapter_ids, hidden, given[4], kept[4], given[5], kept[5], side, 2)
+        y = deliver(adapter_ids, sums, x_mid, all_b, side, scale, 3)
         return y.reshape(x_in.shape)
 
     return jax.shard_map(local_layer, mesh=mesh, in_specs=in_specs, out_specs=P('data', None, None), check_vma=False)

time: 526 us -> 471 us (0.90)
  Pallas kernels: 477 us -> 422 us
    pallas_call x2 -> x1, Pallas kernels: 199 us -> 93.2 us  [row_proj(): pl.pallas_call(functools.partial(row_proj_kernel, side, adapters), out_sh...]
    pallas_call x1, Pallas kernels: 67.9 us -> 115 us  [attend(): pl.pallas_call(functools.partial(attend_kernel, side, adapters, scale, le...]
    pallas_call x1, Pallas kernels: 97 us -> 104 us  [deliver(): pl.pallas_call(functools.partial(deliver_kernel, side, b_all.shape[2], sc...]
  transfers between devices with their start and end apart: 2 -> 2, of which waited for: 0 -> 0; matrix products, arithmetic and copies ran while one was open for 2% -> 2% of each run, Pallas kernels for 32% -> 24%
where the time goes in v3:
time: 471 us
  Pallas kernels  422 us (90%)
  local copies, waits for them, and re-layouts  29.3 us (6%)
  between operations  13.6 us (3%)
  other arithmetic  5.26 us (1%)
    pallas_call x1, Pallas kernels, attend(): pl.pallas_call(functools.partial(attend_kernel, side, adapters, scale, le...  115 us
    pallas_call x1, Pallas kernels, gate_up(): pl.pallas_call(functools.partial(gate_up_kernel, side, adapters, scale),...  110 us
    pallas_call x1, Pallas kernels, deliver(): pl.pallas_call(functools.partial(deliver_kernel, side, b_all.shape[2], sc...  104 us
    pallas_call x1, Pallas kernels, row_proj(): pl.pallas_call(functools.partial(row_proj_kernel, side, adapters), out_sh...  93.2 us
    unnamed x7, local copies, waits for them, and re-layouts  22.9 us
  transfers between devices with their start and end apart: 2, of which 0 were waited for; matrix products, arithmetic and copies ran while one was open for 2% of the time, Pallas kernels for 24%

profile of v3, /device:TPU:97, one launch (start us, length us, event | category | flops | bytes accessed | tf_op | source)
XLA Modules:
  0.0 470.8 jit_solution(16133262085460218732)
XLA Ops:
  6.5 0.0 copy-start
  6.5 0.0 copy-start.1
  6.6 0.0 copy-start.2
  6.6 0.0 all-gather.6.cloned.1.call-start
  6.6 1.6 pad_maximum_fusion.3
  8.1 0.1 all-gather.6.cloned.1.call-update
  8.2 0.1 all-gather.4.cloned.1.call-start
  8.3 1.0 pad_maximum_fusion.2
  9.3 0.7 reshape.23
  10.0 0.1 all-gather.4.cloned.1.call-update
  10.0 0.1 pad.27.clone
  10.1 1.1 maximum_maximum_fusion
  11.2 0.1 copy.34
  11.3 0.8 reshape.21.rest_3_
  12.1 0.0 copy-done
  12.1 0.1 pad_bitcast_fusion.2
  12.2 0.0 copy-done.1
  12.2 0.0 copy-done.2
  12.2 0.2 pad_bitcast_fusion
  12.4 0.7 pad_maximum_fusion
  13.1 0.4 fusion
  13.5 0.5 copy.38
  14.1 0.3 stack.58
  14.4 0.5 copy.39
  14.9 0.3 stack.59
  15.3 1.0 pad_maximum_fusion.1.rest_4_
  16.3 115.1 %attend.1 = (bf16[128,4224]{1,0:T(8,128)(2,1)}, bf16[344,4096]{1,0:T(8,128)(2,1)}, bf16[344,4096]{1,0:T(8,128)(2,1)}, bf16[2,344,128]{2,1,0:T(8,128)(2,1)}, bf16...) custom-call(s32[32]{0:T(128)} %ids_ref.7, bf16[32,128,4096]{2,1,0:T(8,128)(2,1)} %x_ref.1, ...), custom_call_target="tpu_custom_call" | custom-call | tf_op jit(solution)/shard_map/attend/pallas_call | solution.py:447
  131.4 2.3 dynamic-slice_bitcast_fusion.x_ref
  133.7 109.9 %gate_up.1 = (bf16[2,4,256,768]{3,2,1,0:T(8,128)(2,1)}, bf16[128,4096]{1,0:T(8,128)(2,1)}) custom-call(s32[32]{0:T(128)} %ids_ref.7, bf16[128,4224]{1,0:T(8,128)(2,1)} %get-tuple-element.14.sums_ref, bf16[128,4096]{1,0:T(8,128)(2,1)} %dynamic-slice_bitcast_fusion.x_ref, f32[1,4096]{1,0:T(1,128)} %bitcast.85, ...), custom_call_target="tpu_custom_call" | custom-call | tf_op jit(solution)/shard_map/gate_up/pallas_call | solution.py:650
  243.6 93.2 %row_proj.1.sums_ref = bf16[128,4224]{1,0:T(8,128)(2,1)} custom-call(s32[32]{0:T(128)} %ids_ref.7, bf16[2,4,256,768]{3,2,1,0:T(8,128)(2,1)} %get-tuple-element.19.act_ref, bf16[344,4096]{1,0:T(8,128)(2,1)} %w_own.1, bf16[344,4096]{1,0:T(8,128)(2,1)} %get-tuple-element.20.w_par, bf16[2,344,128]{2,1,0:T(8,128)(2,1)} %a_own.1, ...), custom_call_target="tpu_custom_call" | custom-call | tf_op jit(solution)/shard_map/row_proj/pallas_call | solution.py:552
  336.8 104.2 %deliver.1 = bf16[32,2,2,32,4096]{4,3,2,1,0:T(8,128)(2,1)} custom-call(s32[32]{0:T(128)} %ids_ref.7, bf16[128,4224]{1,0:T(8,128)(2,1)} %row_proj.1.sums_ref, bf16[128,4096]{1,0:T(8,128)(2,1)} %get-tuple-element.22.x_ref, bf16[2,32,2,128,128]{4,3,2,1,0:T(8,128)(2,1)} %bitcast.58), custom_call_target="tpu_custom_call" | custom-call | tf_op jit(solution)/shard_map/deliver/pallas_call | solution.py:704
  441.0 22.9 %copy.44 = bf16[32,128,4096]{2,1,0:T(8,128)(2,1)} copy(bf16[32,128,4096]{2,1,0:T(8,128)(2,1)} %bitcast.56) | data formatting | bytes 67108864
  (3 shorter events, 0.1 us)
Async XLA Ops:
  6.5 5.5 %copy-start = (bf16[2,128,1,128]{3,1,2,0:T(8,128)(2,1)S(1)}, bf16[2,128,1,128]{3,1,2,0:T(8,128)(2,1)}, u32[]{:S(2)}) copy-start(bf16[2,128,1,128]{3,1,2,0:T(8,128)(2,1)} %param.39) | copy-start | bytes 196612
  6.5 5.6 %copy-start.1 = (bf16[2,128,1,128]{3,1,2,0:T(8,128)(2,1)S(1)}, bf16[2,128,1,128]{3,1,2,0:T(8,128)(2,1)}, u32[]{:S(2)}) copy-start(bf16[2,128,1,128]{3,1,2,0:T(8,128)(2,1)} %param.43) | copy-start | bytes 196612
  6.6 5.6 %copy-start.2 = (bf16[2,128,1,128]{3,1,2,0:T(8,128)(2,1)S(1)}, bf16[2,128,1,128]{3,1,2,0:T(8,128)(2,1)}, u32[]{:S(2)}) copy-start(bf16[2,128,1,128]{3,1,2,0:T(8,128)(2,1)} %param.41) | copy-start | bytes 196612
  6.6 127.1 %all-gather.6.cloned.1.call-start = ((), (), s32[]{:S(2)}) async-start(), calls=%async_computation.1 | async-start | bytes 4325376 | tf_op jit(solution)/shard_map/all_gather | solution.py:748
  8.2 125.5 %all-gather.4.cloned.1.call-start = ((), (), s32[]{:S(2)}) async-start(), calls=%async_computation | async-start | bytes 4325376 | tf_op jit(solution)/shard_map/all_gather | solution.py:749
Sparse Core Ops, SparseCore 0:
  9.5 51.7 all-gather.5
  63.4 44.7 all-gather.3

commit v4 on v3

--- a/solution.py
+++ b/solution.py
@@ -17,6 +17,8 @@
 LANE = 128
 TILE = 16
 VMEM_MOST = 67043328
+VMEM_SMALL = VMEM_MOST * 3 // 8
+VMEM_LEAST = VMEM_MOST // 32
 MESH = pl.DeviceIdType.MESH
 HBM = pl.BlockSpec(memory_space=pltpu.HBM)
 VMEM = pl.BlockSpec(memory_space=pltpu.VMEM)
@@ -106,67 +108,80 @@
 GATHER_SEMS = [DMA((2, 2, 2, 2, 4))] * 2
 
 
-def gather(place, block, send_sem, recv_sem, absolute=False, seen=None, on_near=None, on_sides=None, on_far=None):
-    def message(part, ring, passed, d, j=OWN):
+class Gather:
+    def __init__(self, place, block, send_sem, recv_sem, absolute=False, seen=None):
+        self.place, self.block, self.sems, self.absolute, self.seen = place, block, (send_sem, recv_sem), absolute, seen
+
+    def message(self, part, ring, passed, d, j=OWN):
         spot = (lambda s: (s, j)) if ring == SLOW else (lambda s: (OWN, s))
         src, dst = (FROM[d], FAR) if passed else (OWN, FROM[d])
-        a, b = block(part, *spot(src)), block(part, *spot(src if absolute else dst))
+        a, b = self.block(part, *spot(src)), self.block(part, *spot(src if self.absolute else dst))
         if passed:
             a, b = a.at[d], b.at[d]
-        sems = (part, ring, passed, d, j)
-        return remote(a, b, send_sem.at[sems], recv_sem.at[sems], place.neighbour(part, ring, STEP[d]))
-
-    def start(*which):
-        for d in BOTH:
-            for part in BOTH:
-                message(part, *which[:2], d, *which[2:]).start()
-
-    def arrived(part, ring, passed, d, j=OWN):
-        message(part, ring, passed, d, j).wait_recv()
-        if seen:
+        return remote(a, b, *(sem.at[part, ring, passed, d, j] for sem in self.sems), self.place.neighbour(part, ring, STEP[d]))
+
+    def arrived(self, part, ring, passed, d, j=OWN):
+        self.message(part, ring, passed, d, j).wait_recv()
+        if self.seen:
             at = FAR if passed else FROM[d]
-            seen(part, *((at, j) if ring == SLOW else (OWN, at)), d if passed else None)
-
-    start(FAST, 0)
-    start(SLOW, 0, OWN)
-    for d in BOTH:
-        for part in BOTH:
-            arrived(part, FAST, 0, d)
-            message(part, FAST, 1, d).start()
-            for e in BOTH:
-                message(part, SLOW, 0, e, FROM[d]).start()
-    for part in BOTH:
-        for d in BOTH:
-            arrived(part, FAST, 1, d)
-        for e in BOTH:
-            message(part, SLOW, 0, e, FAR).start()
-
-    def pass_on(j):
+            self.seen(part, *((at, j) if ring == SLOW else (OWN, at)), d if passed else None)
+
+    def own(self):
+        for ring in BOTH:
+            for d in BOTH:
+                for part in BOTH:
+                    self.message(part, ring, 0, d).start()
+
+    def near(self):
+        for d in BOTH:
+            for part in BOTH:
+                self.arrived(part, FAST, 0, d)
+                self.message(part, FAST, 1, d).start()
+                for e in BOTH:
+                    self.message(part, SLOW, 0, e, FROM[d]).start()
+
+    def row(self):
         for part in BOTH:
             for d in BOTH:
-                arrived(part, SLOW, 0, d, j)
-                message(part, SLOW, 1, d, j).start()
-
-    order = (OWN,) + FROM + (FAR,)
-    pass_on(OWN)
-    if on_near:
-        on_near()
-    for j in order[1:]:
-        pass_on(j)
-    if on_sides:
-        on_sides()
-    for j in order:
+                self.arrived(part, FAST, 1, d)
+            for e in BOTH:
+                self.message(part, SLOW, 0, e, FAR).start()
+        self.sides(OWN)
+
+    def sides(self, *blocks):
+        for j in blocks:
+            for part in BOTH:
+                for d in BOTH:
+                    self.arrived(part, SLOW, 0, d, j)
+                    self.message(part, SLOW, 1, d, j).start()
+
+    def far(self):
+        for j in (OWN,) + FROM + (FAR,):
+            for part in BOTH:
+                for d in BOTH:
+                    self.arrived(part, SLOW, 1, d, j)
+
+    def sent(self):
         for part in BOTH:
             for d in BOTH:
-                arrived(part, SLOW, 1, d, j)
-    if on_far:
-        on_far()
-    for part in BOTH:
-        for d in BOTH:
-            for passed in BOTH:
-                message(part, FAST, passed, d).wait_send()
-                for j in RING:
-                    message(part, SLOW, passed, d, j).wait_send()
+                for passed in BOTH:
+                    self.message(part, FAST, passed, d).wait_send()
+                    for j in RING:
+                        self.message(part, SLOW, passed, d, j).wait_send()
+
+    def run(self, on_row=None, on_sides=None, on_far=None):
+        self.own()
+        self.near()
+        self.row()
+        if on_row:
+            on_row()
+        self.sides(*FROM, FAR)
+        if on_sides:
+            on_sides()
+        self.far()
+        if on_far:
+            on_far()
+        self.sent()
 
 
 def rows_of_adapter(place, ids_ref, part, ds, shape):
@@ -249,31 +264,45 @@
     return [pltpu.VMEM((2, 2, rows // 2, cols), BF), pltpu.VMEM((2, 2, rows, cols), BF)]
 
 
-def comm_params(collective_id):
-    return pltpu.CompilerParams(collective_id=collective_id, has_side_effects=True, vmem_limit_bytes=VMEM_MOST)
-
-
-def attend_kernel(side, adapters, scale, n_keep, ids_ref, x_ref, gain_ref, cos_ref, sin_ref, wo_ref, ao_ref, *rest):
-    heads, rest = rest[:5], rest[5:]
+def comm_params(collective_id, limit=VMEM_MOST):
+    return pltpu.CompilerParams(collective_id=collective_id, has_side_effects=True, vmem_limit_bytes=limit)
+
+
+WO_CHUNKS = 4
+
+
+def attend_kernel(side, adapters, scale, n_keep, ids_ref, x_ref, gain_ref, cos_ref, sin_ref, *rest):
+    w_heads, a_heads, b_heads, (wo_ref, ao_ref), a_mlp, b_rows, rest = rest[:3], rest[3:6], rest[6:9], rest[9:11], rest[11:13], rest[13:15], rest[15:]
     given, rest = rest[:n_keep], rest[n_keep:]
-    out_ref, rest = rest[0], rest[1:]
+    (out_ref, a_all, b_all), rest = rest[:3], rest[3:]
     kept, rest = rest[:n_keep], rest[n_keep:]
-    (w, a_rows, bx, xbuf, h, z, lows, att, act, wo, stage, near, landed, pair_send, pair_recv, load_sem, x_sem, wo_load, wo_send, wo_recv,
-     wo_pair_send, wo_pair_recv, swap_send, swap_recv, send_sem, recv_sem, fast_send, fast_recv) = rest
+    (w, a_raw, b_raw, a_rows, bx, xbuf, h, z, lows, att, act, wo, stage, near, landed, am_raw, am_rows, pair_send, pair_recv, load_sem, x_sem, own_sem,
+     wo_load, wo_send, wo_recv, bulk_send, bulk_recv, swap_send, swap_recv,
+     send_sem, recv_sem, a_send, a_recv, b_send, b_recv, fast_send, fast_recv) = rest
     place = Place(side)
     head, seq_len, depth = cos_ref.shape[1], x_ref.shape[1], x_ref.shape[2]
-    cols = heads[4].shape[-1]
+    cols = len(w_heads) * head
     chips = side * side
-    a_own = a_rows.at[pl.ds(pl.multiple_of(place.core * 2 * TILE, TILE), 2 * TILE)]
-    spots = [[w.at[:, pl.ds(at + i * head, head)] for i in range(3)] + [a_own, bx.at[:, :, :, pl.ds(at, cols)]] for at in (0, cols)]
-    loads = [pltpu.make_async_copy(src, dst, load_sem) for src, dst in zip(heads, spots[0])]
-    ends(loads)
+    per = a_raw.shape[3]
+    half_depth = depth // 4
+    heads = w_heads + a_heads + b_heads
+    spots = [[w.at[:, pl.ds(at * cols + i * head, head)] for i in range(3)] + [a_raw.at[place.core, i] for i in range(3)] + [b_raw.at[at, i] for i in range(3)]
+             for at in BOTH]
+    loads = ends([pltpu.make_async_copy(src, dst, load_sem) for src, dst in zip(heads, spots[0])])
 
     def x_loads(step):
         slot = lax.rem(step, 2)
         return [pltpu.make_async_copy(x_ref.at[4 * step + 2 * i + place.core], xbuf.at[slot, i], x_sem.at[slot]) for i in BOTH]
 
     ends(x_loads(0))
+
+    def every(ref):
+        return lambda part, ds, df: ref.at[place.core, part, place.turn(place.y, df if part else ds), place.turn(place.x, ds if part else df)]
+
+    every_a, every_b = every(a_all), every(b_all)
+    own_loads = ends([pltpu.make_async_copy(a_mlp[i], am_raw.at[i], own_sem) for i in BOTH])
+    own_b = [pltpu.make_async_copy(b_rows[half].at[part], every_b(part, OWN, OWN).at[half], load_sem) for part in BOTH for half in BOTH]
+    ends(own_b)
     width = wo_ref.shape[1]
     rank = ao_ref.shape[2]
     wo_loads = []
@@ -282,49 +311,78 @@
         for a in range(adapters):
             wo_loads.append(pltpu.make_async_copy(ao_ref.at[a], wo.at[part, OWN, 0, :, pl.ds(width + a * rank, rank)], wo_load))
     ends(wo_loads)
+    wait(own_loads)
+    am_rows[...] = jnp.concatenate([am_raw[i, a] for i in BOTH for a in range(adapters)], axis=0)
     place.barrier(place.partner, place.device(0, FAR), place.device(FAR, 0))
-    moves = list(zip(heads, spots[1][:3] + [a_own] + spots[1][4:])) + list(zip(given, kept))
-    pair = [remote(src, dst, pair_send.at[i], pair_recv.at[i], place.partner) for i, (src, dst) in enumerate(moves)]
-    ends(pair)
-
-    def wo_message(part, passed, d):
-        src, dst = (wo.at[part, s, 0] for s in ((FROM[d], FAR) if passed else (OWN, FROM[d])))
-        if passed:
-            at = pl.ds(d * head // 2, head // 2)
-            src, dst = src.at[at], dst.at[at]
-        return remote(src, dst, wo_send.at[part, passed, d], wo_recv.at[part, passed, d], place.neighbour(part, SLOW, STEP[d]))
+    pair = [remote(src, dst, pair_send.at[i], pair_recv.at[i], place.partner) for i, (src, dst) in
+            enumerate(list(zip(heads, spots[1])) + list(zip(given, kept)))]
+    ends(pair[:len(heads)])
+    a_own = ends([pltpu.make_async_copy(am_rows.at[:, pl.ds((2 * part + half) * half_depth, half_depth)], every_a(part, OWN, OWN).at[half], own_sem)
+                  for part in BOTH for half in BOTH])
+
+    piece = head // WO_CHUNKS
+
+    def wo_message(part, passed, d, i):
+        src, dst = (wo.at[part, s, 0, pl.ds(i * piece, piece)] for s in ((FROM[d], FAR) if passed else (OWN, FROM[d])))
+        sems = (part, passed, d, i)
+        return remote(src, dst, wo_send.at[sems], wo_recv.at[sems], place.neighbour(part, SLOW, STEP[d]))
 
     def wo_to_partner(part, s):
-        remote(wo.at[part, s, 0], wo.at[part, s, 1], wo_pair_send, wo_pair_recv, place.partner).start()
-
-    wait(wo_loads)
-    for d in BOTH:
-        for part in BOTH:
-            wo_message(part, 0, d).start()
-    for part in BOTH:
-        wo_to_partner(part, OWN)
-
-    def wo_pass():
-        for d in BOTH:
-            for part in BOTH:
-                wo_message(part, 0, d).wait_recv()
-                wo_message(part, 1, d).start()
+        remote(wo.at[part, s, 0], wo.at[part, s, 1], bulk_send, bulk_recv, place.partner).start()
+
+    passes = [range(d * WO_CHUNKS // 2, (d + 1) * WO_CHUNKS // 2) for d in BOTH]
+
+    def wo_start(i):
+        for d in BOTH:
+            for part in BOTH:
+                wo_message(part, 0, d, i).start()
+
+    def wo_pass(k):
+        for d in BOTH:
+            for part in BOTH:
+                wo_message(part, 0, d, passes[d][k]).wait_recv()
+                wo_message(part, 1, d, passes[d][k]).start()
+
+    def wo_arrived():
+        for d in BOTH:
+            for part in BOTH:
+                for i in passes[1 - d]:
+                    wo_message(part, 0, d, i).wait_recv()
                 wo_to_partner(part, FROM[d])
 
     def wo_last():
         for part in BOTH:
             for d in BOTH:
-                wo_message(part, 1, d).wait_recv()
+                for i in passes[d]:
+                    wo_message(part, 1, d, i).wait_recv()
             wo_to_partner(part, FAR)
 
+    wait(wo_loads)
+    wo_start(0)
+    wait(a_own)
     wait(loads)
+    wait(own_b)
+    gathers = [Gather(place, every_a, a_send, a_recv, absolute=True), Gather(place, every_b, b_send, b_recv, absolute=True)]
+
+    def both(stage_of, *more):
+        return lambda: [getattr(g, stage_of)(*more) for g in gathers]
+
+    both('own')()
+    for part in BOTH:
+        wo_to_partner(part, OWN)
     for copy in pair[:len(heads)]:
         copy.wait_recv()
+    for core in BOTH:
+        pieces = [a_raw[core, i, a] if i < len(w_heads) else jnp.zeros((per, depth), BF) for a in range(adapters) for i in RING]
+        a_rows[core * 2 * TILE:(core + 1) * 2 * TILE, :] = jnp.concatenate(pieces, axis=0)
     mine = [(place.y, place.x), (place.x, place.y)]
     steps = chips // 2
 
     def block(part, ds, df):
         return lows.at[part, place.turn(mine[part][0], ds), place.turn(mine[part][1], df)]
+
+    background = {1: lambda: (wo_start(1), ends(pair[len(heads):])), 2: both('near'), 3: lambda: wo_start(2), 4: both('row'), 5: lambda: wo_start(3),
+                  7: both('sides', *FROM, FAR)}
 
     def project(step):
         slot = lax.rem(step, 2)
@@ -333,6 +391,8 @@
         def _():
             ends(x_loads(step + 1))
 
+        for at, what in background.items():
+            pl.when(step == at)(lambda what=what: (what(), None)[1])
         wait(x_loads(step))
         for i in BOTH:
             h[i * seq_len:(i + 1) * seq_len, :] = normed(xbuf[slot, i].astype(F32), gain_ref[...])
@@ -346,16 +406,32 @@
             pieces = []
             for i in BOTH:
                 options = [low[TILE * (2 * part + a):TILE * (2 * part + a + 1), i * seq_len:(i + 1) * seq_len] for a in range(adapters)]
-                piece = options[0]
+                chosen = options[0]
                 for a in range(1, adapters):
-                    piece = jnp.where(ids_ref[4 * step + 2 * i + place.core] == a, options[a], piece)
-                pieces.append(piece)
+                    chosen = jnp.where(ids_ref[4 * step + 2 * i + place.core] == a, options[a], chosen)
+                pieces.append(chosen)
             lows[part, mine[part][0], mine[part][1], half, :, pl.ds(pl.multiple_of(at, LANE), 2 * seq_len)] = jnp.concatenate(pieces, axis=1).astype(BF)
 
-        pl.when(step == steps - 3)(wo_pass)
-
     loop(steps, project)
-    gather(place, block, send_sem, recv_sem, absolute=True)
+    low_gather = Gather(place, block, send_sem, recv_sem, absolute=True)
+    low_gather.own()
+    row, col = (lax.broadcasted_iota(jnp.int32, (2 * rank, rank), axis) for axis in BOTH)
+    spot, kind = row // TILE, lax.rem(row, TILE) // per
+    for part in BOTH:
+        chip_of = spot if part == 0 else lax.rem(spot, side) * side + spot // side
+        to = chip_of * 2 * per + part * per + lax.rem(row, per)
+        for i in range(3):
+            spread_rows = jnp.where((kind == i) & (col == to), 1.0, 0.0).astype(BF)
+            for a in range(adapters):
+                for o in BOTH:
+                    bx[a, part, :, o * cols + i * head:o * cols + (i + 1) * head] = dot(spread_rows, b_raw[o, i, a]).astype(BF)
+    low_gather.near()
+    wo_pass(0)
+    low_gather.row()
+    wo_pass(1)
+    low_gather.sides(*FROM, FAR)
+    wo_arrived()
+    low_gather.far()
     causal = lax.broadcasted_iota(jnp.int32, (seq_len, seq_len), 0) >= lax.broadcasted_iota(jnp.int32, (seq_len, seq_len), 1)
 
     def swap(part, ds, df):
@@ -393,7 +469,10 @@
     loop(chips // 2, attention_pair)
     for part in BOTH:
         act[part, OWN] = att[part, OWN]
-    pltpu.make_async_copy(wo.at[:, :, 1], wo.at[:, :, 1], wo_pair_recv).wait()
+    both('far')()
+    bulk = [remote(ref.at[place.core], ref.at[place.core], pair_send.at[len(pair) + i], pair_recv.at[len(pair) + i], place.partner) for i, ref in enumerate((a_all, b_all))]
+    ends(bulk)
+    pltpu.make_async_copy(wo.at[:, :, 1], wo.at[:, :, 1], bulk_recv).wait()
     chunk = fit(width, 512)
     rows = seq_len // 2
     blocks = (len(RING), rows)
@@ -418,41 +497,51 @@
             fast.ready(part, df)
     fast.finish()
     fast.store(out_ref, load_sem)
-    for copy in pair[len(heads):]:
+    for copy in pair[len(heads):] + bulk:
         copy.wait_recv()
-    for copy in pair:
+    for copy in pair + bulk:
         copy.wait_send()
-    pltpu.make_async_copy(wo.at[:, :, 1], wo.at[:, :, 1], wo_pair_send).wait()
-    for part in BOTH:
-        for d in BOTH:
-            for passed in BOTH:
-                wo_message(part, passed, d).wait_send()
+    for g in gathers + [low_gather]:
+        g.sent()
+    pltpu.make_async_copy(wo.at[:, :, 1], wo.at[:, :, 1], bulk_send).wait()
+    for part in BOTH:
+        for d in BOTH:
+            for i in range(WO_CHUNKS):
+                wo_message(part, 0, d, i).wait_send()
+            for i in passes[d]:
+                wo_message(part, 1, d, i).wait_send()
         for ds in RING[1:]:
             for df in RING:
                 swap(part, ds, df).wait_send()
 
 
-def attend(ids, x_in, gain, w_o, a_o, heads, given, side, scale, collective_id):
+def attend(ids, x_in, gain, heads, w_o, a_o, a_mlp, b_rows, given, side, scale, collective_id):
     _, seq_len, depth = x_in.shape
-    head, cols = heads[0].shape[1], heads[4].shape[-1]
+    head = heads[0].shape[1]
+    cols = 3 * head
     adapters, _, rank = a_o.shape
+    per = a_mlp[0].shape[1]
     chips = side * side
     half_dim = head // 2
     inv_freq = ROPE_BASE ** (-2.0 * np.arange(half_dim) / head)
     angle = np.arange(seq_len)[:, None] * inv_freq[None, :]
     cos, sin = np.cos(angle), np.sin(angle)
     tables = [jnp.asarray(np.concatenate(pair, axis=1), F32) for pair in ((cos, cos), (-sin, sin))]
-    n_moves = len(heads) + len(given)
+    n_pair = len(heads) + len(given) + 2
     rows, out_cols = seq_len // 2, depth + rank
+    every = (2, 2, side, side, 2)
     return pl.pallas_call(
         functools.partial(attend_kernel, side, adapters, scale, len(given)),
-        out_shape=[jax.ShapeDtypeStruct((seq_len, out_cols), BF)] + [jax.ShapeDtypeStruct(g.shape, g.dtype) for g in given],
-        in_specs=[SMEM, HBM, VMEM, VMEM, VMEM] + [HBM] * (2 + n_moves),
-        out_specs=[HBM] * (1 + len(given)),
+        out_shape=[jax.ShapeDtypeStruct((seq_len, out_cols), BF), jax.ShapeDtypeStruct(every + (2 * adapters * per, depth // 4), BF),
+                   jax.ShapeDtypeStruct(every + b_rows[0].shape[1:], BF)] + [jax.ShapeDtypeStruct(g.shape, g.dtype) for g in given],
+        in_specs=[SMEM, HBM, VMEM, VMEM, VMEM] + [HBM] * (len(heads) + 6 + len(given)),
+        out_specs=[HBM] * (3 + len(given)),
         scratch_shapes=[
             pltpu.VMEM((depth, 2 * cols), BF),
+            pltpu.VMEM((2, 3, adapters, per, depth), BF),
+            pltpu.VMEM((2, 3, adapters, rank, head), BF),
             pltpu.VMEM((2 * 2 * TILE, depth), BF),
-            pltpu.VMEM(heads[4].shape[:3] + (2 * cols,), BF),
+            pltpu.VMEM((adapters, 2, 2 * rank, 2 * cols), BF),
             pltpu.VMEM((2, 2, seq_len, depth), BF),
             pltpu.VMEM((2 * seq_len, depth), BF),
             pltpu.VMEM((chips * seq_len, 2 * cols), F32),
@@ -462,11 +551,13 @@
             pltpu.VMEM((2, side, 2, head, depth + adapters * rank), BF),
             pltpu.VMEM((2, side, rows, out_cols), BF),
         ] + fast_scratch(rows, out_cols) + [
-            DMA((n_moves,)), DMA((n_moves,)), DMA, DMA((2,)), DMA, DMA((2, 2, 2)), DMA((2, 2, 2)), DMA, DMA, DMA((2, 4, 4)), DMA((2, 4, 4)),
-        ] + GATHER_SEMS + FAST_SEMS,
+            pltpu.VMEM((2, adapters, per, depth), BF),
+            pltpu.VMEM((2 * adapters * per, depth), BF),
+            DMA((n_pair,)), DMA((n_pair,)), DMA, DMA((2,)), DMA, DMA, DMA((2, 2, 2, WO_CHUNKS)), DMA((2, 2, 2, WO_CHUNKS)), DMA, DMA, DMA((2, 4, 4)), DMA((2, 4, 4)),
+        ] + GATHER_SEMS * 3 + FAST_SEMS,
         compiler_params=comm_params(collective_id),
         name='attend',
-    )(ids, x_in, gain.reshape(1, depth), *tables, w_o, a_o, *heads, *given)
+    )(ids, x_in, gain.reshape(1, depth), *tables, *heads, w_o, a_o, *a_mlp, *b_rows, *given)
 
 
 def row_proj_kernel(side, adapters, ids_ref, act_ref, w_own, w_par, a_own, a_par, out_ref,
@@ -567,17 +658,21 @@
 
 
 def finish(sums_ref, resid, b_ref, chosen, scale, adapters):
-    devices, _, rank, part = b_ref.shape
-    width = devices * part
+    _, _, side, _, rank, part = b_ref.shape
+    width = sums_ref.shape[1] - rank
     low = spread(sums_ref[:, width:].astype(F32), chosen, adapters)
-    delta = [dot(low, b_ref[j].reshape(adapters * rank, part)) for j in range(devices)]
+    delta = [dot(low, b_ref[core, :, y, x].reshape(adapters * rank, part)) for y in range(side) for x in range(side) for core in BOTH]
     return resid.astype(F32) + (sums_ref[:, :width].astype(F32) + scale * jnp.concatenate(delta, axis=1))
 
 
-def gate_up_kernel(side, adapters, scale, ids_ref, sums_ref, x_ref, gain_ref, a_ref, b_all, wg_own, wg_par, wu_own, wu_par, bg_own, bg_par, bu_own, bu_par,
-                   hid_ref, mid_ref, gbuf, w, b, b_ref, hid, load_sem, b_sem, store_sem, send_sem, recv_sem):
+def own_rows(place, ids_ref, shape):
+    return jnp.full(shape, ids_ref[place.device(0, 0)], jnp.int32)
+
+
+def gate_up_kernel(side, adapters, scale, ids_ref, sums_ref, x_ref, gain_ref, a_all, b_all, wg_own, wg_par, wu_own, wu_par, bg_own, bg_par, bu_own, bu_par,
+                   hid_ref, mid_ref, gbuf, w, b, a_ref, b_ref, hid, load_sem, b_sem, store_sem, send_sem, recv_sem):
     place = Place(side)
-    b_load = ends([pltpu.make_async_copy(b_all.at[0], b_ref, b_sem)])
+    b_load = ends([pltpu.make_async_copy(b_all.at[:, :, :, :, 0], b_ref, b_sem), pltpu.make_async_copy(a_all, a_ref, b_sem)])
     share, width = wg_own.shape
     half = w.shape[1] // 2
     rank = bg_own.shape[2]
@@ -595,19 +690,22 @@
                 loads.append(pltpu.make_async_copy(pieces[2 + i].at[a], b.at[kind, pl.ds(at, share), pl.ds(a * rank, rank)], load_sem))
     ends(loads)
     rows = seq_len // 4
-    chosen = jnp.full((seq_len, rank), ids_ref[place.device(0, 0)], jnp.int32)
+    chosen = own_rows(place, ids_ref, (seq_len, rank))
     wait(b_load)
     mid = finish(sums_ref, x_ref[...], b_ref, chosen, scale, adapters).astype(BF)
     mid_ref[...] = mid
     h2 = normed(mid.astype(F32), gain_ref[...])
-    low = dot_rows(h2, a_ref[...]).astype(BF)
-    n_low = low.shape[1]
+    lows = []
+    for core in BOTH:
+        pieces = [dot_rows(h2[:, i * width // 4:(i + 1) * width // 4], a_ref[core, i // 2, :, :, i % 2].reshape(-1, width // 4)) for i in RING]
+        lows.append(sum(pieces).astype(BF))
+    low = jnp.concatenate(lows, axis=1)
     per = rank // (2 * side * side)
-    to = lax.broadcasted_iota(jnp.int32, (n_low, 2 * rank), 1)
-    frm = lax.broadcasted_iota(jnp.int32, (n_low, 2 * rank), 0)
-    kind, rank_at = to // rank, lax.rem(to, rank)
-    pick = (rank_at // per) * (2 * adapters * per) + ids_ref[place.device(0, 0)] * (2 * per) + kind * per + lax.rem(rank_at, per)
-    low = dot(low, jnp.where(frm == pick, 1.0, 0.0).astype(BF)).astype(BF)
+    row, col = (lax.broadcasted_iota(jnp.int32, (low.shape[1], 2 * rank), axis) for axis in BOTH)
+    kind, rank_at = col // rank, lax.rem(col, rank)
+    chip, core = rank_at // (2 * per), lax.rem(rank_at // per, 2)
+    pick = ((core * side * side + chip) * 2 + kind) * adapters * per + ids_ref[place.device(0, 0)] * per + lax.rem(rank_at, per)
+    low = dot(low, jnp.where(row == pick, 1.0, 0.0).astype(BF)).astype(BF)
     for part in BOTH:
         for piece in BOTH:
             at = (2 * part + piece) * rows
@@ -631,17 +729,16 @@
         loop(2 * half // chunk, columns)
         pltpu.make_async_copy(hid.at[part, ds], hid_ref.at[part, ds], store_sem).start()
 
-    def on_near():
+    def on_row():
         wait(loads)
         loop(2, lambda part: unit(part, OWN))
 
-    gather(place, lambda part, ds, df: gbuf.at[part, ds, df], send_sem, recv_sem, on_near=on_near,
-           on_sides=lambda: loop(len(RING), lambda i: unit(lax.rem(i, 2), NEXT + 2 * (i // 2))),
-           on_far=lambda: loop(2, lambda part: unit(part, FAR)))
+    Gather(place, lambda part, ds, df: gbuf.at[part, ds, df], send_sem, recv_sem).run(
+        on_row, lambda: loop(len(RING), lambda i: unit(lax.rem(i, 2), NEXT + 2 * (i // 2))), lambda: loop(2, lambda part: unit(part, FAR)))
     pltpu.make_async_copy(hid, hid_ref, store_sem).wait()
 
 
-def gate_up(ids, sums, x_own, gain, b_all, a_all, w, side, scale, collective_id):
+def gate_up(ids, sums, x_own, gain, a_all, b_all, w, side, scale, collective_id):
     seq_len, depth = x_own.shape
     share = w[0].shape[0]
     adapters, _, rank = w[4].shape
@@ -650,13 +747,14 @@
     return pl.pallas_call(
         functools.partial(gate_up_kernel, side, adapters, scale),
         out_shape=[hidden, jax.ShapeDtypeStruct(x_own.shape, BF)],
-        in_specs=[SMEM] + [VMEM] * 4 + [HBM] * (1 + len(w)),
+        in_specs=[SMEM] + [VMEM] * 3 + [HBM] * (2 + len(w)),
         out_specs=[HBM, VMEM],
         scratch_shapes=[
             pltpu.VMEM((2, side, side, 2, seq_len // 4, depth + 2 * rank), BF),
             pltpu.VMEM((2, 2 * half, depth), BF),
             pltpu.VMEM((2, 2 * half, adapters * rank), BF),
-            pltpu.VMEM(b_all.shape[1:], BF),
+            pltpu.VMEM(a_all.shape, BF),
+            pltpu.VMEM(b_all.shape[:4] + b_all.shape[5:], BF),
             pltpu.VMEM(hidden.shape, BF),
             DMA, DMA, DMA,
         ] + GATHER_SEMS,
@@ -665,51 +763,59 @@
     )(ids, sums, x_own, gain.reshape(1, depth), a_all, b_all, *w)
 
 
-def deliver_kernel(side, adapters, scale, ids_ref, sums_ref, x_ref, b_all, out_ref, gbuf, b_ref, b_sem, pair_send, pair_recv, store_sem, send_sem, recv_sem):
+def deliver_kernel(side, adapters, scale, ids_ref, sums_ref, x_ref, b_all, out_ref, b_ref, b_sem, pair_send, pair_recv, send_sem, recv_sem):
     place = Place(side)
-    b_load = ends([pltpu.make_async_copy(b_all.at[1], b_ref, b_sem)])
+    b_load = ends([pltpu.make_async_copy(b_all.at[:, :, :, :, 1], b_ref, b_sem)])
     seq_len = sums_ref.shape[0]
     rows = seq_len // 4
-    rank = b_ref.shape[2]
-    chosen = jnp.full((seq_len, rank), ids_ref[place.device(0, 0)], jnp.int32)
+    chosen = own_rows(place, ids_ref, (seq_len, b_ref.shape[4]))
     wait(b_load)
     y = finish(sums_ref, x_ref[...], b_ref, chosen, scale, adapters).astype(BF)
     for part in BOTH:
         for piece in BOTH:
             at = (2 * part + piece) * rows
-            gbuf[part, OWN, OWN, piece] = y[at:at + rows]
+            out_ref[place.device(0, 0), part, piece] = y[at:at + rows]
     place.barrier(place.partner)
 
     def block(part, ds, df):
-        return gbuf.at[part, ds, df]
+        return out_ref.at[place.sequence(part, ds, df), part]
 
     def seen(part, ds, df, half):
-        src, dst = block(part, ds, df), out_ref.at[place.sequence(part, ds, df), part]
-        if half is not None:
-            src, dst = src.at[half], dst.at[half]
-        remote(src, dst, pair_send, pair_recv, place.partner).start()
-        pltpu.make_async_copy(src, dst, store_sem).start()
+        ref = block(part, ds, df) if half is None else block(part, ds, df).at[half]
+        remote(ref, ref, pair_send, pair_recv, place.partner).start()
 
     for part in BOTH:
         seen(part, OWN, OWN, None)
-    gather(place, block, send_sem, recv_sem, seen=seen)
+    Gather(place, block, send_sem, recv_sem, absolute=True, seen=seen).run()
     every = out_ref.at[first(side * side)]
-    for sem in (store_sem, pair_send, pair_recv):
+    for sem in (pair_send, pair_recv):
         pltpu.make_async_copy(every, every, sem).wait()
+
+
+def put_kernel(y_ref, out_ref, sem):
+    wait(ends([pltpu.make_async_copy(y_ref.at[i], out_ref.at[i], sem) for i in range(y_ref.shape[0])]))
 
 
 def deliver(ids, sums, x_mid, b_all, side, scale, collective_id):
     seq_len, depth = x_mid.shape
     rows = seq_len // 4
-    return pl.pallas_call(
-        functools.partial(deliver_kernel, side, b_all.shape[2], scale),
-        out_shape=jax.ShapeDtypeStruct((2 * side * side, 2, 2, rows, depth), BF),
+    y = pl.pallas_call(
+        functools.partial(deliver_kernel, side, b_all.shape[1], scale),
+        out_shape=pltpu.VMEM((2 * side * side, 2, 2, rows, depth), BF),
         in_specs=[SMEM] + [VMEM] * 2 + [HBM],
-        out_specs=HBM,
-        scratch_shapes=[pltpu.VMEM((2, side, side, 2, rows, depth), BF), pltpu.VMEM(b_all.shape[1:], BF), DMA, DMA, DMA, DMA] + GATHER_SEMS,
-        compiler_params=comm_params(collective_id),
+        scratch_shapes=[pltpu.VMEM(b_all.shape[:4] + b_all.shape[5:], BF), DMA, DMA, DMA] + GATHER_SEMS,
+        compiler_params=comm_params(collective_id, VMEM_SMALL),
         name='deliver',
     )(ids, sums, x_mid, b_all)
+    return pl.pallas_call(
+        put_kernel,
+        out_shape=jax.ShapeDtypeStruct(y.shape, BF),
+        in_specs=[pl.BlockSpec(memory_space=pl.ANY)],
+        out_specs=HBM,
+        scratch_shapes=[DMA],
+        compiler_params=pltpu.CompilerParams(vmem_limit_bytes=VMEM_LEAST),
+        name='put',
+    )(y)
 
 
 def solution(mesh):
@@ -728,28 +834,18 @@
                 head_split, last_split)
 
     def local_layer(x_in, adapter_ids, gain_attn, gain_mlp, w_q, w_k, w_v, w_o, w_gate, w_up, w_down, a_q, b_q, a_k, b_k, a_v, b_v, a_o, b_o, a_gate, b_gate, a_up, b_up, a_down, b_down):
-        depth = x_in.shape[2]
-        adapters, rank = b_q.shape[:2]
-        scale = ALPHA / rank
+        scale = ALPHA / b_q.shape[1]
         index = lax.axis_index('tensor')
 
         def across(a):
             return a.swapaxes(-1, -2)
 
-        per = a_q.shape[2]
-        own_a = jnp.stack([across(a) for a in (a_q, a_k, a_v)] + [jnp.zeros((adapters, per, depth), BF)], axis=1).reshape(-1, depth)
-        spread_b = jnp.stack([jnp.pad(b[:, :, 0].reshape(adapters, side, side, 2, 1, per, -1), ((0, 0),) * 4 + ((i, 3 - i),) + ((0, 0),) * 2)
-                              for i, b in enumerate((b_q, b_k, b_v))], axis=-2)
-        own_b = jnp.stack([spread_b[:, :, :, 0], spread_b[:, :, :, 1].swapaxes(1, 2)], axis=1).reshape(adapters, 2, 2 * rank, -1)
-        heads = [w_q[:, 0], w_k[:, 0], w_v[:, 0], own_a, own_b]
+        heads = [w[:, 0] for w in (w_q, w_k, w_v)] + [across(a) for a in (a_q, a_k, a_v)] + [b[:, :, 0] for b in (b_q, b_k, b_v)]
         given = [across(w_gate), across(w_up), across(b_gate), across(b_up), w_down, a_down]
-        sums, *kept = attend(adapter_ids, x_in, gain_attn, w_o[0], a_o[:, 0], heads, given, side, scale, 0)
-
-        all_b = lax.all_gather(jnp.stack([b_o, b_down]), 'tensor', axis=1)
-        all_a = lax.all_gather(jnp.stack([across(a_gate), across(a_up)], axis=1).reshape(-1, depth), 'tensor', axis=0, tiled=True)
+        sums, all_a, all_b, *kept = attend(adapter_ids, x_in, gain_attn, heads, w_o[0], a_o[:, 0], (across(a_gate), across(a_up)), (b_o, b_down), given, side, scale, 0)
         x_own = lax.dynamic_index_in_dim(x_in, index, axis=0, keepdims=False)
         w = [piece for pair in zip(given[:4], kept[:4]) for piece in pair]
-        hidden, x_mid = gate_up(adapter_ids, sums, x_own, gain_mlp, all_b, all_a, w, side, scale, 1)
+        hidden, x_mid = gate_up(adapter_ids, sums, x_own, gain_mlp, all_a, all_b, w, side, scale, 1)
         sums = row_proj(adapter_ids, hidden, given[4], kept[4], given[5], kept[5], side, 2)
         y = deliver(adapter_ids, sums, x_mid, all_b, side, scale, 3)
         return y.reshape(x_in.shape)

time: 471 us -> 445 us (0.945)
  local copies, waits for them, and re-layouts: 29.3 us -> 2.29 us
  Pallas kernels: 422 us -> 442 us
  between operations: 13.6 us -> 0.19 us
  other arithmetic: 5.26 us -> 0 us
    unnamed x7 -> x0, local copies, waits for them, and re-layouts: 22.9 us -> none
    pallas_call x1, Pallas kernels: 115 us -> 122 us  [attend(): pl.pallas_call(functools.partial(attend_kernel, side, adapters, scale, le...]
    pallas_call x1, Pallas kernels: 93.2 us -> 100 us  [row_proj(): pl.pallas_call(functools.partial(row_proj_kernel, side, adapters), out_sh...]
    pallas_call x1 -> x2, Pallas kernels: 104 us -> 110 us  [the longest x1 99.2 us: deliver(): pl.pallas_call(functools.partial(deliver_kernel, side, b_all.shape[1], sc...]
    another operation x5 -> x0, other arithmetic: 5.26 us -> none  [the longest x1 1.57 us: local_layer(): all_b = lax.all_gather(jnp.stack([b_o, b_down]), 'tensor', axis=1)]
  transfers between devices with their start and end apart: 2 -> 0, of which waited for: 0 -> 0; matrix products, arithmetic and copies ran while one was open for 2% -> 0% of each run, Pallas kernels for 24% -> 0%
where the time goes in v4:
time: 445 us
  Pallas kernels  442 us (99%)
    pallas_call x1, Pallas kernels, attend(): pl.pallas_call(functools.partial(attend_kernel, side, adapters, scale, le...  122 us
    pallas_call x1, Pallas kernels, gate_up(): pl.pallas_call(functools.partial(gate_up_kernel, side, adapters, scale),...  110 us
    pallas_call x1, Pallas kernels, row_proj(): pl.pallas_call(functools.partial(row_proj_kernel, side, adapters), out_sh...  100 us
    pallas_call x1, Pallas kernels, deliver(): pl.pallas_call(functools.partial(deliver_kernel, side, b_all.shape[1], sc...  99.2 us
    pallas_call x1, Pallas kernels, deliver(): pl.pallas_call(put_kernel, out_shape=jax.ShapeDtypeStruct(y.shape, BF), i...  10.9 us

profile of v4, /device:TPU:97, one launch (start us, length us, event | category | flops | bytes accessed | tf_op | source)
XLA Modules:
  0.0 444.7 jit_solution(13334575377503899628)
XLA Ops:
  0.0 2.3 dynamic-slice_bitcast_fusion.x_ref
  2.3 122.4 %attend.1 = (bf16[128,4224]{1,0:T(8,128)(2,1)}, bf16[2,2,4,4,2,16,1024]{6,5,4,3,2,1,0:T(8,128)(2,1)}, bf16[2,2,4,4,2,128,128]{6,5,4,3,2,1,0:T(8,128)(2,1)}, bf16...) custom-call(s32[32]{0:T(128)} %ids_ref.7, ...), custom_call_target="tpu_custom_call" | custom-call | tf_op jit(solution)/shard_map/attend/pallas_call | solution.py:533
  124.7 109.7 %gate_up.1 = (bf16[2,4,256,768]{3,2,1,0:T(8,128)(2,1)}, bf16[128,4096]{1,0:T(8,128)(2,1)}) custom-call(s32[32]{0:T(128)} %ids_ref.7, bf16[128,4224]{1,0:T(8,128)(2,1)} %get-tuple-element.16.sums_ref, bf16[128,4096]{1,0:T(8,128)(2,1)} %dynamic-slice_bitcast_fusion.x_ref, f32[1,4096]{1,0:T(1,128)} %bitcast.44, ...), custom_call_target="tpu_custom_call" | custom-call | tf_op jit(solution)/shard_map/gate_up/pallas_call | solution.py:747
  234.5 100.0 %row_proj.1.sums_ref = bf16[128,4224]{1,0:T(8,128)(2,1)} custom-call(s32[32]{0:T(128)} %ids_ref.7, bf16[2,4,256,768]{3,2,1,0:T(8,128)(2,1)} %get-tuple-element.23.act_ref, bf16[344,4096]{1,0:T(8,128)(2,1)} %w_own.1, bf16[344,4096]{1,0:T(8,128)(2,1)} %get-tuple-element.24.w_par, bf16[2,344,128]{2,1,0:T(8,128)(2,1)} %a_own.1, ...), custom_call_target="tpu_custom_call" | custom-call | tf_op jit(solution)/shard_map/row_proj/pallas_call | solution.py:643
  334.5 99.2 %deliver.1.y_ref = bf16[32,2,2,32,4096]{4,3,2,1,0:T(8,128)(2,1)S(1)} custom-call(s32[32]{0:T(128)} %ids_ref.7, bf16[128,4224]{1,0:T(8,128)(2,1)} %row_proj.1.sums_ref, bf16[128,4096]{1,0:T(8,128)(2,1)} %get-tuple-element.26.x_ref, bf16[2,2,4,4,2,128,128]{6,5,4,3,2,1,0:T(8,128)(2,1)} %get-tuple-element.18.b_all), custom_call_target="tpu_custom_call" | custom-call | tf_op jit(solution)/shard_map/deliver/pallas_call | solution.py:802
  433.7 10.9 %put.1 = bf16[32,2,2,32,4096]{4,3,2,1,0:T(8,128)(2,1)} custom-call(bf16[32,2,2,32,4096]{4,3,2,1,0:T(8,128)(2,1)S(1)} %deliver.1.y_ref), custom_call_target="tpu_custom_call" | custom-call | tf_op jit(solution)/shard_map/put/pallas_call | solution.py:810

commit v5 on v4

--- a/solution.py
+++ b/solution.py
@@ -29,6 +29,7 @@
 UP, DOWN = BOTH = range(2)
 STEP = (NEXT, -NEXT)
 FROM = (LAST, NEXT)
+AWAY = (NEXT, LAST, FAR)
 TOWARD = (NEXT, LAST)
 FAST, SLOW = BOTH
 
@@ -93,12 +94,14 @@
     def sequence(self, part, ds, df):
         return self.device(jnp.where(part == 0, ds, df), jnp.where(part == 0, df, ds))
 
-    def barrier(self, *more):
-        sem = pltpu.get_barrier_semaphore()
+    def announce(self, *more):
         to = [self.neighbour(0, ring, step) for ring in BOTH for step in STEP] + list(more)
         for device in to:
-            pl.semaphore_signal(sem, inc=1, device_id={'tensor': device}, device_id_type=MESH)
-        pl.semaphore_wait(sem, len(to))
+            pl.semaphore_signal(pltpu.get_barrier_semaphore(), inc=1, device_id={'tensor': device}, device_id_type=MESH)
+        self.announced = len(to)
+
+    def meet(self):
+        pl.semaphore_wait(pltpu.get_barrier_semaphore(), self.announced)
 
 
 def remote(src, dst, send_sem, recv_sem, to):
@@ -156,7 +159,7 @@
                     self.message(part, SLOW, 1, d, j).start()
 
     def far(self):
-        for j in (OWN,) + FROM + (FAR,):
+        for j in (OWN,) + AWAY:
             for part in BOTH:
                 for d in BOTH:
                     self.arrived(part, SLOW, 1, d, j)
@@ -175,7 +178,7 @@
         self.row()
         if on_row:
             on_row()
-        self.sides(*FROM, FAR)
+        self.sides(*AWAY)
         if on_sides:
             on_sides()
         self.far()
@@ -268,7 +271,7 @@
     return pltpu.CompilerParams(collective_id=collective_id, has_side_effects=True, vmem_limit_bytes=limit)
 
 
-WO_CHUNKS = 4
+WO_CHUNKS = 8
 
 
 def attend_kernel(side, adapters, scale, n_keep, ids_ref, x_ref, gain_ref, cos_ref, sin_ref, *rest):
@@ -280,6 +283,7 @@
      wo_load, wo_send, wo_recv, bulk_send, bulk_recv, swap_send, swap_recv,
      send_sem, recv_sem, a_send, a_recv, b_send, b_recv, fast_send, fast_recv) = rest
     place = Place(side)
+    place.announce(place.partner, place.device(0, FAR), place.device(FAR, 0))
     head, seq_len, depth = cos_ref.shape[1], x_ref.shape[1], x_ref.shape[2]
     cols = len(w_heads) * head
     chips = side * side
@@ -313,7 +317,7 @@
     ends(wo_loads)
     wait(own_loads)
     am_rows[...] = jnp.concatenate([am_raw[i, a] for i in BOTH for a in range(adapters)], axis=0)
-    place.barrier(place.partner, place.device(0, FAR), place.device(FAR, 0))
+    place.meet()
     pair = [remote(src, dst, pair_send.at[i], pair_recv.at[i], place.partner) for i, (src, dst) in
             enumerate(list(zip(heads, spots[1])) + list(zip(given, kept)))]
     ends(pair[:len(heads)])
@@ -358,16 +362,20 @@
             wo_to_partner(part, FAR)
 
     wait(wo_loads)
-    wo_start(0)
+    for i in range(WO_CHUNKS // 2):
+        wo_start(i)
     wait(a_own)
     wait(loads)
     wait(own_b)
     gathers = [Gather(place, every_a, a_send, a_recv, absolute=True), Gather(place, every_b, b_send, b_recv, absolute=True)]
 
     def both(stage_of, *more):
-        return lambda: [getattr(g, stage_of)(*more) for g in gathers]
-
-    both('own')()
+        for g in gathers:
+            getattr(g, stage_of)(*more)
+
+    both('own')
+    for i in range(WO_CHUNKS // 2, WO_CHUNKS):
+        wo_start(i)
     for part in BOTH:
         wo_to_partner(part, OWN)
     for copy in pair[:len(heads)]:
@@ -381,9 +389,6 @@
     def block(part, ds, df):
         return lows.at[part, place.turn(mine[part][0], ds), place.turn(mine[part][1], df)]
 
-    background = {1: lambda: (wo_start(1), ends(pair[len(heads):])), 2: both('near'), 3: lambda: wo_start(2), 4: both('row'), 5: lambda: wo_start(3),
-                  7: both('sides', *FROM, FAR)}
-
     def project(step):
         slot = lax.rem(step, 2)
 
@@ -391,8 +396,10 @@
         def _():
             ends(x_loads(step + 1))
 
-        for at, what in background.items():
-            pl.when(step == at)(lambda what=what: (what(), None)[1])
+        @pl.when(step == 2)
+        def _():
+            ends(pair[len(heads):])
+
         wait(x_loads(step))
         for i in BOTH:
             h[i * seq_len:(i + 1) * seq_len, :] = normed(xbuf[slot, i].astype(F32), gain_ref[...])
@@ -429,9 +436,12 @@
     wo_pass(0)
     low_gather.row()
     wo_pass(1)
-    low_gather.sides(*FROM, FAR)
+    low_gather.sides(*AWAY)
+    wo_pass(2)
+    low_gather.far()
+    wo_pass(3)
     wo_arrived()
-    low_gather.far()
+    both('near')
     causal = lax.broadcasted_iota(jnp.int32, (seq_len, seq_len), 0) >= lax.broadcasted_iota(jnp.int32, (seq_len, seq_len), 1)
 
     def swap(part, ds, df):
@@ -464,14 +474,14 @@
             dy, dx = side - 1 - (2 * k + i) // side, side - 1 - lax.rem(2 * k + i, side)
             for part, (ds, df) in enumerate(((dy, dx), (dx, dy))):
                 pl.when(ds != OWN)(swap(part, ds, df).start)
-        pl.when(k == 2)(wo_last)
+        pl.when(k == chips // 4)(lambda: both('row'))
 
     loop(chips // 2, attention_pair)
+    wo_last()
     for part in BOTH:
         act[part, OWN] = att[part, OWN]
-    both('far')()
+    both('sides', *AWAY)
     bulk = [remote(ref.at[place.core], ref.at[place.core], pair_send.at[len(pair) + i], pair_recv.at[len(pair) + i], place.partner) for i, ref in enumerate((a_all, b_all))]
-    ends(bulk)
     pltpu.make_async_copy(wo.at[:, :, 1], wo.at[:, :, 1], bulk_recv).wait()
     chunk = fit(width, 512)
     rows = seq_len // 2
@@ -495,6 +505,8 @@
         stage[part, :, :, width:] = pick_columns(sum_heads(part, pl.ds(width, adapters * rank)), chosen).reshape(blocks + (rank,)).astype(BF)
         for df in RING[1:]:
             fast.ready(part, df)
+    both('far')
+    ends(bulk)
     fast.finish()
     fast.store(out_ref, load_sem)
     for copy in pair[len(heads):] + bulk:
@@ -563,6 +575,7 @@
 def row_proj_kernel(side, adapters, ids_ref, act_ref, w_own, w_par, a_own, a_par, out_ref,
                     act, w, stage, near, landed, fast_near, fast_landed, slow_send, slow_recv, fast_send, fast_recv, load_sem):
     place = Place(side)
+    place.announce()
     share, width = w_own.shape
     half = w.shape[0] // 2
     rank = a_own.shape[2]
@@ -577,7 +590,6 @@
         for a in range(adapters):
             loads.append(pltpu.make_async_copy(a_part.at[a], w.at[pl.ds(at, share), pl.ds(width + a * rank, rank)], load_sem))
     ends(loads)
-    place.barrier()
     wait(loads)
     chunk = fit(width, 512)
 
@@ -602,6 +614,8 @@
     fast = FastScatter(place, lambda part, df: stage.at[part, OWN, df], fast_near, fast_landed, fast_send, fast_recv)
     for part in BOTH:
         unit(part, FAR)
+        if part == 0:
+            place.meet()
         for i in BOTH:
             for d in BOTH:
                 slow(part, PASS, d, i).start()
@@ -669,10 +683,12 @@
     return jnp.full(shape, ids_ref[place.device(0, 0)], jnp.int32)
 
 
-def gate_up_kernel(side, adapters, scale, ids_ref, sums_ref, x_ref, gain_ref, a_all, b_all, wg_own, wg_par, wu_own, wu_par, bg_own, bg_par, bu_own, bu_par,
-                   hid_ref, mid_ref, gbuf, w, b, a_ref, b_ref, hid, load_sem, b_sem, store_sem, send_sem, recv_sem):
+def gate_up_kernel(side, adapters, scale, ids_ref, sums_ref, gain_ref, x_all, a_all, b_all, wg_own, wg_par, wu_own, wu_par, bg_own, bg_par, bu_own, bu_par,
+                   hid_ref, mid_ref, gbuf, w, b, x_ref, a_ref, b_ref, hid, load_sem, a_sem, b_sem, store_sem, send_sem, recv_sem):
     place = Place(side)
-    b_load = ends([pltpu.make_async_copy(b_all.at[:, :, :, :, 0], b_ref, b_sem), pltpu.make_async_copy(a_all, a_ref, b_sem)])
+    place.announce()
+    b_load = ends([pltpu.make_async_copy(b_all.at[:, :, :, :, 0], b_ref, b_sem), pltpu.make_async_copy(x_all.at[place.device(0, 0)], x_ref, b_sem)])
+    a_load = ends([pltpu.make_async_copy(a_all, a_ref, a_sem)])
     share, width = wg_own.shape
     half = w.shape[1] // 2
     rank = bg_own.shape[2]
@@ -696,6 +712,7 @@
     mid_ref[...] = mid
     h2 = normed(mid.astype(F32), gain_ref[...])
     lows = []
+    wait(a_load)
     for core in BOTH:
         pieces = [dot_rows(h2[:, i * width // 4:(i + 1) * width // 4], a_ref[core, i // 2, :, :, i % 2].reshape(-1, width // 4)) for i in RING]
         lows.append(sum(pieces).astype(BF))
@@ -711,60 +728,62 @@
             at = (2 * part + piece) * rows
             gbuf[part, OWN, OWN, piece, :, :width] = h2[at:at + rows]
             gbuf[part, OWN, OWN, piece, :, width:] = low[at:at + rows]
-    place.barrier()
+    place.meet()
     chunk = fit(2 * half, 256)
 
-    def unit(part, ds):
-        unit_rows = len(RING) * 2 * rows
-        low = gbuf[part, ds, :, :, :, width:].reshape(unit_rows, 2 * rank).astype(F32)
-        chosen = rows_of_adapter(place, ids_ref, part, ds, (unit_rows, rank))
+    def unit(ds):
+        unit_rows = 2 * len(RING) * 2 * rows
+        low = gbuf[:, ds, :, :, :, width:].reshape(unit_rows, 2 * rank).astype(F32)
+        chosen = jnp.concatenate([rows_of_adapter(place, ids_ref, part, ds, (unit_rows // 2, rank)) for part in BOTH], axis=0)
         lows = [spread(low[:, kind * rank:(kind + 1) * rank], chosen, adapters) for kind in BOTH]
 
         def columns(n):
             at = pl.ds(pl.multiple_of(n * chunk, chunk), chunk)
-            act = gbuf[part, ds, :, :, :, :width].reshape(unit_rows, width)
+            act = gbuf[:, ds, :, :, :, :width].reshape(unit_rows, width)
             gate, up = (dot_rows(act, w[kind, at]) + scale * dot_rows(lows[kind], b[kind, at]) for kind in BOTH)
-            hid[part, ds, :, at] = (gate * jax.nn.sigmoid(gate) * up).astype(BF)
+            hid[:, ds, :, at] = (gate * jax.nn.sigmoid(gate) * up).astype(BF).reshape(2, unit_rows // 2, chunk)
 
         loop(2 * half // chunk, columns)
-        pltpu.make_async_copy(hid.at[part, ds], hid_ref.at[part, ds], store_sem).start()
+        ends([pltpu.make_async_copy(hid.at[part, ds], hid_ref.at[part, ds], store_sem) for part in BOTH])
 
     def on_row():
         wait(loads)
-        loop(2, lambda part: unit(part, OWN))
+        unit(OWN)
 
     Gather(place, lambda part, ds, df: gbuf.at[part, ds, df], send_sem, recv_sem).run(
-        on_row, lambda: loop(len(RING), lambda i: unit(lax.rem(i, 2), NEXT + 2 * (i // 2))), lambda: loop(2, lambda part: unit(part, FAR)))
+        on_row, lambda: loop(2, lambda i: unit(NEXT + 2 * i)), lambda: unit(FAR))
     pltpu.make_async_copy(hid, hid_ref, store_sem).wait()
 
 
-def gate_up(ids, sums, x_own, gain, a_all, b_all, w, side, scale, collective_id):
-    seq_len, depth = x_own.shape
+def gate_up(ids, sums, gain, x_in, a_all, b_all, w, side, scale, collective_id):
+    _, seq_len, depth = x_in.shape
     share = w[0].shape[0]
     adapters, _, rank = w[4].shape
     half = (share + LANE - 1) // LANE * LANE
     hidden = jax.ShapeDtypeStruct((2, side, side * seq_len // 2, 2 * half), BF)
     return pl.pallas_call(
         functools.partial(gate_up_kernel, side, adapters, scale),
-        out_shape=[hidden, jax.ShapeDtypeStruct(x_own.shape, BF)],
-        in_specs=[SMEM] + [VMEM] * 3 + [HBM] * (2 + len(w)),
+        out_shape=[hidden, jax.ShapeDtypeStruct((seq_len, depth), BF)],
+        in_specs=[SMEM] + [VMEM] * 2 + [HBM] * (3 + len(w)),
         out_specs=[HBM, VMEM],
         scratch_shapes=[
             pltpu.VMEM((2, side, side, 2, seq_len // 4, depth + 2 * rank), BF),
             pltpu.VMEM((2, 2 * half, depth), BF),
             pltpu.VMEM((2, 2 * half, adapters * rank), BF),
+            pltpu.VMEM((seq_len, depth), BF),
             pltpu.VMEM(a_all.shape, BF),
             pltpu.VMEM(b_all.shape[:4] + b_all.shape[5:], BF),
             pltpu.VMEM(hidden.shape, BF),
-            DMA, DMA, DMA,
+            DMA, DMA, DMA, DMA,
         ] + GATHER_SEMS,
         compiler_params=comm_params(collective_id),
         name='gate_up',
-    )(ids, sums, x_own, gain.reshape(1, depth), a_all, b_all, *w)
+    )(ids, sums, gain.reshape(1, depth), x_in, a_all, b_all, *w)
 
 
 def deliver_kernel(side, adapters, scale, ids_ref, sums_ref, x_ref, b_all, out_ref, b_ref, b_sem, pair_send, pair_recv, send_sem, recv_sem):
     place = Place(side)
+    place.announce(place.partner)
     b_load = ends([pltpu.make_async_copy(b_all.at[:, :, :, :, 1], b_ref, b_sem)])
     seq_len = sums_ref.shape[0]
     rows = seq_len // 4
@@ -775,7 +794,7 @@
         for piece in BOTH:
             at = (2 * part + piece) * rows
             out_ref[place.device(0, 0), part, piece] = y[at:at + rows]
-    place.barrier(place.partner)
+    place.meet()
 
     def block(part, ds, df):
         return out_ref.at[place.sequence(part, ds, df), part]
@@ -835,7 +854,6 @@
 
     def local_layer(x_in, adapter_ids, gain_attn, gain_mlp, w_q, w_k, w_v, w_o, w_gate, w_up, w_down, a_q, b_q, a_k, b_k, a_v, b_v, a_o, b_o, a_gate, b_gate, a_up, b_up, a_down, b_down):
         scale = ALPHA / b_q.shape[1]
-        index = lax.axis_index('tensor')
 
         def across(a):
             return a.swapaxes(-1, -2)
@@ -843,9 +861,8 @@
         heads = [w[:, 0] for w in (w_q, w_k, w_v)] + [across(a) for a in (a_q, a_k, a_v)] + [b[:, :, 0] for b in (b_q, b_k, b_v)]
         given = [across(w_gate), across(w_up), across(b_gate), across(b_up), w_down, a_down]
         sums, all_a, all_b, *kept = attend(adapter_ids, x_in, gain_attn, heads, w_o[0], a_o[:, 0], (across(a_gate), across(a_up)), (b_o, b_down), given, side, scale, 0)
-        x_own = lax.dynamic_index_in_dim(x_in, index, axis=0, keepdims=False)
         w = [piece for pair in zip(given[:4], kept[:4]) for piece in pair]
-        hidden, x_mid = gate_up(adapter_ids, sums, x_own, gain_mlp, all_a, all_b, w, side, scale, 1)
+        hidden, x_mid = gate_up(adapter_ids, sums, gain_mlp, x_in, all_a, all_b, w, side, scale, 1)
         sums = row_proj(adapter_ids, hidden, given[4], kept[4], given[5], kept[5], side, 2)
         y = deliver(adapter_ids, sums, x_mid, all_b, side, scale, 3)
         return y.reshape(x_in.shape)

time: 445 us -> 439 us (0.987)
  no operation moved by 1% of the time
where the time goes in v5:
time: 439 us
  Pallas kernels  439 us (100%)
    pallas_call x1, Pallas kernels, attend(): pl.pallas_call(functools.partial(attend_kernel, side, adapters, scale, le...  118 us
    pallas_call x1, Pallas kernels, gate_up(): pl.pallas_call(functools.partial(gate_up_kernel, side, adapters, scale),...  114 us
    pallas_call x1, Pallas kernels, row_proj(): pl.pallas_call(functools.partial(row_proj_kernel, side, adapters), out_sh...  100 us
    pallas_call x1, Pallas kernels, deliver(): pl.pallas_call(functools.partial(deliver_kernel, side, b_all.shape[1], sc...  95.5 us
    pallas_call x1, Pallas kernels, deliver(): pl.pallas_call(put_kernel, out_shape=jax.ShapeDtypeStruct(y.shape, BF), i...  10.9 us

profile of v5, /device:TPU:97, one launch (start us, length us, event | category | flops | bytes accessed | tf_op | source)
XLA Modules:
  0.0 438.8 jit_solution(1522791694590850743)
XLA Ops:
  0.0 118.0 %attend.1 = (bf16[128,4224]{1,0:T(8,128)(2,1)}, bf16[2,2,4,4,2,16,1024]{6,5,4,3,2,1,0:T(8,128)(2,1)}, bf16[2,2,4,4,2,128,128]{6,5,4,3,2,1,0:T(8,128)(2,1)}, bf16...) custom-call(s32[32]{0:T(128)} %ids_ref.7, ...), custom_call_target="tpu_custom_call" | custom-call | tf_op jit(solution)/shard_map/attend/pallas_call | solution.py:545
  118.0 114.0 %gate_up.1 = (bf16[2,4,256,768]{3,2,1,0:T(8,128)(2,1)}, bf16[128,4096]{1,0:T(8,128)(2,1)}) custom-call(s32[32]{0:T(128)} %ids_ref.7, bf16[128,4224]{1,0:T(8,128)(2,1)} %get-tuple-element.16.sums_ref, f32[1,4096]{1,0:T(1,128)} %bitcast.41, bf16[32,128,4096]{2,1,0:T(8,128)(2,1)} %x_all.1, bf16[2,2,4,4,2,16,1024]{6,5,4,3,2,1,0:T(8,128)(2,1)} %get-tuple-element.17.a_all, ...), custom_call_target="tpu_custom_call" | custom-call | tf_op jit(solution)/shard_map/gate_up/pallas_call | solution.py:764
  232.1 100.2 %row_proj.1.sums_ref = bf16[128,4224]{1,0:T(8,128)(2,1)} custom-call(s32[32]{0:T(128)} %ids_ref.7, bf16[2,4,256,768]{3,2,1,0:T(8,128)(2,1)} %get-tuple-element.23.act_ref, bf16[344,4096]{1,0:T(8,128)(2,1)} %w_own.1, bf16[344,4096]{1,0:T(8,128)(2,1)} %get-tuple-element.24.w_par, bf16[2,344,128]{2,1,0:T(8,128)(2,1)} %a_own.1, ...), custom_call_target="tpu_custom_call" | custom-call | tf_op jit(solution)/shard_map/row_proj/pallas_call | solution.py:657
  332.3 95.5 %deliver.1.y_ref = bf16[32,2,2,32,4096]{4,3,2,1,0:T(8,128)(2,1)S(1)} custom-call(s32[32]{0:T(128)} %ids_ref.7, bf16[128,4224]{1,0:T(8,128)(2,1)} %row_proj.1.sums_ref, bf16[128,4096]{1,0:T(8,128)(2,1)} %get-tuple-element.26.x_ref, bf16[2,2,4,4,2,128,128]{6,5,4,3,2,1,0:T(8,128)(2,1)} %get-tuple-element.18.b_all), custom_call_target="tpu_custom_call" | custom-call | tf_op jit(solution)/shard_map/deliver/pallas_call | solution.py:821
  427.8 10.9 %put.1 = bf16[32,2,2,32,4096]{4,3,2,1,0:T(8,128)(2,1)} custom-call(bf16[32,2,2,32,4096]{4,3,2,1,0:T(8,128)(2,1)S(1)} %deliver.1.y_ref), custom_call_target="tpu_custom_call" | custom-call | tf_op jit(solution)/shard_map/put/pallas_call | solution.py:829

commit v6 on v5

--- a/solution.py
+++ b/solution.py
@@ -17,7 +17,7 @@
 LANE = 128
 TILE = 16
 VMEM_MOST = 67043328
-VMEM_SMALL = VMEM_MOST * 3 // 8
+VMEM_SMALL = VMEM_MOST // 6
 VMEM_LEAST = VMEM_MOST // 32
 MESH = pl.DeviceIdType.MESH
 HBM = pl.BlockSpec(memory_space=pltpu.HBM)
@@ -30,6 +30,7 @@
 STEP = (NEXT, -NEXT)
 FROM = (LAST, NEXT)
 AWAY = (NEXT, LAST, FAR)
+PAIRS = ((OWN, NEXT), (LAST, FAR))
 TOWARD = (NEXT, LAST)
 FAST, SLOW = BOTH
 
@@ -158,8 +159,8 @@
                     self.arrived(part, SLOW, 0, d, j)
                     self.message(part, SLOW, 1, d, j).start()
 
-    def far(self):
-        for j in (OWN,) + AWAY:
+    def far(self, *blocks):
+        for j in blocks:
             for part in BOTH:
                 for d in BOTH:
                     self.arrived(part, SLOW, 1, d, j)
@@ -171,20 +172,6 @@
                     self.message(part, FAST, passed, d).wait_send()
                     for j in RING:
                         self.message(part, SLOW, passed, d, j).wait_send()
-
-    def run(self, on_row=None, on_sides=None, on_far=None):
-        self.own()
-        self.near()
-        self.row()
-        if on_row:
-            on_row()
-        self.sides(*AWAY)
-        if on_sides:
-            on_sides()
-        self.far()
-        if on_far:
-            on_far()
-        self.sent()
 
 
 def rows_of_adapter(place, ids_ref, part, ds, shape):
@@ -254,9 +241,10 @@
                 self.message(part, SUM, d).wait_recv()
             add(self.stage(part, OWN), self.landed.at[part, UP], self.landed.at[part, DOWN])
 
-    def store(self, out_ref, sem):
+    def store(self, out_ref):
         rows = self.landed.shape[2]
-        wait(ends([pltpu.make_async_copy(self.stage(part, OWN), out_ref.at[pl.ds(part * rows, rows)], sem) for part in BOTH]))
+        for part in BOTH:
+            out_ref[part * rows:(part + 1) * rows] = self.stage(part, OWN)[...]
         for part in BOTH:
             for kind in range(3):
                 for d in BOTH:
@@ -438,10 +426,9 @@
     wo_pass(1)
     low_gather.sides(*AWAY)
     wo_pass(2)
-    low_gather.far()
+    low_gather.far(*RING)
     wo_pass(3)
     wo_arrived()
-    both('near')
     causal = lax.broadcasted_iota(jnp.int32, (seq_len, seq_len), 0) >= lax.broadcasted_iota(jnp.int32, (seq_len, seq_len), 1)
 
     def swap(part, ds, df):
@@ -474,13 +461,12 @@
             dy, dx = side - 1 - (2 * k + i) // side, side - 1 - lax.rem(2 * k + i, side)
             for part, (ds, df) in enumerate(((dy, dx), (dx, dy))):
                 pl.when(ds != OWN)(swap(part, ds, df).start)
-        pl.when(k == chips // 4)(lambda: both('row'))
 
     loop(chips // 2, attention_pair)
+    both('near')
     wo_last()
     for part in BOTH:
         act[part, OWN] = att[part, OWN]
-    both('sides', *AWAY)
     bulk = [remote(ref.at[place.core], ref.at[place.core], pair_send.at[len(pair) + i], pair_recv.at[len(pair) + i], place.partner) for i, ref in enumerate((a_all, b_all))]
     pltpu.make_async_copy(wo.at[:, :, 1], wo.at[:, :, 1], bulk_recv).wait()
     chunk = fit(width, 512)
@@ -505,10 +491,13 @@
         stage[part, :, :, width:] = pick_columns(sum_heads(part, pl.ds(width, adapters * rank)), chosen).reshape(blocks + (rank,)).astype(BF)
         for df in RING[1:]:
             fast.ready(part, df)
-    both('far')
+        if part == 0:
+            both('row')
+    both('sides', *AWAY)
+    fast.finish()
+    both('far', *RING)
     ends(bulk)
-    fast.finish()
-    fast.store(out_ref, load_sem)
+    fast.store(out_ref)
     for copy in pair[len(heads):] + bulk:
         copy.wait_recv()
     for copy in pair + bulk:
@@ -547,7 +536,7 @@
         out_shape=[jax.ShapeDtypeStruct((seq_len, out_cols), BF), jax.ShapeDtypeStruct(every + (2 * adapters * per, depth // 4), BF),
                    jax.ShapeDtypeStruct(every + b_rows[0].shape[1:], BF)] + [jax.ShapeDtypeStruct(g.shape, g.dtype) for g in given],
         in_specs=[SMEM, HBM, VMEM, VMEM, VMEM] + [HBM] * (len(heads) + 6 + len(given)),
-        out_specs=[HBM] * (3 + len(given)),
+        out_specs=[VMEM] + [HBM] * (2 + len(given)),
         scratch_shapes=[
             pltpu.VMEM((depth, 2 * cols), BF),
             pltpu.VMEM((2, 3, adapters, per, depth), BF),
@@ -572,25 +561,12 @@
     )(ids, x_in, gain.reshape(1, depth), *tables, *heads, w_o, a_o, *a_mlp, *b_rows, *given)
 
 
-def row_proj_kernel(side, adapters, ids_ref, act_ref, w_own, w_par, a_own, a_par, out_ref,
-                    act, w, stage, near, landed, fast_near, fast_landed, slow_send, slow_recv, fast_send, fast_recv, load_sem):
+def row_proj_kernel(side, adapters, rank, ids_ref, act, w, out_ref, stage, near, landed, fast_near, fast_landed, slow_send, slow_recv, fast_send, fast_recv):
     place = Place(side)
     place.announce()
-    share, width = w_own.shape
-    half = w.shape[0] // 2
-    rank = a_own.shape[2]
-    rows = stage.shape[3]
+    rows, cols = stage.shape[3:]
     quarter = rows // 2
-    if share < half:
-        for at in (0, half):
-            w[at + share // TILE * TILE:at + half, :] = jnp.zeros((half - share // TILE * TILE, w.shape[1]), BF)
-    loads = [pltpu.make_async_copy(act_ref, act, load_sem)]
-    for at, w_part, a_part in ((0, w_own, a_own), (half, w_par, a_par)):
-        loads.append(pltpu.make_async_copy(w_part, w.at[pl.ds(at, share), first(width)], load_sem))
-        for a in range(adapters):
-            loads.append(pltpu.make_async_copy(a_part.at[a], w.at[pl.ds(at, share), pl.ds(width + a * rank, rank)], load_sem))
-    ends(loads)
-    wait(loads)
+    width = cols - rank
     chunk = fit(width, 512)
 
     def unit(part, ds):
@@ -640,7 +616,7 @@
                 add(stage.at[part, OWN, df], landed.at[part, UP, df], landed.at[part, DOWN, df])
                 fast.ready(part, df)
     fast.finish()
-    fast.store(out_ref, load_sem)
+    fast.store(out_ref)
     for part in BOTH:
         for kind in range(3):
             for d in BOTH:
@@ -648,27 +624,23 @@
                     slow(part, kind, d, i).wait_send()
 
 
-def row_proj(ids, act, w_own, w_par, a_own, a_par, side, collective_id):
-    adapters, _, rank = a_own.shape
-    width = w_own.shape[1]
+def row_proj(ids, act, w, adapters, rank, side, collective_id):
     rows = act.shape[2] // side
-    cols = width + rank
+    cols = w.shape[1] - (adapters - 1) * rank
     blocks = (rows, cols)
     return pl.pallas_call(
-        functools.partial(row_proj_kernel, side, adapters),
-        out_shape=jax.ShapeDtypeStruct((2 * rows, cols), BF),
-        in_specs=[SMEM] + [HBM] * 5,
-        out_specs=HBM,
+        functools.partial(row_proj_kernel, side, adapters, rank),
+        out_shape=pltpu.VMEM((2 * rows, cols), BF),
+        in_specs=[SMEM, VMEM, VMEM],
+        out_specs=VMEM,
         scratch_shapes=[
-            pltpu.VMEM(act.shape, BF),
-            pltpu.VMEM((act.shape[3], width + adapters * rank), BF),
             pltpu.VMEM((2, side, side) + blocks, BF),
             pltpu.VMEM((2, 2, 2) + blocks, BF),
             pltpu.VMEM((2, 2, side) + blocks, BF),
-        ] + fast_scratch(rows, cols) + [DMA((2, 3, 2, 2))] * 2 + FAST_SEMS + [DMA],
-        compiler_params=comm_params(collective_id),
+        ] + fast_scratch(rows, cols) + [DMA((2, 3, 2, 2))] * 2 + FAST_SEMS,
+        compiler_params=comm_params(collective_id, VMEM_MOST * 5 // 8),
         name='row_proj',
-    )(ids, act, w_own, w_par, a_own, a_par)
+    )(ids, act, w)
 
 
 def finish(sums_ref, resid, b_ref, chosen, scale, adapters):
@@ -684,26 +656,34 @@
 
 
 def gate_up_kernel(side, adapters, scale, ids_ref, sums_ref, gain_ref, x_all, a_all, b_all, wg_own, wg_par, wu_own, wu_par, bg_own, bg_par, bu_own, bu_par,
-                   hid_ref, mid_ref, gbuf, w, b, x_ref, a_ref, b_ref, hid, load_sem, a_sem, b_sem, store_sem, send_sem, recv_sem):
+                   wd_own, wd_par, ad_own, ad_par, hid, mid_ref, wd, gbuf, raw, w, b, x_ref, a_ref, b_ref, raw_sem, load_sem, a_sem, b_sem, wd_sem, send_sem, recv_sem):
     place = Place(side)
     place.announce()
     b_load = ends([pltpu.make_async_copy(b_all.at[:, :, :, :, 0], b_ref, b_sem), pltpu.make_async_copy(x_all.at[place.device(0, 0)], x_ref, b_sem)])
     a_load = ends([pltpu.make_async_copy(a_all, a_ref, a_sem)])
     share, width = wg_own.shape
-    half = w.shape[1] // 2
+    half = raw.shape[1]
     rank = bg_own.shape[2]
     seq_len = sums_ref.shape[0]
     edge = share // TILE * TILE
-    for at in (0, half):
+    shares = (wg_own, wg_par, wu_own, wu_par)
+
+    def raw_load(i):
+        return pltpu.make_async_copy(shares[i], raw.at[i % 2, first(share)], raw_sem.at[i % 2])
+
+    for i in BOTH:
+        raw[i, edge:] = jnp.zeros((half - edge, width), BF)
+        raw_load(i).start()
         for kind in BOTH:
-            w[kind, at + edge:at + half, :] = jnp.zeros((half - edge, width), BF)
-            b[kind, at + edge:at + half, :] = jnp.zeros((half - edge, adapters * rank), BF)
-    loads = []
-    for kind, pieces in enumerate(((wg_own, wg_par, bg_own, bg_par), (wu_own, wu_par, bu_own, bu_par))):
-        for i, at in enumerate((0, half)):
-            loads.append(pltpu.make_async_copy(pieces[i], w.at[kind, pl.ds(at, share)], load_sem))
-            for a in range(adapters):
-                loads.append(pltpu.make_async_copy(pieces[2 + i].at[a], b.at[kind, pl.ds(at, share), pl.ds(a * rank, rank)], load_sem))
+            b[kind, i * half + edge:(i + 1) * half] = jnp.zeros((half - edge, adapters * rank), BF)
+        wd[i * half + edge:(i + 1) * half] = jnp.zeros((half - edge, wd.shape[1]), BF)
+    loads, wd_loads = [], []
+    for i, at in enumerate((0, half)):
+        wd_loads.append(pltpu.make_async_copy((wd_own, wd_par)[i], wd.at[pl.ds(at, share), first(width)], wd_sem))
+        for a in range(adapters):
+            wd_loads.append(pltpu.make_async_copy((ad_own, ad_par)[i].at[a], wd.at[pl.ds(at, share), pl.ds(width + a * rank, rank)], wd_sem))
+            for kind, pair in enumerate(((bg_own, bg_par), (bu_own, bu_par))):
+                loads.append(pltpu.make_async_copy(pair[i].at[a], b.at[kind, pl.ds(at, share), pl.ds(a * rank, rank)], load_sem))
     ends(loads)
     rows = seq_len // 4
     chosen = own_rows(place, ids_ref, (seq_len, rank))
@@ -731,28 +711,45 @@
     place.meet()
     chunk = fit(2 * half, 256)
 
-    def unit(ds):
-        unit_rows = 2 * len(RING) * 2 * rows
-        low = gbuf[:, ds, :, :, :, width:].reshape(unit_rows, 2 * rank).astype(F32)
-        chosen = jnp.concatenate([rows_of_adapter(place, ids_ref, part, ds, (unit_rows // 2, rank)) for part in BOTH], axis=0)
+    def unit(ds, blocks=RING):
+        lo, hi = min(blocks), max(blocks) + 1
+        unit_rows = (hi - lo) * 2 * rows
+        low = gbuf[:, ds, lo:hi, :, :, width:].reshape(2 * unit_rows, 2 * rank).astype(F32)
+        chosen = jnp.concatenate([rows_of_adapter(place, ids_ref, part, ds, (len(RING) * 2 * rows, rank))[lo * 2 * rows:hi * 2 * rows] for part in BOTH], axis=0)
         lows = [spread(low[:, kind * rank:(kind + 1) * rank], chosen, adapters) for kind in BOTH]
 
         def columns(n):
             at = pl.ds(pl.multiple_of(n * chunk, chunk), chunk)
-            act = gbuf[:, ds, :, :, :, :width].reshape(unit_rows, width)
-            gate, up = (dot_rows(act, w[kind, at]) + scale * dot_rows(lows[kind], b[kind, at]) for kind in BOTH)
-            hid[:, ds, :, at] = (gate * jax.nn.sigmoid(gate) * up).astype(BF).reshape(2, unit_rows // 2, chunk)
+            act = gbuf[:, ds, lo:hi, :, :, :width].reshape(2 * unit_rows, width)
+            gate, up = (dot(act, w[kind, :, at]) + scale * dot_rows(lows[kind], b[kind, at]) for kind in BOTH)
+            hid[:, ds, lo * 2 * rows:hi * 2 * rows, at] = (gate * jax.nn.sigmoid(gate) * up).astype(BF).reshape(2, unit_rows, chunk)
 
         loop(2 * half // chunk, columns)
-        ends([pltpu.make_async_copy(hid.at[part, ds], hid_ref.at[part, ds], store_sem) for part in BOTH])
-
-    def on_row():
-        wait(loads)
-        unit(OWN)
-
-    Gather(place, lambda part, ds, df: gbuf.at[part, ds, df], send_sem, recv_sem).run(
-        on_row, lambda: loop(2, lambda i: unit(NEXT + 2 * i)), lambda: unit(FAR))
-    pltpu.make_async_copy(hid, hid_ref, store_sem).wait()
+
+    gather = Gather(place, lambda part, ds, df: gbuf.at[part, ds, df], send_sem, recv_sem)
+    gather.own()
+    for i in range(len(shares)):
+        raw_load(i).wait()
+
+        def turn(n):
+            at = pl.ds(pl.multiple_of(n * LANE, LANE), LANE)
+            w[i // 2, at, i % 2 * half:(i % 2 + 1) * half] = raw[i % 2, :, at].T
+
+        loop(width // LANE, turn)
+        if i + 2 < len(shares):
+            raw_load(i + 2).start()
+    gather.near()
+    gather.row()
+    ends(wd_loads)
+    wait(loads)
+    unit(OWN)
+    gather.sides(*AWAY)
+    loop(2, lambda i: unit(NEXT + 2 * i))
+    wait(wd_loads)
+    for pair in PAIRS:
+        gather.far(*pair)
+        unit(FAR, pair)
+    gather.sent()
 
 
 def gate_up(ids, sums, gain, x_in, a_all, b_all, w, side, scale, collective_id):
@@ -760,23 +757,23 @@
     share = w[0].shape[0]
     adapters, _, rank = w[4].shape
     half = (share + LANE - 1) // LANE * LANE
-    hidden = jax.ShapeDtypeStruct((2, side, side * seq_len // 2, 2 * half), BF)
+    hidden = (2, side, side * seq_len // 2, 2 * half)
     return pl.pallas_call(
         functools.partial(gate_up_kernel, side, adapters, scale),
-        out_shape=[hidden, jax.ShapeDtypeStruct((seq_len, depth), BF)],
+        out_shape=[pltpu.VMEM(hidden, BF), pltpu.VMEM((seq_len, depth), BF), pltpu.VMEM((2 * half, depth + adapters * rank), BF)],
         in_specs=[SMEM] + [VMEM] * 2 + [HBM] * (3 + len(w)),
-        out_specs=[HBM, VMEM],
+        out_specs=[VMEM] * 3,
         scratch_shapes=[
             pltpu.VMEM((2, side, side, 2, seq_len // 4, depth + 2 * rank), BF),
-            pltpu.VMEM((2, 2 * half, depth), BF),
+            pltpu.VMEM((2, half, depth), BF),
+            pltpu.VMEM((2, depth, 2 * half), BF),
             pltpu.VMEM((2, 2 * half, adapters * rank), BF),
             pltpu.VMEM((seq_len, depth), BF),
             pltpu.VMEM(a_all.shape, BF),
             pltpu.VMEM(b_all.shape[:4] + b_all.shape[5:], BF),
-            pltpu.VMEM(hidden.shape, BF),
-            DMA, DMA, DMA, DMA,
+            DMA((2,)), DMA, DMA, DMA, DMA,
         ] + GATHER_SEMS,
-        compiler_params=comm_params(collective_id),
+        compiler_params=comm_params(collective_id, VMEM_MOST * 51 // 64),
         name='gate_up',
     )(ids, sums, gain.reshape(1, depth), x_in, a_all, b_all, *w)
 
@@ -805,7 +802,13 @@
 
     for part in BOTH:
         seen(part, OWN, OWN, None)
-    Gather(place, block, send_sem, recv_sem, absolute=True, seen=seen).run()
+    gather = Gather(place, block, send_sem, recv_sem, absolute=True, seen=seen)
+    gather.own()
+    gather.near()
+    gather.row()
+    gather.sides(*AWAY)
+    gather.far(*RING)
+    gather.sent()
     every = out_ref.at[first(side * side)]
     for sem in (pair_send, pair_recv):
         pltpu.make_async_copy(every, every, sem).wait()
@@ -861,10 +864,10 @@
         heads = [w[:, 0] for w in (w_q, w_k, w_v)] + [across(a) for a in (a_q, a_k, a_v)] + [b[:, :, 0] for b in (b_q, b_k, b_v)]
         given = [across(w_gate), across(w_up), across(b_gate), across(b_up), w_down, a_down]
         sums, all_a, all_b, *kept = attend(adapter_ids, x_in, gain_attn, heads, w_o[0], a_o[:, 0], (across(a_gate), across(a_up)), (b_o, b_down), given, side, scale, 0)
-        w = [piece for pair in zip(given[:4], kept[:4]) for piece in pair]
-        hidden, x_mid = gate_up(adapter_ids, sums, gain_mlp, x_in, all_a, all_b, w, side, scale, 1)
-        sums = row_proj(adapter_ids, hidden, given[4], kept[4], given[5], kept[5], side, 2)
-        y = deliver(adapter_ids, sums, x_mid, all_b, side, scale, 3)
+        w = [piece for pair in zip(given, kept) for piece in pair]
+        hidden, x_mid, w_d = gate_up(adapter_ids, sums, gain_mlp, x_in, all_a, all_b, w, side, scale, 1)
+        sums = row_proj(adapter_ids, hidden, w_d, *a_o.shape[::3], side, 2)
+        y = deliver(adapter_ids, sums, x_mid, pltpu.with_memory_space_constraint(all_b, pltpu.HBM), side, scale, 3)
         return y.reshape(x_in.shape)
 
     return jax.shard_map(local_layer, mesh=mesh, in_specs=in_specs, out_specs=P('data', None, None), check_vma=False)

time: 439 us -> 430 us (0.979)
  Pallas kernels: 439 us -> 429 us
    pallas_call x1, Pallas kernels: 114 us -> 104 us  [gate_up(): pl.pallas_call(functools.partial(gate_up_kernel, side, adapters, scale),...]
    pallas_call x1, Pallas kernels: 100 us -> 95.8 us  [row_proj(): pl.pallas_call(functools.partial(row_proj_kernel, side, adapters, rank),...]
where the time goes in v6:
time: 430 us
  Pallas kernels  429 us (100%)
    pallas_call x1, Pallas kernels, attend(): pl.pallas_call(functools.partial(attend_kernel, side, adapters, scale, le...  122 us
    pallas_call x1, Pallas kernels, gate_up(): pl.pallas_call(functools.partial(gate_up_kernel, side, adapters, scale),...  104 us
    pallas_call x1, Pallas kernels, deliver(): pl.pallas_call(functools.partial(deliver_kernel, side, b_all.shape[1], sc...  96.6 us
    pallas_call x1, Pallas kernels, row_proj(): pl.pallas_call(functools.partial(row_proj_kernel, side, adapters, rank),...  95.8 us
    pallas_call x1, Pallas kernels, deliver(): pl.pallas_call(put_kernel, out_shape=jax.ShapeDtypeStruct(y.shape, BF), i...  10.9 us

profile of v6, /device:TPU:97, one launch (start us, length us, event | category | flops | bytes accessed | tf_op | source)
XLA Modules:
  0.0 429.6 jit_solution(9720244147330513104)
XLA Ops:
  0.0 122.1 %attend.1 = (bf16[128,4224]{1,0:T(8,128)(2,1)}, bf16[2,2,4,4,2,16,1024]{6,5,4,3,2,1,0:T(8,128)(2,1)}, bf16[2,2,4,4,2,128,128]{6,5,4,3,2,1,0:T(8,128)(2,1)}, bf16...) custom-call(s32[32]{0:T(128)} %ids_ref.7, ...), custom_call_target="tpu_custom_call" | custom-call | tf_op jit(solution)/shard_map/attend/pallas_call | solution.py:534
  122.1 0.0 copy-start
  122.1 104.1 %gate_up.1 = (bf16[2,4,256,768]{3,2,1,0:T(8,128)(2,1)S(1)}, bf16[128,4096]{1,0:T(8,128)(2,1)S(1)}, bf16[768,4352]{1,0:T(8,128)(2,1)S(1)}) custom-call(s32[32]{0:T(128)} %ids_ref.7, bf16[128,4224]{1,0:T(8,128)(2,1)} %get-tuple-element.17.sums_ref, f32[1,4096]{1,0:T(1,128)} %bitcast.42, bf16[32,128,4096]{2,1,0:T(8,128)(2,1)} %x_all.1, ...), custom_call_target="tpu_custom_call" | custom-call | tf_op jit(solution)/shard_map/gate_up/pallas_call | solution.py:761
  226.2 0.0 copy-done
  226.2 95.8 %row_proj.1.sums_ref = bf16[128,4224]{1,0:T(8,128)(2,1)S(1)} custom-call(s32[32]{0:T(128)S(1)} %copy-done, bf16[2,4,256,768]{3,2,1,0:T(8,128)(2,1)S(1)} %get-tuple-element.26.act, bf16[768,4352]{1,0:T(8,128)(2,1)S(1)} %get-tuple-element.27.w), custom_call_target="tpu_custom_call" | custom-call | tf_op jit(solution)/shard_map/row_proj/pallas_call | solution.py:631
  322.0 96.6 %deliver.1.y_ref = bf16[32,2,2,32,4096]{4,3,2,1,0:T(8,128)(2,1)S(1)} custom-call(s32[32]{0:T(128)S(1)} %copy-done, bf16[128,4224]{1,0:T(8,128)(2,1)S(1)} %row_proj.1.sums_ref, bf16[128,4096]{1,0:T(8,128)(2,1)S(1)} %get-tuple-element.28.x_ref, bf16[2,2,4,4,2,128,128]{6,5,4,3,2,1,0:T(8,128)(2,1)} %get-tuple-element.19.b_all), custom_call_target="tpu_custom_call" | custom-call | tf_op jit(solution)/shard_map/deliver/pallas_call | solution.py:824
  418.6 10.9 %put.1 = bf16[32,2,2,32,4096]{4,3,2,1,0:T(8,128)(2,1)} custom-call(bf16[32,2,2,32,4096]{4,3,2,1,0:T(8,128)(2,1)S(1)} %deliver.1.y_ref), custom_call_target="tpu_custom_call" | custom-call | tf_op jit(solution)/shard_map/put/pallas_call | solution.py:832
Async XLA Ops:
  122.1 104.1 %copy-start = (s32[32]{0:T(128)S(1)}, s32[32]{0:T(128)}, u32[]{:S(2)}) copy-start(s32[32]{0:T(128)} %ids_ref.7) | copy-start | bytes 388

commit v7 on v6

--- a/solution.py
+++ b/solution.py
@@ -277,14 +277,16 @@
     chips = side * side
     per = a_raw.shape[3]
     half_depth = depth // 4
-    heads = w_heads + a_heads + b_heads
-    spots = [[w.at[:, pl.ds(at * cols + i * head, head)] for i in range(3)] + [a_raw.at[place.core, i] for i in range(3)] + [b_raw.at[at, i] for i in range(3)]
+    heads = a_heads + b_heads + w_heads
+    spots = [[a_raw.at[place.core, i] for i in range(3)] + [b_raw.at[at, i] for i in range(3)] + [w.at[:, pl.ds(at * cols + i * head, head)] for i in range(3)]
              for at in BOTH]
+    few = len(a_heads) + len(b_heads)
+    steps = chips // 2
     loads = ends([pltpu.make_async_copy(src, dst, load_sem) for src, dst in zip(heads, spots[0])])
 
     def x_loads(step):
         slot = lax.rem(step, 2)
-        return [pltpu.make_async_copy(x_ref.at[4 * step + 2 * i + place.core], xbuf.at[slot, i], x_sem.at[slot]) for i in BOTH]
+        return [pltpu.make_async_copy(x_ref.at[4 * lax.rem(step, steps) + 2 * i + place.core], xbuf.at[slot, i], x_sem.at[slot]) for i in BOTH]
 
     ends(x_loads(0))
 
@@ -343,14 +345,16 @@
                 wo_to_partner(part, FROM[d])
 
     def wo_last():
-        for part in BOTH:
-            for d in BOTH:
-                for i in passes[d]:
-                    wo_message(part, 1, d, i).wait_recv()
-            wo_to_partner(part, FAR)
+        for k in range(WO_CHUNKS // 2):
+            for part in BOTH:
+                for d in BOTH:
+                    wo_message(part, 1, d, passes[d][k]).wait_recv()
+                    at = pl.ds(passes[d][k] * piece, piece)
+                    remote(wo.at[part, FAR, 0, at], wo.at[part, FAR, 1, at], bulk_send, bulk_recv, place.partner).start()
 
     wait(wo_loads)
-    for i in range(WO_CHUNKS // 2):
+    early = WO_CHUNKS // 2 + 1
+    for i in range(early):
         wo_start(i)
     wait(a_own)
     wait(loads)
@@ -361,40 +365,31 @@
         for g in gathers:
             getattr(g, stage_of)(*more)
 
-    both('own')
-    for i in range(WO_CHUNKS // 2, WO_CHUNKS):
-        wo_start(i)
-    for part in BOTH:
-        wo_to_partner(part, OWN)
-    for copy in pair[:len(heads)]:
+    for copy in pair[:few]:
         copy.wait_recv()
     for core in BOTH:
         pieces = [a_raw[core, i, a] if i < len(w_heads) else jnp.zeros((per, depth), BF) for a in range(adapters) for i in RING]
         a_rows[core * 2 * TILE:(core + 1) * 2 * TILE, :] = jnp.concatenate(pieces, axis=0)
     mine = [(place.y, place.x), (place.x, place.y)]
-    steps = chips // 2
 
     def block(part, ds, df):
         return lows.at[part, place.turn(mine[part][0], ds), place.turn(mine[part][1], df)]
 
-    def project(step):
+    low_gather = Gather(place, block, send_sem, recv_sem, absolute=True)
+
+    def norm(step, last):
         slot = lax.rem(step, 2)
 
-        @pl.when(step + 1 < steps)
+        @pl.when(step + 1 < last)
         def _():
             ends(x_loads(step + 1))
-
-        @pl.when(step == 2)
-        def _():
-            ends(pair[len(heads):])
 
         wait(x_loads(step))
         for i in BOTH:
             h[i * seq_len:(i + 1) * seq_len, :] = normed(xbuf[slot, i].astype(F32), gain_ref[...])
-        rows = pl.ds(pl.multiple_of(step * 2 * seq_len, LANE), 2 * seq_len)
-        chunk = fit(2 * cols, 256)
-        for n in range(2 * cols // chunk):
-            z[rows, n * chunk:(n + 1) * chunk] = dot(h[...], w[:, n * chunk:(n + 1) * chunk])
+
+    def products(step):
+        norm(step, 2 * steps)
         low = dot_rows(a_rows[...], h[...])
         half, at = step // (steps // 2), lax.rem(step, steps // 2) * 2 * seq_len
         for part in BOTH:
@@ -407,9 +402,25 @@
                 pieces.append(chosen)
             lows[part, mine[part][0], mine[part][1], half, :, pl.ds(pl.multiple_of(at, LANE), 2 * seq_len)] = jnp.concatenate(pieces, axis=1).astype(BF)
 
+    loop(steps, products)
+    low_gather.own()
+    for copy in pair[few:len(heads)]:
+        copy.wait_recv()
+    for part in BOTH:
+        wo_to_partner(part, OWN)
+    events = [lambda: ends(pair[len(heads):]), lambda: wo_start(early), low_gather.near, lambda: wo_start(early + 1), low_gather.row, lambda: wo_start(early + 2),
+              lambda: low_gather.sides(*AWAY), lambda: wo_pass(0)]
+
+    def project(step):
+        for at, what in enumerate(events):
+            pl.when(step == at)(lambda what=what: (what(), None)[1])
+        norm(step + steps, 2 * steps)
+        rows = pl.ds(pl.multiple_of(step * 2 * seq_len, LANE), 2 * seq_len)
+        chunk = fit(2 * cols, 256)
+        for n in range(2 * cols // chunk):
+            z[rows, n * chunk:(n + 1) * chunk] = dot(h[...], w[:, n * chunk:(n + 1) * chunk])
+
     loop(steps, project)
-    low_gather = Gather(place, block, send_sem, recv_sem, absolute=True)
-    low_gather.own()
     row, col = (lax.broadcasted_iota(jnp.int32, (2 * rank, rank), axis) for axis in BOTH)
     spot, kind = row // TILE, lax.rem(row, TILE) // per
     for part in BOTH:
@@ -420,15 +431,7 @@
             for a in range(adapters):
                 for o in BOTH:
                     bx[a, part, :, o * cols + i * head:o * cols + (i + 1) * head] = dot(spread_rows, b_raw[o, i, a]).astype(BF)
-    low_gather.near()
-    wo_pass(0)
-    low_gather.row()
-    wo_pass(1)
-    low_gather.sides(*AWAY)
-    wo_pass(2)
     low_gather.far(*RING)
-    wo_pass(3)
-    wo_arrived()
     causal = lax.broadcasted_iota(jnp.int32, (seq_len, seq_len), 0) >= lax.broadcasted_iota(jnp.int32, (seq_len, seq_len), 1)
 
     def swap(part, ds, df):
@@ -461,9 +464,12 @@
             dy, dx = side - 1 - (2 * k + i) // side, side - 1 - lax.rem(2 * k + i, side)
             for part, (ds, df) in enumerate(((dy, dx), (dx, dy))):
                 pl.when(ds != OWN)(swap(part, ds, df).start)
+        for i in range(1, WO_CHUNKS // 2):
+            pl.when(k == 2 * i)(lambda i=i: wo_pass(i))
 
     loop(chips // 2, attention_pair)
-    both('near')
+    wo_arrived()
+    both('own')
     wo_last()
     for part in BOTH:
         act[part, OWN] = att[part, OWN]
@@ -491,8 +497,7 @@
         stage[part, :, :, width:] = pick_columns(sum_heads(part, pl.ds(width, adapters * rank)), chosen).reshape(blocks + (rank,)).astype(BF)
         for df in RING[1:]:
             fast.ready(part, df)
-        if part == 0:
-            both('row')
+        both(('near', 'row')[part])
     both('sides', *AWAY)
     fast.finish()
     both('far', *RING)

time: 430 us -> 431 us (level)
  no operation moved by 1% of the time
where the time goes in v7:
time: 431 us; the launch traced here: 430 us
  Pallas kernels  430 us (100%)
    pallas_call x1, Pallas kernels, attend(): pl.pallas_call(functools.partial(attend_kernel, side, adapters, scale, le...  123 us
    pallas_call x1, Pallas kernels, gate_up(): pl.pallas_call(functools.partial(gate_up_kernel, side, adapters, scale),...  105 us
    pallas_call x1, Pallas kernels, row_proj(): pl.pallas_call(functools.partial(row_proj_kernel, side, adapters, rank),...  96.1 us
    pallas_call x1, Pallas kernels, deliver(): pl.pallas_call(functools.partial(deliver_kernel, side, b_all.shape[1], sc...  95.4 us
    pallas_call x1, Pallas kernels, deliver(): pl.pallas_call(put_kernel, out_shape=jax.ShapeDtypeStruct(y.shape, BF), i...  10.9 us

profile of v7, /device:TPU:97, one launch (start us, length us, event | category | flops | bytes accessed | tf_op | source)
XLA Modules:
  0.0 430.4 jit_solution(15943773202006670170)
XLA Ops:
  0.0 122.8 %attend.1 = (bf16[128,4224]{1,0:T(8,128)(2,1)}, bf16[2,2,4,4,2,16,1024]{6,5,4,3,2,1,0:T(8,128)(2,1)}, bf16[2,2,4,4,2,128,128]{6,5,4,3,2,1,0:T(8,128)(2,1)}, bf16...) custom-call(s32[32]{0:T(128)} %ids_ref.7, ...), custom_call_target="tpu_custom_call" | custom-call | tf_op jit(solution)/shard_map/attend/pallas_call | solution.py:539
  122.8 0.0 copy-start
  122.8 105.0 %gate_up.1 = (bf16[2,4,256,768]{3,2,1,0:T(8,128)(2,1)S(1)}, bf16[128,4096]{1,0:T(8,128)(2,1)S(1)}, bf16[768,4352]{1,0:T(8,128)(2,1)S(1)}) custom-call(s32[32]{0:T(128)} %ids_ref.7, bf16[128,4224]{1,0:T(8,128)(2,1)} %get-tuple-element.17.sums_ref, f32[1,4096]{1,0:T(1,128)} %bitcast.42, bf16[32,128,4096]{2,1,0:T(8,128)(2,1)} %x_all.1, ...), custom_call_target="tpu_custom_call" | custom-call | tf_op jit(solution)/shard_map/gate_up/pallas_call | solution.py:766
  227.8 0.0 copy-done
  227.8 96.1 %row_proj.1.sums_ref = bf16[128,4224]{1,0:T(8,128)(2,1)S(1)} custom-call(s32[32]{0:T(128)S(1)} %copy-done, bf16[2,4,256,768]{3,2,1,0:T(8,128)(2,1)S(1)} %get-tuple-element.26.act, bf16[768,4352]{1,0:T(8,128)(2,1)S(1)} %get-tuple-element.27.w), custom_call_target="tpu_custom_call" | custom-call | tf_op jit(solution)/shard_map/row_proj/pallas_call | solution.py:636
  323.9 95.4 %deliver.1.y_ref = bf16[32,2,2,32,4096]{4,3,2,1,0:T(8,128)(2,1)S(1)} custom-call(s32[32]{0:T(128)S(1)} %copy-done, bf16[128,4224]{1,0:T(8,128)(2,1)S(1)} %row_proj.1.sums_ref, bf16[128,4096]{1,0:T(8,128)(2,1)S(1)} %get-tuple-element.28.x_ref, bf16[2,2,4,4,2,128,128]{6,5,4,3,2,1,0:T(8,128)(2,1)} %get-tuple-element.19.b_all), custom_call_target="tpu_custom_call" | custom-call | tf_op jit(solution)/shard_map/deliver/pallas_call | solution.py:829
  419.3 10.9 %put.1 = bf16[32,2,2,32,4096]{4,3,2,1,0:T(8,128)(2,1)} custom-call(bf16[32,2,2,32,4096]{4,3,2,1,0:T(8,128)(2,1)S(1)} %deliver.1.y_ref), custom_call_target="tpu_custom_call" | custom-call | tf_op jit(solution)/shard_map/put/pallas_call | solution.py:837
Async XLA Ops:
  122.8 105.0 %copy-start = (s32[32]{0:T(128)S(1)}, s32[32]{0:T(128)}, u32[]{:S(2)}) copy-start(s32[32]{0:T(128)} %ids_ref.7) | copy-start | bytes 388

commit v8 on v7

--- a/solution.py
+++ b/solution.py
@@ -174,6 +174,64 @@
                         self.message(part, SLOW, passed, d, j).wait_send()
 
 
+ROW_SEMS = [DMA((2, 2, 2, 2))] * 2
+
+
+class RowGather:
+    def __init__(self, place, row, mine, send_sem, recv_sem):
+        self.place, self.row_at, self.mine, self.sems = place, row, mine, (send_sem, recv_sem)
+
+    def message(self, part, ring, passed, d):
+        if ring == SLOW:
+            ref = self.row_at(part, FROM[d] if passed else OWN)
+            ref = ref.at[:, d] if passed else ref
+        else:
+            ref = self.row_at(part, OWN).at[self.place.turn(self.mine(part), FROM[d] if passed else OWN)]
+            ref = ref.at[d] if passed else ref
+        return remote(ref, ref, *(sem.at[part, ring, passed, d] for sem in self.sems), self.place.neighbour(part, ring, STEP[d]))
+
+    def pass_on(self, ring, passed):
+        for part in BOTH:
+            for d in BOTH:
+                self.landing(part, ring, passed, d).wait_recv()
+                if not passed:
+                    self.message(part, ring, 1, d).start()
+            if passed and ring == FAST:
+                for d in BOTH:
+                    self.message(part, SLOW, 0, d).start()
+
+    def landing(self, part, ring, passed, d):
+        at = FAR if passed else FROM[d]
+        ref = self.row_at(part, at) if ring == SLOW else self.row_at(part, OWN).at[self.place.turn(self.mine(part), at)]
+        if passed:
+            ref = ref.at[:, d] if ring == SLOW else ref.at[d]
+        return remote(ref, ref, *(sem.at[part, ring, passed, d] for sem in self.sems), self.place.neighbour(part, ring, STEP[d]))
+
+    def own(self):
+        for d in BOTH:
+            for part in BOTH:
+                self.message(part, FAST, 0, d).start()
+
+    def near(self):
+        self.pass_on(FAST, 0)
+
+    def row(self):
+        self.pass_on(FAST, 1)
+
+    def sides(self):
+        self.pass_on(SLOW, 0)
+
+    def far(self):
+        self.pass_on(SLOW, 1)
+
+    def sent(self):
+        for part in BOTH:
+            for ring in BOTH:
+                for passed in BOTH:
+                    for d in BOTH:
+                        self.message(part, ring, passed, d).wait_send()
+
+
 def rows_of_adapter(place, ids_ref, part, ds, shape):
     block = lax.broadcasted_iota(jnp.int32, shape, 0) // (shape[0] // len(RING))
     chosen = jnp.zeros(shape, jnp.int32)
@@ -229,12 +287,14 @@
             elif df == TOWARD[d]:
                 self.message(part, FREE, d).start()
 
-    def finish(self):
+    def sum(self):
         for d in BOTH:
             for part in BOTH:
                 self.message(part, PASS, d).wait_recv()
                 add(self.stage(part, TOWARD[d]).at[self.halves[d]], self.near.at[part, d])
                 self.message(part, SUM, d).start()
+
+    def finish(self):
         for part in BOTH:
             for d in BOTH:
                 self.message(part, FREE, d).wait_recv()
@@ -259,7 +319,7 @@
     return pltpu.CompilerParams(collective_id=collective_id, has_side_effects=True, vmem_limit_bytes=limit)
 
 
-WO_CHUNKS = 8
+WO_CHUNKS = 4
 
 
 def attend_kernel(side, adapters, scale, n_keep, ids_ref, x_ref, gain_ref, cos_ref, sin_ref, *rest):
@@ -277,10 +337,10 @@
     chips = side * side
     per = a_raw.shape[3]
     half_depth = depth // 4
-    heads = a_heads + b_heads + w_heads
-    spots = [[a_raw.at[place.core, i] for i in range(3)] + [b_raw.at[at, i] for i in range(3)] + [w.at[:, pl.ds(at * cols + i * head, head)] for i in range(3)]
+    heads = a_heads + w_heads + b_heads
+    spots = [[a_raw.at[place.core, i] for i in range(3)] + [w.at[:, pl.ds(at * cols + i * head, head)] for i in range(3)] + [b_raw.at[at, i] for i in range(3)]
              for at in BOTH]
-    few = len(a_heads) + len(b_heads)
+    few = len(a_heads)
     steps = chips // 2
     loads = ends([pltpu.make_async_copy(src, dst, load_sem) for src, dst in zip(heads, spots[0])])
 
@@ -291,11 +351,16 @@
     ends(x_loads(0))
 
     def every(ref):
-        return lambda part, ds, df: ref.at[place.core, part, place.turn(place.y, df if part else ds), place.turn(place.x, ds if part else df)]
-
-    every_a, every_b = every(a_all), every(b_all)
+        return lambda part, ds: ref.at[place.core, part, :, place.turn(place.x, ds)] if part else ref.at[place.core, part, place.turn(place.y, ds)]
+
+    def spot_of(part):
+        return place.y if part else place.x
+
+    def own_of(ref, part):
+        return ref.at[place.core, part, place.y, place.x]
+
     own_loads = ends([pltpu.make_async_copy(a_mlp[i], am_raw.at[i], own_sem) for i in BOTH])
-    own_b = [pltpu.make_async_copy(b_rows[half].at[part], every_b(part, OWN, OWN).at[half], load_sem) for part in BOTH for half in BOTH]
+    own_b = [pltpu.make_async_copy(b_rows[half].at[part], own_of(b_all, part).at[half], load_sem) for part in BOTH for half in BOTH]
     ends(own_b)
     width = wo_ref.shape[1]
     rank = ao_ref.shape[2]
@@ -311,7 +376,7 @@
     pair = [remote(src, dst, pair_send.at[i], pair_recv.at[i], place.partner) for i, (src, dst) in
             enumerate(list(zip(heads, spots[1])) + list(zip(given, kept)))]
     ends(pair[:len(heads)])
-    a_own = ends([pltpu.make_async_copy(am_rows.at[:, pl.ds((2 * part + half) * half_depth, half_depth)], every_a(part, OWN, OWN).at[half], own_sem)
+    a_own = ends([pltpu.make_async_copy(am_rows.at[:, pl.ds((2 * part + half) * half_depth, half_depth)], own_of(a_all, part).at[half], own_sem)
                   for part in BOTH for half in BOTH])
 
     piece = head // WO_CHUNKS
@@ -345,25 +410,24 @@
                 wo_to_partner(part, FROM[d])
 
     def wo_last():
-        for k in range(WO_CHUNKS // 2):
-            for part in BOTH:
-                for d in BOTH:
-                    wo_message(part, 1, d, passes[d][k]).wait_recv()
-                    at = pl.ds(passes[d][k] * piece, piece)
-                    remote(wo.at[part, FAR, 0, at], wo.at[part, FAR, 1, at], bulk_send, bulk_recv, place.partner).start()
+        for part in BOTH:
+            for d in BOTH:
+                for i in passes[d]:
+                    wo_message(part, 1, d, i).wait_recv()
+            wo_to_partner(part, FAR)
 
     wait(wo_loads)
-    early = WO_CHUNKS // 2 + 1
+    early = WO_CHUNKS - 1
     for i in range(early):
         wo_start(i)
     wait(a_own)
     wait(loads)
     wait(own_b)
-    gathers = [Gather(place, every_a, a_send, a_recv, absolute=True), Gather(place, every_b, b_send, b_recv, absolute=True)]
-
-    def both(stage_of, *more):
+    gathers = [RowGather(place, every(a_all), spot_of, a_send, a_recv), RowGather(place, every(b_all), spot_of, b_send, b_recv)]
+
+    def both(stage_of):
         for g in gathers:
-            getattr(g, stage_of)(*more)
+            getattr(g, stage_of)()
 
     for copy in pair[:few]:
         copy.wait_recv()
@@ -372,10 +436,7 @@
         a_rows[core * 2 * TILE:(core + 1) * 2 * TILE, :] = jnp.concatenate(pieces, axis=0)
     mine = [(place.y, place.x), (place.x, place.y)]
 
-    def block(part, ds, df):
-        return lows.at[part, place.turn(mine[part][0], ds), place.turn(mine[part][1], df)]
-
-    low_gather = Gather(place, block, send_sem, recv_sem, absolute=True)
+    low_gather = RowGather(place, lambda part, ds: lows.at[part, place.turn(mine[part][0], ds)], spot_of, send_sem, recv_sem)
 
     def norm(step, last):
         slot = lax.rem(step, 2)
@@ -408,11 +469,10 @@
         copy.wait_recv()
     for part in BOTH:
         wo_to_partner(part, OWN)
-    events = [lambda: ends(pair[len(heads):]), lambda: wo_start(early), low_gather.near, lambda: wo_start(early + 1), low_gather.row, lambda: wo_start(early + 2),
-              lambda: low_gather.sides(*AWAY), lambda: wo_pass(0)]
+    events = {0: lambda: ends(pair[len(heads):]), 3: low_gather.near, 5: lambda: (low_gather.row(), wo_start(early))}
 
     def project(step):
-        for at, what in enumerate(events):
+        for at, what in events.items():
             pl.when(step == at)(lambda what=what: (what(), None)[1])
         norm(step + steps, 2 * steps)
         rows = pl.ds(pl.multiple_of(step * 2 * seq_len, LANE), 2 * seq_len)
@@ -431,13 +491,15 @@
             for a in range(adapters):
                 for o in BOTH:
                     bx[a, part, :, o * cols + i * head:o * cols + (i + 1) * head] = dot(spread_rows, b_raw[o, i, a]).astype(BF)
-    low_gather.far(*RING)
+    low_gather.sides()
+    wo_pass(0)
+    low_gather.far()
     causal = lax.broadcasted_iota(jnp.int32, (seq_len, seq_len), 0) >= lax.broadcasted_iota(jnp.int32, (seq_len, seq_len), 1)
 
-    def swap(part, ds, df):
-        sems = (part, ds, df)
+    def swap(part, ds):
+        sems = (part, ds)
         to = place.neighbour(part, SLOW, ds)
-        return remote(att.at[sems], act.at[part, lax.rem(len(RING) - ds, len(RING)), df], swap_send.at[sems], swap_recv.at[sems], to)
+        return remote(att.at[sems], act.at[part, lax.rem(len(RING) - ds, len(RING))], swap_send.at[sems], swap_recv.at[sems], to)
 
     def attention(i):
         dy, dx = side - 1 - i // side, side - 1 - lax.rem(i, side)
@@ -460,14 +522,13 @@
     def attention_pair(k):
         for i in BOTH:
             attention(2 * k + i)
-        for i in BOTH:
-            dy, dx = side - 1 - (2 * k + i) // side, side - 1 - lax.rem(2 * k + i, side)
-            for part, (ds, df) in enumerate(((dy, dx), (dx, dy))):
-                pl.when(ds != OWN)(swap(part, ds, df).start)
-        for i in range(1, WO_CHUNKS // 2):
-            pl.when(k == 2 * i)(lambda i=i: wo_pass(i))
+        row = side - 1 - 2 * k // side
+        pl.when((lax.rem(2 * k + 2, side) == 0) & (row != OWN))(lambda: swap(0, row).start())
+        pl.when(k == 1)(lambda: wo_pass(1))
 
     loop(chips // 2, attention_pair)
+    for ds in AWAY:
+        swap(1, ds).start()
     wo_arrived()
     both('own')
     wo_last()
@@ -484,9 +545,8 @@
         return sum(dot(act[part, s].reshape(-1, 2 * head), wo[part, s, :, :, at].reshape(2 * head, -1)) for s in RING)
 
     for part in BOTH:
-        for ds in RING[1:]:
-            for df in RING:
-                swap(part, ds, df).wait_recv()
+        for ds in AWAY:
+            swap(part, ds).wait_recv()
 
         def columns(n):
             at = pl.ds(pl.multiple_of(n * chunk, chunk), chunk)
@@ -495,13 +555,14 @@
         loop(width // chunk, columns)
         chosen = rows_of_adapter(place, ids_ref, part, OWN, (len(RING) * rows, rank))
         stage[part, :, :, width:] = pick_columns(sum_heads(part, pl.ds(width, adapters * rank)), chosen).reshape(blocks + (rank,)).astype(BF)
-        for df in RING[1:]:
+        for df in (FAR, NEXT, LAST):
             fast.ready(part, df)
         both(('near', 'row')[part])
-    both('sides', *AWAY)
+    both('sides')
+    fast.sum()
+    both('far')
+    ends(bulk)
     fast.finish()
-    both('far', *RING)
-    ends(bulk)
     fast.store(out_ref)
     for copy in pair[len(heads):] + bulk:
         copy.wait_recv()
@@ -516,9 +577,8 @@
                 wo_message(part, 0, d, i).wait_send()
             for i in passes[d]:
                 wo_message(part, 1, d, i).wait_send()
-        for ds in RING[1:]:
-            for df in RING:
-                swap(part, ds, df).wait_send()
+        for ds in AWAY:
+            swap(part, ds).wait_send()
 
 
 def attend(ids, x_in, gain, heads, w_o, a_o, a_mlp, b_rows, given, side, scale, collective_id):
@@ -559,8 +619,8 @@
         ] + fast_scratch(rows, out_cols) + [
             pltpu.VMEM((2, adapters, per, depth), BF),
             pltpu.VMEM((2 * adapters * per, depth), BF),
-            DMA((n_pair,)), DMA((n_pair,)), DMA, DMA((2,)), DMA, DMA, DMA((2, 2, 2, WO_CHUNKS)), DMA((2, 2, 2, WO_CHUNKS)), DMA, DMA, DMA((2, 4, 4)), DMA((2, 4, 4)),
-        ] + GATHER_SEMS * 3 + FAST_SEMS,
+            DMA((n_pair,)), DMA((n_pair,)), DMA, DMA((2,)), DMA, DMA, DMA((2, 2, 2, WO_CHUNKS)), DMA((2, 2, 2, WO_CHUNKS)), DMA, DMA, DMA((2, 4)), DMA((2, 4)),
+        ] + ROW_SEMS * 3 + FAST_SEMS,
         compiler_params=comm_params(collective_id),
         name='attend',
     )(ids, x_in, gain.reshape(1, depth), *tables, *heads, w_o, a_o, *a_mlp, *b_rows, *given)
@@ -620,6 +680,7 @@
                 slow(part, FREE, 1 - d, i).wait_recv()
                 add(stage.at[part, OWN, df], landed.at[part, UP, df], landed.at[part, DOWN, df])
                 fast.ready(part, df)
+    fast.sum()
     fast.finish()
     fast.store(out_ref)
     for part in BOTH:

time: 431 us -> 433 us (level)
  no operation moved by 1% of the time
where the time goes in v8:
time: 433 us; the launch traced here: 432 us
  Pallas kernels  432 us (100%)
    pallas_call x1, Pallas kernels, attend(): pl.pallas_call(functools.partial(attend_kernel, side, adapters, scale, le...  125 us
    pallas_call x1, Pallas kernels, gate_up(): pl.pallas_call(functools.partial(gate_up_kernel, side, adapters, scale),...  104 us
    pallas_call x1, Pallas kernels, deliver(): pl.pallas_call(functools.partial(deliver_kernel, side, b_all.shape[1], sc...  96.4 us
    pallas_call x1, Pallas kernels, row_proj(): pl.pallas_call(functools.partial(row_proj_kernel, side, adapters, rank),...  95.7 us
    pallas_call x1, Pallas kernels, deliver(): pl.pallas_call(put_kernel, out_shape=jax.ShapeDtypeStruct(y.shape, BF), i...  10.9 us

profile of v8, /device:TPU:97, one launch (start us, length us, event | category | flops | bytes accessed | tf_op | source)
XLA Modules:
  0.0 432.4 jit_solution(1806590104583551937)
XLA Ops:
  0.0 124.8 %attend.1 = (bf16[128,4224]{1,0:T(8,128)(2,1)}, bf16[2,2,4,4,2,16,1024]{6,5,4,3,2,1,0:T(8,128)(2,1)}, bf16[2,2,4,4,2,128,128]{6,5,4,3,2,1,0:T(8,128)(2,1)}, bf16...) custom-call(s32[32]{0:T(128)} %ids_ref.7, ...), custom_call_target="tpu_custom_call" | custom-call | tf_op jit(solution)/shard_map/attend/pallas_call | solution.py:599
  124.8 0.0 copy-start
  124.9 104.3 %gate_up.1 = (bf16[2,4,256,768]{3,2,1,0:T(8,128)(2,1)S(1)}, bf16[128,4096]{1,0:T(8,128)(2,1)S(1)}, bf16[768,4352]{1,0:T(8,128)(2,1)S(1)}) custom-call(s32[32]{0:T(128)} %ids_ref.7, bf16[128,4224]{1,0:T(8,128)(2,1)} %get-tuple-element.17.sums_ref, f32[1,4096]{1,0:T(1,128)} %bitcast.42, bf16[32,128,4096]{2,1,0:T(8,128)(2,1)} %x_all.1, ...), custom_call_target="tpu_custom_call" | custom-call | tf_op jit(solution)/shard_map/gate_up/pallas_call | solution.py:827
  229.2 0.0 copy-done
  229.2 95.7 %row_proj.1.sums_ref = bf16[128,4224]{1,0:T(8,128)(2,1)S(1)} custom-call(s32[32]{0:T(128)S(1)} %copy-done, bf16[2,4,256,768]{3,2,1,0:T(8,128)(2,1)S(1)} %get-tuple-element.26.act, bf16[768,4352]{1,0:T(8,128)(2,1)S(1)} %get-tuple-element.27.w), custom_call_target="tpu_custom_call" | custom-call | tf_op jit(solution)/shard_map/row_proj/pallas_call | solution.py:697
  324.9 96.4 %deliver.1.y_ref = bf16[32,2,2,32,4096]{4,3,2,1,0:T(8,128)(2,1)S(1)} custom-call(s32[32]{0:T(128)S(1)} %copy-done, bf16[128,4224]{1,0:T(8,128)(2,1)S(1)} %row_proj.1.sums_ref, bf16[128,4096]{1,0:T(8,128)(2,1)S(1)} %get-tuple-element.28.x_ref, bf16[2,2,4,4,2,128,128]{6,5,4,3,2,1,0:T(8,128)(2,1)} %get-tuple-element.19.b_all), custom_call_target="tpu_custom_call" | custom-call | tf_op jit(solution)/shard_map/deliver/pallas_call | solution.py:890
  421.4 10.9 %put.1 = bf16[32,2,2,32,4096]{4,3,2,1,0:T(8,128)(2,1)} custom-call(bf16[32,2,2,32,4096]{4,3,2,1,0:T(8,128)(2,1)S(1)} %deliver.1.y_ref), custom_call_target="tpu_custom_call" | custom-call | tf_op jit(solution)/shard_map/put/pallas_call | solution.py:898
Async XLA Ops:
  124.8 104.4 %copy-start = (s32[32]{0:T(128)S(1)}, s32[32]{0:T(128)}, u32[]{:S(2)}) copy-start(s32[32]{0:T(128)} %ids_ref.7) | copy-start | bytes 388

commit v9 on v8

--- a/solution.py
+++ b/solution.py
@@ -322,12 +322,10 @@
 WO_CHUNKS = 4
 
 
-def attend_kernel(side, adapters, scale, n_keep, ids_ref, x_ref, gain_ref, cos_ref, sin_ref, *rest):
+def attend_kernel(side, adapters, scale, ids_ref, x_ref, gain_ref, cos_ref, sin_ref, *rest):
     w_heads, a_heads, b_heads, (wo_ref, ao_ref), a_mlp, b_rows, rest = rest[:3], rest[3:6], rest[6:9], rest[9:11], rest[11:13], rest[13:15], rest[15:]
-    given, rest = rest[:n_keep], rest[n_keep:]
     (out_ref, a_all, b_all), rest = rest[:3], rest[3:]
-    kept, rest = rest[:n_keep], rest[n_keep:]
-    (w, a_raw, b_raw, a_rows, bx, xbuf, h, z, lows, att, act, wo, stage, near, landed, am_raw, am_rows, pair_send, pair_recv, load_sem, x_sem, own_sem,
+    (w, a_raw, b_raw, a_rows, bx, xbuf, h, z, lows, att, act, wo, stage, near, landed, am_raw, a_mine, b_mine, pair_send, pair_recv, load_sem, x_sem, own_sem,
      wo_load, wo_send, wo_recv, bulk_send, bulk_recv, swap_send, swap_recv,
      send_sem, recv_sem, a_send, a_recv, b_send, b_recv, fast_send, fast_recv) = rest
     place = Place(side)
@@ -337,12 +335,9 @@
     chips = side * side
     per = a_raw.shape[3]
     half_depth = depth // 4
-    heads = a_heads + w_heads + b_heads
-    spots = [[a_raw.at[place.core, i] for i in range(3)] + [w.at[:, pl.ds(at * cols + i * head, head)] for i in range(3)] + [b_raw.at[at, i] for i in range(3)]
-             for at in BOTH]
-    few = len(a_heads)
+    loads = ends([pltpu.make_async_copy(src, dst, load_sem) for i in range(3) for src, dst in
+                  ((a_heads[i], a_raw.at[place.core, i]), (w_heads[i], w.at[:, pl.ds(i * head, head)]), (b_heads[i], b_raw.at[0, i]))])
     steps = chips // 2
-    loads = ends([pltpu.make_async_copy(src, dst, load_sem) for src, dst in zip(heads, spots[0])])
 
     def x_loads(step):
         slot = lax.rem(step, 2)
@@ -351,17 +346,13 @@
     ends(x_loads(0))
 
     def every(ref):
-        return lambda part, ds: ref.at[place.core, part, :, place.turn(place.x, ds)] if part else ref.at[place.core, part, place.turn(place.y, ds)]
+        return lambda part, ds: ref.at[part, :, place.turn(place.x, ds)] if part else ref.at[part, place.turn(place.y, ds)]
 
     def spot_of(part):
         return place.y if part else place.x
 
-    def own_of(ref, part):
-        return ref.at[place.core, part, place.y, place.x]
-
-    own_loads = ends([pltpu.make_async_copy(a_mlp[i], am_raw.at[i], own_sem) for i in BOTH])
-    own_b = [pltpu.make_async_copy(b_rows[half].at[part], own_of(b_all, part).at[half], load_sem) for part in BOTH for half in BOTH]
-    ends(own_b)
+    own_loads = ends([pltpu.make_async_copy(a_mlp[i], am_raw.at[i], own_sem) for i in BOTH] +
+                     [pltpu.make_async_copy(b_rows[half].at[part], b_mine.at[part, place.y, place.x, half], own_sem) for part in BOTH for half in BOTH])
     width = wo_ref.shape[1]
     rank = ao_ref.shape[2]
     wo_loads = []
@@ -371,13 +362,15 @@
             wo_loads.append(pltpu.make_async_copy(ao_ref.at[a], wo.at[part, OWN, 0, :, pl.ds(width + a * rank, rank)], wo_load))
     ends(wo_loads)
     wait(own_loads)
-    am_rows[...] = jnp.concatenate([am_raw[i, a] for i in BOTH for a in range(adapters)], axis=0)
+    wait(loads)
+    am_rows = jnp.concatenate([am_raw[i, a] for i in BOTH for a in range(adapters)], axis=0)
+    for part in BOTH:
+        for half in BOTH:
+            at = (2 * part + half) * half_depth
+            a_mine[part, place.y, place.x, half] = am_rows[:, at:at + half_depth]
     place.meet()
-    pair = [remote(src, dst, pair_send.at[i], pair_recv.at[i], place.partner) for i, (src, dst) in
-            enumerate(list(zip(heads, spots[1])) + list(zip(given, kept)))]
-    ends(pair[:len(heads)])
-    a_own = ends([pltpu.make_async_copy(am_rows.at[:, pl.ds((2 * part + half) * half_depth, half_depth)], own_of(a_all, part).at[half], own_sem)
-                  for part in BOTH for half in BOTH])
+    moves = [(a_raw.at[place.core], a_raw.at[place.core]), (w.at[:, first(cols)], w.at[:, pl.ds(cols, cols)]), (b_raw.at[0], b_raw.at[1])]
+    pair = ends([remote(src, dst, pair_send.at[i], pair_recv.at[i], place.partner) for i, (src, dst) in enumerate(moves)])
 
     piece = head // WO_CHUNKS
 
@@ -420,17 +413,13 @@
     early = WO_CHUNKS - 1
     for i in range(early):
         wo_start(i)
-    wait(a_own)
-    wait(loads)
-    wait(own_b)
-    gathers = [RowGather(place, every(a_all), spot_of, a_send, a_recv), RowGather(place, every(b_all), spot_of, b_send, b_recv)]
+    gathers = [RowGather(place, every(a_mine), spot_of, a_send, a_recv), RowGather(place, every(b_mine), spot_of, b_send, b_recv)]
 
     def both(stage_of):
         for g in gathers:
             getattr(g, stage_of)()
 
-    for copy in pair[:few]:
-        copy.wait_recv()
+    pair[0].wait_recv()
     for core in BOTH:
         pieces = [a_raw[core, i, a] if i < len(w_heads) else jnp.zeros((per, depth), BF) for a in range(adapters) for i in RING]
         a_rows[core * 2 * TILE:(core + 1) * 2 * TILE, :] = jnp.concatenate(pieces, axis=0)
@@ -465,11 +454,11 @@
 
     loop(steps, products)
     low_gather.own()
-    for copy in pair[few:len(heads)]:
+    for copy in pair[1:]:
         copy.wait_recv()
     for part in BOTH:
         wo_to_partner(part, OWN)
-    events = {0: lambda: ends(pair[len(heads):]), 3: low_gather.near, 5: lambda: (low_gather.row(), wo_start(early))}
+    events = {3: low_gather.near, 5: lambda: (low_gather.row(), wo_start(early))}
 
     def project(step):
         for at, what in events.items():
@@ -534,7 +523,9 @@
     wo_last()
     for part in BOTH:
         act[part, OWN] = att[part, OWN]
-    bulk = [remote(ref.at[place.core], ref.at[place.core], pair_send.at[len(pair) + i], pair_recv.at[len(pair) + i], place.partner) for i, ref in enumerate((a_all, b_all))]
+    bulk = [remote(src, dst.at[place.core], pair_send.at[len(pair) + i], pair_recv.at[len(pair) + i], place.partner)
+            for i, (src, dst) in enumerate(((a_mine, a_all), (b_mine, b_all)))]
+    kept = [pltpu.make_async_copy(src, dst.at[place.core], load_sem) for src, dst in ((a_mine, a_all), (b_mine, b_all))]
     pltpu.make_async_copy(wo.at[:, :, 1], wo.at[:, :, 1], bulk_recv).wait()
     chunk = fit(width, 512)
     rows = seq_len // 2
@@ -562,9 +553,11 @@
     fast.sum()
     both('far')
     ends(bulk)
+    ends(kept)
     fast.finish()
     fast.store(out_ref)
-    for copy in pair[len(heads):] + bulk:
+    wait(kept)
+    for copy in bulk:
         copy.wait_recv()
     for copy in pair + bulk:
         copy.wait_send()
@@ -581,7 +574,7 @@
             swap(part, ds).wait_send()
 
 
-def attend(ids, x_in, gain, heads, w_o, a_o, a_mlp, b_rows, given, side, scale, collective_id):
+def attend(ids, x_in, gain, heads, w_o, a_o, a_mlp, b_rows, side, scale, collective_id):
     _, seq_len, depth = x_in.shape
     head = heads[0].shape[1]
     cols = 3 * head
@@ -593,15 +586,15 @@
     angle = np.arange(seq_len)[:, None] * inv_freq[None, :]
     cos, sin = np.cos(angle), np.sin(angle)
     tables = [jnp.asarray(np.concatenate(pair, axis=1), F32) for pair in ((cos, cos), (-sin, sin))]
-    n_pair = len(heads) + len(given) + 2
+    n_pair = 3 + 2
     rows, out_cols = seq_len // 2, depth + rank
     every = (2, 2, side, side, 2)
     return pl.pallas_call(
-        functools.partial(attend_kernel, side, adapters, scale, len(given)),
+        functools.partial(attend_kernel, side, adapters, scale),
         out_shape=[jax.ShapeDtypeStruct((seq_len, out_cols), BF), jax.ShapeDtypeStruct(every + (2 * adapters * per, depth // 4), BF),
-                   jax.ShapeDtypeStruct(every + b_rows[0].shape[1:], BF)] + [jax.ShapeDtypeStruct(g.shape, g.dtype) for g in given],
-        in_specs=[SMEM, HBM, VMEM, VMEM, VMEM] + [HBM] * (len(heads) + 6 + len(given)),
-        out_specs=[VMEM] + [HBM] * (2 + len(given)),
+                   jax.ShapeDtypeStruct(every + b_rows[0].shape[1:], BF)],
+        in_specs=[SMEM, HBM, VMEM, VMEM, VMEM] + [HBM] * (len(heads) + 6),
+        out_specs=[VMEM] + [HBM] * 2,
         scratch_shapes=[
             pltpu.VMEM((depth, 2 * cols), BF),
             pltpu.VMEM((2, 3, adapters, per, depth), BF),
@@ -618,12 +611,13 @@
             pltpu.VMEM((2, side, rows, out_cols), BF),
         ] + fast_scratch(rows, out_cols) + [
             pltpu.VMEM((2, adapters, per, depth), BF),
-            pltpu.VMEM((2 * adapters * per, depth), BF),
+            pltpu.VMEM(every[1:] + (2 * adapters * per, depth // 4), BF),
+            pltpu.VMEM(every[1:] + b_rows[0].shape[1:], BF),
             DMA((n_pair,)), DMA((n_pair,)), DMA, DMA((2,)), DMA, DMA, DMA((2, 2, 2, WO_CHUNKS)), DMA((2, 2, 2, WO_CHUNKS)), DMA, DMA, DMA((2, 4)), DMA((2, 4)),
         ] + ROW_SEMS * 3 + FAST_SEMS,
         compiler_params=comm_params(collective_id),
         name='attend',
-    )(ids, x_in, gain.reshape(1, depth), *tables, *heads, w_o, a_o, *a_mlp, *b_rows, *given)
+    )(ids, x_in, gain.reshape(1, depth), *tables, *heads, w_o, a_o, *a_mlp, *b_rows)
 
 
 def row_proj_kernel(side, adapters, rank, ids_ref, act, w, out_ref, stage, near, landed, fast_near, fast_landed, slow_send, slow_recv, fast_send, fast_recv):
@@ -721,36 +715,37 @@
     return jnp.full(shape, ids_ref[place.device(0, 0)], jnp.int32)
 
 
-def gate_up_kernel(side, adapters, scale, ids_ref, sums_ref, gain_ref, x_all, a_all, b_all, wg_own, wg_par, wu_own, wu_par, bg_own, bg_par, bu_own, bu_par,
-                   wd_own, wd_par, ad_own, ad_par, hid, mid_ref, wd, gbuf, raw, w, b, x_ref, a_ref, b_ref, raw_sem, load_sem, a_sem, b_sem, wd_sem, send_sem, recv_sem):
+def gate_up_kernel(side, adapters, scale, ids_ref, sums_ref, gain_ref, x_all, a_all, b_all, wg_ref, wu_ref, bg_ref, bu_ref, wd_ref, ad_ref,
+                   hid, mid_ref, wd, gbuf, raw, w, b, x_ref, a_ref, b_ref, raw_sem, load_sem, a_sem, b_sem, credit, pair_send, pair_recv, send_sem, recv_sem):
     place = Place(side)
-    place.announce()
-    b_load = ends([pltpu.make_async_copy(b_all.at[:, :, :, :, 0], b_ref, b_sem), pltpu.make_async_copy(x_all.at[place.device(0, 0)], x_ref, b_sem)])
-    a_load = ends([pltpu.make_async_copy(a_all, a_ref, a_sem)])
-    share, width = wg_own.shape
+    share, width = wg_ref.shape
     half = raw.shape[1]
-    rank = bg_own.shape[2]
+    rank = bg_ref.shape[2]
     seq_len = sums_ref.shape[0]
     edge = share // TILE * TILE
-    shares = (wg_own, wg_par, wu_own, wu_par)
-
-    def raw_load(i):
-        return pltpu.make_async_copy(shares[i], raw.at[i % 2, first(share)], raw_sem.at[i % 2])
-
     for i in BOTH:
         raw[i, edge:] = jnp.zeros((half - edge, width), BF)
-        raw_load(i).start()
         for kind in BOTH:
             b[kind, i * half + edge:(i + 1) * half] = jnp.zeros((half - edge, adapters * rank), BF)
         wd[i * half + edge:(i + 1) * half] = jnp.zeros((half - edge, wd.shape[1]), BF)
-    loads, wd_loads = [], []
-    for i, at in enumerate((0, half)):
-        wd_loads.append(pltpu.make_async_copy((wd_own, wd_par)[i], wd.at[pl.ds(at, share), first(width)], wd_sem))
-        for a in range(adapters):
-            wd_loads.append(pltpu.make_async_copy((ad_own, ad_par)[i].at[a], wd.at[pl.ds(at, share), pl.ds(width + a * rank, rank)], wd_sem))
-            for kind, pair in enumerate(((bg_own, bg_par), (bu_own, bu_par))):
-                loads.append(pltpu.make_async_copy(pair[i].at[a], b.at[kind, pl.ds(at, share), pl.ds(a * rank, rank)], load_sem))
+    place.announce(place.partner)
+    b_load = ends([pltpu.make_async_copy(b_all.at[:, :, :, :, 0], b_ref, b_sem), pltpu.make_async_copy(x_all.at[place.device(0, 0)], x_ref, b_sem)])
+    a_load = ends([pltpu.make_async_copy(a_all, a_ref, a_sem)])
+    mine = first(share)
+
+    def raw_load(kind):
+        return pltpu.make_async_copy((wg_ref, wu_ref)[kind], raw.at[0, mine], raw_sem)
+
+    raw_load(0).start()
+    loads = [pltpu.make_async_copy(wd_ref, wd.at[mine, first(width)], load_sem)]
+    for a in range(adapters):
+        loads.append(pltpu.make_async_copy(ad_ref.at[a], wd.at[mine, pl.ds(width + a * rank, rank)], load_sem))
+        for kind, ref in enumerate((bg_ref, bu_ref)):
+            loads.append(pltpu.make_async_copy(ref.at[a], b.at[kind, mine, pl.ds(a * rank, rank)], load_sem))
     ends(loads)
+    other = pl.ds(half, share)
+    moves = [(raw.at[0, mine], raw.at[1, mine])] * 2 + [(wd.at[mine], wd.at[other])] + [(b.at[kind, mine], b.at[kind, other]) for kind in BOTH]
+    pair = [remote(src, dst, pair_send.at[i], pair_recv.at[i], place.partner) for i, (src, dst) in enumerate(moves)]
     rows = seq_len // 4
     chosen = own_rows(place, ids_ref, (seq_len, rank))
     wait(b_load)
@@ -794,34 +789,47 @@
 
     gather = Gather(place, lambda part, ds, df: gbuf.at[part, ds, df], send_sem, recv_sem)
     gather.own()
-    for i in range(len(shares)):
-        raw_load(i).wait()
-
+    def turned(kind, i):
         def turn(n):
             at = pl.ds(pl.multiple_of(n * LANE, LANE), LANE)
-            w[i // 2, at, i % 2 * half:(i % 2 + 1) * half] = raw[i % 2, :, at].T
+            w[kind, at, i * half:(i + 1) * half] = raw[i, :, at].T
 
         loop(width // LANE, turn)
-        if i + 2 < len(shares):
-            raw_load(i + 2).start()
+
+    for kind in BOTH:
+        raw_load(kind).wait()
+        if kind:
+            pl.semaphore_wait(credit, 1)
+        pair[kind].start()
+        turned(kind, 0)
+        if kind == 0:
+            wait(loads)
+            ends(pair[2:])
+        pair[kind].wait_recv()
+        turned(kind, 1)
+        pair[kind].wait_send()
+        if kind == 0:
+            pl.semaphore_signal(credit, inc=1, device_id={'tensor': place.partner}, device_id_type=MESH)
+            raw_load(1).start()
     gather.near()
     gather.row()
-    ends(wd_loads)
-    wait(loads)
+    for copy in pair[2:]:
+        copy.wait_recv()
     unit(OWN)
     gather.sides(*AWAY)
     loop(2, lambda i: unit(NEXT + 2 * i))
-    wait(wd_loads)
-    for pair in PAIRS:
-        gather.far(*pair)
-        unit(FAR, pair)
+    for blocks in PAIRS:
+        gather.far(*blocks)
+        unit(FAR, blocks)
     gather.sent()
+    for copy in pair[2:]:
+        copy.wait_send()
 
 
 def gate_up(ids, sums, gain, x_in, a_all, b_all, w, side, scale, collective_id):
     _, seq_len, depth = x_in.shape
     share = w[0].shape[0]
-    adapters, _, rank = w[4].shape
+    adapters, _, rank = w[2].shape
     half = (share + LANE - 1) // LANE * LANE
     hidden = (2, side, side * seq_len // 2, 2 * half)
     return pl.pallas_call(
@@ -837,7 +845,7 @@
             pltpu.VMEM((seq_len, depth), BF),
             pltpu.VMEM(a_all.shape, BF),
             pltpu.VMEM(b_all.shape[:4] + b_all.shape[5:], BF),
-            DMA((2,)), DMA, DMA, DMA, DMA,
+            DMA, DMA, DMA, DMA, pltpu.SemaphoreType.REGULAR, DMA((5,)), DMA((5,)),
         ] + GATHER_SEMS,
         compiler_params=comm_params(collective_id, VMEM_MOST * 51 // 64),
         name='gate_up',
@@ -928,9 +936,9 @@
             return a.swapaxes(-1, -2)
 
         heads = [w[:, 0] for w in (w_q, w_k, w_v)] + [across(a) for a in (a_q, a_k, a_v)] + [b[:, :, 0] for b in (b_q, b_k, b_v)]
-        given = [across(w_gate), across(w_up), across(b_gate), across(b_up), w_down, a_down]
-        sums, all_a, all_b, *kept = attend(adapter_ids, x_in, gain_attn, heads, w_o[0], a_o[:, 0], (across(a_gate), across(a_up)), (b_o, b_down), given, side, scale, 0)
-        w = [piece for pair in zip(given, kept) for piece in pair]
+        sums, all_a, all_b = attend(adapter_ids, x_in, gain_attn, heads, w_o[0], a_o[:, 0], (across(a_gate), across(a_up)), (b_o, b_down), side, scale, 0)
+
+        w = [across(w_gate), across(w_up), across(b_gate), across(b_up), w_down, a_down]
         hidden, x_mid, w_d = gate_up(adapter_ids, sums, gain_mlp, x_in, all_a, all_b, w, side, scale, 1)
         sums = row_proj(adapter_ids, hidden, w_d, *a_o.shape[::3], side, 2)
         y = deliver(adapter_ids, sums, x_mid, pltpu.with_memory_space_constraint(all_b, pltpu.HBM), side, scale, 3)

time: 433 us -> 432 us (level)
  no operation moved by 1% of the time
where the time goes in v9:
time: 432 us
  Pallas kernels  432 us (100%)
    pallas_call x1, Pallas kernels, attend(): pl.pallas_call(functools.partial(attend_kernel, side, adapters, scale), o...  124 us
    pallas_call x1, Pallas kernels, gate_up(): pl.pallas_call(functools.partial(gate_up_kernel, side, adapters, scale),...  104 us
    pallas_call x1, Pallas kernels, deliver(): pl.pallas_call(functools.partial(deliver_kernel, side, b_all.shape[1], sc...  96.4 us
    pallas_call x1, Pallas kernels, row_proj(): pl.pallas_call(functools.partial(row_proj_kernel, side, adapters, rank),...  95.9 us
    pallas_call x1, Pallas kernels, deliver(): pl.pallas_call(put_kernel, out_shape=jax.ShapeDtypeStruct(y.shape, BF), i...  10.9 us

profile of v9, /device:TPU:97, one launch (start us, length us, event | category | flops | bytes accessed | tf_op | source)
XLA Modules:
  0.0 431.7 jit_solution(9856665653237379324)
XLA Ops:
  0.0 124.2 %attend.1 = (bf16[128,4224]{1,0:T(8,128)(2,1)}, bf16[2,2,4,4,2,16,1024]{6,5,4,3,2,1,0:T(8,128)(2,1)}, bf16[2,2,4,4,2,128,128]{6,5,4,3,2,1,0:T(8,128)(2,1)}) custom-call(s32[32]{0:T(128)} %ids_ref.7, bf16[32,128,4096]{2,1,0:T(8,128)(2,1)} %x_all.1, f32[1,4096]{1,0:T(1,128)} %bitcast.37, f32[128,128]{1,0:T(8,128)} %constant.4.clone.cos_ref, ...), custom_call_target="tpu_custom_call" | custom-call | tf_op jit(solution)/shard_map/attend/pallas_call | solution.py:592
  124.2 0.0 copy-start
  124.2 104.2 %gate_up.1 = (bf16[2,4,256,768]{3,2,1,0:T(8,128)(2,1)S(1)}, bf16[128,4096]{1,0:T(8,128)(2,1)S(1)}, bf16[768,4352]{1,0:T(8,128)(2,1)S(1)}) custom-call(s32[32]{0:T(128)} %ids_ref.7, bf16[128,4224]{1,0:T(8,128)(2,1)} %get-tuple-element.11.sums_ref, f32[1,4096]{1,0:T(1,128)} %bitcast.38, bf16[32,128,4096]{2,1,0:T(8,128)(2,1)} %x_all.1, ...), custom_call_target="tpu_custom_call" | custom-call | tf_op jit(solution)/shard_map/gate_up/pallas_call | solution.py:835
  228.4 0.0 copy-done
  228.4 95.9 %row_proj.1.sums_ref = bf16[128,4224]{1,0:T(8,128)(2,1)S(1)} custom-call(s32[32]{0:T(128)S(1)} %copy-done, bf16[2,4,256,768]{3,2,1,0:T(8,128)(2,1)S(1)} %get-tuple-element.14.act, bf16[768,4352]{1,0:T(8,128)(2,1)S(1)} %get-tuple-element.15.w), custom_call_target="tpu_custom_call" | custom-call | tf_op jit(solution)/shard_map/row_proj/pallas_call | solution.py:691
  324.3 96.4 %deliver.1.y_ref = bf16[32,2,2,32,4096]{4,3,2,1,0:T(8,128)(2,1)S(1)} custom-call(s32[32]{0:T(128)S(1)} %copy-done, bf16[128,4224]{1,0:T(8,128)(2,1)S(1)} %row_proj.1.sums_ref, bf16[128,4096]{1,0:T(8,128)(2,1)S(1)} %get-tuple-element.16.x_ref, bf16[2,2,4,4,2,128,128]{6,5,4,3,2,1,0:T(8,128)(2,1)} %get-tuple-element.13.b_all), custom_call_target="tpu_custom_call" | custom-call | tf_op jit(solution)/shard_map/deliver/pallas_call | solution.py:898
  420.7 10.9 %put.1 = bf16[32,2,2,32,4096]{4,3,2,1,0:T(8,128)(2,1)} custom-call(bf16[32,2,2,32,4096]{4,3,2,1,0:T(8,128)(2,1)S(1)} %deliver.1.y_ref), custom_call_target="tpu_custom_call" | custom-call | tf_op jit(solution)/shard_map/put/pallas_call | solution.py:906
Async XLA Ops:
  124.2 104.2 %copy-start = (s32[32]{0:T(128)S(1)}, s32[32]{0:T(128)}, u32[]{:S(2)}) copy-start(s32[32]{0:T(128)} %ids_ref.7) | copy-start | bytes 388

commit v10 on v9

--- a/solution.py
+++ b/solution.py
@@ -326,7 +326,7 @@
     w_heads, a_heads, b_heads, (wo_ref, ao_ref), a_mlp, b_rows, rest = rest[:3], rest[3:6], rest[6:9], rest[9:11], rest[11:13], rest[13:15], rest[15:]
     (out_ref, a_all, b_all), rest = rest[:3], rest[3:]
     (w, a_raw, b_raw, a_rows, bx, xbuf, h, z, lows, att, act, wo, stage, near, landed, am_raw, a_mine, b_mine, pair_send, pair_recv, load_sem, x_sem, own_sem,
-     wo_load, wo_send, wo_recv, bulk_send, bulk_recv, swap_send, swap_recv,
+     kept_sem, hand_send, hand_recv, wo_load, wo_send, wo_recv, bulk_send, bulk_recv, swap_send, swap_recv,
      send_sem, recv_sem, a_send, a_recv, b_send, b_recv, fast_send, fast_recv) = rest
     place = Place(side)
     place.announce(place.partner, place.device(0, FAR), place.device(FAR, 0))
@@ -410,15 +410,24 @@
             wo_to_partner(part, FAR)
 
     wait(wo_loads)
-    early = WO_CHUNKS - 1
-    for i in range(early):
-        wo_start(i)
+    early = WO_CHUNKS // 2
     gathers = [RowGather(place, every(a_mine), spot_of, a_send, a_recv), RowGather(place, every(b_mine), spot_of, b_send, b_recv)]
 
     def both(stage_of):
         for g in gathers:
             getattr(g, stage_of)()
 
+    def hand(*distances):
+        for ds in distances:
+            for part in BOTH:
+                for i, dst in enumerate((a_all, b_all)):
+                    here, there = gathers[i].row_at(part, ds), every(dst.at[place.core])(part, ds)
+                    pltpu.make_async_copy(here, there, kept_sem.at[i]).start()
+                    remote(here, there, hand_send.at[i], hand_recv.at[i], place.partner).start()
+
+    both('own')
+    for i in range(early):
+        wo_start(i)
     pair[0].wait_recv()
     for core in BOTH:
         pieces = [a_raw[core, i, a] if i < len(w_heads) else jnp.zeros((per, depth), BF) for a in range(adapters) for i in RING]
@@ -439,6 +448,7 @@
             h[i * seq_len:(i + 1) * seq_len, :] = normed(xbuf[slot, i].astype(F32), gain_ref[...])
 
     def products(step):
+        pl.when(step == 3)(lambda: both('near'))
         norm(step, 2 * steps)
         low = dot_rows(a_rows[...], h[...])
         half, at = step // (steps // 2), lax.rem(step, steps // 2) * 2 * seq_len
@@ -458,7 +468,7 @@
         copy.wait_recv()
     for part in BOTH:
         wo_to_partner(part, OWN)
-    events = {3: low_gather.near, 5: lambda: (low_gather.row(), wo_start(early))}
+    events = {1: lambda: wo_start(early), 4: lambda: (low_gather.near(), wo_start(early + 1)), 7: low_gather.row}
 
     def project(step):
         for at, what in events.items():
@@ -482,6 +492,7 @@
                     bx[a, part, :, o * cols + i * head:o * cols + (i + 1) * head] = dot(spread_rows, b_raw[o, i, a]).astype(BF)
     low_gather.sides()
     wo_pass(0)
+    wo_pass(1)
     low_gather.far()
     causal = lax.broadcasted_iota(jnp.int32, (seq_len, seq_len), 0) >= lax.broadcasted_iota(jnp.int32, (seq_len, seq_len), 1)
 
@@ -513,19 +524,16 @@
             attention(2 * k + i)
         row = side - 1 - 2 * k // side
         pl.when((lax.rem(2 * k + 2, side) == 0) & (row != OWN))(lambda: swap(0, row).start())
-        pl.when(k == 1)(lambda: wo_pass(1))
 
     loop(chips // 2, attention_pair)
     for ds in AWAY:
         swap(1, ds).start()
+    both('row')
+    hand(OWN)
     wo_arrived()
-    both('own')
     wo_last()
     for part in BOTH:
         act[part, OWN] = att[part, OWN]
-    bulk = [remote(src, dst.at[place.core], pair_send.at[len(pair) + i], pair_recv.at[len(pair) + i], place.partner)
-            for i, (src, dst) in enumerate(((a_mine, a_all), (b_mine, b_all)))]
-    kept = [pltpu.make_async_copy(src, dst.at[place.core], load_sem) for src, dst in ((a_mine, a_all), (b_mine, b_all))]
     pltpu.make_async_copy(wo.at[:, :, 1], wo.at[:, :, 1], bulk_recv).wait()
     chunk = fit(width, 512)
     rows = seq_len // 2
@@ -548,18 +556,17 @@
         stage[part, :, :, width:] = pick_columns(sum_heads(part, pl.ds(width, adapters * rank)), chosen).reshape(blocks + (rank,)).astype(BF)
         for df in (FAR, NEXT, LAST):
             fast.ready(part, df)
-        both(('near', 'row')[part])
     both('sides')
+    hand(NEXT, LAST)
     fast.sum()
     both('far')
-    ends(bulk)
-    ends(kept)
+    hand(FAR)
     fast.finish()
     fast.store(out_ref)
-    wait(kept)
-    for copy in bulk:
-        copy.wait_recv()
-    for copy in pair + bulk:
+    for sem in (kept_sem, hand_send, hand_recv):
+        for i, ref in enumerate((a_mine, b_mine)):
+            pltpu.make_async_copy(ref, ref, sem.at[i]).wait()
+    for copy in pair:
         copy.wait_send()
     for g in gathers + [low_gather]:
         g.sent()
@@ -586,7 +593,7 @@
     angle = np.arange(seq_len)[:, None] * inv_freq[None, :]
     cos, sin = np.cos(angle), np.sin(angle)
     tables = [jnp.asarray(np.concatenate(pair, axis=1), F32) for pair in ((cos, cos), (-sin, sin))]
-    n_pair = 3 + 2
+    n_pair = 3
     rows, out_cols = seq_len // 2, depth + rank
     every = (2, 2, side, side, 2)
     return pl.pallas_call(
@@ -613,7 +620,7 @@
             pltpu.VMEM((2, adapters, per, depth), BF),
             pltpu.VMEM(every[1:] + (2 * adapters * per, depth // 4), BF),
             pltpu.VMEM(every[1:] + b_rows[0].shape[1:], BF),
-            DMA((n_pair,)), DMA((n_pair,)), DMA, DMA((2,)), DMA, DMA, DMA((2, 2, 2, WO_CHUNKS)), DMA((2, 2, 2, WO_CHUNKS)), DMA, DMA, DMA((2, 4)), DMA((2, 4)),
+            DMA((n_pair,)), DMA((n_pair,)), DMA, DMA((2,)), DMA, DMA((2,)), DMA((2,)), DMA((2,)), DMA, DMA((2, 2, 2, WO_CHUNKS)), DMA((2, 2, 2, WO_CHUNKS)), DMA, DMA, DMA((2, 4)), DMA((2, 4)),
         ] + ROW_SEMS * 3 + FAST_SEMS,
         compiler_params=comm_params(collective_id),
         name='attend',

time: 432 us -> 424 us (0.981)
  Pallas kernels: 432 us -> 423 us
    pallas_call x1, Pallas kernels: 124 us -> 112 us  [attend(): pl.pallas_call(functools.partial(attend_kernel, side, adapters, scale), o...]
where the time goes in v10:
time: 424 us; the launch traced here: 423 us
  Pallas kernels  423 us (100%)
    pallas_call x1, Pallas kernels, attend(): pl.pallas_call(functools.partial(attend_kernel, side, adapters, scale), o...  112 us
    pallas_call x1, Pallas kernels, gate_up(): pl.pallas_call(functools.partial(gate_up_kernel, side, adapters, scale),...  106 us
    pallas_call x1, Pallas kernels, row_proj(): pl.pallas_call(functools.partial(row_proj_kernel, side, adapters, rank),...  98.5 us
    pallas_call x1, Pallas kernels, deliver(): pl.pallas_call(functools.partial(deliver_kernel, side, b_all.shape[1], sc...  95.3 us
    pallas_call x1, Pallas kernels, deliver(): pl.pallas_call(put_kernel, out_shape=jax.ShapeDtypeStruct(y.shape, BF), i...  10.9 us

profile of v10, /device:TPU:97, one launch (start us, length us, event | category | flops | bytes accessed | tf_op | source)
XLA Modules:
  0.0 423.4 jit_solution(15498534646834740986)
XLA Ops:
  0.0 112.3 %attend.1 = (bf16[128,4224]{1,0:T(8,128)(2,1)}, bf16[2,2,4,4,2,16,1024]{6,5,4,3,2,1,0:T(8,128)(2,1)}, bf16[2,2,4,4,2,128,128]{6,5,4,3,2,1,0:T(8,128)(2,1)}) custom-call(s32[32]{0:T(128)} %ids_ref.7, bf16[32,128,4096]{2,1,0:T(8,128)(2,1)} %x_all.1, f32[1,4096]{1,0:T(1,128)} %bitcast.37, f32[128,128]{1,0:T(8,128)} %constant.4.clone.cos_ref, ...), custom_call_target="tpu_custom_call" | custom-call | tf_op jit(solution)/shard_map/attend/pallas_call | solution.py:599
  112.3 0.0 copy-start
  112.3 106.2 %gate_up.1 = (bf16[2,4,256,768]{3,2,1,0:T(8,128)(2,1)S(1)}, bf16[128,4096]{1,0:T(8,128)(2,1)S(1)}, bf16[768,4352]{1,0:T(8,128)(2,1)S(1)}) custom-call(s32[32]{0:T(128)} %ids_ref.7, bf16[128,4224]{1,0:T(8,128)(2,1)} %get-tuple-element.11.sums_ref, f32[1,4096]{1,0:T(1,128)} %bitcast.38, bf16[32,128,4096]{2,1,0:T(8,128)(2,1)} %x_all.1, ...), custom_call_target="tpu_custom_call" | custom-call | tf_op jit(solution)/shard_map/gate_up/pallas_call | solution.py:842
  218.5 0.0 copy-done
  218.6 98.5 %row_proj.1.sums_ref = bf16[128,4224]{1,0:T(8,128)(2,1)S(1)} custom-call(s32[32]{0:T(128)S(1)} %copy-done, bf16[2,4,256,768]{3,2,1,0:T(8,128)(2,1)S(1)} %get-tuple-element.14.act, bf16[768,4352]{1,0:T(8,128)(2,1)S(1)} %get-tuple-element.15.w), custom_call_target="tpu_custom_call" | custom-call | tf_op jit(solution)/shard_map/row_proj/pallas_call | solution.py:698
  317.1 95.3 %deliver.1.y_ref = bf16[32,2,2,32,4096]{4,3,2,1,0:T(8,128)(2,1)S(1)} custom-call(s32[32]{0:T(128)S(1)} %copy-done, bf16[128,4224]{1,0:T(8,128)(2,1)S(1)} %row_proj.1.sums_ref, bf16[128,4096]{1,0:T(8,128)(2,1)S(1)} %get-tuple-element.16.x_ref, bf16[2,2,4,4,2,128,128]{6,5,4,3,2,1,0:T(8,128)(2,1)} %get-tuple-element.13.b_all), custom_call_target="tpu_custom_call" | custom-call | tf_op jit(solution)/shard_map/deliver/pallas_call | solution.py:905
  412.4 10.9 %put.1 = bf16[32,2,2,32,4096]{4,3,2,1,0:T(8,128)(2,1)} custom-call(bf16[32,2,2,32,4096]{4,3,2,1,0:T(8,128)(2,1)S(1)} %deliver.1.y_ref), custom_call_target="tpu_custom_call" | custom-call | tf_op jit(solution)/shard_map/put/pallas_call | solution.py:913
Async XLA Ops:
  112.3 106.2 %copy-start = (s32[32]{0:T(128)S(1)}, s32[32]{0:T(128)}, u32[]{:S(2)}) copy-start(s32[32]{0:T(128)} %ids_ref.7) | copy-start | bytes 388

commit v11 on v10

--- a/solution.py
+++ b/solution.py
@@ -95,6 +95,12 @@
     def sequence(self, part, ds, df):
         return self.device(jnp.where(part == 0, ds, df), jnp.where(part == 0, df, ds))
 
+    def rows(self, ref):
+        return lambda part, ds: ref.at[part, :, self.turn(self.x, ds)] if part else ref.at[part, self.turn(self.y, ds)]
+
+    def spot(self, part):
+        return self.y if part else self.x
+
     def announce(self, *more):
         to = [self.neighbour(0, ring, step) for ring in BOTH for step in STEP] + list(more)
         for device in to:
@@ -323,18 +329,17 @@
 
 
 def attend_kernel(side, adapters, scale, ids_ref, x_ref, gain_ref, cos_ref, sin_ref, *rest):
-    w_heads, a_heads, b_heads, (wo_ref, ao_ref), a_mlp, b_rows, rest = rest[:3], rest[3:6], rest[6:9], rest[9:11], rest[11:13], rest[13:15], rest[15:]
-    (out_ref, a_all, b_all), rest = rest[:3], rest[3:]
-    (w, a_raw, b_raw, a_rows, bx, xbuf, h, z, lows, att, act, wo, stage, near, landed, am_raw, a_mine, b_mine, pair_send, pair_recv, load_sem, x_sem, own_sem,
+    w_heads, a_heads, b_heads, (wo_ref, ao_ref), b_rows, rest = rest[:3], rest[3:6], rest[6:9], rest[9:11], rest[11:13], rest[13:]
+    (out_ref, b_all), rest = rest[:2], rest[2:]
+    (w, a_raw, b_raw, a_rows, bx, xbuf, h, z, lows, att, act, wo, stage, near, landed, b_mine, pair_send, pair_recv, load_sem, x_sem, own_sem,
      kept_sem, hand_send, hand_recv, wo_load, wo_send, wo_recv, bulk_send, bulk_recv, swap_send, swap_recv,
-     send_sem, recv_sem, a_send, a_recv, b_send, b_recv, fast_send, fast_recv) = rest
+     send_sem, recv_sem, b_send, b_recv, fast_send, fast_recv) = rest
     place = Place(side)
     place.announce(place.partner, place.device(0, FAR), place.device(FAR, 0))
     head, seq_len, depth = cos_ref.shape[1], x_ref.shape[1], x_ref.shape[2]
     cols = len(w_heads) * head
     chips = side * side
     per = a_raw.shape[3]
-    half_depth = depth // 4
     loads = ends([pltpu.make_async_copy(src, dst, load_sem) for i in range(3) for src, dst in
                   ((a_heads[i], a_raw.at[place.core, i]), (w_heads[i], w.at[:, pl.ds(i * head, head)]), (b_heads[i], b_raw.at[0, i]))])
     steps = chips // 2
@@ -345,14 +350,7 @@
 
     ends(x_loads(0))
 
-    def every(ref):
-        return lambda part, ds: ref.at[part, :, place.turn(place.x, ds)] if part else ref.at[part, place.turn(place.y, ds)]
-
-    def spot_of(part):
-        return place.y if part else place.x
-
-    own_loads = ends([pltpu.make_async_copy(a_mlp[i], am_raw.at[i], own_sem) for i in BOTH] +
-                     [pltpu.make_async_copy(b_rows[half].at[part], b_mine.at[part, place.y, place.x, half], own_sem) for part in BOTH for half in BOTH])
+    own_loads = ends([pltpu.make_async_copy(b_rows[half].at[part], b_mine.at[part, place.y, place.x, half], own_sem) for part in BOTH for half in BOTH])
     width = wo_ref.shape[1]
     rank = ao_ref.shape[2]
     wo_loads = []
@@ -363,11 +361,6 @@
     ends(wo_loads)
     wait(own_loads)
     wait(loads)
-    am_rows = jnp.concatenate([am_raw[i, a] for i in BOTH for a in range(adapters)], axis=0)
-    for part in BOTH:
-        for half in BOTH:
-            at = (2 * part + half) * half_depth
-            a_mine[part, place.y, place.x, half] = am_rows[:, at:at + half_depth]
     place.meet()
     moves = [(a_raw.at[place.core], a_raw.at[place.core]), (w.at[:, first(cols)], w.at[:, pl.ds(cols, cols)]), (b_raw.at[0], b_raw.at[1])]
     pair = ends([remote(src, dst, pair_send.at[i], pair_recv.at[i], place.partner) for i, (src, dst) in enumerate(moves)])
@@ -411,21 +404,16 @@
 
     wait(wo_loads)
     early = WO_CHUNKS // 2
-    gathers = [RowGather(place, every(a_mine), spot_of, a_send, a_recv), RowGather(place, every(b_mine), spot_of, b_send, b_recv)]
-
-    def both(stage_of):
-        for g in gathers:
-            getattr(g, stage_of)()
+    b_gather = RowGather(place, place.rows(b_mine), place.spot, b_send, b_recv)
 
     def hand(*distances):
         for ds in distances:
             for part in BOTH:
-                for i, dst in enumerate((a_all, b_all)):
-                    here, there = gathers[i].row_at(part, ds), every(dst.at[place.core])(part, ds)
-                    pltpu.make_async_copy(here, there, kept_sem.at[i]).start()
-                    remote(here, there, hand_send.at[i], hand_recv.at[i], place.partner).start()
-
-    both('own')
+                here, there = b_gather.row_at(part, ds), place.rows(b_all.at[place.core])(part, ds)
+                pltpu.make_async_copy(here, there, kept_sem).start()
+                remote(here, there, hand_send, hand_recv, place.partner).start()
+
+    b_gather.own()
     for i in range(early):
         wo_start(i)
     pair[0].wait_recv()
@@ -434,7 +422,7 @@
         a_rows[core * 2 * TILE:(core + 1) * 2 * TILE, :] = jnp.concatenate(pieces, axis=0)
     mine = [(place.y, place.x), (place.x, place.y)]
 
-    low_gather = RowGather(place, lambda part, ds: lows.at[part, place.turn(mine[part][0], ds)], spot_of, send_sem, recv_sem)
+    low_gather = RowGather(place, lambda part, ds: lows.at[part, place.turn(mine[part][0], ds)], place.spot, send_sem, recv_sem)
 
     def norm(step, last):
         slot = lax.rem(step, 2)
@@ -448,7 +436,7 @@
             h[i * seq_len:(i + 1) * seq_len, :] = normed(xbuf[slot, i].astype(F32), gain_ref[...])
 
     def products(step):
-        pl.when(step == 3)(lambda: both('near'))
+        pl.when(step == 3)(b_gather.near)
         norm(step, 2 * steps)
         low = dot_rows(a_rows[...], h[...])
         half, at = step // (steps // 2), lax.rem(step, steps // 2) * 2 * seq_len
@@ -528,7 +516,7 @@
     loop(chips // 2, attention_pair)
     for ds in AWAY:
         swap(1, ds).start()
-    both('row')
+    b_gather.row()
     hand(OWN)
     wo_arrived()
     wo_last()
@@ -556,19 +544,18 @@
         stage[part, :, :, width:] = pick_columns(sum_heads(part, pl.ds(width, adapters * rank)), chosen).reshape(blocks + (rank,)).astype(BF)
         for df in (FAR, NEXT, LAST):
             fast.ready(part, df)
-    both('sides')
+    b_gather.sides()
     hand(NEXT, LAST)
     fast.sum()
-    both('far')
+    b_gather.far()
     hand(FAR)
     fast.finish()
     fast.store(out_ref)
     for sem in (kept_sem, hand_send, hand_recv):
-        for i, ref in enumerate((a_mine, b_mine)):
-            pltpu.make_async_copy(ref, ref, sem.at[i]).wait()
+        pltpu.make_async_copy(b_mine, b_mine, sem).wait()
     for copy in pair:
         copy.wait_send()
-    for g in gathers + [low_gather]:
+    for g in (b_gather, low_gather):
         g.sent()
     pltpu.make_async_copy(wo.at[:, :, 1], wo.at[:, :, 1], bulk_send).wait()
     for part in BOTH:
@@ -581,12 +568,12 @@
             swap(part, ds).wait_send()
 
 
-def attend(ids, x_in, gain, heads, w_o, a_o, a_mlp, b_rows, side, scale, collective_id):
+def attend(ids, x_in, gain, heads, w_o, a_o, b_rows, side, scale, collective_id):
     _, seq_len, depth = x_in.shape
     head = heads[0].shape[1]
     cols = 3 * head
     adapters, _, rank = a_o.shape
-    per = a_mlp[0].shape[1]
+    per = heads[3].shape[1]
     chips = side * side
     half_dim = head // 2
     inv_freq = ROPE_BASE ** (-2.0 * np.arange(half_dim) / head)
@@ -598,10 +585,10 @@
     every = (2, 2, side, side, 2)
     return pl.pallas_call(
         functools.partial(attend_kernel, side, adapters, scale),
-        out_shape=[jax.ShapeDtypeStruct((seq_len, out_cols), BF), jax.ShapeDtypeStruct(every + (2 * adapters * per, depth // 4), BF),
+        out_shape=[jax.ShapeDtypeStruct((seq_len, out_cols), BF),
                    jax.ShapeDtypeStruct(every + b_rows[0].shape[1:], BF)],
-        in_specs=[SMEM, HBM, VMEM, VMEM, VMEM] + [HBM] * (len(heads) + 6),
-        out_specs=[VMEM] + [HBM] * 2,
+        in_specs=[SMEM, HBM, VMEM, VMEM, VMEM] + [HBM] * (len(heads) + 4),
+        out_specs=[VMEM, HBM],
         scratch_shapes=[
             pltpu.VMEM((depth, 2 * cols), BF),
             pltpu.VMEM((2, 3, adapters, per, depth), BF),
@@ -617,14 +604,12 @@
             pltpu.VMEM((2, side, 2, head, depth + adapters * rank), BF),
             pltpu.VMEM((2, side, rows, out_cols), BF),
         ] + fast_scratch(rows, out_cols) + [
-            pltpu.VMEM((2, adapters, per, depth), BF),
-            pltpu.VMEM(every[1:] + (2 * adapters * per, depth // 4), BF),
             pltpu.VMEM(every[1:] + b_rows[0].shape[1:], BF),
-            DMA((n_pair,)), DMA((n_pair,)), DMA, DMA((2,)), DMA, DMA((2,)), DMA((2,)), DMA((2,)), DMA, DMA((2, 2, 2, WO_CHUNKS)), DMA((2, 2, 2, WO_CHUNKS)), DMA, DMA, DMA((2, 4)), DMA((2, 4)),
-        ] + ROW_SEMS * 3 + FAST_SEMS,
+            DMA((n_pair,)), DMA((n_pair,)), DMA, DMA((2,)), DMA, DMA, DMA, DMA, DMA, DMA((2, 2, 2, WO_CHUNKS)), DMA((2, 2, 2, WO_CHUNKS)), DMA, DMA, DMA((2, 4)), DMA((2, 4)),
+        ] + ROW_SEMS * 2 + FAST_SEMS,
         compiler_params=comm_params(collective_id),
         name='attend',
-    )(ids, x_in, gain.reshape(1, depth), *tables, *heads, w_o, a_o, *a_mlp, *b_rows)
+    )(ids, x_in, gain.reshape(1, depth), *tables, *heads, w_o, a_o, *b_rows)
 
 
 def row_proj_kernel(side, adapters, rank, ids_ref, act, w, out_ref, stage, near, landed, fast_near, fast_landed, slow_send, slow_recv, fast_send, fast_recv):
@@ -722,8 +707,9 @@
     return jnp.full(shape, ids_ref[place.device(0, 0)], jnp.int32)
 
 
-def gate_up_kernel(side, adapters, scale, ids_ref, sums_ref, gain_ref, x_all, a_all, b_all, wg_ref, wu_ref, bg_ref, bu_ref, wd_ref, ad_ref,
-                   hid, mid_ref, wd, gbuf, raw, w, b, x_ref, a_ref, b_ref, raw_sem, load_sem, a_sem, b_sem, credit, pair_send, pair_recv, send_sem, recv_sem):
+def gate_up_kernel(side, adapters, scale, ids_ref, sums_ref, gain_ref, x_all, b_all, ag_ref, au_ref, wg_ref, wu_ref, bg_ref, bu_ref, wd_ref, ad_ref,
+                   hid, mid_ref, wd, gbuf, raw, w, b, bx, x_ref, a_raw, a_ref, a_cols, b_ref, raw_sem, load_sem, a_sem, b_sem, credit, pair_send, pair_recv, hand_send, hand_recv,
+                   send_sem, recv_sem, a_send, a_recv):
     place = Place(side)
     share, width = wg_ref.shape
     half = raw.shape[1]
@@ -737,7 +723,7 @@
         wd[i * half + edge:(i + 1) * half] = jnp.zeros((half - edge, wd.shape[1]), BF)
     place.announce(place.partner)
     b_load = ends([pltpu.make_async_copy(b_all.at[:, :, :, :, 0], b_ref, b_sem), pltpu.make_async_copy(x_all.at[place.device(0, 0)], x_ref, b_sem)])
-    a_load = ends([pltpu.make_async_copy(a_all, a_ref, a_sem)])
+    a_load = ends([pltpu.make_async_copy(ref, a_raw.at[i], a_sem) for i, ref in enumerate((ag_ref, au_ref))])
     mine = first(share)
 
     def raw_load(kind):
@@ -753,49 +739,56 @@
     other = pl.ds(half, share)
     moves = [(raw.at[0, mine], raw.at[1, mine])] * 2 + [(wd.at[mine], wd.at[other])] + [(b.at[kind, mine], b.at[kind, other]) for kind in BOTH]
     pair = [remote(src, dst, pair_send.at[i], pair_recv.at[i], place.partner) for i, (src, dst) in enumerate(moves)]
+    quarter = width // 4
+    wait(a_load)
+    a_own = jnp.concatenate([a_raw[i, a] for i in BOTH for a in range(adapters)], axis=0)
+    group = a_own.shape[0]
+    for i in RING:
+        a_ref[place.core, i // 2, place.y, place.x, i % 2] = a_own[:, i * quarter:(i + 1) * quarter]
+    a_gather = RowGather(place, place.rows(a_ref.at[place.core]), place.spot, a_send, a_recv)
+
+    def hand(*distances):
+        for ds in distances:
+            for part in BOTH:
+                ref = a_gather.row_at(part, ds)
+                remote(ref, ref, hand_send, hand_recv, place.partner).start()
+
+    place.meet()
+    a_gather.own()
     rows = seq_len // 4
     chosen = own_rows(place, ids_ref, (seq_len, rank))
     wait(b_load)
     mid = finish(sums_ref, x_ref[...], b_ref, chosen, scale, adapters).astype(BF)
     mid_ref[...] = mid
     h2 = normed(mid.astype(F32), gain_ref[...])
-    lows = []
-    wait(a_load)
-    for core in BOTH:
-        pieces = [dot_rows(h2[:, i * width // 4:(i + 1) * width // 4], a_ref[core, i // 2, :, :, i % 2].reshape(-1, width // 4)) for i in RING]
-        lows.append(sum(pieces).astype(BF))
-    low = jnp.concatenate(lows, axis=1)
-    per = rank // (2 * side * side)
-    row, col = (lax.broadcasted_iota(jnp.int32, (low.shape[1], 2 * rank), axis) for axis in BOTH)
-    kind, rank_at = col // rank, lax.rem(col, rank)
-    chip, core = rank_at // (2 * per), lax.rem(rank_at // per, 2)
-    pick = ((core * side * side + chip) * 2 + kind) * adapters * per + ids_ref[place.device(0, 0)] * per + lax.rem(rank_at, per)
-    low = dot(low, jnp.where(row == pick, 1.0, 0.0).astype(BF)).astype(BF)
     for part in BOTH:
         for piece in BOTH:
             at = (2 * part + piece) * rows
-            gbuf[part, OWN, OWN, piece, :, :width] = h2[at:at + rows]
-            gbuf[part, OWN, OWN, piece, :, width:] = low[at:at + rows]
-    place.meet()
+            gbuf[part, OWN, OWN, piece] = h2[at:at + rows]
     chunk = fit(2 * half, 256)
+
+    n_low = 2 * side * side * group
+    per = group // (2 * adapters)
 
     def unit(ds, blocks=RING):
         lo, hi = min(blocks), max(blocks) + 1
         unit_rows = (hi - lo) * 2 * rows
-        low = gbuf[:, ds, lo:hi, :, :, width:].reshape(2 * unit_rows, 2 * rank).astype(F32)
-        chosen = jnp.concatenate([rows_of_adapter(place, ids_ref, part, ds, (len(RING) * 2 * rows, rank))[lo * 2 * rows:hi * 2 * rows] for part in BOTH], axis=0)
-        lows = [spread(low[:, kind * rank:(kind + 1) * rank], chosen, adapters) for kind in BOTH]
+        act_of = lambda: gbuf[:, ds, lo:hi].reshape(2 * unit_rows, width)
+        chosen = jnp.concatenate([rows_of_adapter(place, ids_ref, part, ds, (len(RING) * 2 * rows, n_low))[lo * 2 * rows:hi * 2 * rows] for part in BOTH], axis=0)
+        adapter = lax.rem(lax.broadcasted_iota(jnp.int32, chosen.shape, 1) // per, adapters)
+        lows = jnp.where(adapter == chosen, dot(act_of(), a_cols[...]), 0.0).astype(BF)
 
         def columns(n):
             at = pl.ds(pl.multiple_of(n * chunk, chunk), chunk)
-            act = gbuf[:, ds, lo:hi, :, :, :width].reshape(2 * unit_rows, width)
-            gate, up = (dot(act, w[kind, :, at]) + scale * dot_rows(lows[kind], b[kind, at]) for kind in BOTH)
+            act = act_of()
+            gate, up = (dot(act, w[kind, :, at]) + scale * dot_rows(lows, bx[kind, at]) for kind in BOTH)
             hid[:, ds, lo * 2 * rows:hi * 2 * rows, at] = (gate * jax.nn.sigmoid(gate) * up).astype(BF).reshape(2, unit_rows, chunk)
 
         loop(2 * half // chunk, columns)
 
     gather = Gather(place, lambda part, ds, df: gbuf.at[part, ds, df], send_sem, recv_sem)
     gather.own()
+    a_gather.near()
     def turned(kind, i):
         def turn(n):
             at = pl.ds(pl.multiple_of(n * LANE, LANE), LANE)
@@ -812,6 +805,8 @@
         if kind == 0:
             wait(loads)
             ends(pair[2:])
+            a_gather.row()
+            hand(OWN)
         pair[kind].wait_recv()
         turned(kind, 1)
         pair[kind].wait_send()
@@ -820,43 +815,70 @@
             raw_load(1).start()
     gather.near()
     gather.row()
+    a_gather.sides()
+    hand(NEXT, LAST)
     for copy in pair[2:]:
         copy.wait_recv()
+    row, col = (lax.broadcasted_iota(jnp.int32, (adapters * rank, n_low), axis) for axis in BOTH)
+    core, chip = col // (n_low // 2), lax.rem(col, n_low // 2) // group
+    kind_of, a_of = lax.rem(col, group) // (group // 2), lax.rem(col // per, adapters)
+    to = a_of * rank + chip * 2 * per + core * per + lax.rem(col, per)
+    for kind in BOTH:
+        bx[kind] = dot(b[kind], jnp.where((row == to) & (kind_of == kind), 1.0, 0.0).astype(BF)).astype(BF)
+    a_gather.far()
+    hand(FAR)
+    pltpu.make_async_copy(a_ref.at[0], a_ref.at[0], hand_recv).wait()
+    for core in BOTH:
+        for i in RING:
+
+            def turn_a(n):
+                at = pl.ds(pl.multiple_of(n * LANE, LANE), LANE)
+                to = pl.ds(pl.multiple_of(i * quarter + n * LANE, LANE), LANE)
+                a_cols[to, core * n_low // 2:(core + 1) * n_low // 2] = a_ref[core, i // 2, :, :, i % 2, :, at].reshape(n_low // 2, LANE).T
+
+            loop(quarter // LANE, turn_a)
     unit(OWN)
-    gather.sides(*AWAY)
-    loop(2, lambda i: unit(NEXT + 2 * i))
+    for blocks in PAIRS:
+        gather.sides(*(j for j in blocks if j != OWN))
+        loop(2, lambda i: unit(NEXT + 2 * i, blocks))
     for blocks in PAIRS:
         gather.far(*blocks)
         unit(FAR, blocks)
     gather.sent()
+    a_gather.sent()
+    pltpu.make_async_copy(a_ref.at[0], a_ref.at[0], hand_send).wait()
     for copy in pair[2:]:
         copy.wait_send()
 
 
-def gate_up(ids, sums, gain, x_in, a_all, b_all, w, side, scale, collective_id):
+def gate_up(ids, sums, gain, x_in, b_all, a_mlp, w, side, scale, collective_id):
     _, seq_len, depth = x_in.shape
     share = w[0].shape[0]
     adapters, _, rank = w[2].shape
     half = (share + LANE - 1) // LANE * LANE
     hidden = (2, side, side * seq_len // 2, 2 * half)
+    n_low = 2 * adapters * rank
     return pl.pallas_call(
         functools.partial(gate_up_kernel, side, adapters, scale),
         out_shape=[pltpu.VMEM(hidden, BF), pltpu.VMEM((seq_len, depth), BF), pltpu.VMEM((2 * half, depth + adapters * rank), BF)],
-        in_specs=[SMEM] + [VMEM] * 2 + [HBM] * (3 + len(w)),
+        in_specs=[SMEM] + [VMEM] * 2 + [HBM] * (4 + len(w)),
         out_specs=[VMEM] * 3,
         scratch_shapes=[
-            pltpu.VMEM((2, side, side, 2, seq_len // 4, depth + 2 * rank), BF),
+            pltpu.VMEM((2, side, side, 2, seq_len // 4, depth), BF),
             pltpu.VMEM((2, half, depth), BF),
             pltpu.VMEM((2, depth, 2 * half), BF),
             pltpu.VMEM((2, 2 * half, adapters * rank), BF),
+            pltpu.VMEM((2, 2 * half, n_low), BF),
             pltpu.VMEM((seq_len, depth), BF),
-            pltpu.VMEM(a_all.shape, BF),
+            pltpu.VMEM((2,) + a_mlp[0].shape, BF),
+            pltpu.VMEM((2, 2, side, side, 2, n_low // (2 * side * side), depth // 4), BF),
+            pltpu.VMEM((depth, n_low), BF),
             pltpu.VMEM(b_all.shape[:4] + b_all.shape[5:], BF),
-            DMA, DMA, DMA, DMA, pltpu.SemaphoreType.REGULAR, DMA((5,)), DMA((5,)),
-        ] + GATHER_SEMS,
+            DMA, DMA, DMA, DMA, pltpu.SemaphoreType.REGULAR, DMA((5,)), DMA((5,)), DMA, DMA,
+        ] + GATHER_SEMS + ROW_SEMS,
         compiler_params=comm_params(collective_id, VMEM_MOST * 51 // 64),
         name='gate_up',
-    )(ids, sums, gain.reshape(1, depth), x_in, a_all, b_all, *w)
+    )(ids, sums, gain.reshape(1, depth), x_in, b_all, *a_mlp, *w)
 
 
 def deliver_kernel(side, adapters, scale, ids_ref, sums_ref, x_ref, b_all, out_ref, b_ref, b_sem, pair_send, pair_recv, send_sem, recv_sem):
@@ -943,10 +965,10 @@
             return a.swapaxes(-1, -2)
 
         heads = [w[:, 0] for w in (w_q, w_k, w_v)] + [across(a) for a in (a_q, a_k, a_v)] + [b[:, :, 0] for b in (b_q, b_k, b_v)]
-        sums, all_a, all_b = attend(adapter_ids, x_in, gain_attn, heads, w_o[0], a_o[:, 0], (across(a_gate), across(a_up)), (b_o, b_down), side, scale, 0)
+        sums, all_b = attend(adapter_ids, x_in, gain_attn, heads, w_o[0], a_o[:, 0], (b_o, b_down), side, scale, 0)
 
         w = [across(w_gate), across(w_up), across(b_gate), across(b_up), w_down, a_down]
-        hidden, x_mid, w_d = gate_up(adapter_ids, sums, gain_mlp, x_in, all_a, all_b, w, side, scale, 1)
+        hidden, x_mid, w_d = gate_up(adapter_ids, sums, gain_mlp, x_in, all_b, (across(a_gate), across(a_up)), w, side, scale, 1)
         sums = row_proj(adapter_ids, hidden, w_d, *a_o.shape[::3], side, 2)
         y = deliver(adapter_ids, sums, x_mid, pltpu.with_memory_space_constraint(all_b, pltpu.HBM), side, scale, 3)
         return y.reshape(x_in.shape)

time: 424 us -> 462 us (1.090)
  Pallas kernels: 423 us -> 462 us
    pallas_call x1, Pallas kernels: 106 us -> 149 us  [gate_up(): pl.pallas_call(functools.partial(gate_up_kernel, side, adapters, scale),...]
where the time goes in v11:
time: 462 us
  Pallas kernels  462 us (100%)
    pallas_call x1, Pallas kernels, gate_up(): pl.pallas_call(functools.partial(gate_up_kernel, side, adapters, scale),...  149 us
    pallas_call x1, Pallas kernels, attend(): pl.pallas_call(functools.partial(attend_kernel, side, adapters, scale), o...  109 us
    pallas_call x1, Pallas kernels, row_proj(): pl.pallas_call(functools.partial(row_proj_kernel, side, adapters, rank),...  96.5 us
    pallas_call x1, Pallas kernels, deliver(): pl.pallas_call(functools.partial(deliver_kernel, side, b_all.shape[1], sc...  96.5 us
    pallas_call x1, Pallas kernels, deliver(): pl.pallas_call(put_kernel, out_shape=jax.ShapeDtypeStruct(y.shape, BF), i...  10.9 us

profile of v11, /device:TPU:97, one launch (start us, length us, event | category | flops | bytes accessed | tf_op | source)
XLA Modules:
  0.0 461.8 jit_solution(7557536739740834397)
XLA Ops:
  0.0 108.8 %attend.1 = (bf16[128,4224]{1,0:T(8,128)(2,1)}, bf16[2,2,4,4,2,128,128]{6,5,4,3,2,1,0:T(8,128)(2,1)}) custom-call(s32[32]{0:T(128)} %ids_ref.7, bf16[32,128,4096]{2,1,0:T(8,128)(2,1)} %x_all.1, f32[1,4096]{1,0:T(1,128)} %bitcast.37, f32[128,128]{1,0:T(8,128)} %constant.4.clone.cos_ref, f32[128,128]{1,0:T(8,128)} %constant.5.clone.sin_ref, ...), custom_call_target="tpu_custom_call" | custom-call | tf_op jit(solution)/shard_map/attend/pallas_call | solution.py:586
  108.8 0.0 copy-start
  108.8 148.9 %gate_up.1 = (bf16[2,4,256,768]{3,2,1,0:T(8,128)(2,1)S(1)}, bf16[128,4096]{1,0:T(8,128)(2,1)S(1)}, bf16[768,4352]{1,0:T(8,128)(2,1)S(1)}) custom-call(s32[32]{0:T(128)} %ids_ref.7, bf16[128,4224]{1,0:T(8,128)(2,1)} %get-tuple-element.10.sums_ref, f32[1,4096]{1,0:T(1,128)} %bitcast.38, bf16[32,128,4096]{2,1,0:T(8,128)(2,1)} %x_all.1, ...), custom_call_target="tpu_custom_call" | custom-call | tf_op jit(solution)/shard_map/gate_up/pallas_call | solution.py:861
  257.7 0.0 copy-done
  257.7 96.5 %row_proj.1.sums_ref = bf16[128,4224]{1,0:T(8,128)(2,1)S(1)} custom-call(s32[32]{0:T(128)S(1)} %copy-done, bf16[2,4,256,768]{3,2,1,0:T(8,128)(2,1)S(1)} %get-tuple-element.12.act, bf16[768,4352]{1,0:T(8,128)(2,1)S(1)} %get-tuple-element.13.w), custom_call_target="tpu_custom_call" | custom-call | tf_op jit(solution)/shard_map/row_proj/pallas_call | solution.py:683
  354.3 96.5 %deliver.1.y_ref = bf16[32,2,2,32,4096]{4,3,2,1,0:T(8,128)(2,1)S(1)} custom-call(s32[32]{0:T(128)S(1)} %copy-done, bf16[128,4224]{1,0:T(8,128)(2,1)S(1)} %row_proj.1.sums_ref, bf16[128,4096]{1,0:T(8,128)(2,1)S(1)} %get-tuple-element.14.x_ref, bf16[2,2,4,4,2,128,128]{6,5,4,3,2,1,0:T(8,128)(2,1)} %get-tuple-element.11.b_all), custom_call_target="tpu_custom_call" | custom-call | tf_op jit(solution)/shard_map/deliver/pallas_call | solution.py:927
  450.8 10.9 %put.1 = bf16[32,2,2,32,4096]{4,3,2,1,0:T(8,128)(2,1)} custom-call(bf16[32,2,2,32,4096]{4,3,2,1,0:T(8,128)(2,1)S(1)} %deliver.1.y_ref), custom_call_target="tpu_custom_call" | custom-call | tf_op jit(solution)/shard_map/put/pallas_call | solution.py:935
Async XLA Ops:
  108.8 148.9 %copy-start = (s32[32]{0:T(128)S(1)}, s32[32]{0:T(128)}, u32[]{:S(2)}) copy-start(s32[32]{0:T(128)} %ids_ref.7) | copy-start | bytes 388

commit v12 on v11

--- a/solution.py
+++ b/solution.py
@@ -136,8 +136,8 @@
             at = FAR if passed else FROM[d]
             self.seen(part, *((at, j) if ring == SLOW else (OWN, at)), d if passed else None)
 
-    def own(self):
-        for ring in BOTH:
+    def own(self, *rings):
+        for ring in rings:
             for d in BOTH:
                 for part in BOTH:
                     self.message(part, ring, 0, d).start()
@@ -325,7 +325,8 @@
     return pltpu.CompilerParams(collective_id=collective_id, has_side_effects=True, vmem_limit_bytes=limit)
 
 
-WO_CHUNKS = 4
+WO_CHUNKS = 8
+X_SLOTS = 3
 
 
 def attend_kernel(side, adapters, scale, ids_ref, x_ref, gain_ref, cos_ref, sin_ref, *rest):
@@ -345,10 +346,11 @@
     steps = chips // 2
 
     def x_loads(step):
-        slot = lax.rem(step, 2)
+        slot = lax.rem(step, X_SLOTS)
         return [pltpu.make_async_copy(x_ref.at[4 * lax.rem(step, steps) + 2 * i + place.core], xbuf.at[slot, i], x_sem.at[slot]) for i in BOTH]
 
-    ends(x_loads(0))
+    for step in range(X_SLOTS - 1):
+        ends(x_loads(step))
 
     own_loads = ends([pltpu.make_async_copy(b_rows[half].at[part], b_mine.at[part, place.y, place.x, half], own_sem) for part in BOTH for half in BOTH])
     width = wo_ref.shape[1]
@@ -425,11 +427,11 @@
     low_gather = RowGather(place, lambda part, ds: lows.at[part, place.turn(mine[part][0], ds)], place.spot, send_sem, recv_sem)
 
     def norm(step, last):
-        slot = lax.rem(step, 2)
-
-        @pl.when(step + 1 < last)
+        slot = lax.rem(step, X_SLOTS)
+
+        @pl.when(step + X_SLOTS - 1 < last)
         def _():
-            ends(x_loads(step + 1))
+            ends(x_loads(step + X_SLOTS - 1))
 
         wait(x_loads(step))
         for i in BOTH:
@@ -456,12 +458,17 @@
         copy.wait_recv()
     for part in BOTH:
         wo_to_partner(part, OWN)
-    events = {1: lambda: wo_start(early), 4: lambda: (low_gather.near(), wo_start(early + 1)), 7: low_gather.row}
+    events = {0: lambda: wo_start(early), 3: lambda: (low_gather.near(), wo_start(early + 1)), 7: lambda: (low_gather.row(), wo_start(early + 2)),
+              14: lambda: (low_gather.sides(), wo_start(early + 3))}
+
+    def happen(half_step):
+        for at, what in events.items():
+            pl.when(half_step == at)(lambda what=what: (what(), None)[1])
 
     def project(step):
-        for at, what in events.items():
-            pl.when(step == at)(lambda what=what: (what(), None)[1])
+        happen(2 * step)
         norm(step + steps, 2 * steps)
+        happen(2 * step + 1)
         rows = pl.ds(pl.multiple_of(step * 2 * seq_len, LANE), 2 * seq_len)
         chunk = fit(2 * cols, 256)
         for n in range(2 * cols // chunk):
@@ -478,10 +485,11 @@
             for a in range(adapters):
                 for o in BOTH:
                     bx[a, part, :, o * cols + i * head:o * cols + (i + 1) * head] = dot(spread_rows, b_raw[o, i, a]).astype(BF)
-    low_gather.sides()
     wo_pass(0)
     wo_pass(1)
     low_gather.far()
+    wo_pass(2)
+    wo_pass(3)
     causal = lax.broadcasted_iota(jnp.int32, (seq_len, seq_len), 0) >= lax.broadcasted_iota(jnp.int32, (seq_len, seq_len), 1)
 
     def swap(part, ds):
@@ -595,7 +603,7 @@
             pltpu.VMEM((2, 3, adapters, rank, head), BF),
             pltpu.VMEM((2 * 2 * TILE, depth), BF),
             pltpu.VMEM((adapters, 2, 2 * rank, 2 * cols), BF),
-            pltpu.VMEM((2, 2, seq_len, depth), BF),
+            pltpu.VMEM((X_SLOTS, 2, seq_len, depth), BF),
             pltpu.VMEM((2 * seq_len, depth), BF),
             pltpu.VMEM((chips * seq_len, 2 * cols), F32),
             pltpu.VMEM((2, side, side, 2, TILE, chips * seq_len // 2), BF),
@@ -605,7 +613,7 @@
             pltpu.VMEM((2, side, rows, out_cols), BF),
         ] + fast_scratch(rows, out_cols) + [
             pltpu.VMEM(every[1:] + b_rows[0].shape[1:], BF),
-            DMA((n_pair,)), DMA((n_pair,)), DMA, DMA((2,)), DMA, DMA, DMA, DMA, DMA, DMA((2, 2, 2, WO_CHUNKS)), DMA((2, 2, 2, WO_CHUNKS)), DMA, DMA, DMA((2, 4)), DMA((2, 4)),
+            DMA((n_pair,)), DMA((n_pair,)), DMA, DMA((X_SLOTS,)), DMA, DMA, DMA, DMA, DMA, DMA((2, 2, 2, WO_CHUNKS)), DMA((2, 2, 2, WO_CHUNKS)), DMA, DMA, DMA((2, 4)), DMA((2, 4)),
         ] + ROW_SEMS * 2 + FAST_SEMS,
         compiler_params=comm_params(collective_id),
         name='attend',
@@ -787,8 +795,11 @@
         loop(2 * half // chunk, columns)
 
     gather = Gather(place, lambda part, ds, df: gbuf.at[part, ds, df], send_sem, recv_sem)
-    gather.own()
     a_gather.near()
+    gather.own(FAST)
+    a_gather.row()
+    hand(OWN)
+    gather.own(SLOW)
     def turned(kind, i):
         def turn(n):
             at = pl.ds(pl.multiple_of(n * LANE, LANE), LANE)
@@ -805,17 +816,14 @@
         if kind == 0:
             wait(loads)
             ends(pair[2:])
-            a_gather.row()
-            hand(OWN)
         pair[kind].wait_recv()
         turned(kind, 1)
         pair[kind].wait_send()
         if kind == 0:
             pl.semaphore_signal(credit, inc=1, device_id={'tensor': place.partner}, device_id_type=MESH)
             raw_load(1).start()
+    a_gather.sides()
     gather.near()
-    gather.row()
-    a_gather.sides()
     hand(NEXT, LAST)
     for copy in pair[2:]:
         copy.wait_recv()
@@ -837,6 +845,7 @@
                 a_cols[to, core * n_low // 2:(core + 1) * n_low // 2] = a_ref[core, i // 2, :, :, i % 2, :, at].reshape(n_low // 2, LANE).T
 
             loop(quarter // LANE, turn_a)
+    gather.row()
     unit(OWN)
     for blocks in PAIRS:
         gather.sides(*(j for j in blocks if j != OWN))
@@ -906,7 +915,7 @@
     for part in BOTH:
         seen(part, OWN, OWN, None)
     gather = Gather(place, block, send_sem, recv_sem, absolute=True, seen=seen)
-    gather.own()
+    gather.own(*BOTH)
     gather.near()
     gather.row()
     gather.sides(*AWAY)

time: 462 us -> 427 us (0.924)
  Pallas kernels: 462 us -> 427 us
    pallas_call x1, Pallas kernels: 149 us -> 116 us  [gate_up(): pl.pallas_call(functools.partial(gate_up_kernel, side, adapters, scale),...]
where the time goes in v12:
time: 427 us
  Pallas kernels  427 us (100%)
    pallas_call x1, Pallas kernels, gate_up(): pl.pallas_call(functools.partial(gate_up_kernel, side, adapters, scale),...  116 us
    pallas_call x1, Pallas kernels, attend(): pl.pallas_call(functools.partial(attend_kernel, side, adapters, scale), o...  106 us
    pallas_call x1, Pallas kernels, row_proj(): pl.pallas_call(functools.partial(row_proj_kernel, side, adapters, rank),...  97.3 us
    pallas_call x1, Pallas kernels, deliver(): pl.pallas_call(functools.partial(deliver_kernel, side, b_all.shape[1], sc...  96.3 us
    pallas_call x1, Pallas kernels, deliver(): pl.pallas_call(put_kernel, out_shape=jax.ShapeDtypeStruct(y.shape, BF), i...  10.9 us

profile of v12, /device:TPU:97, one launch (start us, length us, event | category | flops | bytes accessed | tf_op | source)
XLA Modules:
  0.0 426.9 jit_solution(1469975187311032747)
XLA Ops:
  0.0 106.1 %attend.1 = (bf16[128,4224]{1,0:T(8,128)(2,1)}, bf16[2,2,4,4,2,128,128]{6,5,4,3,2,1,0:T(8,128)(2,1)}) custom-call(s32[32]{0:T(128)} %ids_ref.7, bf16[32,128,4096]{2,1,0:T(8,128)(2,1)} %x_all.1, f32[1,4096]{1,0:T(1,128)} %bitcast.37, f32[128,128]{1,0:T(8,128)} %constant.4.clone.cos_ref, f32[128,128]{1,0:T(8,128)} %constant.5.clone.sin_ref, ...), custom_call_target="tpu_custom_call" | custom-call | tf_op jit(solution)/shard_map/attend/pallas_call | solution.py:594
  106.1 0.0 copy-start
  106.1 116.1 %gate_up.1 = (bf16[2,4,256,768]{3,2,1,0:T(8,128)(2,1)S(1)}, bf16[128,4096]{1,0:T(8,128)(2,1)S(1)}, bf16[768,4352]{1,0:T(8,128)(2,1)S(1)}) custom-call(s32[32]{0:T(128)} %ids_ref.7, bf16[128,4224]{1,0:T(8,128)(2,1)} %get-tuple-element.10.sums_ref, f32[1,4096]{1,0:T(1,128)} %bitcast.38, bf16[32,128,4096]{2,1,0:T(8,128)(2,1)} %x_all.1, ...), custom_call_target="tpu_custom_call" | custom-call | tf_op jit(solution)/shard_map/gate_up/pallas_call | solution.py:870
  222.3 0.0 copy-done
  222.3 97.3 %row_proj.1.sums_ref = bf16[128,4224]{1,0:T(8,128)(2,1)S(1)} custom-call(s32[32]{0:T(128)S(1)} %copy-done, bf16[2,4,256,768]{3,2,1,0:T(8,128)(2,1)S(1)} %get-tuple-element.12.act, bf16[768,4352]{1,0:T(8,128)(2,1)S(1)} %get-tuple-element.13.w), custom_call_target="tpu_custom_call" | custom-call | tf_op jit(solution)/shard_map/row_proj/pallas_call | solution.py:691
  319.5 96.3 %deliver.1.y_ref = bf16[32,2,2,32,4096]{4,3,2,1,0:T(8,128)(2,1)S(1)} custom-call(s32[32]{0:T(128)S(1)} %copy-done, bf16[128,4224]{1,0:T(8,128)(2,1)S(1)} %row_proj.1.sums_ref, bf16[128,4096]{1,0:T(8,128)(2,1)S(1)} %get-tuple-element.14.x_ref, bf16[2,2,4,4,2,128,128]{6,5,4,3,2,1,0:T(8,128)(2,1)} %get-tuple-element.11.b_all), custom_call_target="tpu_custom_call" | custom-call | tf_op jit(solution)/shard_map/deliver/pallas_call | solution.py:936
  415.8 10.9 %put.1 = bf16[32,2,2,32,4096]{4,3,2,1,0:T(8,128)(2,1)} custom-call(bf16[32,2,2,32,4096]{4,3,2,1,0:T(8,128)(2,1)S(1)} %deliver.1.y_ref), custom_call_target="tpu_custom_call" | custom-call | tf_op jit(solution)/shard_map/put/pallas_call | solution.py:944
Async XLA Ops:
  106.1 116.2 %copy-start = (s32[32]{0:T(128)S(1)}, s32[32]{0:T(128)}, u32[]{:S(2)}) copy-start(s32[32]{0:T(128)} %ids_ref.7) | copy-start | bytes 388

commit v13 on v12

--- a/solution.py
+++ b/solution.py
@@ -330,11 +330,11 @@
 
 
 def attend_kernel(side, adapters, scale, ids_ref, x_ref, gain_ref, cos_ref, sin_ref, *rest):
-    w_heads, a_heads, b_heads, (wo_ref, ao_ref), b_rows, rest = rest[:3], rest[3:6], rest[6:9], rest[9:11], rest[11:13], rest[13:]
-    (out_ref, b_all), rest = rest[:2], rest[2:]
-    (w, a_raw, b_raw, a_rows, bx, xbuf, h, z, lows, att, act, wo, stage, near, landed, b_mine, pair_send, pair_recv, load_sem, x_sem, own_sem,
+    w_heads, a_heads, b_heads, (wo_ref, ao_ref), a_mlp, b_rows, rest = rest[:3], rest[3:6], rest[6:9], rest[9:11], rest[11:13], rest[13:15], rest[15:]
+    (out_ref, a_all, b_all), rest = rest[:3], rest[3:]
+    (w, a_raw, b_raw, a_rows, bx, xbuf, h, z, lows, att, act, wo, stage, near, landed, am_raw, a_mine, b_mine, pair_send, pair_recv, load_sem, x_sem, own_sem,
      kept_sem, hand_send, hand_recv, wo_load, wo_send, wo_recv, bulk_send, bulk_recv, swap_send, swap_recv,
-     send_sem, recv_sem, b_send, b_recv, fast_send, fast_recv) = rest
+     send_sem, recv_sem, a_send, a_recv, b_send, b_recv, fast_send, fast_recv) = rest
     place = Place(side)
     place.announce(place.partner, place.device(0, FAR), place.device(FAR, 0))
     head, seq_len, depth = cos_ref.shape[1], x_ref.shape[1], x_ref.shape[2]
@@ -352,7 +352,8 @@
     for step in range(X_SLOTS - 1):
         ends(x_loads(step))
 
-    own_loads = ends([pltpu.make_async_copy(b_rows[half].at[part], b_mine.at[part, place.y, place.x, half], own_sem) for part in BOTH for half in BOTH])
+    own_loads = ends([pltpu.make_async_copy(a_mlp[i], am_raw.at[i], own_sem) for i in BOTH] +
+                     [pltpu.make_async_copy(b_rows[half].at[part], b_mine.at[part, place.y, place.x, half], own_sem) for part in BOTH for half in BOTH])
     width = wo_ref.shape[1]
     rank = ao_ref.shape[2]
     wo_loads = []
@@ -363,6 +364,9 @@
     ends(wo_loads)
     wait(own_loads)
     wait(loads)
+    am_rows = jnp.concatenate([am_raw[i, a] for i in BOTH for a in range(adapters)], axis=0)
+    for i in RING:
+        a_mine[i // 2, place.y, place.x, i % 2] = am_rows[:, i * depth // 4:(i + 1) * depth // 4]
     place.meet()
     moves = [(a_raw.at[place.core], a_raw.at[place.core]), (w.at[:, first(cols)], w.at[:, pl.ds(cols, cols)]), (b_raw.at[0], b_raw.at[1])]
     pair = ends([remote(src, dst, pair_send.at[i], pair_recv.at[i], place.partner) for i, (src, dst) in enumerate(moves)])
@@ -406,16 +410,21 @@
 
     wait(wo_loads)
     early = WO_CHUNKS // 2
-    b_gather = RowGather(place, place.rows(b_mine), place.spot, b_send, b_recv)
+    gathers = [RowGather(place, place.rows(a_mine), place.spot, a_send, a_recv), RowGather(place, place.rows(b_mine), place.spot, b_send, b_recv)]
+
+    def both(stage_of):
+        for g in gathers:
+            getattr(g, stage_of)()
 
     def hand(*distances):
         for ds in distances:
             for part in BOTH:
-                here, there = b_gather.row_at(part, ds), place.rows(b_all.at[place.core])(part, ds)
-                pltpu.make_async_copy(here, there, kept_sem).start()
-                remote(here, there, hand_send, hand_recv, place.partner).start()
-
-    b_gather.own()
+                for i, dst in enumerate((a_all, b_all)):
+                    here, there = gathers[i].row_at(part, ds), place.rows(dst.at[place.core])(part, ds)
+                    pltpu.make_async_copy(here, there, kept_sem.at[i]).start()
+                    remote(here, there, hand_send.at[i], hand_recv.at[i], place.partner).start()
+
+    both('own')
     for i in range(early):
         wo_start(i)
     pair[0].wait_recv()
@@ -438,7 +447,7 @@
             h[i * seq_len:(i + 1) * seq_len, :] = normed(xbuf[slot, i].astype(F32), gain_ref[...])
 
     def products(step):
-        pl.when(step == 3)(b_gather.near)
+        pl.when(step == 3)(lambda: both('near'))
         norm(step, 2 * steps)
         low = dot_rows(a_rows[...], h[...])
         half, at = step // (steps // 2), lax.rem(step, steps // 2) * 2 * seq_len
@@ -524,7 +533,7 @@
     loop(chips // 2, attention_pair)
     for ds in AWAY:
         swap(1, ds).start()
-    b_gather.row()
+    both('row')
     hand(OWN)
     wo_arrived()
     wo_last()
@@ -552,18 +561,19 @@
         stage[part, :, :, width:] = pick_columns(sum_heads(part, pl.ds(width, adapters * rank)), chosen).reshape(blocks + (rank,)).astype(BF)
         for df in (FAR, NEXT, LAST):
             fast.ready(part, df)
-    b_gather.sides()
+    both('sides')
     hand(NEXT, LAST)
     fast.sum()
-    b_gather.far()
+    both('far')
     hand(FAR)
     fast.finish()
     fast.store(out_ref)
     for sem in (kept_sem, hand_send, hand_recv):
-        pltpu.make_async_copy(b_mine, b_mine, sem).wait()
+        for i, ref in enumerate((a_mine, b_mine)):
+            pltpu.make_async_copy(ref, ref, sem.at[i]).wait()
     for copy in pair:
         copy.wait_send()
-    for g in (b_gather, low_gather):
+    for g in gathers + [low_gather]:
         g.sent()
     pltpu.make_async_copy(wo.at[:, :, 1], wo.at[:, :, 1], bulk_send).wait()
     for part in BOTH:
@@ -576,7 +586,7 @@
             swap(part, ds).wait_send()
 
 
-def attend(ids, x_in, gain, heads, w_o, a_o, b_rows, side, scale, collective_id):
+def attend(ids, x_in, gain, heads, w_o, a_o, a_mlp, b_rows, side, scale, collective_id):
     _, seq_len, depth = x_in.shape
     head = heads[0].shape[1]
     cols = 3 * head
@@ -593,10 +603,10 @@
     every = (2, 2, side, side, 2)
     return pl.pallas_call(
         functools.partial(attend_kernel, side, adapters, scale),
-        out_shape=[jax.ShapeDtypeStruct((seq_len, out_cols), BF),
+        out_shape=[jax.ShapeDtypeStruct((seq_len, out_cols), BF), jax.ShapeDtypeStruct(every + (2 * adapters * per, depth // 4), BF),
                    jax.ShapeDtypeStruct(every + b_rows[0].shape[1:], BF)],
-        in_specs=[SMEM, HBM, VMEM, VMEM, VMEM] + [HBM] * (len(heads) + 4),
-        out_specs=[VMEM, HBM],
+        in_specs=[SMEM, HBM, VMEM, VMEM, VMEM] + [HBM] * (len(heads) + 6),
+        out_specs=[VMEM] + [HBM] * 2,
         scratch_shapes=[
             pltpu.VMEM((depth, 2 * cols), BF),
             pltpu.VMEM((2, 3, adapters, per, depth), BF),
@@ -612,12 +622,14 @@
             pltpu.VMEM((2, side, 2, head, depth + adapters * rank), BF),
             pltpu.VMEM((2, side, rows, out_cols), BF),
         ] + fast_scratch(rows, out_cols) + [
+            pltpu.VMEM((2, adapters, per, depth), BF),
+            pltpu.VMEM(every[1:] + (2 * adapters * per, depth // 4), BF),
             pltpu.VMEM(every[1:] + b_rows[0].shape[1:], BF),
-            DMA((n_pair,)), DMA((n_pair,)), DMA, DMA((X_SLOTS,)), DMA, DMA, DMA, DMA, DMA, DMA((2, 2, 2, WO_CHUNKS)), DMA((2, 2, 2, WO_CHUNKS)), DMA, DMA, DMA((2, 4)), DMA((2, 4)),
-        ] + ROW_SEMS * 2 + FAST_SEMS,
+            DMA((n_pair,)), DMA((n_pair,)), DMA, DMA((X_SLOTS,)), DMA, DMA((2,)), DMA((2,)), DMA((2,)), DMA, DMA((2, 2, 2, WO_CHUNKS)), DMA((2, 2, 2, WO_CHUNKS)), DMA, DMA, DMA((2, 4)), DMA((2, 4)),
+        ] + ROW_SEMS * 3 + FAST_SEMS,
         compiler_params=comm_params(collective_id),
         name='attend',
-    )(ids, x_in, gain.reshape(1, depth), *tables, *heads, w_o, a_o, *b_rows)
+    )(ids, x_in, gain.reshape(1, depth), *tables, *heads, w_o, a_o, *a_mlp, *b_rows)
 
 
 def row_proj_kernel(side, adapters, rank, ids_ref, act, w, out_ref, stage, near, landed, fast_near, fast_landed, slow_send, slow_recv, fast_send, fast_recv):
@@ -626,7 +638,7 @@
     rows, cols = stage.shape[3:]
     quarter = rows // 2
     width = cols - rank
-    chunk = fit(width, 512)
+    chunk = fit(width, 1024)
 
     def unit(part, ds):
         def columns(n):
@@ -715,9 +727,8 @@
     return jnp.full(shape, ids_ref[place.device(0, 0)], jnp.int32)
 
 
-def gate_up_kernel(side, adapters, scale, ids_ref, sums_ref, gain_ref, x_all, b_all, ag_ref, au_ref, wg_ref, wu_ref, bg_ref, bu_ref, wd_ref, ad_ref,
-                   hid, mid_ref, wd, gbuf, raw, w, b, bx, x_ref, a_raw, a_ref, a_cols, b_ref, raw_sem, load_sem, a_sem, b_sem, credit, pair_send, pair_recv, hand_send, hand_recv,
-                   send_sem, recv_sem, a_send, a_recv):
+def gate_up_kernel(side, adapters, scale, ids_ref, sums_ref, gain_ref, x_all, a_all, b_all, wg_ref, wu_ref, bg_ref, bu_ref, wd_ref, ad_ref,
+                   hid, mid_ref, wd, gbuf, raw, w, b, bx, x_ref, a_ref, a_cols, b_ref, raw_sem, load_sem, a_sem, b_sem, credit, pair_send, pair_recv, send_sem, recv_sem):
     place = Place(side)
     share, width = wg_ref.shape
     half = raw.shape[1]
@@ -731,7 +742,7 @@
         wd[i * half + edge:(i + 1) * half] = jnp.zeros((half - edge, wd.shape[1]), BF)
     place.announce(place.partner)
     b_load = ends([pltpu.make_async_copy(b_all.at[:, :, :, :, 0], b_ref, b_sem), pltpu.make_async_copy(x_all.at[place.device(0, 0)], x_ref, b_sem)])
-    a_load = ends([pltpu.make_async_copy(ref, a_raw.at[i], a_sem) for i, ref in enumerate((ag_ref, au_ref))])
+    a_load = ends([pltpu.make_async_copy(a_all, a_ref, a_sem)])
     mine = first(share)
 
     def raw_load(kind):
@@ -747,22 +758,6 @@
     other = pl.ds(half, share)
     moves = [(raw.at[0, mine], raw.at[1, mine])] * 2 + [(wd.at[mine], wd.at[other])] + [(b.at[kind, mine], b.at[kind, other]) for kind in BOTH]
     pair = [remote(src, dst, pair_send.at[i], pair_recv.at[i], place.partner) for i, (src, dst) in enumerate(moves)]
-    quarter = width // 4
-    wait(a_load)
-    a_own = jnp.concatenate([a_raw[i, a] for i in BOTH for a in range(adapters)], axis=0)
-    group = a_own.shape[0]
-    for i in RING:
-        a_ref[place.core, i // 2, place.y, place.x, i % 2] = a_own[:, i * quarter:(i + 1) * quarter]
-    a_gather = RowGather(place, place.rows(a_ref.at[place.core]), place.spot, a_send, a_recv)
-
-    def hand(*distances):
-        for ds in distances:
-            for part in BOTH:
-                ref = a_gather.row_at(part, ds)
-                remote(ref, ref, hand_send, hand_recv, place.partner).start()
-
-    place.meet()
-    a_gather.own()
     rows = seq_len // 4
     chosen = own_rows(place, ids_ref, (seq_len, rank))
     wait(b_load)
@@ -773,8 +768,10 @@
         for piece in BOTH:
             at = (2 * part + piece) * rows
             gbuf[part, OWN, OWN, piece] = h2[at:at + rows]
+    place.meet()
     chunk = fit(2 * half, 256)
 
+    group, quarter = a_ref.shape[5:]
     n_low = 2 * side * side * group
     per = group // (2 * adapters)
 
@@ -795,11 +792,7 @@
         loop(2 * half // chunk, columns)
 
     gather = Gather(place, lambda part, ds, df: gbuf.at[part, ds, df], send_sem, recv_sem)
-    a_gather.near()
-    gather.own(FAST)
-    a_gather.row()
-    hand(OWN)
-    gather.own(SLOW)
+    gather.own(*BOTH)
     def turned(kind, i):
         def turn(n):
             at = pl.ds(pl.multiple_of(n * LANE, LANE), LANE)
@@ -822,9 +815,8 @@
         if kind == 0:
             pl.semaphore_signal(credit, inc=1, device_id={'tensor': place.partner}, device_id_type=MESH)
             raw_load(1).start()
-    a_gather.sides()
     gather.near()
-    hand(NEXT, LAST)
+    wait(a_load)
     for copy in pair[2:]:
         copy.wait_recv()
     row, col = (lax.broadcasted_iota(jnp.int32, (adapters * rank, n_low), axis) for axis in BOTH)
@@ -833,9 +825,6 @@
     to = a_of * rank + chip * 2 * per + core * per + lax.rem(col, per)
     for kind in BOTH:
         bx[kind] = dot(b[kind], jnp.where((row == to) & (kind_of == kind), 1.0, 0.0).astype(BF)).astype(BF)
-    a_gather.far()
-    hand(FAR)
-    pltpu.make_async_copy(a_ref.at[0], a_ref.at[0], hand_recv).wait()
     for core in BOTH:
         for i in RING:
 
@@ -854,13 +843,11 @@
         gather.far(*blocks)
         unit(FAR, blocks)
     gather.sent()
-    a_gather.sent()
-    pltpu.make_async_copy(a_ref.at[0], a_ref.at[0], hand_send).wait()
     for copy in pair[2:]:
         copy.wait_send()
 
 
-def gate_up(ids, sums, gain, x_in, b_all, a_mlp, w, side, scale, collective_id):
+def gate_up(ids, sums, gain, x_in, a_all, b_all, w, side, scale, collective_id):
     _, seq_len, depth = x_in.shape
     share = w[0].shape[0]
     adapters, _, rank = w[2].shape
@@ -870,7 +857,7 @@
     return pl.pallas_call(
         functools.partial(gate_up_kernel, side, adapters, scale),
         out_shape=[pltpu.VMEM(hidden, BF), pltpu.VMEM((seq_len, depth), BF), pltpu.VMEM((2 * half, depth + adapters * rank), BF)],
-        in_specs=[SMEM] + [VMEM] * 2 + [HBM] * (4 + len(w)),
+        in_specs=[SMEM] + [VMEM] * 2 + [HBM] * (3 + len(w)),
         out_specs=[VMEM] * 3,
         scratch_shapes=[
             pltpu.VMEM((2, side, side, 2, seq_len // 4, depth), BF),
@@ -879,15 +866,14 @@
             pltpu.VMEM((2, 2 * half, adapters * rank), BF),
             pltpu.VMEM((2, 2 * half, n_low), BF),
             pltpu.VMEM((seq_len, depth), BF),
-            pltpu.VMEM((2,) + a_mlp[0].shape, BF),
-            pltpu.VMEM((2, 2, side, side, 2, n_low // (2 * side * side), depth // 4), BF),
+            pltpu.VMEM(a_all.shape, BF),
             pltpu.VMEM((depth, n_low), BF),
             pltpu.VMEM(b_all.shape[:4] + b_all.shape[5:], BF),
-            DMA, DMA, DMA, DMA, pltpu.SemaphoreType.REGULAR, DMA((5,)), DMA((5,)), DMA, DMA,
-        ] + GATHER_SEMS + ROW_SEMS,
+            DMA, DMA, DMA, DMA, pltpu.SemaphoreType.REGULAR, DMA((5,)), DMA((5,)),
+        ] + GATHER_SEMS,
         compiler_params=comm_params(collective_id, VMEM_MOST * 51 // 64),
         name='gate_up',
-    )(ids, sums, gain.reshape(1, depth), x_in, b_all, *a_mlp, *w)
+    )(ids, sums, gain.reshape(1, depth), x_in, a_all, b_all, *w)
 
 
 def deliver_kernel(side, adapters, scale, ids_ref, sums_ref, x_ref, b_all, out_ref, b_ref, b_sem, pair_send, pair_recv, send_sem, recv_sem):
@@ -974,10 +960,10 @@
             return a.swapaxes(-1, -2)
 
         heads = [w[:, 0] for w in (w_q, w_k, w_v)] + [across(a) for a in (a_q, a_k, a_v)] + [b[:, :, 0] for b in (b_q, b_k, b_v)]
-        sums, all_b = attend(adapter_ids, x_in, gain_attn, heads, w_o[0], a_o[:, 0], (b_o, b_down), side, scale, 0)
+        sums, all_a, all_b = attend(adapter_ids, x_in, gain_attn, heads, w_o[0], a_o[:, 0], (across(a_gate), across(a_up)), (b_o, b_down), side, scale, 0)
 
         w = [across(w_gate), across(w_up), across(b_gate), across(b_up), w_down, a_down]
-        hidden, x_mid, w_d = gate_up(adapter_ids, sums, gain_mlp, x_in, all_b, (across(a_gate), across(a_up)), w, side, scale, 1)
+        hidden, x_mid, w_d = gate_up(adapter_ids, sums, gain_mlp, x_in, all_a, all_b, w, side, scale, 1)
         sums = row_proj(adapter_ids, hidden, w_d, *a_o.shape[::3], side, 2)
         y = deliver(adapter_ids, sums, x_mid, pltpu.with_memory_space_constraint(all_b, pltpu.HBM), side, scale, 3)
         return y.reshape(x_in.shape)

time: 427 us -> 421 us (0.986)
  Pallas kernels: 427 us -> 420 us
    pallas_call x1, Pallas kernels: 116 us -> 104 us  [gate_up(): pl.pallas_call(functools.partial(gate_up_kernel, side, adapters, scale),...]
    pallas_call x1, Pallas kernels: 106 us -> 112 us  [attend(): pl.pallas_call(functools.partial(attend_kernel, side, adapters, scale), o...]
where the time goes in v13:
time: 421 us
  Pallas kernels  420 us (100%)
    pallas_call x1, Pallas kernels, attend(): pl.pallas_call(functools.partial(attend_kernel, side, adapters, scale), o...  112 us
    pallas_call x1, Pallas kernels, gate_up(): pl.pallas_call(functools.partial(gate_up_kernel, side, adapters, scale),...  104 us
    pallas_call x1, Pallas kernels, row_proj(): pl.pallas_call(functools.partial(row_proj_kernel, side, adapters, rank),...  97 us
    pallas_call x1, Pallas kernels, deliver(): pl.pallas_call(functools.partial(deliver_kernel, side, b_all.shape[1], sc...  96.2 us
    pallas_call x1, Pallas kernels, deliver(): pl.pallas_call(put_kernel, out_shape=jax.ShapeDtypeStruct(y.shape, BF), i...  10.9 us

profile of v13, /device:TPU:97, one launch (start us, length us, event | category | flops | bytes accessed | tf_op | source)
XLA Modules:
  0.0 420.6 jit_solution(12981890934033541186)
XLA Ops:
  0.0 112.5 %attend.1 = (bf16[128,4224]{1,0:T(8,128)(2,1)}, bf16[2,2,4,4,2,16,1024]{6,5,4,3,2,1,0:T(8,128)(2,1)}, bf16[2,2,4,4,2,128,128]{6,5,4,3,2,1,0:T(8,128)(2,1)}) custom-call(s32[32]{0:T(128)} %ids_ref.7, bf16[32,128,4096]{2,1,0:T(8,128)(2,1)} %x_all.1, f32[1,4096]{1,0:T(1,128)} %bitcast.37, f32[128,128]{1,0:T(8,128)} %constant.4.clone.cos_ref, ...), custom_call_target="tpu_custom_call" | custom-call | tf_op jit(solution)/shard_map/attend/pallas_call | solution.py:604
  112.5 0.0 copy-start
  112.5 103.8 %gate_up.1 = (bf16[2,4,256,768]{3,2,1,0:T(8,128)(2,1)S(1)}, bf16[128,4096]{1,0:T(8,128)(2,1)S(1)}, bf16[768,4352]{1,0:T(8,128)(2,1)S(1)}) custom-call(s32[32]{0:T(128)} %ids_ref.7, bf16[128,4224]{1,0:T(8,128)(2,1)} %get-tuple-element.11.sums_ref, f32[1,4096]{1,0:T(1,128)} %bitcast.38, bf16[32,128,4096]{2,1,0:T(8,128)(2,1)} %x_all.1, ...), custom_call_target="tpu_custom_call" | custom-call | tf_op jit(solution)/shard_map/gate_up/pallas_call | solution.py:857
  216.3 0.0 copy-done
  216.3 97.0 %row_proj.1.sums_ref = bf16[128,4224]{1,0:T(8,128)(2,1)S(1)} custom-call(s32[32]{0:T(128)S(1)} %copy-done, bf16[2,4,256,768]{3,2,1,0:T(8,128)(2,1)S(1)} %get-tuple-element.14.act, bf16[768,4352]{1,0:T(8,128)(2,1)S(1)} %get-tuple-element.15.w), custom_call_target="tpu_custom_call" | custom-call | tf_op jit(solution)/shard_map/row_proj/pallas_call | solution.py:703
  313.3 96.2 %deliver.1.y_ref = bf16[32,2,2,32,4096]{4,3,2,1,0:T(8,128)(2,1)S(1)} custom-call(s32[32]{0:T(128)S(1)} %copy-done, bf16[128,4224]{1,0:T(8,128)(2,1)S(1)} %row_proj.1.sums_ref, bf16[128,4096]{1,0:T(8,128)(2,1)S(1)} %get-tuple-element.16.x_ref, bf16[2,2,4,4,2,128,128]{6,5,4,3,2,1,0:T(8,128)(2,1)} %get-tuple-element.13.b_all), custom_call_target="tpu_custom_call" | custom-call | tf_op jit(solution)/shard_map/deliver/pallas_call | solution.py:922
  409.5 10.9 %put.1 = bf16[32,2,2,32,4096]{4,3,2,1,0:T(8,128)(2,1)} custom-call(bf16[32,2,2,32,4096]{4,3,2,1,0:T(8,128)(2,1)S(1)} %deliver.1.y_ref), custom_call_target="tpu_custom_call" | custom-call | tf_op jit(solution)/shard_map/put/pallas_call | solution.py:930
Async XLA Ops:
  112.5 103.8 %copy-start = (s32[32]{0:T(128)S(1)}, s32[32]{0:T(128)}, u32[]{:S(2)}) copy-start(s32[32]{0:T(128)} %ids_ref.7) | copy-start | bytes 388

commit v14 on v13

--- a/solution.py
+++ b/solution.py
@@ -311,6 +311,8 @@
         rows = self.landed.shape[2]
         for part in BOTH:
             out_ref[part * rows:(part + 1) * rows] = self.stage(part, OWN)[...]
+
+    def sent(self):
         for part in BOTH:
             for kind in range(3):
                 for d in BOTH:
@@ -329,10 +331,10 @@
 X_SLOTS = 3
 
 
-def attend_kernel(side, adapters, scale, ids_ref, x_ref, gain_ref, cos_ref, sin_ref, *rest):
+def attend_kernel(side, adapters, scale, ids_ref, x_ref, gain_in, cos_in, sin_in, *rest):
     w_heads, a_heads, b_heads, (wo_ref, ao_ref), a_mlp, b_rows, rest = rest[:3], rest[3:6], rest[6:9], rest[9:11], rest[11:13], rest[13:15], rest[15:]
     (out_ref, a_all, b_all), rest = rest[:3], rest[3:]
-    (w, a_raw, b_raw, a_rows, bx, xbuf, h, z, lows, att, act, wo, stage, near, landed, am_raw, a_mine, b_mine, pair_send, pair_recv, load_sem, x_sem, own_sem,
+    (w, a_raw, b_raw, a_rows, bx, xbuf, h, z, lows, att, act, wo, stage, near, landed, am_raw, a_mine, b_mine, gain_ref, cos_ref, sin_ref, pair_send, pair_recv, table_sem, load_sem, x_sem, own_sem,
      kept_sem, hand_send, hand_recv, wo_load, wo_send, wo_recv, bulk_send, bulk_recv, swap_send, swap_recv,
      send_sem, recv_sem, a_send, a_recv, b_send, b_recv, fast_send, fast_recv) = rest
     place = Place(side)
@@ -351,6 +353,7 @@
 
     for step in range(X_SLOTS - 1):
         ends(x_loads(step))
+    tables = ends([pltpu.make_async_copy(src, dst, table_sem) for src, dst in ((gain_in, gain_ref), (cos_in, cos_ref), (sin_in, sin_ref))])
 
     own_loads = ends([pltpu.make_async_copy(a_mlp[i], am_raw.at[i], own_sem) for i in BOTH] +
                      [pltpu.make_async_copy(b_rows[half].at[part], b_mine.at[part, place.y, place.x, half], own_sem) for part in BOTH for half in BOTH])
@@ -427,6 +430,7 @@
     both('own')
     for i in range(early):
         wo_start(i)
+    wait(tables)
     pair[0].wait_recv()
     for core in BOTH:
         pieces = [a_raw[core, i, a] if i < len(w_heads) else jnp.zeros((per, depth), BF) for a in range(adapters) for i in RING]
@@ -567,7 +571,8 @@
     both('far')
     hand(FAR)
     fast.finish()
-    fast.store(out_ref)
+    out = ends([pltpu.make_async_copy(stage.at[part, OWN], out_ref.at[pl.ds(part * rows, rows)], load_sem) for part in BOTH])
+    fast.sent()
     for sem in (kept_sem, hand_send, hand_recv):
         for i, ref in enumerate((a_mine, b_mine)):
             pltpu.make_async_copy(ref, ref, sem.at[i]).wait()
@@ -584,6 +589,7 @@
                 wo_message(part, 1, d, i).wait_send()
         for ds in AWAY:
             swap(part, ds).wait_send()
+    wait(out)
 
 
 def attend(ids, x_in, gain, heads, w_o, a_o, a_mlp, b_rows, side, scale, collective_id):
@@ -605,8 +611,8 @@
         functools.partial(attend_kernel, side, adapters, scale),
         out_shape=[jax.ShapeDtypeStruct((seq_len, out_cols), BF), jax.ShapeDtypeStruct(every + (2 * adapters * per, depth // 4), BF),
                    jax.ShapeDtypeStruct(every + b_rows[0].shape[1:], BF)],
-        in_specs=[SMEM, HBM, VMEM, VMEM, VMEM] + [HBM] * (len(heads) + 6),
-        out_specs=[VMEM] + [HBM] * 2,
+        in_specs=[SMEM] + [HBM] * (4 + len(heads) + 6),
+        out_specs=[HBM] * 3,
         scratch_shapes=[
             pltpu.VMEM((depth, 2 * cols), BF),
             pltpu.VMEM((2, 3, adapters, per, depth), BF),
@@ -625,7 +631,10 @@
             pltpu.VMEM((2, adapters, per, depth), BF),
             pltpu.VMEM(every[1:] + (2 * adapters * per, depth // 4), BF),
             pltpu.VMEM(every[1:] + b_rows[0].shape[1:], BF),
-            DMA((n_pair,)), DMA((n_pair,)), DMA, DMA((X_SLOTS,)), DMA, DMA((2,)), DMA((2,)), DMA((2,)), DMA, DMA((2, 2, 2, WO_CHUNKS)), DMA((2, 2, 2, WO_CHUNKS)), DMA, DMA, DMA((2, 4)), DMA((2, 4)),
+            pltpu.VMEM((1, depth), F32),
+            pltpu.VMEM(tables[0].shape, F32),
+            pltpu.VMEM(tables[0].shape, F32),
+            DMA((n_pair,)), DMA((n_pair,)), DMA, DMA, DMA((X_SLOTS,)), DMA, DMA((2,)), DMA((2,)), DMA((2,)), DMA, DMA((2, 2, 2, WO_CHUNKS)), DMA((2, 2, 2, WO_CHUNKS)), DMA, DMA, DMA((2, 4)), DMA((2, 4)),
         ] + ROW_SEMS * 3 + FAST_SEMS,
         compiler_params=comm_params(collective_id),
         name='attend',
@@ -689,6 +698,7 @@
     fast.sum()
     fast.finish()
     fast.store(out_ref)
+    fast.sent()
     for part in BOTH:
         for kind in range(3):
             for d in BOTH:
@@ -727,8 +737,8 @@
     return jnp.full(shape, ids_ref[place.device(0, 0)], jnp.int32)
 
 
-def gate_up_kernel(side, adapters, scale, ids_ref, sums_ref, gain_ref, x_all, a_all, b_all, wg_ref, wu_ref, bg_ref, bu_ref, wd_ref, ad_ref,
-                   hid, mid_ref, wd, gbuf, raw, w, b, bx, x_ref, a_ref, a_cols, b_ref, raw_sem, load_sem, a_sem, b_sem, credit, pair_send, pair_recv, send_sem, recv_sem):
+def gate_up_kernel(side, adapters, scale, ids_ref, sums_in, gain_in, x_all, a_all, b_all, wg_ref, wu_ref, bg_ref, bu_ref, wd_ref, ad_ref,
+                   hid, mid_ref, wd, gbuf, raw, w, b, bx, gain_ref, sums_ref, a_ref, a_cols, b_ref, raw_sem, load_sem, a_sem, b_sem, credit, pair_send, pair_recv, send_sem, recv_sem):
     place = Place(side)
     share, width = wg_ref.shape
     half = raw.shape[1]
@@ -741,7 +751,8 @@
             b[kind, i * half + edge:(i + 1) * half] = jnp.zeros((half - edge, adapters * rank), BF)
         wd[i * half + edge:(i + 1) * half] = jnp.zeros((half - edge, wd.shape[1]), BF)
     place.announce(place.partner)
-    b_load = ends([pltpu.make_async_copy(b_all.at[:, :, :, :, 0], b_ref, b_sem), pltpu.make_async_copy(x_all.at[place.device(0, 0)], x_ref, b_sem)])
+    b_load = ends([pltpu.make_async_copy(b_all.at[:, :, :, :, 0], b_ref, b_sem), pltpu.make_async_copy(x_all.at[place.device(0, 0)], mid_ref, b_sem),
+                   pltpu.make_async_copy(gain_in, gain_ref, b_sem), pltpu.make_async_copy(sums_in, sums_ref, b_sem)])
     a_load = ends([pltpu.make_async_copy(a_all, a_ref, a_sem)])
     mine = first(share)
 
@@ -761,7 +772,7 @@
     rows = seq_len // 4
     chosen = own_rows(place, ids_ref, (seq_len, rank))
     wait(b_load)
-    mid = finish(sums_ref, x_ref[...], b_ref, chosen, scale, adapters).astype(BF)
+    mid = finish(sums_ref, mid_ref[...], b_ref, chosen, scale, adapters).astype(BF)
     mid_ref[...] = mid
     h2 = normed(mid.astype(F32), gain_ref[...])
     for part in BOTH:
@@ -857,7 +868,7 @@
     return pl.pallas_call(
         functools.partial(gate_up_kernel, side, adapters, scale),
         out_shape=[pltpu.VMEM(hidden, BF), pltpu.VMEM((seq_len, depth), BF), pltpu.VMEM((2 * half, depth + adapters * rank), BF)],
-        in_specs=[SMEM] + [VMEM] * 2 + [HBM] * (3 + len(w)),
+        in_specs=[SMEM] + [HBM] * (5 + len(w)),
         out_specs=[VMEM] * 3,
         scratch_shapes=[
             pltpu.VMEM((2, side, side, 2, seq_len // 4, depth), BF),
@@ -865,7 +876,8 @@
             pltpu.VMEM((2, depth, 2 * half), BF),
             pltpu.VMEM((2, 2 * half, adapters * rank), BF),
             pltpu.VMEM((2, 2 * half, n_low), BF),
-            pltpu.VMEM((seq_len, depth), BF),
+            pltpu.VMEM((1, depth), F32),
+            pltpu.VMEM(sums.shape, BF),
             pltpu.VMEM(a_all.shape, BF),
             pltpu.VMEM((depth, n_low), BF),
             pltpu.VMEM(b_all.shape[:4] + b_all.shape[5:], BF),

time: 421 us -> 418 us (level)
  no operation moved by 1% of the time
where the time goes in v14:
time: 418 us; the launch traced here: 417 us
  Pallas kernels  417 us (100%)
    pallas_call x1, Pallas kernels, attend(): pl.pallas_call(functools.partial(attend_kernel, side, adapters, scale), o...  113 us
    pallas_call x1, Pallas kernels, gate_up(): pl.pallas_call(functools.partial(gate_up_kernel, side, adapters, scale),...  104 us
    pallas_call x1, Pallas kernels, row_proj(): pl.pallas_call(functools.partial(row_proj_kernel, side, adapters, rank),...  95.3 us
    pallas_call x1, Pallas kernels, deliver(): pl.pallas_call(functools.partial(deliver_kernel, side, b_all.shape[1], sc...  94.8 us
    pallas_call x1, Pallas kernels, deliver(): pl.pallas_call(put_kernel, out_shape=jax.ShapeDtypeStruct(y.shape, BF), i...  10.9 us

profile of v14, /device:TPU:97, one launch (start us, length us, event | category | flops | bytes accessed | tf_op | source)
XLA Modules:
  0.0 417.4 jit_solution(7842113224150846714)
XLA Ops:
  0.0 112.6 %attend.1 = (bf16[128,4224]{1,0:T(8,128)(2,1)}, bf16[2,2,4,4,2,16,1024]{6,5,4,3,2,1,0:T(8,128)(2,1)}, bf16[2,2,4,4,2,128,128]{6,5,4,3,2,1,0:T(8,128)(2,1)}) custom-call(s32[32]{0:T(128)} %ids_ref.7, bf16[32,128,4096]{2,1,0:T(8,128)(2,1)} %x_all.1, f32[1,4096]{1,0:T(1,128)} %bitcast.37, f32[128,128]{1,0:T(8,128)} %constant.4.clone.cos_in, ...), custom_call_target="tpu_custom_call" | custom-call | tf_op jit(solution)/shard_map/attend/pallas_call | solution.py:610
  112.7 0.0 copy-start
  112.7 103.6 %gate_up.1 = (bf16[2,4,256,768]{3,2,1,0:T(8,128)(2,1)S(1)}, bf16[128,4096]{1,0:T(8,128)(2,1)S(1)}, bf16[768,4352]{1,0:T(8,128)(2,1)S(1)}) custom-call(s32[32]{0:T(128)} %ids_ref.7, bf16[128,4224]{1,0:T(8,128)(2,1)} %get-tuple-element.11.sums_in, f32[1,4096]{1,0:T(1,128)} %bitcast.38, bf16[32,128,4096]{2,1,0:T(8,128)(2,1)} %x_all.1, ...), custom_call_target="tpu_custom_call" | custom-call | tf_op jit(solution)/shard_map/gate_up/pallas_call | solution.py:868
  216.3 0.0 copy-done
  216.3 95.3 %row_proj.1.sums_ref = bf16[128,4224]{1,0:T(8,128)(2,1)S(1)} custom-call(s32[32]{0:T(128)S(1)} %copy-done, bf16[2,4,256,768]{3,2,1,0:T(8,128)(2,1)S(1)} %get-tuple-element.14.act, bf16[768,4352]{1,0:T(8,128)(2,1)S(1)} %get-tuple-element.15.w), custom_call_target="tpu_custom_call" | custom-call | tf_op jit(solution)/shard_map/row_proj/pallas_call | solution.py:713
  311.6 94.8 %deliver.1.y_ref = bf16[32,2,2,32,4096]{4,3,2,1,0:T(8,128)(2,1)S(1)} custom-call(s32[32]{0:T(128)S(1)} %copy-done, bf16[128,4224]{1,0:T(8,128)(2,1)S(1)} %row_proj.1.sums_ref, bf16[128,4096]{1,0:T(8,128)(2,1)S(1)} %get-tuple-element.16.x_ref, bf16[2,2,4,4,2,128,128]{6,5,4,3,2,1,0:T(8,128)(2,1)} %get-tuple-element.13.b_all), custom_call_target="tpu_custom_call" | custom-call | tf_op jit(solution)/shard_map/deliver/pallas_call | solution.py:934
  406.4 10.9 %put.1 = bf16[32,2,2,32,4096]{4,3,2,1,0:T(8,128)(2,1)} custom-call(bf16[32,2,2,32,4096]{4,3,2,1,0:T(8,128)(2,1)S(1)} %deliver.1.y_ref), custom_call_target="tpu_custom_call" | custom-call | tf_op jit(solution)/shard_map/put/pallas_call | solution.py:942
Async XLA Ops:
  112.7 103.6 %copy-start = (s32[32]{0:T(128)S(1)}, s32[32]{0:T(128)}, u32[]{:S(2)}) copy-start(s32[32]{0:T(128)} %ids_ref.7) | copy-start | bytes 388

commit v15 on v14

--- a/solution.py
+++ b/solution.py
@@ -343,17 +343,11 @@
     cols = len(w_heads) * head
     chips = side * side
     per = a_raw.shape[3]
-    loads = ends([pltpu.make_async_copy(src, dst, load_sem) for i in range(3) for src, dst in
-                  ((a_heads[i], a_raw.at[place.core, i]), (w_heads[i], w.at[:, pl.ds(i * head, head)]), (b_heads[i], b_raw.at[0, i]))])
     steps = chips // 2
 
     def x_loads(step):
         slot = lax.rem(step, X_SLOTS)
         return [pltpu.make_async_copy(x_ref.at[4 * lax.rem(step, steps) + 2 * i + place.core], xbuf.at[slot, i], x_sem.at[slot]) for i in BOTH]
-
-    for step in range(X_SLOTS - 1):
-        ends(x_loads(step))
-    tables = ends([pltpu.make_async_copy(src, dst, table_sem) for src, dst in ((gain_in, gain_ref), (cos_in, cos_ref), (sin_in, sin_ref))])
 
     own_loads = ends([pltpu.make_async_copy(a_mlp[i], am_raw.at[i], own_sem) for i in BOTH] +
                      [pltpu.make_async_copy(b_rows[half].at[part], b_mine.at[part, place.y, place.x, half], own_sem) for part in BOTH for half in BOTH])
@@ -365,15 +359,16 @@
         for a in range(adapters):
             wo_loads.append(pltpu.make_async_copy(ao_ref.at[a], wo.at[part, OWN, 0, :, pl.ds(width + a * rank, rank)], wo_load))
     ends(wo_loads)
+    loads = ends([pltpu.make_async_copy(src, dst, load_sem) for i in range(3) for src, dst in
+                  ((a_heads[i], a_raw.at[place.core, i]), (w_heads[i], w.at[:, pl.ds(i * head, head)]), (b_heads[i], b_raw.at[0, i]))])
+    for step in range(X_SLOTS - 1):
+        ends(x_loads(step))
+    tables = ends([pltpu.make_async_copy(src, dst, table_sem) for src, dst in ((gain_in, gain_ref), (cos_in, cos_ref), (sin_in, sin_ref))])
     wait(own_loads)
-    wait(loads)
     am_rows = jnp.concatenate([am_raw[i, a] for i in BOTH for a in range(adapters)], axis=0)
     for i in RING:
         a_mine[i // 2, place.y, place.x, i % 2] = am_rows[:, i * depth // 4:(i + 1) * depth // 4]
     place.meet()
-    moves = [(a_raw.at[place.core], a_raw.at[place.core]), (w.at[:, first(cols)], w.at[:, pl.ds(cols, cols)]), (b_raw.at[0], b_raw.at[1])]
-    pair = ends([remote(src, dst, pair_send.at[i], pair_recv.at[i], place.partner) for i, (src, dst) in enumerate(moves)])
-
     piece = head // WO_CHUNKS
 
     def wo_message(part, passed, d, i):
@@ -411,7 +406,6 @@
                     wo_message(part, 1, d, i).wait_recv()
             wo_to_partner(part, FAR)
 
-    wait(wo_loads)
     early = WO_CHUNKS // 2
     gathers = [RowGather(place, place.rows(a_mine), place.spot, a_send, a_recv), RowGather(place, place.rows(b_mine), place.spot, b_send, b_recv)]
 
@@ -428,8 +422,12 @@
                     remote(here, there, hand_send.at[i], hand_recv.at[i], place.partner).start()
 
     both('own')
+    wait(wo_loads)
     for i in range(early):
         wo_start(i)
+    wait(loads)
+    moves = [(a_raw.at[place.core], a_raw.at[place.core]), (w.at[:, first(cols)], w.at[:, pl.ds(cols, cols)]), (b_raw.at[0], b_raw.at[1])]
+    pair = ends([remote(src, dst, pair_send.at[i], pair_recv.at[i], place.partner) for i, (src, dst) in enumerate(moves)])
     wait(tables)
     pair[0].wait_recv()
     for core in BOTH:
@@ -641,11 +639,12 @@
     )(ids, x_in, gain.reshape(1, depth), *tables, *heads, w_o, a_o, *a_mlp, *b_rows)
 
 
-def row_proj_kernel(side, adapters, rank, ids_ref, act, w, out_ref, stage, near, landed, fast_near, fast_landed, slow_send, slow_recv, fast_send, fast_recv):
+def row_proj_kernel(side, adapters, rank, ids_ref, act, w, b_all, out_ref, b_ref, b_sem, stage, near, landed, fast_near, fast_landed, slow_send, slow_recv, fast_send, fast_recv):
     place = Place(side)
     place.announce()
     rows, cols = stage.shape[3:]
     quarter = rows // 2
+    b_load = ends([pltpu.make_async_copy(b_all.at[:, :, :, :, 1], b_ref, b_sem)])
     width = cols - rank
     chunk = fit(width, 1024)
 
@@ -699,6 +698,7 @@
     fast.finish()
     fast.store(out_ref)
     fast.sent()
+    wait(b_load)
     for part in BOTH:
         for kind in range(3):
             for d in BOTH:
@@ -706,23 +706,24 @@
                     slow(part, kind, d, i).wait_send()
 
 
-def row_proj(ids, act, w, adapters, rank, side, collective_id):
+def row_proj(ids, act, w, b_all, adapters, rank, side, collective_id):
     rows = act.shape[2] // side
     cols = w.shape[1] - (adapters - 1) * rank
     blocks = (rows, cols)
     return pl.pallas_call(
         functools.partial(row_proj_kernel, side, adapters, rank),
-        out_shape=pltpu.VMEM((2 * rows, cols), BF),
-        in_specs=[SMEM, VMEM, VMEM],
-        out_specs=VMEM,
+        out_shape=[pltpu.VMEM((2 * rows, cols), BF), pltpu.VMEM(b_all.shape[:4] + b_all.shape[5:], BF)],
+        in_specs=[SMEM, VMEM, VMEM, HBM],
+        out_specs=[VMEM, VMEM],
         scratch_shapes=[
+            DMA,
             pltpu.VMEM((2, side, side) + blocks, BF),
             pltpu.VMEM((2, 2, 2) + blocks, BF),
             pltpu.VMEM((2, 2, side) + blocks, BF),
         ] + fast_scratch(rows, cols) + [DMA((2, 3, 2, 2))] * 2 + FAST_SEMS,
-        compiler_params=comm_params(collective_id, VMEM_MOST * 5 // 8),
+        compiler_params=comm_params(collective_id, VMEM_MOST * 9 // 16),
         name='row_proj',
-    )(ids, act, w)
+    )(ids, act, w, b_all)
 
 
 def finish(sums_ref, resid, b_ref, chosen, scale, adapters):
@@ -888,14 +889,12 @@
     )(ids, sums, gain.reshape(1, depth), x_in, a_all, b_all, *w)
 
 
-def deliver_kernel(side, adapters, scale, ids_ref, sums_ref, x_ref, b_all, out_ref, b_ref, b_sem, pair_send, pair_recv, send_sem, recv_sem):
+def deliver_kernel(side, adapters, scale, ids_ref, sums_ref, x_ref, b_ref, out_ref, pair_send, pair_recv, send_sem, recv_sem):
     place = Place(side)
     place.announce(place.partner)
-    b_load = ends([pltpu.make_async_copy(b_all.at[:, :, :, :, 1], b_ref, b_sem)])
     seq_len = sums_ref.shape[0]
     rows = seq_len // 4
     chosen = own_rows(place, ids_ref, (seq_len, b_ref.shape[4]))
-    wait(b_load)
     y = finish(sums_ref, x_ref[...], b_ref, chosen, scale, adapters).astype(BF)
     for part in BOTH:
         for piece in BOTH:
@@ -928,17 +927,17 @@
     wait(ends([pltpu.make_async_copy(y_ref.at[i], out_ref.at[i], sem) for i in range(y_ref.shape[0])]))
 
 
-def deliver(ids, sums, x_mid, b_all, side, scale, collective_id):
+def deliver(ids, sums, x_mid, b_down, side, scale, collective_id):
     seq_len, depth = x_mid.shape
     rows = seq_len // 4
     y = pl.pallas_call(
-        functools.partial(deliver_kernel, side, b_all.shape[1], scale),
+        functools.partial(deliver_kernel, side, b_down.shape[1], scale),
         out_shape=pltpu.VMEM((2 * side * side, 2, 2, rows, depth), BF),
-        in_specs=[SMEM] + [VMEM] * 2 + [HBM],
-        scratch_shapes=[pltpu.VMEM(b_all.shape[:4] + b_all.shape[5:], BF), DMA, DMA, DMA] + GATHER_SEMS,
+        in_specs=[SMEM] + [VMEM] * 3,
+        scratch_shapes=[DMA, DMA] + GATHER_SEMS,
         compiler_params=comm_params(collective_id, VMEM_SMALL),
         name='deliver',
-    )(ids, sums, x_mid, b_all)
+    )(ids, sums, x_mid, b_down)
     return pl.pallas_call(
         put_kernel,
         out_shape=jax.ShapeDtypeStruct(y.shape, BF),
@@ -976,8 +975,8 @@
 
         w = [across(w_gate), across(w_up), across(b_gate), across(b_up), w_down, a_down]
         hidden, x_mid, w_d = gate_up(adapter_ids, sums, gain_mlp, x_in, all_a, all_b, w, side, scale, 1)
-        sums = row_proj(adapter_ids, hidden, w_d, *a_o.shape[::3], side, 2)
-        y = deliver(adapter_ids, sums, x_mid, pltpu.with_memory_space_constraint(all_b, pltpu.HBM), side, scale, 3)
+        sums, b_d = row_proj(adapter_ids, hidden, w_d, pltpu.with_memory_space_constraint(all_b, pltpu.HBM), *a_o.shape[::3], side, 2)
+        y = deliver(adapter_ids, sums, x_mid, b_d, side, scale, 3)
         return y.reshape(x_in.shape)
 
     return jax.shard_map(local_layer, mesh=mesh, in_specs=in_specs, out_specs=P('data', None, None), check_vma=False)

time: 418 us -> 417 us (level)
  no operation moved by 1% of the time
where the time goes in v15:
time: 417 us; the launch traced here: 416 us
  Pallas kernels  416 us (100%)
    pallas_call x1, Pallas kernels, attend(): pl.pallas_call(functools.partial(attend_kernel, side, adapters, scale), o...  112 us
    pallas_call x1, Pallas kernels, gate_up(): pl.pallas_call(functools.partial(gate_up_kernel, side, adapters, scale),...  104 us
    pallas_call x1, Pallas kernels, row_proj(): pl.pallas_call(functools.partial(row_proj_kernel, side, adapters, rank),...  95.2 us
    pallas_call x1, Pallas kernels, deliver(): pl.pallas_call(functools.partial(deliver_kernel, side, b_down.shape[1], s...  94.3 us
    pallas_call x1, Pallas kernels, deliver(): pl.pallas_call(put_kernel, out_shape=jax.ShapeDtypeStruct(y.shape, BF), i...  10.9 us

profile of v15, /device:TPU:97, one launch (start us, length us, event | category | flops | bytes accessed | tf_op | source)
XLA Modules:
  0.0 416.5 jit_solution(15565393111568887382)
XLA Ops:
  0.0 112.2 %attend.1 = (bf16[128,4224]{1,0:T(8,128)(2,1)}, bf16[2,2,4,4,2,16,1024]{6,5,4,3,2,1,0:T(8,128)(2,1)}, bf16[2,2,4,4,2,128,128]{6,5,4,3,2,1,0:T(8,128)(2,1)}) custom-call(s32[32]{0:T(128)} %ids_ref.7, bf16[32,128,4096]{2,1,0:T(8,128)(2,1)} %x_all.1, f32[1,4096]{1,0:T(1,128)} %bitcast.37, f32[128,128]{1,0:T(8,128)} %constant.4.clone.cos_in, ...), custom_call_target="tpu_custom_call" | custom-call | tf_op jit(solution)/shard_map/attend/pallas_call | solution.py:608
  112.2 0.0 copy-start
  112.2 103.6 %gate_up.1 = (bf16[2,4,256,768]{3,2,1,0:T(8,128)(2,1)S(1)}, bf16[128,4096]{1,0:T(8,128)(2,1)S(1)}, bf16[768,4352]{1,0:T(8,128)(2,1)S(1)}) custom-call(s32[32]{0:T(128)} %ids_ref.7, bf16[128,4224]{1,0:T(8,128)(2,1)} %get-tuple-element.13.sums_in, f32[1,4096]{1,0:T(1,128)} %bitcast.38, bf16[32,128,4096]{2,1,0:T(8,128)(2,1)} %x_all.1, ...), custom_call_target="tpu_custom_call" | custom-call | tf_op jit(solution)/shard_map/gate_up/pallas_call | solution.py:869
  215.9 0.0 copy-done
  215.9 95.2 %row_proj.1 = (bf16[128,4224]{1,0:T(8,128)(2,1)S(1)}, bf16[2,2,4,4,128,128]{5,4,3,2,1,0:T(8,128)(2,1)S(1)}) custom-call(s32[32]{0:T(128)S(1)} %copy-done, bf16[2,4,256,768]{3,2,1,0:T(8,128)(2,1)S(1)} %get-tuple-element.16.act, bf16[768,4352]{1,0:T(8,128)(2,1)S(1)} %get-tuple-element.17.w, bf16[2,2,4,4,2,128,128]{6,5,4,3,2,1,0:T(8,128)(2,1)} %get-tuple-element.15.b_all), custom_call_target="tpu_custom_call" | custom-call | tf_op jit(solution)/shard_map/row_proj/pallas_call | solution.py:713
  311.1 94.3 %deliver.1.y_ref = bf16[32,2,2,32,4096]{4,3,2,1,0:T(8,128)(2,1)S(1)} custom-call(s32[32]{0:T(128)S(1)} %copy-done, bf16[128,4224]{1,0:T(8,128)(2,1)S(1)} %get-tuple-element.18.sums_ref, bf16[128,4096]{1,0:T(8,128)(2,1)S(1)} %get-tuple-element.19.x_ref, bf16[2,2,4,4,128,128]{5,4,3,2,1,0:T(8,128)(2,1)S(1)} %get-tuple-element.20.b_ref), custom_call_target="tpu_custom_call" | custom-call | tf_op jit(solution)/shard_map/deliver/pallas_call | solution.py:933
  405.4 10.9 %put.1 = bf16[32,2,2,32,4096]{4,3,2,1,0:T(8,128)(2,1)} custom-call(bf16[32,2,2,32,4096]{4,3,2,1,0:T(8,128)(2,1)S(1)} %deliver.1.y_ref), custom_call_target="tpu_custom_call" | custom-call | tf_op jit(solution)/shard_map/put/pallas_call | solution.py:941
Async XLA Ops:
  112.2 103.7 %copy-start = (s32[32]{0:T(128)S(1)}, s32[32]{0:T(128)}, u32[]{:S(2)}) copy-start(s32[32]{0:T(128)} %ids_ref.7) | copy-start | bytes 388

commit v16 on v15

--- a/solution.py
+++ b/solution.py
@@ -821,13 +821,14 @@
         if kind == 0:
             wait(loads)
             ends(pair[2:])
+        else:
+            gather.near()
         pair[kind].wait_recv()
         turned(kind, 1)
         pair[kind].wait_send()
         if kind == 0:
             pl.semaphore_signal(credit, inc=1, device_id={'tensor': place.partner}, device_id_type=MESH)
             raw_load(1).start()
-    gather.near()
     wait(a_load)
     for copy in pair[2:]:
         copy.wait_recv()

time: 417 us -> 417 us (level)
  no operation moved by 1% of the time
where the time goes in v16:
time: 417 us; the launch traced here: 416 us
  Pallas kernels  416 us (100%)
    pallas_call x1, Pallas kernels, attend(): pl.pallas_call(functools.partial(attend_kernel, side, adapters, scale), o...  112 us
    pallas_call x1, Pallas kernels, gate_up(): pl.pallas_call(functools.partial(gate_up_kernel, side, adapters, scale),...  104 us
    pallas_call x1, Pallas kernels, row_proj(): pl.pallas_call(functools.partial(row_proj_kernel, side, adapters, rank),...  95.2 us
    pallas_call x1, Pallas kernels, deliver(): pl.pallas_call(functools.partial(deliver_kernel, side, b_down.shape[1], s...  94.3 us
    pallas_call x1, Pallas kernels, deliver(): pl.pallas_call(put_kernel, out_shape=jax.ShapeDtypeStruct(y.shape, BF), i...  10.9 us

profile of v16, /device:TPU:97, one launch (start us, length us, event | category | flops | bytes accessed | tf_op | source)
XLA Modules:
  0.0 416.5 jit_solution(11923913876608490736)
XLA Ops:
  0.0 112.2 %attend.1 = (bf16[128,4224]{1,0:T(8,128)(2,1)}, bf16[2,2,4,4,2,16,1024]{6,5,4,3,2,1,0:T(8,128)(2,1)}, bf16[2,2,4,4,2,128,128]{6,5,4,3,2,1,0:T(8,128)(2,1)}) custom-call(s32[32]{0:T(128)} %ids_ref.7, bf16[32,128,4096]{2,1,0:T(8,128)(2,1)} %x_all.1, f32[1,4096]{1,0:T(1,128)} %bitcast.37, f32[128,128]{1,0:T(8,128)} %constant.4.clone.cos_in, ...), custom_call_target="tpu_custom_call" | custom-call | tf_op jit(solution)/shard_map/attend/pallas_call | solution.py:608
  112.2 0.0 copy-start
  112.2 103.6 %gate_up.1 = (bf16[2,4,256,768]{3,2,1,0:T(8,128)(2,1)S(1)}, bf16[128,4096]{1,0:T(8,128)(2,1)S(1)}, bf16[768,4352]{1,0:T(8,128)(2,1)S(1)}) custom-call(s32[32]{0:T(128)} %ids_ref.7, bf16[128,4224]{1,0:T(8,128)(2,1)} %get-tuple-element.13.sums_in, f32[1,4096]{1,0:T(1,128)} %bitcast.38, bf16[32,128,4096]{2,1,0:T(8,128)(2,1)} %x_all.1, ...), custom_call_target="tpu_custom_call" | custom-call | tf_op jit(solution)/shard_map/gate_up/pallas_call | solution.py:870
  215.9 0.0 copy-done
  215.9 95.2 %row_proj.1 = (bf16[128,4224]{1,0:T(8,128)(2,1)S(1)}, bf16[2,2,4,4,128,128]{5,4,3,2,1,0:T(8,128)(2,1)S(1)}) custom-call(s32[32]{0:T(128)S(1)} %copy-done, bf16[2,4,256,768]{3,2,1,0:T(8,128)(2,1)S(1)} %get-tuple-element.16.act, bf16[768,4352]{1,0:T(8,128)(2,1)S(1)} %get-tuple-element.17.w, bf16[2,2,4,4,2,128,128]{6,5,4,3,2,1,0:T(8,128)(2,1)} %get-tuple-element.15.b_all), custom_call_target="tpu_custom_call" | custom-call | tf_op jit(solution)/shard_map/row_proj/pallas_call | solution.py:713
  311.1 94.3 %deliver.1.y_ref = bf16[32,2,2,32,4096]{4,3,2,1,0:T(8,128)(2,1)S(1)} custom-call(s32[32]{0:T(128)S(1)} %copy-done, bf16[128,4224]{1,0:T(8,128)(2,1)S(1)} %get-tuple-element.18.sums_ref, bf16[128,4096]{1,0:T(8,128)(2,1)S(1)} %get-tuple-element.19.x_ref, bf16[2,2,4,4,128,128]{5,4,3,2,1,0:T(8,128)(2,1)S(1)} %get-tuple-element.20.b_ref), custom_call_target="tpu_custom_call" | custom-call | tf_op jit(solution)/shard_map/deliver/pallas_call | solution.py:934
  405.4 10.9 %put.1 = bf16[32,2,2,32,4096]{4,3,2,1,0:T(8,128)(2,1)} custom-call(bf16[32,2,2,32,4096]{4,3,2,1,0:T(8,128)(2,1)S(1)} %deliver.1.y_ref), custom_call_target="tpu_custom_call" | custom-call | tf_op jit(solution)/shard_map/put/pallas_call | solution.py:942
Async XLA Ops:
  112.2 103.7 %copy-start = (s32[32]{0:T(128)S(1)}, s32[32]{0:T(128)}, u32[]{:S(2)}) copy-start(s32[32]{0:T(128)} %ids_ref.7) | copy-start | bytes 388

commit v17 on v16

--- a/solution.py
+++ b/solution.py
@@ -27,6 +27,7 @@
 
 OWN, NEXT, FAR, LAST = RING = range(4)
 UP, DOWN = BOTH = range(2)
+THREE = range(3)
 STEP = (NEXT, -NEXT)
 FROM = (LAST, NEXT)
 AWAY = (NEXT, LAST, FAR)
@@ -258,7 +259,7 @@
     return jnp.concatenate([jnp.where(chosen == a, low, 0.0) for a in range(adapters)], axis=1).astype(BF)
 
 
-PASS, FREE, SUM = range(3)
+PASS, FREE, SUM = THREE
 FAST_SEMS = [DMA((2, 3, 2))] * 2
 
 
@@ -314,7 +315,7 @@
 
     def sent(self):
         for part in BOTH:
-            for kind in range(3):
+            for kind in THREE:
                 for d in BOTH:
                     self.message(part, kind, d).wait_send()
 
@@ -359,7 +360,7 @@
         for a in range(adapters):
             wo_loads.append(pltpu.make_async_copy(ao_ref.at[a], wo.at[part, OWN, 0, :, pl.ds(width + a * rank, rank)], wo_load))
     ends(wo_loads)
-    loads = ends([pltpu.make_async_copy(src, dst, load_sem) for i in range(3) for src, dst in
+    loads = ends([pltpu.make_async_copy(src, dst, load_sem) for i in THREE for src, dst in
                   ((a_heads[i], a_raw.at[place.core, i]), (w_heads[i], w.at[:, pl.ds(i * head, head)]), (b_heads[i], b_raw.at[0, i]))])
     for step in range(X_SLOTS - 1):
         ends(x_loads(step))
@@ -406,25 +407,26 @@
                     wo_message(part, 1, d, i).wait_recv()
             wo_to_partner(part, FAR)
 
-    early = WO_CHUNKS // 2
     gathers = [RowGather(place, place.rows(a_mine), place.spot, a_send, a_recv), RowGather(place, place.rows(b_mine), place.spot, b_send, b_recv)]
 
-    def both(stage_of):
-        for g in gathers:
-            getattr(g, stage_of)()
-
-    def hand(*distances):
+    of_a, of_b = gathers
+
+    def hand(i, *distances):
+        dst = (a_all, b_all)[i]
         for ds in distances:
             for part in BOTH:
-                for i, dst in enumerate((a_all, b_all)):
-                    here, there = gathers[i].row_at(part, ds), place.rows(dst.at[place.core])(part, ds)
-                    pltpu.make_async_copy(here, there, kept_sem.at[i]).start()
-                    remote(here, there, hand_send.at[i], hand_recv.at[i], place.partner).start()
-
-    both('own')
+                here, there = gathers[i].row_at(part, ds), place.rows(dst.at[place.core])(part, ds)
+                pltpu.make_async_copy(here, there, kept_sem.at[i]).start()
+                remote(here, there, hand_send.at[i], hand_recv.at[i], place.partner).start()
+
+    def happen(events, step):
+        for at, what in events.items():
+            pl.when(step == at)(lambda what=what: ([f(*args) for f, *args in what], None)[1])
+
     wait(wo_loads)
-    for i in range(early):
+    for i in BOTH:
         wo_start(i)
+    of_a.own()
     wait(loads)
     moves = [(a_raw.at[place.core], a_raw.at[place.core]), (w.at[:, first(cols)], w.at[:, pl.ds(cols, cols)]), (b_raw.at[0], b_raw.at[1])]
     pair = ends([remote(src, dst, pair_send.at[i], pair_recv.at[i], place.partner) for i, (src, dst) in enumerate(moves)])
@@ -449,7 +451,7 @@
             h[i * seq_len:(i + 1) * seq_len, :] = normed(xbuf[slot, i].astype(F32), gain_ref[...])
 
     def products(step):
-        pl.when(step == 3)(lambda: both('near'))
+        happen({0: [(wo_start, 2)], 2: [(of_b.own,), (wo_start, 3)], 3: [(wo_start, 4)]}, step)
         norm(step, 2 * steps)
         low = dot_rows(a_rows[...], h[...])
         half, at = step // (steps // 2), lax.rem(step, steps // 2) * 2 * seq_len
@@ -469,17 +471,13 @@
         copy.wait_recv()
     for part in BOTH:
         wo_to_partner(part, OWN)
-    events = {0: lambda: wo_start(early), 3: lambda: (low_gather.near(), wo_start(early + 1)), 7: lambda: (low_gather.row(), wo_start(early + 2)),
-              14: lambda: (low_gather.sides(), wo_start(early + 3))}
-
-    def happen(half_step):
-        for at, what in events.items():
-            pl.when(half_step == at)(lambda what=what: (what(), None)[1])
+    second = {1: [(wo_start, 5)], 2: [(low_gather.near,), (wo_start, 6)], 3: [(of_a.near,)], 4: [(low_gather.row,)], 5: [(of_b.near,)],
+              6: [(wo_start, 7), (wo_pass, 0)], 9: [(low_gather.sides,), (of_b.row,), (hand, 1, OWN)], 13: [(wo_pass, 1)], 15: [(wo_pass, 2)]}
 
     def project(step):
-        happen(2 * step)
+        happen(second, 2 * step)
         norm(step + steps, 2 * steps)
-        happen(2 * step + 1)
+        happen(second, 2 * step + 1)
         rows = pl.ds(pl.multiple_of(step * 2 * seq_len, LANE), 2 * seq_len)
         chunk = fit(2 * cols, 256)
         for n in range(2 * cols // chunk):
@@ -491,16 +489,12 @@
     for part in BOTH:
         chip_of = spot if part == 0 else lax.rem(spot, side) * side + spot // side
         to = chip_of * 2 * per + part * per + lax.rem(row, per)
-        for i in range(3):
+        for i in THREE:
             spread_rows = jnp.where((kind == i) & (col == to), 1.0, 0.0).astype(BF)
             for a in range(adapters):
                 for o in BOTH:
                     bx[a, part, :, o * cols + i * head:o * cols + (i + 1) * head] = dot(spread_rows, b_raw[o, i, a]).astype(BF)
-    wo_pass(0)
-    wo_pass(1)
     low_gather.far()
-    wo_pass(2)
-    wo_pass(3)
     causal = lax.broadcasted_iota(jnp.int32, (seq_len, seq_len), 0) >= lax.broadcasted_iota(jnp.int32, (seq_len, seq_len), 1)
 
     def swap(part, ds):
@@ -517,7 +511,7 @@
         for part in BOTH:
             zs += scale * dot_columns(lows[part, :, :, half, :, at].reshape(-1, seq_len), bx[adapter, part])
         for i_head in BOTH:
-            q, k, v = (zs[:, i_head * cols + i * head:i_head * cols + (i + 1) * head] for i in range(3))
+            q, k, v = (zs[:, i_head * cols + i * head:i_head * cols + (i + 1) * head] for i in THREE)
             q, k = ((r * cos_ref[...] + pltpu.roll(r, head // 2, axis=1) * sin_ref[...]).astype(BF) for r in (q, k))
             scores = jnp.where(causal, dot_rows(q, k) * head ** -0.5, -1e30)
             e = jnp.exp(scores - jnp.max(scores, axis=-1, keepdims=True))
@@ -529,14 +523,17 @@
     def attention_pair(k):
         for i in BOTH:
             attention(2 * k + i)
+        happen({0: [(wo_pass, 3)]}, k)
         row = side - 1 - 2 * k // side
         pl.when((lax.rem(2 * k + 2, side) == 0) & (row != OWN))(lambda: swap(0, row).start())
 
     loop(chips // 2, attention_pair)
     for ds in AWAY:
         swap(1, ds).start()
-    both('row')
-    hand(OWN)
+    of_a.row()
+    hand(0, OWN)
+    of_b.sides()
+    hand(1, NEXT, LAST)
     wo_arrived()
     wo_last()
     for part in BOTH:
@@ -563,11 +560,12 @@
         stage[part, :, :, width:] = pick_columns(sum_heads(part, pl.ds(width, adapters * rank)), chosen).reshape(blocks + (rank,)).astype(BF)
         for df in (FAR, NEXT, LAST):
             fast.ready(part, df)
-    both('sides')
-    hand(NEXT, LAST)
+    of_a.sides()
+    hand(0, NEXT, LAST)
     fast.sum()
-    both('far')
-    hand(FAR)
+    for i in BOTH:
+        gathers[1 - i].far()
+        hand(1 - i, FAR)
     fast.finish()
     out = ends([pltpu.make_async_copy(stage.at[part, OWN], out_ref.at[pl.ds(part * rows, rows)], load_sem) for part in BOTH])
     fast.sent()
@@ -700,7 +698,7 @@
     fast.sent()
     wait(b_load)
     for part in BOTH:
-        for kind in range(3):
+        for kind in THREE:
             for d in BOTH:
                 for i in BOTH:
                     slow(part, kind, d, i).wait_send()

time: 417 us -> 421 us (level)
  Pallas kernels: 416 us -> 421 us
where the time goes in v17:
time: 421 us
  Pallas kernels  421 us (100%)
    pallas_call x1, Pallas kernels, attend(): pl.pallas_call(functools.partial(attend_kernel, side, adapters, scale), o...  116 us
    pallas_call x1, Pallas kernels, gate_up(): pl.pallas_call(functools.partial(gate_up_kernel, side, adapters, scale),...  102 us
    pallas_call x1, Pallas kernels, row_proj(): pl.pallas_call(functools.partial(row_proj_kernel, side, adapters, rank),...  97.1 us
    pallas_call x1, Pallas kernels, deliver(): pl.pallas_call(functools.partial(deliver_kernel, side, b_down.shape[1], s...  95.5 us
    pallas_call x1, Pallas kernels, deliver(): pl.pallas_call(put_kernel, out_shape=jax.ShapeDtypeStruct(y.shape, BF), i...  10.9 us

profile of v17, /device:TPU:97, one launch (start us, length us, event | category | flops | bytes accessed | tf_op | source)
XLA Modules:
  0.0 421.2 jit_solution(15617165154658590472)
XLA Ops:
  0.0 115.6 %attend.1 = (bf16[128,4224]{1,0:T(8,128)(2,1)}, bf16[2,2,4,4,2,16,1024]{6,5,4,3,2,1,0:T(8,128)(2,1)}, bf16[2,2,4,4,2,128,128]{6,5,4,3,2,1,0:T(8,128)(2,1)}) custom-call(s32[32]{0:T(128)} %ids_ref.7, bf16[32,128,4096]{2,1,0:T(8,128)(2,1)} %x_all.1, f32[1,4096]{1,0:T(1,128)} %bitcast.37, f32[128,128]{1,0:T(8,128)} %constant.4.clone.cos_in, ...), custom_call_target="tpu_custom_call" | custom-call | tf_op jit(solution)/shard_map/attend/pallas_call | solution.py:606
  115.6 0.0 copy-start
  115.6 101.9 %gate_up.1 = (bf16[2,4,256,768]{3,2,1,0:T(8,128)(2,1)S(1)}, bf16[128,4096]{1,0:T(8,128)(2,1)S(1)}, bf16[768,4352]{1,0:T(8,128)(2,1)S(1)}) custom-call(s32[32]{0:T(128)} %ids_ref.7, bf16[128,4224]{1,0:T(8,128)(2,1)} %get-tuple-element.13.sums_in, f32[1,4096]{1,0:T(1,128)} %bitcast.38, bf16[32,128,4096]{2,1,0:T(8,128)(2,1)} %x_all.1, ...), custom_call_target="tpu_custom_call" | custom-call | tf_op jit(solution)/shard_map/gate_up/pallas_call | solution.py:868
  217.5 0.0 copy-done
  217.5 97.1 %row_proj.1 = (bf16[128,4224]{1,0:T(8,128)(2,1)S(1)}, bf16[2,2,4,4,128,128]{5,4,3,2,1,0:T(8,128)(2,1)S(1)}) custom-call(s32[32]{0:T(128)S(1)} %copy-done, bf16[2,4,256,768]{3,2,1,0:T(8,128)(2,1)S(1)} %get-tuple-element.16.act, bf16[768,4352]{1,0:T(8,128)(2,1)S(1)} %get-tuple-element.17.w, bf16[2,2,4,4,2,128,128]{6,5,4,3,2,1,0:T(8,128)(2,1)} %get-tuple-element.15.b_all), custom_call_target="tpu_custom_call" | custom-call | tf_op jit(solution)/shard_map/row_proj/pallas_call | solution.py:711
  314.6 95.5 %deliver.1.y_ref = bf16[32,2,2,32,4096]{4,3,2,1,0:T(8,128)(2,1)S(1)} custom-call(s32[32]{0:T(128)S(1)} %copy-done, bf16[128,4224]{1,0:T(8,128)(2,1)S(1)} %get-tuple-element.18.sums_ref, bf16[128,4096]{1,0:T(8,128)(2,1)S(1)} %get-tuple-element.19.x_ref, bf16[2,2,4,4,128,128]{5,4,3,2,1,0:T(8,128)(2,1)S(1)} %get-tuple-element.20.b_ref), custom_call_target="tpu_custom_call" | custom-call | tf_op jit(solution)/shard_map/deliver/pallas_call | solution.py:932
  410.1 10.9 %put.1 = bf16[32,2,2,32,4096]{4,3,2,1,0:T(8,128)(2,1)} custom-call(bf16[32,2,2,32,4096]{4,3,2,1,0:T(8,128)(2,1)S(1)} %deliver.1.y_ref), custom_call_target="tpu_custom_call" | custom-call | tf_op jit(solution)/shard_map/put/pallas_call | solution.py:940
Async XLA Ops:
  115.6 101.9 %copy-start = (s32[32]{0:T(128)S(1)}, s32[32]{0:T(128)}, u32[]{:S(2)}) copy-start(s32[32]{0:T(128)} %ids_ref.7) | copy-start | bytes 388
